TPU v7x, 256 devices: a whole 4x4x8 slice. The times are simulated.
256 devices in a mesh: node: 4 (over x), sx: 16 (over z_hi, y), sy: 4 (over z_lo, core).
Axes of the slice: x: 4, y: 4, z: 8 (z_hi: 4, z_lo: 2; z = z_hi * 2 + z_lo), core: 2. Of those that a mesh axis runs over, the one named last changes fastest.
Arguments:
- previous: float32 [4, 2, 256, 128, 256], P('node', None, 'sx', 'sy'), may hold values from 0 to 1
- feed_rate: float32 [256, 128, 256], P('sx', 'sy'), may hold values from 0.01 to 0.1
- kill_rate: float32 [256, 128, 256], P('sx', 'sy'), may hold values from 0.03 to 0.1
Outputs:
- sections: float32 [4, 2, 256, 128, 256], P('node', None, 'sx', 'sy')
All inputs are finite; a program needn't handle non-finite values.
Results may differ from a plain program's by a relative error of at most 0.00011.
Values sent between devices are 32-bit elements; how exact they have to be, the bound alone decides.
No kernel may reach another device: no remote copies, remote signals or barrier semaphores. Data moves between devices by JAX's collectives and lax.ppermute only.
A program may use at most 64 MiB of HBM per device.

v0:
```python
import jax
import jax.numpy as jnp
from jax import lax
from jax.sharding import PartitionSpec as P

SWEEPS = 2
JACOBI = 12


radau_points = [0.088587959512704, 0.409466864440735, 0.787659461760847, 1.0]
time_step = 4.0
diffusion_values = [1.0, 0.5]


def picked(array, axis, root):
    return lax.dynamic_index_in_dim(lax.all_gather(array, axis), root, 0, keepdims=False)


def padded_2(array, sides, width):
    edges = {}
    for axis, dim in sides:
        count, length = (lax.axis_size(axis), array.shape[dim])
        up = [(i, (i + 1) % count) for i in range(count)]
        last = lax.slice_in_dim(array, length - width, length, axis=dim)
        leading = lax.slice_in_dim(array, 0, width, axis=dim)
        edges[dim] = (
            lax.ppermute(last, axis, up),
            lax.ppermute(leading, axis, [(b, a) for a, b in up]),
        )
    done = []
    for _, dim in sides:
        low, high = edges[dim]
        around = [(width, width) if d in done else (0, 0) for d in range(array.ndim)]
        array = jnp.concatenate([jnp.pad(low, around), array, jnp.pad(high, around)], axis=dim)
        done.append(dim)
    return array


def split_up(array, dim, count):
    lengths = array.shape
    blocks = array.reshape(*lengths[:dim], count, lengths[dim] // count, *lengths[dim + 1 :])
    return jnp.moveaxis(blocks, dim, 0)


def sent_and_summed(array, axis, dim):
    count = lax.axis_size(axis)
    blocks = lax.all_to_all(split_up(array, dim, count), axis, 0, 0, tiled=True)
    return jnp.sum(blocks, axis=0)


def padded_3(block, sides, width):
    for axis, dim in sides:
        count = lax.axis_size(axis)
        forward = [(i, i + 1) for i in range(count - 1)]
        forward.append((count - 1, 0))
        backward = [(target, source) for source, target in forward]
        low = lax.ppermute(
            lax.slice_in_dim(block, block.shape[dim] - width, None, axis=dim), axis, forward
        )
        high = lax.ppermute(lax.slice_in_dim(block, 0, width, axis=dim), axis, backward)
        block = jnp.concatenate([low, block, high], axis=dim)
    return block


def collocation():
    count = len(radau_points)
    table = []
    for row in range(count):
        table.append([0.0] * count)
    for column in range(count):
        poly = [1.0]
        denom = 1.0
        for other in range(count):
            if other != column:
                longer = [0.0] * (len(poly) + 1)
                for place in range(len(poly)):
                    longer[place + 1] = longer[place + 1] + poly[place]
                    longer[place] = longer[place] - radau_points[other] * poly[place]
                poly = longer
                denom = denom * (radau_points[column] - radau_points[other])
        for row in range(count):
            point = radau_points[row]
            total = 0.0
            for place in range(len(poly)):
                total = total + poly[place] * point ** (place + 1) / (place + 1)
            table[row][column] = total / denom
    return table


def beside(padded):
    center = padded[:, 1:-1, 1:-1]
    total = padded[:, 2:, 1:-1] + padded[:, :-2, 1:-1]
    total = total + padded[:, 1:-1, 2:] + padded[:, 1:-1, :-2]
    return total + jnp.roll(center, 1, 3) + jnp.roll(center, -1, 3)


def body(previous, feed_rate, kill_rate):
    node_index = lax.axis_index("node")
    qmatrix = jnp.asarray(collocation(), jnp.float32)
    points = jnp.asarray(radau_points, jnp.float32)
    diag_weight = points[node_index]
    diffusion = jnp.asarray(diffusion_values, jnp.float32)[:, None, None, None]
    coef = time_step * diag_weight * diffusion
    start_value = picked(previous[0], "node", len(radau_points) - 1)
    iterate = previous[0]
    for sweep in range(SWEEPS):
        padded = padded_2(iterate, (("sx", 1), ("sy", 2)), 1)
        diff = diffusion * (beside(padded) - 6.0 * iterate)
        upart = iterate[0]
        vpart = iterate[1]
        uvv = upart * vpart * vpart
        react = jnp.stack(
            [-uvv + feed_rate * (1.0 - upart), uvv - (feed_rate + kill_rate) * vpart], 0
        )
        force = diff + react
        weights = qmatrix[:, node_index][:, None, None, None, None]
        section_terms = weights * force[None]
        summed = sent_and_summed(section_terms, "node", 0)[0]
        right_side = start_value + time_step * (summed - diag_weight * diff)
        extended = padded_2(right_side, (("sx", 1), ("sy", 2)), 1)

        def double_turn(turn, current):
            beside_all = padded_3(current, (("sx", 1), ("sy", 2)), 2)
            midway = (extended + coef * beside(beside_all)) / (1.0 + 6.0 * coef)
            return (right_side + coef * beside(midway)) / (1.0 + 6.0 * coef)

        iterate = lax.fori_loop(0, JACOBI // 2, double_turn, iterate)
    return iterate[None]


def solution(mesh):
    return jax.shard_map(
        body,
        mesh=mesh,
        in_specs=(P("node", None, "sx", "sy", None), P("sx", "sy", None), P("sx", "sy", None)),
        out_specs=P("node", None, "sx", "sy", None),
        check_vma=False,
    )
```

profile of v0, /device:TPU:1, one launch (start us, length us, event | category | flops | bytes accessed | tf_op | source)
XLA Modules:
  0.0 478.6 jit_solution(6320649349242898416)
XLA Ops:
  6.5 2.3 copy.27
  10.1 3.3 collective-permute-start.10
  15.6 6.7 %collective-permute-start.8 = (f32[2,1,32,256]{3,2,1,0:T(8,128)S(1)}, f32[2,1,32,256]{3,2,1,0:T(8,128)S(1)}, u32[]{:S(2)}, u32[]{:S(2)}) collective-permute-start(f32[2,1,32,256]{3,2,1,0:T(8,128)S(1)} %get-tuple-element.163), channel_id=1, source_target_pairs={{4,0},{8,4},{12,8},{16,12},{20,16},{24,20},{28,24},{32,28},{36,32}... | collective-permute-start | bytes 196616 | tf_op jit(solution)/shard_map/ppermute | solution.py:28
  25.5 2.4 maximum_add_fusion
  27.9 2.7 broadcast_multiply_fusion.3
  30.6 5.0 %all-to-all-start = ((f32[4,1,2,16,32,256]{5,4,3,2,1,0:T(8,128)}), f32[4,1,2,16,32,256]{5,4,3,2,1,0:T(8,128)}, u32[]{:S(2)}, u32[]{:S(2)}) async-start(f32[4,1,2,16,32,256]{5,4,3,2,1,0:T(8,128)} %broadcast_multiply_fusion.3), calls=%async_computation | async-start | bytes 8388608 | tf_op jit(solution)/shard_map/all_to_all | solution.py:47
  36.2 72.7 %all-to-all-done = f32[4,1,2,16,32,256]{5,4,3,2,1,0:T(8,128)} async-done(((f32[4,1,2,16,32,256]{5,4,3,2,1,0:T(8,128)}), f32[4,1,2,16,32,256]{5,4,3,2,1,0:T(8,128)}, u32[]{:S(2)}, u32[]{:S(2)}) %all-to-all-start) | async-done | bytes 4194336 | tf_op jit(solution)/shard_map/all_to_all | solution.py:47
  108.9 2.7 reduce_sum.18
  111.6 2.4 multiply_add_fusion.3
  115.0 5.1 %collective-permute-start.14 = (f32[2,1,32,256]{3,2,1,0:T(8,128)S(1)}, f32[2,1,32,256]{3,2,1,0:T(8,128)S(1)}, u32[]{:S(2)}, u32[]{:S(2)}) collective-permute-start(f32[2,1,32,256]{3,2,1,0:T(8,128)S(1)} %get-tuple-element.157), channel_id=1, source_target_pairs={{4,0},{8,4},{12,8},{16,12},{20,16},{24,20},{28,24},{32,28},{36,32}... | collective-permute-start | bytes 196616 | tf_op jit(solution)/shard_map/ppermute | solution.py:28
  120.1 2.0 collective-permute-start.12
  123.2 2.3 collective-permute-done.15
  126.8 131.0 %while.22 = (s32[]{:T(128)}, f32[2,16,32,256]{3,2,1,0:T(8,128)S(1)}, f32[2,18,34,256]{3,2,1,0:T(8,128)}, f32[2,16,32,256]{3,2,1,0:T(8,128)S(1)}, f32[]{:T(128)}, /*index=5*/s32[]{:T(128)}, f32[2]{0:T(128)S(1)}) while((s32[]{:T(128)}, f32[2,16,32,256]{3,2,1,0:T(8,128)S(1)}, f32[2,18,34,256]{3,2,1,0:T(8,128)}, ...), condition=%wide.region_2.3_spmd.clone, body=%wide.region_1.2_spmd.clone.sunk | while | flops 7118856 | bytes 39731524 | solution.py:127
  127.0 5.7 %collective-permute-start.1 = (f32[2,2,32,256]{3,2,1,0:T(8,128)S(1)}, f32[2,2,32,256]{3,2,1,0:T(8,128)S(1)}, u32[]{:S(2)}, u32[]{:S(2)}) collective-permute-start(f32[2,2,32,256]{3,2,1,0:T(8,128)S(1)} %get-tuple-element.254), channel_id=1, source_target_pairs={{4,0},{8,4},{12,8},{16,12},{20,16},{24,20},{28,24},{32,28},{36,32}... | collective-permute-start | bytes 393224 | tf_op jit(solution)/shard_map/while/body/eval_jaxpr/ppermute | solution.py:60
  132.6 4.7 collective-permute-done
  138.3 2.1 collective-permute-start.2
  142.2 2.0 collective-permute-done.3
  148.7 5.7 %collective-permute-start.1 = (f32[2,2,32,256]{3,2,1,0:T(8,128)S(1)}, f32[2,2,32,256]{3,2,1,0:T(8,128)S(1)}, u32[]{:S(2)}, u32[]{:S(2)}) collective-permute-start(f32[2,2,32,256]{3,2,1,0:T(8,128)S(1)} %get-tuple-element.254), channel_id=1, source_target_pairs={{4,0},{8,4},{12,8},{16,12},{20,16},{24,20},{28,24},{32,28},{36,32}... | collective-permute-start | bytes 393224 | tf_op jit(solution)/shard_map/while/body/eval_jaxpr/ppermute | solution.py:60
  154.4 5.0 %collective-permute-done = f32[2,2,32,256]{3,2,1,0:T(8,128)S(1)} collective-permute-done((f32[2,2,32,256]{3,2,1,0:T(8,128)S(1)}, f32[2,2,32,256]{3,2,1,0:T(8,128)S(1)}, u32[]{:S(2)}, u32[]{:S(2)}) %collective-permute-start) | collective-permute-done | bytes 131104 | tf_op jit(solution)/shard_map/while/body/eval_jaxpr/ppermute | solution.py:57
  159.6 2.8 collective-permute-start.2
  170.8 5.7 %collective-permute-start.1 = (f32[2,2,32,256]{3,2,1,0:T(8,128)S(1)}, f32[2,2,32,256]{3,2,1,0:T(8,128)S(1)}, u32[]{:S(2)}, u32[]{:S(2)}) collective-permute-start(f32[2,2,32,256]{3,2,1,0:T(8,128)S(1)} %get-tuple-element.254), channel_id=1, source_target_pairs={{4,0},{8,4},{12,8},{16,12},{20,16},{24,20},{28,24},{32,28},{36,32}... | collective-permute-start | bytes 393224 | tf_op jit(solution)/shard_map/while/body/eval_jaxpr/ppermute | solution.py:60
  176.4 4.6 collective-permute-done
  181.2 3.0 collective-permute-start.2
  184.2 2.1 collective-permute-done.2
  192.5 5.7 %collective-permute-start.1 = (f32[2,2,32,256]{3,2,1,0:T(8,128)S(1)}, f32[2,2,32,256]{3,2,1,0:T(8,128)S(1)}, u32[]{:S(2)}, u32[]{:S(2)}) collective-permute-start(f32[2,2,32,256]{3,2,1,0:T(8,128)S(1)} %get-tuple-element.254), channel_id=1, source_target_pairs={{4,0},{8,4},{12,8},{16,12},{20,16},{24,20},{28,24},{32,28},{36,32}... | collective-permute-start | bytes 393224 | tf_op jit(solution)/shard_map/while/body/eval_jaxpr/ppermute | solution.py:60
  198.2 4.7 collective-permute-done
  203.9 2.1 collective-permute-start.2
  206.0 2.0 collective-permute-done.2
  214.4 5.7 %collective-permute-start.1 = (f32[2,2,32,256]{3,2,1,0:T(8,128)S(1)}, f32[2,2,32,256]{3,2,1,0:T(8,128)S(1)}, u32[]{:S(2)}, u32[]{:S(2)}) collective-permute-start(f32[2,2,32,256]{3,2,1,0:T(8,128)S(1)} %get-tuple-element.254), channel_id=1, source_target_pairs={{4,0},{8,4},{12,8},{16,12},{20,16},{24,20},{28,24},{32,28},{36,32}... | collective-permute-start | bytes 393224 | tf_op jit(solution)/shard_map/while/body/eval_jaxpr/ppermute | solution.py:60
  220.1 4.2 collective-permute-done
  225.8 2.2 collective-permute-start.2
  228.0 2.0 collective-permute-done.2
  236.3 5.7 %collective-permute-start.1 = (f32[2,2,32,256]{3,2,1,0:T(8,128)S(1)}, f32[2,2,32,256]{3,2,1,0:T(8,128)S(1)}, u32[]{:S(2)}, u32[]{:S(2)}) collective-permute-start(f32[2,2,32,256]{3,2,1,0:T(8,128)S(1)} %get-tuple-element.254), channel_id=1, source_target_pairs={{4,0},{8,4},{12,8},{16,12},{20,16},{24,20},{28,24},{32,28},{36,32}... | collective-permute-start | bytes 393224 | tf_op jit(solution)/shard_map/while/body/eval_jaxpr/ppermute | solution.py:60
  242.0 3.7 collective-permute-done
  249.6 2.3 collective-permute-done.2
  260.6 5.8 %collective-permute-start.16 = (f32[2,1,32,256]{3,2,1,0:T(8,128)S(1)}, f32[2,1,32,256]{3,2,1,0:T(8,128)S(1)}, u32[]{:S(2)}, u32[]{:S(2)}) collective-permute-start(f32[2,1,32,256]{3,2,1,0:T(8,128)S(1)} %get-tuple-element.148), channel_id=1, source_target_pairs={{4,0},{8,4},{12,8},{16,12},{20,16},{24,20},{28,24},{32,28},{36,32}... | collective-permute-start | bytes 196616 | tf_op jit(solution)/shard_map/ppermute | solution.py:28
  271.0 52.0 %all_to_all.10 = f32[4,1,2,16,32,256]{5,4,3,2,1,0:T(8,128)} all-to-all(f32[4,1,2,16,32,256]{5,4,3,2,1,0:T(8,128)S(1)} %broadcast_multiply_fusion.2), channel_id=1, replica_groups=mesh['node'=4,'sx'=16,'sy'=4] {'node'}, dimensions={0} | all-to-all | bytes 8388608 | tf_op jit(solution)/shard_map/all_to_all | solution.py:47
  323.0 3.7 reduce_sum.19
  326.7 2.4 multiply_add_fusion.2
  329.2 6.2 %collective-permute-start.22 = (f32[2,1,32,256]{3,2,1,0:T(8,128)S(1)}, f32[2,1,32,256]{3,2,1,0:T(8,128)S(1)}, u32[]{:S(2)}, u32[]{:S(2)}) collective-permute-start(f32[2,1,32,256]{3,2,1,0:T(8,128)S(1)} %get-tuple-element.143), channel_id=1, source_target_pairs={{4,0},{8,4},{12,8},{16,12},{20,16},{24,20},{28,24},{32,28},{36,32}... | collective-permute-start | bytes 196616 | tf_op jit(solution)/shard_map/ppermute | solution.py:28
  338.4 2.3 collective-permute-done.23
  342.1 128.7 %while.23 = (s32[]{:T(128)}, f32[2,16,32,256]{3,2,1,0:T(8,128)S(1)}, f32[2,18,34,256]{3,2,1,0:T(8,128)}, f32[2,16,32,256]{3,2,1,0:T(8,128)S(1)}, f32[]{:T(128)}, /*index=5*/s32[]{:T(128)}, f32[2]{0:T(128)S(1)}) while((s32[]{:T(128)}, f32[2,16,32,256]{3,2,1,0:T(8,128)S(1)}, f32[2,18,34,256]{3,2,1,0:T(8,128)}, ...), condition=%wide.region_5.6_spmd.clone, body=%wide.region_4.5_spmd.clone.sunk | while | flops 7118856 | bytes 39731524 | solution.py:127
  342.2 5.7 %collective-permute-start.5 = (f32[2,2,32,256]{3,2,1,0:T(8,128)S(1)}, f32[2,2,32,256]{3,2,1,0:T(8,128)S(1)}, u32[]{:S(2)}, u32[]{:S(2)}) collective-permute-start(f32[2,2,32,256]{3,2,1,0:T(8,128)S(1)} %get-tuple-element.273), channel_id=1, source_target_pairs={{4,0},{8,4},{12,8},{16,12},{20,16},{24,20},{28,24},{32,28},{36,32}... | collective-permute-start | bytes 393224 | tf_op jit(solution)/shard_map/while/body/eval_jaxpr/ppermute | solution.py:60
  347.9 4.0 collective-permute-done.4
  357.1 2.4 collective-permute-done.7
  363.9 6.0 %collective-permute-start.5 = (f32[2,2,32,256]{3,2,1,0:T(8,128)S(1)}, f32[2,2,32,256]{3,2,1,0:T(8,128)S(1)}, u32[]{:S(2)}, u32[]{:S(2)}) collective-permute-start(f32[2,2,32,256]{3,2,1,0:T(8,128)S(1)} %get-tuple-element.273), channel_id=1, source_target_pairs={{4,0},{8,4},{12,8},{16,12},{20,16},{24,20},{28,24},{32,28},{36,32}... | collective-permute-start | bytes 393224 | tf_op jit(solution)/shard_map/while/body/eval_jaxpr/ppermute | solution.py:60
  369.9 2.4 collective-permute-done.4
  373.7 2.5 collective-permute-start.6
  377.7 3.0 collective-permute-done.7
  385.1 5.8 %collective-permute-start.5 = (f32[2,2,32,256]{3,2,1,0:T(8,128)S(1)}, f32[2,2,32,256]{3,2,1,0:T(8,128)S(1)}, u32[]{:S(2)}, u32[]{:S(2)}) collective-permute-start(f32[2,2,32,256]{3,2,1,0:T(8,128)S(1)} %get-tuple-element.273), channel_id=1, source_target_pairs={{4,0},{8,4},{12,8},{16,12},{20,16},{24,20},{28,24},{32,28},{36,32}... | collective-permute-start | bytes 393224 | tf_op jit(solution)/shard_map/while/body/eval_jaxpr/ppermute | solution.py:60
  391.0 2.4 collective-permute-done.4
  398.5 3.5 collective-permute-done.7
  406.5 5.7 %collective-permute-start.5 = (f32[2,2,32,256]{3,2,1,0:T(8,128)S(1)}, f32[2,2,32,256]{3,2,1,0:T(8,128)S(1)}, u32[]{:S(2)}, u32[]{:S(2)}) collective-permute-start(f32[2,2,32,256]{3,2,1,0:T(8,128)S(1)} %get-tuple-element.273), channel_id=1, source_target_pairs={{4,0},{8,4},{12,8},{16,12},{20,16},{24,20},{28,24},{32,28},{36,32}... | collective-permute-start | bytes 393224 | tf_op jit(solution)/shard_map/while/body/eval_jaxpr/ppermute | solution.py:60
  412.1 3.2 collective-permute-done.4
  415.5 2.3 collective-permute-done.5
  420.1 2.7 collective-permute-done.7
  427.3 6.7 %collective-permute-start.5 = (f32[2,2,32,256]{3,2,1,0:T(8,128)S(1)}, f32[2,2,32,256]{3,2,1,0:T(8,128)S(1)}, u32[]{:S(2)}, u32[]{:S(2)}) collective-permute-start(f32[2,2,32,256]{3,2,1,0:T(8,128)S(1)} %get-tuple-element.273), channel_id=1, source_target_pairs={{4,0},{8,4},{12,8},{16,12},{20,16},{24,20},{28,24},{32,28},{36,32}... | collective-permute-start | bytes 393224 | tf_op jit(solution)/shard_map/while/body/eval_jaxpr/ppermute | solution.py:60
  434.0 3.4 collective-permute-done.4
  437.5 2.2 collective-permute-done.5
  441.5 3.5 collective-permute-done.7
  449.5 6.3 %collective-permute-start.5 = (f32[2,2,32,256]{3,2,1,0:T(8,128)S(1)}, f32[2,2,32,256]{3,2,1,0:T(8,128)S(1)}, u32[]{:S(2)}, u32[]{:S(2)}) collective-permute-start(f32[2,2,32,256]{3,2,1,0:T(8,128)S(1)} %get-tuple-element.273), channel_id=1, source_target_pairs={{4,0},{8,4},{12,8},{16,12},{20,16},{24,20},{28,24},{32,28},{36,32}... | collective-permute-start | bytes 393224 | tf_op jit(solution)/shard_map/while/body/eval_jaxpr/ppermute | solution.py:60
  455.8 3.3 collective-permute-done.4
  459.2 2.5 collective-permute-done.5
  463.4 3.0 collective-permute-done.7
  (298 shorter events, 115.3 us)
Async XLA Ops:
  6.5 105.1 %all-gather.2.cloned.1.call-start = ((), (), s32[]{:S(2)}) async-start(), calls=%async_computation.2 | async-start | bytes 5242880 | tf_op jit(solution)/shard_map/all_gather | solution.py:16
  10.1 14.5 %collective-permute-start.10 = (f32[2,16,1,256]{3,2,1,0:T(1,128)S(1)}, f32[2,16,1,256]{3,2,1,0:T(1,128)S(1)}, u32[]{:S(2)}, u32[]{:S(2)}) collective-permute-start(f32[2,16,1,256]{3,2,1,0:T(1,128)S(1)} %get-tuple-element.160), channel_id=1, source_target_pairs={{1,0},{2,1},{3,2},{0,3},{5,4},{6,5},{7,6},{4,7},{9,8},{10,9},{11,1... | collective-permute-start | bytes 98312 | tf_op jit(solution)/shard_map/ppermute | solution.py:28
  13.4 11.2 %collective-permute-start.11 = (f32[2,16,1,256]{3,2,1,0:T(1,128)S(1)}, f32[2,16,1,256]{3,2,1,0:T(1,128)S(1)}, u32[]{:S(2)}, u32[]{:S(2)}) collective-permute-start(f32[2,16,1,256]{3,2,1,0:T(1,128)S(1)} %get-tuple-element.161), channel_id=1, source_target_pairs={{0,1},{1,2},{2,3},{3,0},{4,5},{5,6},{6,7},{7,4},{8,9},{9,10},{10,1... | collective-permute-start | bytes 98312 | tf_op jit(solution)/shard_map/ppermute | solution.py:27
  14.3 10.3 %collective-permute-start.9 = (f32[2,1,32,256]{3,2,1,0:T(8,128)S(1)}, f32[2,1,32,256]{3,2,1,0:T(8,128)S(1)}, u32[]{:S(2)}, u32[]{:S(2)}) collective-permute-start(f32[2,1,32,256]{3,2,1,0:T(8,128)S(1)} %get-tuple-element.162), channel_id=1, source_target_pairs={{0,4},{4,8},{8,12},{12,16},{16,20},{20,24},{24,28},{28,32},{32,36}... | collective-permute-start | bytes 196616 | tf_op jit(solution)/shard_map/ppermute | solution.py:27
  15.6 10.0 %collective-permute-start.8 = (f32[2,1,32,256]{3,2,1,0:T(8,128)S(1)}, f32[2,1,32,256]{3,2,1,0:T(8,128)S(1)}, u32[]{:S(2)}, u32[]{:S(2)}) collective-permute-start(f32[2,1,32,256]{3,2,1,0:T(8,128)S(1)} %get-tuple-element.163), channel_id=1, source_target_pairs={{4,0},{8,4},{12,8},{16,12},{20,16},{24,20},{28,24},{32,28},{36,32}... | collective-permute-start | bytes 196616 | tf_op jit(solution)/shard_map/ppermute | solution.py:28
  30.6 78.3 %all-to-all-start = ((f32[4,1,2,16,32,256]{5,4,3,2,1,0:T(8,128)}), f32[4,1,2,16,32,256]{5,4,3,2,1,0:T(8,128)}, u32[]{:S(2)}, u32[]{:S(2)}) async-start(f32[4,1,2,16,32,256]{5,4,3,2,1,0:T(8,128)} %broadcast_multiply_fusion.3), calls=%async_computation | async-start | bytes 8388608 | tf_op jit(solution)/shard_map/all_to_all | solution.py:47
  114.1 11.4 %collective-permute-start.13 = (f32[2,1,32,256]{3,2,1,0:T(8,128)S(1)}, f32[2,1,32,256]{3,2,1,0:T(8,128)S(1)}, u32[]{:S(2)}, u32[]{:S(2)}) collective-permute-start(f32[2,1,32,256]{3,2,1,0:T(8,128)S(1)} %get-tuple-element.156), channel_id=1, source_target_pairs={{0,4},{4,8},{8,12},{12,16},{16,20},{20,24},{24,28},{28,32},{32,36}... | collective-permute-start | bytes 196616 | tf_op jit(solution)/shard_map/ppermute | solution.py:27
  115.0 10.5 %collective-permute-start.14 = (f32[2,1,32,256]{3,2,1,0:T(8,128)S(1)}, f32[2,1,32,256]{3,2,1,0:T(8,128)S(1)}, u32[]{:S(2)}, u32[]{:S(2)}) collective-permute-start(f32[2,1,32,256]{3,2,1,0:T(8,128)S(1)} %get-tuple-element.157), channel_id=1, source_target_pairs={{4,0},{8,4},{12,8},{16,12},{20,16},{24,20},{28,24},{32,28},{36,32}... | collective-permute-start | bytes 196616 | tf_op jit(solution)/shard_map/ppermute | solution.py:28
  120.1 3.0 collective-permute-start.12
  122.1 3.3 collective-permute-start.15
  126.9 10.4 %collective-permute-start = (f32[2,2,32,256]{3,2,1,0:T(8,128)S(1)}, f32[2,2,32,256]{3,2,1,0:T(8,128)S(1)}, u32[]{:S(2)}, u32[]{:S(2)}) collective-permute-start(f32[2,2,32,256]{3,2,1,0:T(8,128)S(1)} %get-tuple-element.253), channel_id=1, source_target_pairs={{0,4},{4,8},{8,12},{12,16},{16,20},{20,24},{24,28},{28,32},{32,36}... | collective-permute-start | bytes 393224 | tf_op jit(solution)/shard_map/while/body/eval_jaxpr/ppermute | solution.py:57
  127.0 11.2 %collective-permute-start.1 = (f32[2,2,32,256]{3,2,1,0:T(8,128)S(1)}, f32[2,2,32,256]{3,2,1,0:T(8,128)S(1)}, u32[]{:S(2)}, u32[]{:S(2)}) collective-permute-start(f32[2,2,32,256]{3,2,1,0:T(8,128)S(1)} %get-tuple-element.254), channel_id=1, source_target_pairs={{4,0},{8,4},{12,8},{16,12},{20,16},{24,20},{28,24},{32,28},{36,32}... | collective-permute-start | bytes 393224 | tf_op jit(solution)/shard_map/while/body/eval_jaxpr/ppermute | solution.py:60
  138.3 4.0 collective-permute-start.2
  140.4 3.9 collective-permute-start.3
  148.6 10.8 %collective-permute-start = (f32[2,2,32,256]{3,2,1,0:T(8,128)S(1)}, f32[2,2,32,256]{3,2,1,0:T(8,128)S(1)}, u32[]{:S(2)}, u32[]{:S(2)}) collective-permute-start(f32[2,2,32,256]{3,2,1,0:T(8,128)S(1)} %get-tuple-element.253), channel_id=1, source_target_pairs={{0,4},{4,8},{8,12},{12,16},{16,20},{20,24},{24,28},{28,32},{32,36}... | collective-permute-start | bytes 393224 | tf_op jit(solution)/shard_map/while/body/eval_jaxpr/ppermute | solution.py:57
  148.7 10.8 %collective-permute-start.1 = (f32[2,2,32,256]{3,2,1,0:T(8,128)S(1)}, f32[2,2,32,256]{3,2,1,0:T(8,128)S(1)}, u32[]{:S(2)}, u32[]{:S(2)}) collective-permute-start(f32[2,2,32,256]{3,2,1,0:T(8,128)S(1)} %get-tuple-element.254), channel_id=1, source_target_pairs={{4,0},{8,4},{12,8},{16,12},{20,16},{24,20},{28,24},{32,28},{36,32}... | collective-permute-start | bytes 393224 | tf_op jit(solution)/shard_map/while/body/eval_jaxpr/ppermute | solution.py:60
  159.6 4.8 collective-permute-start.2
  162.4 3.9 collective-permute-start.3
  170.7 10.3 %collective-permute-start = (f32[2,2,32,256]{3,2,1,0:T(8,128)S(1)}, f32[2,2,32,256]{3,2,1,0:T(8,128)S(1)}, u32[]{:S(2)}, u32[]{:S(2)}) collective-permute-start(f32[2,2,32,256]{3,2,1,0:T(8,128)S(1)} %get-tuple-element.253), channel_id=1, source_target_pairs={{0,4},{4,8},{8,12},{12,16},{16,20},{20,24},{24,28},{28,32},{32,36}... | collective-permute-start | bytes 393224 | tf_op jit(solution)/shard_map/while/body/eval_jaxpr/ppermute | solution.py:57
  170.8 10.4 %collective-permute-start.1 = (f32[2,2,32,256]{3,2,1,0:T(8,128)S(1)}, f32[2,2,32,256]{3,2,1,0:T(8,128)S(1)}, u32[]{:S(2)}, u32[]{:S(2)}) collective-permute-start(f32[2,2,32,256]{3,2,1,0:T(8,128)S(1)} %get-tuple-element.254), channel_id=1, source_target_pairs={{4,0},{8,4},{12,8},{16,12},{20,16},{24,20},{28,24},{32,28},{36,32}... | collective-permute-start | bytes 393224 | tf_op jit(solution)/shard_map/while/body/eval_jaxpr/ppermute | solution.py:60
  181.2 5.0 %collective-permute-start.2 = (f32[2,20,2,256]{3,2,1,0:T(2,128)S(1)}, f32[2,20,2,256]{3,2,1,0:T(2,128)S(1)}, u32[]{:S(2)}, u32[]{:S(2)}) collective-permute-start(f32[2,20,2,256]{3,2,1,0:T(2,128)S(1)} %get-tuple-element.255), channel_id=1, source_target_pairs={{0,1},{1,2},{2,3},{3,0},{4,5},{5,6},{6,7},{7,4},{8,9},{9,10},{10,1... | collective-permute-start | bytes 245768 | tf_op jit(solution)/shard_map/while/body/eval_jaxpr/ppermute | solution.py:57
  184.2 3.9 collective-permute-start.3
  192.4 10.4 %collective-permute-start = (f32[2,2,32,256]{3,2,1,0:T(8,128)S(1)}, f32[2,2,32,256]{3,2,1,0:T(8,128)S(1)}, u32[]{:S(2)}, u32[]{:S(2)}) collective-permute-start(f32[2,2,32,256]{3,2,1,0:T(8,128)S(1)} %get-tuple-element.253), channel_id=1, source_target_pairs={{0,4},{4,8},{8,12},{12,16},{16,20},{20,24},{24,28},{28,32},{32,36}... | collective-permute-start | bytes 393224 | tf_op jit(solution)/shard_map/while/body/eval_jaxpr/ppermute | solution.py:57
  192.5 11.3 %collective-permute-start.1 = (f32[2,2,32,256]{3,2,1,0:T(8,128)S(1)}, f32[2,2,32,256]{3,2,1,0:T(8,128)S(1)}, u32[]{:S(2)}, u32[]{:S(2)}) collective-permute-start(f32[2,2,32,256]{3,2,1,0:T(8,128)S(1)} %get-tuple-element.254), channel_id=1, source_target_pairs={{4,0},{8,4},{12,8},{16,12},{20,16},{24,20},{28,24},{32,28},{36,32}... | collective-permute-start | bytes 393224 | tf_op jit(solution)/shard_map/while/body/eval_jaxpr/ppermute | solution.py:60
  203.9 4.2 collective-permute-start.2
  206.0 3.9 collective-permute-start.3
  214.3 10.0 %collective-permute-start = (f32[2,2,32,256]{3,2,1,0:T(8,128)S(1)}, f32[2,2,32,256]{3,2,1,0:T(8,128)S(1)}, u32[]{:S(2)}, u32[]{:S(2)}) collective-permute-start(f32[2,2,32,256]{3,2,1,0:T(8,128)S(1)} %get-tuple-element.253), channel_id=1, source_target_pairs={{0,4},{4,8},{8,12},{12,16},{16,20},{20,24},{24,28},{28,32},{32,36}... | collective-permute-start | bytes 393224 | tf_op jit(solution)/shard_map/while/body/eval_jaxpr/ppermute | solution.py:57
  214.4 11.3 %collective-permute-start.1 = (f32[2,2,32,256]{3,2,1,0:T(8,128)S(1)}, f32[2,2,32,256]{3,2,1,0:T(8,128)S(1)}, u32[]{:S(2)}, u32[]{:S(2)}) collective-permute-start(f32[2,2,32,256]{3,2,1,0:T(8,128)S(1)} %get-tuple-element.254), channel_id=1, source_target_pairs={{4,0},{8,4},{12,8},{16,12},{20,16},{24,20},{28,24},{32,28},{36,32}... | collective-permute-start | bytes 393224 | tf_op jit(solution)/shard_map/while/body/eval_jaxpr/ppermute | solution.py:60
  225.8 4.2 collective-permute-start.2
  228.0 3.9 collective-permute-start.3
  236.2 9.4 %collective-permute-start = (f32[2,2,32,256]{3,2,1,0:T(8,128)S(1)}, f32[2,2,32,256]{3,2,1,0:T(8,128)S(1)}, u32[]{:S(2)}, u32[]{:S(2)}) collective-permute-start(f32[2,2,32,256]{3,2,1,0:T(8,128)S(1)} %get-tuple-element.253), channel_id=1, source_target_pairs={{0,4},{4,8},{8,12},{12,16},{16,20},{20,24},{24,28},{28,32},{32,36}... | collective-permute-start | bytes 393224 | tf_op jit(solution)/shard_map/while/body/eval_jaxpr/ppermute | solution.py:57
  236.3 11.2 %collective-permute-start.1 = (f32[2,2,32,256]{3,2,1,0:T(8,128)S(1)}, f32[2,2,32,256]{3,2,1,0:T(8,128)S(1)}, u32[]{:S(2)}, u32[]{:S(2)}) collective-permute-start(f32[2,2,32,256]{3,2,1,0:T(8,128)S(1)} %get-tuple-element.254), channel_id=1, source_target_pairs={{4,0},{8,4},{12,8},{16,12},{20,16},{24,20},{28,24},{32,28},{36,32}... | collective-permute-start | bytes 393224 | tf_op jit(solution)/shard_map/while/body/eval_jaxpr/ppermute | solution.py:60
  247.6 4.2 collective-permute-start.2
  249.6 3.9 collective-permute-start.3
  258.3 11.2 %collective-permute-start.18 = (f32[2,16,1,256]{3,2,1,0:T(1,128)S(1)}, f32[2,16,1,256]{3,2,1,0:T(1,128)S(1)}, u32[]{:S(2)}, u32[]{:S(2)}) collective-permute-start(f32[2,16,1,256]{3,2,1,0:T(1,128)S(1)} %get-tuple-element.146), channel_id=1, source_target_pairs={{1,0},{2,1},{3,2},{0,3},{5,4},{6,5},{7,6},{4,7},{9,8},{10,9},{11,1... | collective-permute-start | bytes 98312 | tf_op jit(solution)/shard_map/ppermute | solution.py:28
  258.4 11.1 %collective-permute-start.19 = (f32[2,16,1,256]{3,2,1,0:T(1,128)S(1)}, f32[2,16,1,256]{3,2,1,0:T(1,128)S(1)}, u32[]{:S(2)}, u32[]{:S(2)}) collective-permute-start(f32[2,16,1,256]{3,2,1,0:T(1,128)S(1)} %get-tuple-element.147), channel_id=1, source_target_pairs={{0,1},{1,2},{2,3},{3,0},{4,5},{5,6},{6,7},{7,4},{8,9},{9,10},{10,1... | collective-permute-start | bytes 98312 | tf_op jit(solution)/shard_map/ppermute | solution.py:27
  260.1 7.7 %collective-permute-start.17 = (f32[2,1,32,256]{3,2,1,0:T(8,128)S(1)}, f32[2,1,32,256]{3,2,1,0:T(8,128)S(1)}, u32[]{:S(2)}, u32[]{:S(2)}) collective-permute-start(f32[2,1,32,256]{3,2,1,0:T(8,128)S(1)} %get-tuple-element.149), channel_id=1, source_target_pairs={{0,4},{4,8},{8,12},{12,16},{16,20},{20,24},{24,28},{28,32},{32,36}... | collective-permute-start | bytes 196616 | tf_op jit(solution)/shard_map/ppermute | solution.py:27
  260.6 8.9 %collective-permute-start.16 = (f32[2,1,32,256]{3,2,1,0:T(8,128)S(1)}, f32[2,1,32,256]{3,2,1,0:T(8,128)S(1)}, u32[]{:S(2)}, u32[]{:S(2)}) collective-permute-start(f32[2,1,32,256]{3,2,1,0:T(8,128)S(1)} %get-tuple-element.148), channel_id=1, source_target_pairs={{4,0},{8,4},{12,8},{16,12},{20,16},{24,20},{28,24},{32,28},{36,32}... | collective-permute-start | bytes 196616 | tf_op jit(solution)/shard_map/ppermute | solution.py:28
  329.1 11.6 %collective-permute-start.21 = (f32[2,1,32,256]{3,2,1,0:T(8,128)S(1)}, f32[2,1,32,256]{3,2,1,0:T(8,128)S(1)}, u32[]{:S(2)}, u32[]{:S(2)}) collective-permute-start(f32[2,1,32,256]{3,2,1,0:T(8,128)S(1)} %get-tuple-element.142), channel_id=1, source_target_pairs={{0,4},{4,8},{8,12},{12,16},{16,20},{20,24},{24,28},{28,32},{32,36}... | collective-permute-start | bytes 196616 | tf_op jit(solution)/shard_map/ppermute | solution.py:27
  329.2 11.6 %collective-permute-start.22 = (f32[2,1,32,256]{3,2,1,0:T(8,128)S(1)}, f32[2,1,32,256]{3,2,1,0:T(8,128)S(1)}, u32[]{:S(2)}, u32[]{:S(2)}) collective-permute-start(f32[2,1,32,256]{3,2,1,0:T(8,128)S(1)} %get-tuple-element.143), channel_id=1, source_target_pairs={{4,0},{8,4},{12,8},{16,12},{20,16},{24,20},{28,24},{32,28},{36,32}... | collective-permute-start | bytes 196616 | tf_op jit(solution)/shard_map/ppermute | solution.py:28
  335.5 3.0 collective-permute-start.20
  337.4 3.3 collective-permute-start.23
  342.1 9.7 %collective-permute-start.4 = (f32[2,2,32,256]{3,2,1,0:T(8,128)S(1)}, f32[2,2,32,256]{3,2,1,0:T(8,128)S(1)}, u32[]{:S(2)}, u32[]{:S(2)}) collective-permute-start(f32[2,2,32,256]{3,2,1,0:T(8,128)S(1)} %get-tuple-element.272), channel_id=1, source_target_pairs={{0,4},{4,8},{8,12},{12,16},{16,20},{20,24},{24,28},{28,32},{32,36}... | collective-permute-start | bytes 393224 | tf_op jit(solution)/shard_map/while/body/eval_jaxpr/ppermute | solution.py:57
  342.2 11.4 %collective-permute-start.5 = (f32[2,2,32,256]{3,2,1,0:T(8,128)S(1)}, f32[2,2,32,256]{3,2,1,0:T(8,128)S(1)}, u32[]{:S(2)}, u32[]{:S(2)}) collective-permute-start(f32[2,2,32,256]{3,2,1,0:T(8,128)S(1)} %get-tuple-element.273), channel_id=1, source_target_pairs={{4,0},{8,4},{12,8},{16,12},{20,16},{24,20},{28,24},{32,28},{36,32}... | collective-permute-start | bytes 393224 | tf_op jit(solution)/shard_map/while/body/eval_jaxpr/ppermute | solution.py:60
  353.7 3.3 collective-permute-start.6
  355.6 3.9 collective-permute-start.7
  363.8 8.4 %collective-permute-start.4 = (f32[2,2,32,256]{3,2,1,0:T(8,128)S(1)}, f32[2,2,32,256]{3,2,1,0:T(8,128)S(1)}, u32[]{:S(2)}, u32[]{:S(2)}) collective-permute-start(f32[2,2,32,256]{3,2,1,0:T(8,128)S(1)} %get-tuple-element.272), channel_id=1, source_target_pairs={{0,4},{4,8},{8,12},{12,16},{16,20},{20,24},{24,28},{28,32},{32,36}... | collective-permute-start | bytes 393224 | tf_op jit(solution)/shard_map/while/body/eval_jaxpr/ppermute | solution.py:57
  363.9 9.7 %collective-permute-start.5 = (f32[2,2,32,256]{3,2,1,0:T(8,128)S(1)}, f32[2,2,32,256]{3,2,1,0:T(8,128)S(1)}, u32[]{:S(2)}, u32[]{:S(2)}) collective-permute-start(f32[2,2,32,256]{3,2,1,0:T(8,128)S(1)} %get-tuple-element.273), channel_id=1, source_target_pairs={{4,0},{8,4},{12,8},{16,12},{20,16},{24,20},{28,24},{32,28},{36,32}... | collective-permute-start | bytes 393224 | tf_op jit(solution)/shard_map/while/body/eval_jaxpr/ppermute | solution.py:60
  373.7 4.0 collective-permute-start.6
  376.2 4.4 collective-permute-start.7
  385.0 8.3 %collective-permute-start.4 = (f32[2,2,32,256]{3,2,1,0:T(8,128)S(1)}, f32[2,2,32,256]{3,2,1,0:T(8,128)S(1)}, u32[]{:S(2)}, u32[]{:S(2)}) collective-permute-start(f32[2,2,32,256]{3,2,1,0:T(8,128)S(1)} %get-tuple-element.272), channel_id=1, source_target_pairs={{0,4},{4,8},{8,12},{12,16},{16,20},{20,24},{24,28},{28,32},{32,36}... | collective-permute-start | bytes 393224 | tf_op jit(solution)/shard_map/while/body/eval_jaxpr/ppermute | solution.py:57
  385.1 9.3 %collective-permute-start.5 = (f32[2,2,32,256]{3,2,1,0:T(8,128)S(1)}, f32[2,2,32,256]{3,2,1,0:T(8,128)S(1)}, u32[]{:S(2)}, u32[]{:S(2)}) collective-permute-start(f32[2,2,32,256]{3,2,1,0:T(8,128)S(1)} %get-tuple-element.273), channel_id=1, source_target_pairs={{4,0},{8,4},{12,8},{16,12},{20,16},{24,20},{28,24},{32,28},{36,32}... | collective-permute-start | bytes 393224 | tf_op jit(solution)/shard_map/while/body/eval_jaxpr/ppermute | solution.py:60
  394.5 3.9 collective-permute-start.6
  395.8 6.1 %collective-permute-start.7 = (f32[2,20,2,256]{3,2,1,0:T(2,128)S(1)}, f32[2,20,2,256]{3,2,1,0:T(2,128)S(1)}, u32[]{:S(2)}, u32[]{:S(2)}) collective-permute-start(f32[2,20,2,256]{3,2,1,0:T(2,128)S(1)} %get-tuple-element.275), channel_id=1, source_target_pairs={{1,0},{2,1},{3,2},{0,3},{5,4},{6,5},{7,6},{4,7},{9,8},{10,9},{11,1... | collective-permute-start | bytes 245768 | tf_op jit(solution)/shard_map/while/body/eval_jaxpr/ppermute | solution.py:60
  406.4 9.0 %collective-permute-start.4 = (f32[2,2,32,256]{3,2,1,0:T(8,128)S(1)}, f32[2,2,32,256]{3,2,1,0:T(8,128)S(1)}, u32[]{:S(2)}, u32[]{:S(2)}) collective-permute-start(f32[2,2,32,256]{3,2,1,0:T(8,128)S(1)} %get-tuple-element.272), channel_id=1, source_target_pairs={{0,4},{4,8},{8,12},{12,16},{16,20},{20,24},{24,28},{28,32},{32,36}... | collective-permute-start | bytes 393224 | tf_op jit(solution)/shard_map/while/body/eval_jaxpr/ppermute | solution.py:57
  406.5 11.3 %collective-permute-start.5 = (f32[2,2,32,256]{3,2,1,0:T(8,128)S(1)}, f32[2,2,32,256]{3,2,1,0:T(8,128)S(1)}, u32[]{:S(2)}, u32[]{:S(2)}) collective-permute-start(f32[2,2,32,256]{3,2,1,0:T(8,128)S(1)} %get-tuple-element.273), channel_id=1, source_target_pairs={{4,0},{8,4},{12,8},{16,12},{20,16},{24,20},{28,24},{32,28},{36,32}... | collective-permute-start | bytes 393224 | tf_op jit(solution)/shard_map/while/body/eval_jaxpr/ppermute | solution.py:60
  417.9 2.3 collective-permute-start.6
  418.6 4.2 collective-permute-start.7
  427.3 10.1 %collective-permute-start.4 = (f32[2,2,32,256]{3,2,1,0:T(8,128)S(1)}, f32[2,2,32,256]{3,2,1,0:T(8,128)S(1)}, u32[]{:S(2)}, u32[]{:S(2)}) collective-permute-start(f32[2,2,32,256]{3,2,1,0:T(8,128)S(1)} %get-tuple-element.272), channel_id=1, source_target_pairs={{0,4},{4,8},{8,12},{12,16},{16,20},{20,24},{24,28},{28,32},{32,36}... | collective-permute-start | bytes 393224 | tf_op jit(solution)/shard_map/while/body/eval_jaxpr/ppermute | solution.py:57
  427.3 12.3 %collective-permute-start.5 = (f32[2,2,32,256]{3,2,1,0:T(8,128)S(1)}, f32[2,2,32,256]{3,2,1,0:T(8,128)S(1)}, u32[]{:S(2)}, u32[]{:S(2)}) collective-permute-start(f32[2,2,32,256]{3,2,1,0:T(8,128)S(1)} %get-tuple-element.273), channel_id=1, source_target_pairs={{4,0},{8,4},{12,8},{16,12},{20,16},{24,20},{28,24},{32,28},{36,32}... | collective-permute-start | bytes 393224 | tf_op jit(solution)/shard_map/while/body/eval_jaxpr/ppermute | solution.py:60
  440.0 5.0 %collective-permute-start.7 = (f32[2,20,2,256]{3,2,1,0:T(2,128)S(1)}, f32[2,20,2,256]{3,2,1,0:T(2,128)S(1)}, u32[]{:S(2)}, u32[]{:S(2)}) collective-permute-start(f32[2,20,2,256]{3,2,1,0:T(2,128)S(1)} %get-tuple-element.275), channel_id=1, source_target_pairs={{1,0},{2,1},{3,2},{0,3},{5,4},{6,5},{7,6},{4,7},{9,8},{10,9},{11,1... | collective-permute-start | bytes 245768 | tf_op jit(solution)/shard_map/while/body/eval_jaxpr/ppermute | solution.py:60
  449.4 9.7 %collective-permute-start.4 = (f32[2,2,32,256]{3,2,1,0:T(8,128)S(1)}, f32[2,2,32,256]{3,2,1,0:T(8,128)S(1)}, u32[]{:S(2)}, u32[]{:S(2)}) collective-permute-start(f32[2,2,32,256]{3,2,1,0:T(8,128)S(1)} %get-tuple-element.272), channel_id=1, source_target_pairs={{0,4},{4,8},{8,12},{12,16},{16,20},{20,24},{24,28},{28,32},{32,36}... | collective-permute-start | bytes 393224 | tf_op jit(solution)/shard_map/while/body/eval_jaxpr/ppermute | solution.py:57
  449.5 12.3 %collective-permute-start.5 = (f32[2,2,32,256]{3,2,1,0:T(8,128)S(1)}, f32[2,2,32,256]{3,2,1,0:T(8,128)S(1)}, u32[]{:S(2)}, u32[]{:S(2)}) collective-permute-start(f32[2,2,32,256]{3,2,1,0:T(8,128)S(1)} %get-tuple-element.273), channel_id=1, source_target_pairs={{4,0},{8,4},{12,8},{16,12},{20,16},{24,20},{28,24},{32,28},{36,32}... | collective-permute-start | bytes 393224 | tf_op jit(solution)/shard_map/while/body/eval_jaxpr/ppermute | solution.py:60
  461.9 4.5 collective-permute-start.7
  (22 other events, 72.9 us)
Sparse Core Ops, SparseCore 0:
  9.1 77.7 all-gather.1
where the time goes:
time: 482 us; the launch traced here: 479 us
  waiting for transfers between devices  191 us (40%)
  starting transfers between devices  136 us (28%)
  blocking collectives  52 us (11%)
  other arithmetic  46.1 us (10%)
  local copies, waits for them, and re-layouts  37.5 us (8%)
  between operations  14.2 us (3%)
    ppermute x24, starting transfers between devices, padded_3(): lax.ppermute(lax.slice_in_dim(block, 0, width, axis=dim), axis, backward)  74.2 us
    all_to_all x1, waiting for transfers between devices, sent_and_summed(): blocks = lax.all_to_all(split_up(array, dim, count), axis, 0, 0, tiled=True)  72.7 us
    ppermute x24, waiting for transfers between devices, padded_3(): lax.ppermute(lax.slice_in_dim(block, block.shape[dim] - width, None, axis...  63.7 us
    all_to_all x1, blocking collectives, sent_and_summed(): blocks = lax.all_to_all(split_up(array, dim, count), axis, 0, 0, tiled=True)  52 us
    ppermute x24, waiting for transfers between devices, padded_3(): lax.ppermute(lax.slice_in_dim(block, 0, width, axis=dim), axis, backward)  44.9 us
    ppermute x8, starting transfers between devices, padded_2(): lax.ppermute(leading, axis, [(b, a) for a, b in up])  27.1 us
    ppermute x24, starting transfers between devices, padded_3(): lax.ppermute(lax.slice_in_dim(block, block.shape[dim] - width, None, axis...  21.9 us
    slice x52, local copies, waits for them, and re-layouts, beside(): return total + jnp.roll(center, 1, 3) + jnp.roll(center, -1, 3)  18.7 us
  transfers between devices with their start and end apart: 66, of which 54 were waited for; matrix products, arithmetic and copies ran while one was open for 3% of the time, Pallas kernels for 0%

commit v1 on v0

v1 whole, which is shorter than its diff:
```python
import jax
import jax.numpy as jnp
from jax import lax
from jax.experimental import pallas as pl
from jax.experimental.pallas import tpu as pltpu
from jax.sharding import PartitionSpec as P

SWEEPS = 2
JACOBI = 12


radau_points = [0.088587959512704, 0.409466864440735, 0.787659461760847, 1.0]
time_step = 4.0
diffusion_values = [1.0, 0.5]

XB, YB, ZB = 16, 32, 256
HALF = XB // 2
LANES = 128
PLANES = XB + 2 * (JACOBI + 1)
FIRST = JACOBI + 1
ROW0 = 24
ROWS = YB + 2 * ROW0
NEAR = (FIRST - 11, FIRST + XB + 11)
FAR = (FIRST - 3, FIRST + XB + 3)
NNEAR = NEAR[1] - NEAR[0]
NFAR = FAR[1] - FAR[0]
STRIP = NNEAR + NFAR


def collocation():
    count = len(radau_points)
    table = []
    for row in range(count):
        table.append([0.0] * count)
    for column in range(count):
        poly = [1.0]
        denom = 1.0
        for other in range(count):
            if other != column:
                longer = [0.0] * (len(poly) + 1)
                for place in range(len(poly)):
                    longer[place + 1] = longer[place + 1] + poly[place]
                    longer[place] = longer[place] - radau_points[other] * poly[place]
                poly = longer
                denom = denom * (radau_points[column] - radau_points[other])
        for row in range(count):
            point = radau_points[row]
            total = 0.0
            for place in range(len(poly)):
                total = total + poly[place] * point ** (place + 1) / (place + 1)
            table[row][column] = total / denom
    return table


def node_table():
    q = collocation()
    rows = []
    for n in range(4):
        a, b = n ^ 1, 3 - n
        row = [
            time_step * q[n][n], time_step * q[n][a], time_step * q[n][b],
            time_step * q[b][n], time_step * q[b][a],
            time_step * q[a][n], time_step * q[a][b],
            0.0,
        ]
        for d in diffusion_values:
            c = time_step * radau_points[n] * d
            row += [-c, c / (1.0 + 6.0 * c), 1.0 / (1.0 + 6.0 * c), d]
        rows.append(row)
    return rows


def ring(count, step):
    return [(i, (i + step) % count) for i in range(count)]


def shifted(array, axis, step):
    return lax.ppermute(array, axis, ring(lax.axis_size(axis), step))


def z_sum(c0, c1, lane):
    first, last = lane == 0, lane == LANES - 1
    up0, up1 = pltpu.roll(c0, 1, 1), pltpu.roll(c1, 1, 1)
    dn0, dn1 = pltpu.roll(c0, LANES - 1, 1), pltpu.roll(c1, LANES - 1, 1)
    low = jnp.where(first, up1, up0) + jnp.where(last, dn1, dn0)
    high = jnp.where(first, up0, up1) + jnp.where(last, dn0, dn1)
    return low, high


def force_kernel(sc, x, xlo, xhi, ylo, yhi, feed, kill,
                 fua, fub, fva, fvb, du, dv, work):
    def fill(p, carry):
        for s in range(2):
            for h in range(2):
                lanes = slice(h * LANES, (h + 1) * LANES)
                work[s, p + 1, h, 8:8 + YB, :] = x[s, p, :, lanes]
        return carry

    lax.fori_loop(0, XB, fill, 0)
    for s in range(2):
        for h in range(2):
            lanes = slice(h * LANES, (h + 1) * LANES)
            work[s, 0, h, 8:8 + YB, :] = xlo[s, 0, :, lanes]
            work[s, XB + 1, h, 8:8 + YB, :] = xhi[s, 0, :, lanes]
            for p in range(XB):
                work[s, p + 1, h, 7:8, :] = ylo[s, p:p + 1, lanes]
                work[s, p + 1, h, 8 + YB:9 + YB, :] = yhi[s, p:p + 1, lanes]
    lane = lax.broadcasted_iota(jnp.int32, (8, LANES), 1)

    def run(base, fu, fv):
        def plane(i, carry):
            p = base + i
            for t in range(YB // 8):
                r = 8 + 8 * t
                out = slice(8 * t, 8 * t + 8)
                field = []
                lap = []
                for s in range(2):
                    c = [work[s, p + 1, h, r:r + 8, :] for h in range(2)]
                    z = z_sum(c[0], c[1], lane)
                    terms = []
                    for h in range(2):
                        total = work[s, p, h, r:r + 8, :] + work[s, p + 2, h, r:r + 8, :]
                        total = total + work[s, p + 1, h, r - 1:r + 7, :]
                        total = total + work[s, p + 1, h, r + 1:r + 9, :]
                        terms.append(total + z[h] - 6.0 * c[h])
                    field.append(c)
                    lap.append(terms)
                for h in range(2):
                    lanes = slice(h * LANES, (h + 1) * LANES)
                    u, v = field[0][h], field[1][h]
                    fr, kr = feed[p, out, lanes], kill[p, out, lanes]
                    uvv = u * v * v
                    fu[i, out, lanes] = sc[11] * lap[0][h] + (fr * (1.0 - u) - uvv)
                    fv[i, out, lanes] = sc[15] * lap[1][h] + (uvv - (fr + kr) * v)
                    du[p, out, lanes] = sc[8] * lap[0][h]
                    dv[p, out, lanes] = sc[12] * lap[1][h]
            return carry

        lax.fori_loop(0, HALF, plane, 0)

    run(0, fua, fva)
    run(HALF, fub, fvb)


def forces(sc, x, xlo, xhi, ylo, yhi, feed, kill):
    half = jax.ShapeDtypeStruct((HALF, YB, ZB), jnp.float32)
    full = jax.ShapeDtypeStruct((XB, YB, ZB), jnp.float32)
    vmem = pl.BlockSpec(memory_space=pltpu.VMEM)
    return pl.pallas_call(
        force_kernel,
        out_shape=(half, half, half, half, full, full),
        in_specs=[pl.BlockSpec(memory_space=pltpu.SMEM)] + [vmem] * 7,
        out_specs=(vmem,) * 6,
        scratch_shapes=[pltpu.VMEM((2, XB + 2, 2, YB + 16, LANES), jnp.float32)],
        cost_estimate=pl.CostEstimate(flops=8_000_000, bytes_accessed=6_000_000, transcendentals=0),
        name="forces",
    )(sc, x, xlo, xhi, ylo, yhi, feed, kill)


def jacobi_kernel(species, sc, x, own, ra, rb, core, yhi, ylo, one, two, bs):
    spread = sc[8 + 4 * species + 1]
    scale = sc[8 + 4 * species + 2]
    zero = jnp.zeros((ROWS, LANES), jnp.float32)

    def clear(p, carry):
        for h in range(2):
            one[p, h] = zero
            two[p, h] = zero
        return carry

    lax.fori_loop(0, PLANES, clear, 0)

    def fill(half, recv):
        def plane(i, carry):
            p = half * HALF + i
            for h in range(2):
                lanes = slice(h * LANES, (h + 1) * LANES)
                one[FIRST + p, h, ROW0:ROW0 + YB, :] = x[0, p, :, lanes]
                bs[p, h] = scale * (own[p, :, lanes] + recv[i, :, lanes])
            return carry

        lax.fori_loop(0, HALF, plane, 0)

    fill(0, ra)
    fill(1, rb)
    lane = lax.broadcasted_iota(jnp.int32, (8, LANES), 1)

    def plane_of(src, dst, p, tiles, inside):
        for t in range(-tiles, YB // 8 + tiles):
            r = ROW0 + 8 * t
            c = [src[p, h, r:r + 8, :] for h in range(2)]
            z = z_sum(c[0], c[1], lane)
            for h in range(2):
                total = src[p - 1, h, r:r + 8, :] + src[p + 1, h, r:r + 8, :]
                total = total + (src[p, h, r - 1:r + 7, :] + src[p, h, r + 1:r + 9, :])
                new = spread * (total + z[h])
                if inside and 0 <= t < YB // 8:
                    new = new + bs[p - FIRST, h, 8 * t:8 * t + 8, :]
                dst[p, h, r:r + 8, :] = new

    def turn(src, dst, k, tiles):
        def outside(i, carry):
            plane_of(src, dst, FIRST - 1 - i, tiles, False)
            plane_of(src, dst, FIRST + XB + i, tiles, False)
            return carry

        def inside(i, carry):
            plane_of(src, dst, FIRST + i, tiles, True)
            return carry

        lax.fori_loop(0, k, outside, 0)
        lax.fori_loop(0, XB, inside, 0)

    def pair(tiles):
        def run(i, carry):
            turn(one, two, 2 * i + 1, tiles)
            turn(two, one, 2 * i + 2, tiles)
            return carry

        return run

    lax.fori_loop(0, 4, pair(1), 0)
    lax.fori_loop(4, JACOBI // 2, pair(2), 0)

    def give(p, carry):
        for h in range(2):
            lanes = slice(h * LANES, (h + 1) * LANES)
            core[p, :, lanes] = one[p + 1, h, ROW0:ROW0 + YB, :]
        return carry

    lax.fori_loop(0, XB + 2 * JACOBI, give, 0)

    def near(i, carry):
        for h in range(2):
            lanes = slice(h * LANES, (h + 1) * LANES)
            yhi[i, :, lanes] = one[NEAR[0] + i, h, ROW0 + YB:ROW0 + YB + 8, :]
            ylo[i, :, lanes] = one[NEAR[0] + i, h, ROW0 - 8:ROW0, :]
        return carry

    def far(i, carry):
        for h in range(2):
            lanes = slice(h * LANES, (h + 1) * LANES)
            yhi[NNEAR + i, :, lanes] = one[FAR[0] + i, h, ROW0 + YB + 8:ROW0 + YB + 16, :]
            ylo[NNEAR + i, :, lanes] = one[FAR[0] + i, h, ROW0 - 16:ROW0 - 8, :]
        return carry

    lax.fori_loop(0, NNEAR, near, 0)
    lax.fori_loop(0, NFAR, far, 0)


def jacobi(species, sc, x, own, ra, rb):
    vmem = pl.BlockSpec(memory_space=pltpu.VMEM)
    strip = jax.ShapeDtypeStruct((STRIP, 8, ZB), jnp.float32)
    return pl.pallas_call(
        lambda *refs: jacobi_kernel(species, *refs),
        grid=(1,),
        out_shape=(jax.ShapeDtypeStruct((XB + 2 * JACOBI, YB, ZB), jnp.float32), strip, strip),
        in_specs=[
            pl.BlockSpec(memory_space=pltpu.SMEM),
            pl.BlockSpec((1, XB, YB, ZB), lambda i: (species, 0, 0, 0)),
            vmem, vmem, vmem,
        ],
        out_specs=(vmem,) * 3,
        scratch_shapes=[
            pltpu.VMEM((PLANES, 2, ROWS, LANES), jnp.float32),
            pltpu.VMEM((PLANES, 2, ROWS, LANES), jnp.float32),
            pltpu.VMEM((XB, 2, YB, LANES), jnp.float32),
        ],
        cost_estimate=pl.CostEstimate(flops=60_000_000, bytes_accessed=5_000_000, transcendentals=0),
        name="jacobi",
    )(sc, x, own, ra, rb)


def gather_kernel(core, low, high, xlo, xhi, center):
    wide = XB + 2 * JACOBI
    for p in range(wide):
        if p < JACOBI:
            dst, q = xlo, p
        elif p < JACOBI + XB:
            dst, q = center, p - JACOBI
        else:
            dst, q = xhi, p - JACOBI - XB
        near = p + 1 - NEAR[0]
        far = p + 1 - FAR[0]
        has_near = 0 <= near < NNEAR
        has_far = 0 <= far < NFAR
        parts = [core[p, 8 * t:8 * t + 8, :] for t in range(4)]
        if has_near:
            parts[0] = parts[0] + low[near]
            parts[3] = parts[3] + high[near]
        if has_far:
            parts[1] = parts[1] + low[NNEAR + far]
            parts[2] = parts[2] + high[NNEAR + far]
        for t in range(4):
            dst[q, 8 * t:8 * t + 8, :] = parts[t]


def gathered(core, low, high):
    vmem = pl.BlockSpec(memory_space=pltpu.VMEM)
    side = jax.ShapeDtypeStruct((JACOBI, YB, ZB), jnp.float32)
    return pl.pallas_call(
        gather_kernel,
        out_shape=(side, side, jax.ShapeDtypeStruct((XB, YB, ZB), jnp.float32)),
        in_specs=[vmem] * 3,
        out_specs=(vmem,) * 3,
        cost_estimate=pl.CostEstimate(flops=1_000_000, bytes_accessed=4_000_000, transcendentals=0),
        name="gathered",
    )(core, low, high)


def final_kernel(cu, lu, hu, cv, lv, hv, out, *edges):
    gap = XB - JACOBI
    for s, (c, low, high) in enumerate(((cu, lu, hu), (cv, lv, hv))):
        for p in range(XB):
            value = c[p]
            if p < JACOBI:
                value = value + low[p]
            if p >= gap:
                value = value + high[p - gap]
            out[s, p] = value
            if edges:
                xfirst, xlast, yfirst, ylast = edges
                if p == 0:
                    xfirst[s, 0] = value
                if p == XB - 1:
                    xlast[s, 0] = value
                yfirst[s, p:p + 1, :] = value[0:1, :]
                ylast[s, p:p + 1, :] = value[YB - 1:YB, :]


def final(cu, lu, hu, cv, lv, hv, edges):
    vmem = pl.BlockSpec(memory_space=pltpu.VMEM)
    shapes = [jax.ShapeDtypeStruct((2, XB, YB, ZB), jnp.float32)]
    if edges:
        shapes += [jax.ShapeDtypeStruct((2, 1, YB, ZB), jnp.float32)] * 2
        shapes += [jax.ShapeDtypeStruct((2, XB, ZB), jnp.float32)] * 2
    return pl.pallas_call(
        final_kernel,
        out_shape=tuple(shapes),
        in_specs=[vmem] * 6,
        out_specs=(vmem,) * len(shapes),
        cost_estimate=pl.CostEstimate(flops=1_000_000, bytes_accessed=4_000_000, transcendentals=0),
        name="final",
    )(cu, lu, hu, cv, lv, hv)


PAIR_A = [(0, 1), (1, 0), (2, 3), (3, 2)]
PAIR_B = [(0, 3), (3, 0), (1, 2), (2, 1)]


def body(previous, feed_rate, kill_rate):
    node = lax.axis_index("node")
    sc = jnp.asarray(node_table(), jnp.float32)[node]
    x = previous[0]
    sent_a = lax.ppermute(x[:, :HALF], "node", [(3, 2)])
    sent_b = lax.ppermute(x[:, HALF:], "node", [(3, 0)])
    last = node == 3
    edges = (x[:, :1], x[:, XB - 1:], x[:, :, 0], x[:, :, YB - 1])
    for sweep in range(SWEEPS):
        xfirst, xlast, yfirst, ylast = edges
        xlo = shifted(xlast, "sx", 1)
        xhi = shifted(xfirst, "sx", -1)
        ylo = shifted(ylast, "sy", 1)
        yhi = shifted(yfirst, "sy", -1)
        if sweep == 0:
            start_a = jnp.where(last, x[:, :HALF], sent_a)
            start_b = jnp.where(last, x[:, HALF:], sent_b)
        fua, fub, fva, fvb, du, dv = forces(sc, x, xlo, xhi, ylo, yhi, feed_rate, kill_rate)
        cores = []
        for s, (fa, fb, d) in enumerate(((fua, fub, du), (fva, fvb, dv))):
            ga = lax.ppermute(fa, "node", PAIR_A)
            gb = lax.ppermute(fb, "node", PAIR_B)
            ra = lax.ppermute(sc[3] * fa + sc[4] * ga + start_a[s], "node", PAIR_B)
            rb = lax.ppermute(sc[5] * fb + sc[6] * gb + start_b[s], "node", PAIR_A)
            own = jnp.concatenate(
                [
                    sc[0] * fa + sc[1] * ga + start_a[s] + d[:HALF],
                    sc[0] * fb + sc[2] * gb + start_b[s] + d[HALF:],
                ],
                0,
            )
            core, up, down = jacobi(s, sc, x, own, ra, rb)
            low = shifted(up, "sy", 1)
            high = shifted(down, "sy", -1)
            left, right, center = gathered(core, low, high)
            cores += [center, shifted(right, "sx", 1), shifted(left, "sx", -1)]
        x, *edges = final(*cores, sweep + 1 < SWEEPS)
    return x[None]


def solution(mesh):
    return jax.shard_map(
        body,
        mesh=mesh,
        in_specs=(P("node", None, "sx", "sy", None), P("sx", "sy", None), P("sx", "sy", None)),
        out_specs=P("node", None, "sx", "sy", None),
        check_vma=False,
    )
```

time: 482 us -> 361 us (0.75)
  Pallas kernels: 0 us -> 158 us
  waiting for transfers between devices: 191 us -> 96.3 us
  starting transfers between devices: 136 us -> 74.2 us
  blocking collectives: 52 us -> 0 us
  other arithmetic: 46.1 us -> 15.4 us
  local copies, waits for them, and re-layouts: 37.5 us -> 14.8 us
  between operations: 14.2 us -> 0.36 us
    pallas_call x0 -> x12, Pallas kernels: none -> 158 us  [the longest x4 132 us: jacobi(): pl.pallas_call(lambda *refs: jacobi_kernel(species, *refs), grid=(1,), ou...]
    all_to_all x1 -> x0, waiting for transfers between devices: 72.7 us -> none  [sent_and_summed(): blocks = lax.all_to_all(split_up(array, dim, count), axis, 0, 0, tiled=True)]
    ppermute x64 -> x42, starting transfers between devices: 131 us -> 74.2 us  [the longest x24 51.9 us: shifted(): return lax.ppermute(array, axis, ring(lax.axis_size(axis), step))]
    all_to_all x1 -> x0, blocking collectives: 52 us -> none  [sent_and_summed(): blocks = lax.all_to_all(split_up(array, dim, count), axis, 0, 0, tiled=True)]
    ppermute x64 -> x42, waiting for transfers between devices: 119 us -> 96.3 us  [the longest x24 64.6 us: shifted(): return lax.ppermute(array, axis, ring(lax.axis_size(axis), step))]
    div x24 -> x0, other arithmetic: 21.9 us -> none  [the longest x12 12.1 us: double_turn(): midway = (extended + coef * beside(beside_all)) / (1.0 + 6.0 * coef)]
    slice x84 -> x4, local copies, waits for them, and re-layouts: 21.9 us -> 3.71 us  [the longest x2 1.97 us: body(): edges = (x[:, :1], x[:, XB - 1:], x[:, :, 0], x[:, :, YB - 1])]
    while x48 -> x0, local copies, waits for them, and re-layouts: 10.8 us -> none
  transfers between devices with their start and end apart: 66 -> 42, of which waited for: 54 -> 20; matrix products, arithmetic and copies ran while one was open for 3% -> 5% of each run, Pallas kernels for 0% -> 41%
where the time goes in v1:
time: 361 us; the launch traced here: 359 us
  Pallas kernels  158 us (44%)
  waiting for transfers between devices  96.3 us (27%)
  starting transfers between devices  74.2 us (21%)
  other arithmetic  15.4 us (4%)
  local copies, waits for them, and re-layouts  14.8 us (4%)
    pallas_call x4, Pallas kernels, jacobi(): pl.pallas_call(lambda *refs: jacobi_kernel(species, *refs), grid=(1,), ou...  132 us
    ppermute x24, waiting for transfers between devices, shifted(): return lax.ppermute(array, axis, ring(lax.axis_size(axis), step))  64.6 us
    ppermute x24, starting transfers between devices, shifted(): return lax.ppermute(array, axis, ring(lax.axis_size(axis), step))  51.9 us
    ppermute x4, waiting for transfers between devices, body(): ga = lax.ppermute(fa, 'node', PAIR_A)  14.8 us
    pallas_call x4, Pallas kernels, gathered(): pl.pallas_call(gather_kernel, out_shape=(side, side, jax.ShapeDtypeStruct...  10.8 us
    unnamed x88, local copies, waits for them, and re-layouts  9.82 us
    ppermute x4, waiting for transfers between devices, body(): gb = lax.ppermute(fb, 'node', PAIR_B)  9.7 us
    pallas_call x2, Pallas kernels, forces(): pl.pallas_call(force_kernel, out_shape=(half, half, half, half, full, ful...  9.41 us
  transfers between devices with their start and end apart: 42, of which 20 were waited for; matrix products, arithmetic and copies ran while one was open for 5% of the time, Pallas kernels for 41%

profile of v1, /device:TPU:1, one launch (start us, length us, event | category | flops | bytes accessed | tf_op | source)
XLA Modules:
  0.0 359.1 jit_solution(8430264946726831330)
XLA Ops:
  0.0 1.1 slice.150
  1.8 0.9 fusion.2
  2.7 2.2 collective-permute-start
  4.9 7.3 %collective-permute-start.1 = (f32[2,1,32,256]{3,2,1,0:T(8,128)S(1)}, f32[2,1,32,256]{3,2,1,0:T(8,128)S(1)}, u32[]{:S(2)}, u32[]{:S(2)}) collective-permute-start(f32[2,1,32,256]{3,2,1,0:T(8,128)S(1)} %get-tuple-element.107), channel_id=1, source_target_pairs={{0,60},{4,0},{8,4},{12,8},{16,12},{20,16},{24,20},{28,24},{32,28},... | collective-permute-start | bytes 196616 | tf_op jit(solution)/shard_map/ppermute | solution.py:78
  12.1 1.1 fusion.1
  13.2 1.7 collective-permute-start.2
  14.9 1.2 constant_dynamic-slice_fusion
  16.1 2.1 collective-permute-done.3.yhi
  18.9 4.7 %forces.2 = (f32[8,32,256]{2,1,0:T(8,128)}, f32[8,32,256]{2,1,0:T(8,128)}, f32[8,32,256]{2,1,0:T(8,128)}, f32[8,32,256]{2,1,0:T(8,128)}, f32[16,32,256]{2,1,0:T(8,128)}, /*index=5*/f32[16,32,256]{2,1,0:T(8,128)}) custom-call(f32[16]{0:T(128)} %get-tuple-element.118.sc.refs_0_, f32[2,16,32,256]{3,2,1,0:T(8,128)} %bitcast.60, f32[2,1,32,256]{3,2,1,0:T(8,128)} %copy-done.35, ...), custom_call_target="tpu_custom_call" | custom-call | flops 8000000 | bytes 6000000 | tf_op jit(solution)/shard_map/forces/pallas_call | solution.py:150
  23.6 1.2 collective-permute-start.14
  25.4 1.4 collective-permute-start.7
  27.5 4.5 %collective-permute-start.15 = (f32[8,32,256]{2,1,0:T(8,128)S(1)}, f32[8,32,256]{2,1,0:T(8,128)S(1)}, u32[]{:S(2)}, u32[]{:S(2)}) collective-permute-start(f32[8,32,256]{2,1,0:T(8,128)S(1)} %copy-done.30), channel_id=1, source_target_pairs={{0,192},{192,0},{64,128},{128,64},{1,193},{193,1},{65,129},{129,65... | collective-permute-start | bytes 786440 | tf_op jit(solution)/shard_map/ppermute | solution.py:373
  32.1 5.5 %collective-permute-done.4 = f32[8,32,256]{2,1,0:T(8,128)S(1)} collective-permute-done((f32[8,32,256]{2,1,0:T(8,128)}, f32[8,32,256]{2,1,0:T(8,128)S(1)}, u32[]{:S(2)}, u32[]{:S(2)}) %collective-permute-start.4) | collective-permute-done | bytes 262176 | tf_op jit(solution)/shard_map/ppermute | solution.py:372
  37.6 2.7 add_add_fusion.5
  40.3 4.6 %collective-permute-start.16 = (f32[8,32,256]{2,1,0:T(8,128)S(1)}, f32[8,32,256]{2,1,0:T(8,128)S(1)}, u32[]{:S(2)}, u32[]{:S(2)}) collective-permute-start(f32[8,32,256]{2,1,0:T(8,128)S(1)} %get-tuple-element.97), channel_id=1, source_target_pairs={{0,192},{192,0},{64,128},{128,64},{1,193},{193,1},{65,129},{129,65... | collective-permute-start | bytes 786440 | tf_op jit(solution)/shard_map/ppermute | solution.py:374
  45.1 4.1 %collective-permute-done.15 = f32[8,32,256]{2,1,0:T(8,128)S(1)} collective-permute-done((f32[8,32,256]{2,1,0:T(8,128)S(1)}, f32[8,32,256]{2,1,0:T(8,128)S(1)}, u32[]{:S(2)}, u32[]{:S(2)}) %collective-permute-start.15) | collective-permute-done | bytes 262176 | tf_op jit(solution)/shard_map/ppermute | solution.py:373
  49.2 5.6 %collective-permute-done.6 = f32[8,32,256]{2,1,0:T(8,128)S(1)} collective-permute-done((f32[8,32,256]{2,1,0:T(8,128)S(1)}, f32[8,32,256]{2,1,0:T(8,128)S(1)}, u32[]{:S(2)}, u32[]{:S(2)}) %collective-permute-start.6) | collective-permute-done | bytes 262176 | tf_op jit(solution)/shard_map/ppermute | solution.py:373
  54.8 2.9 add_add_fusion.4
  57.9 1.4 collective-permute-start.9
  59.3 1.0 pad_maximum_fusion
  60.4 4.6 %collective-permute-done.17.refs_4_ = f32[8,32,256]{2,1,0:T(8,128)S(1)} collective-permute-done((f32[8,32,256]{2,1,0:T(8,128)S(1)}, f32[8,32,256]{2,1,0:T(8,128)S(1)}, u32[]{:S(2)}, u32[]{:S(2)}) %collective-permute-start.17) | collective-permute-done | bytes 262176 | tf_op jit(solution)/shard_map/ppermute | solution.py:375
  65.7 33.1 %jacobi.5 = (f32[40,32,256]{2,1,0:T(8,128)}, f32[60,8,256]{2,1,0:T(8,128)}, f32[60,8,256]{2,1,0:T(8,128)}) custom-call(f32[16]{0:T(128)} %get-tuple-element.118.sc.refs_0_, f32[2,16,32,256]{3,2,1,0:T(8,128)} %bitcast.61, f32[16,32,256]{2,1,0:T(8,128)} %get-tuple-element.127.refs_2_, f32[8,32,256]{2,1,0:T(8,128)} %copy-done.21, f32[8,32,256]{2,1,0:T(8,128)} %copy-done.27), custom_call_target="tpu_custom_call" | custom-call | flops 60000000 | bytes 5000000 | tf_op jit(solution)/shard_map/jacobi/pallas_call | solution.py:255
  98.8 3.2 collective-permute-start.18
  102.8 33.1 %jacobi.4 = (f32[40,32,256]{2,1,0:T(8,128)}, f32[60,8,256]{2,1,0:T(8,128)}, f32[60,8,256]{2,1,0:T(8,128)}) custom-call(f32[16]{0:T(128)} %get-tuple-element.118.sc.refs_0_, f32[2,16,32,256]{3,2,1,0:T(8,128)} %bitcast.62, f32[16,32,256]{2,1,0:T(8,128)} %get-tuple-element.126.refs_2_, f32[8,32,256]{2,1,0:T(8,128)} %copy-done.23, f32[8,32,256]{2,1,0:T(8,128)} %copy-done.25), custom_call_target="tpu_custom_call" | custom-call | flops 60000000 | bytes 5000000 | tf_op jit(solution)/shard_map/jacobi/pallas_call | solution.py:255
  135.9 1.7 collective-permute-start.10
  138.6 2.7 gathered.5
  141.3 5.7 %collective-permute-start.21 = (f32[12,32,256]{2,1,0:T(8,128)}, f32[12,32,256]{2,1,0:T(8,128)S(1)}, u32[]{:S(2)}, u32[]{:S(2)}) collective-permute-start(f32[12,32,256]{2,1,0:T(8,128)} %get-tuple-element.63), channel_id=1, source_target_pairs={{0,60},{4,0},{8,4},{12,8},{16,12},{20,16},{24,20},{28,24},{32,28},... | collective-permute-start | bytes 1179656 | tf_op jit(solution)/shard_map/ppermute | solution.py:78
  147.7 4.9 %collective-permute-done.11.high = f32[60,8,256]{2,1,0:T(8,128)S(1)} collective-permute-done((f32[60,8,256]{2,1,0:T(8,128)}, f32[60,8,256]{2,1,0:T(8,128)S(1)}, u32[]{:S(2)}, u32[]{:S(2)}) %collective-permute-start.11) | collective-permute-done | bytes 491552 | tf_op jit(solution)/shard_map/ppermute | solution.py:78
  152.6 0.8 copy-done.11
  153.4 2.7 gathered.4
  156.1 5.7 %collective-permute-start.13 = (f32[12,32,256]{2,1,0:T(8,128)}, f32[12,32,256]{2,1,0:T(8,128)S(1)}, u32[]{:S(2)}, u32[]{:S(2)}) collective-permute-start(f32[12,32,256]{2,1,0:T(8,128)} %get-tuple-element.54), channel_id=1, source_target_pairs={{0,60},{4,0},{8,4},{12,8},{16,12},{20,16},{24,20},{28,24},{32,28},... | collective-permute-start | bytes 1179656 | tf_op jit(solution)/shard_map/ppermute | solution.py:78
  161.8 5.5 %collective-permute-done.20.lv = f32[12,32,256]{2,1,0:T(8,128)S(1)} collective-permute-done((f32[12,32,256]{2,1,0:T(8,128)}, f32[12,32,256]{2,1,0:T(8,128)S(1)}, u32[]{:S(2)}, u32[]{:S(2)}) %collective-permute-start.20) | collective-permute-done | bytes 393248 | tf_op jit(solution)/shard_map/ppermute | solution.py:78
  167.3 12.2 %collective-permute-done.12.lu = f32[12,32,256]{2,1,0:T(8,128)S(1)} collective-permute-done((f32[12,32,256]{2,1,0:T(8,128)}, f32[12,32,256]{2,1,0:T(8,128)S(1)}, u32[]{:S(2)}, u32[]{:S(2)}) %collective-permute-start.12) | collective-permute-done | bytes 393248 | tf_op jit(solution)/shard_map/ppermute | solution.py:78
  179.6 4.5 %collective-permute-done.13.hu = f32[12,32,256]{2,1,0:T(8,128)S(1)} collective-permute-done((f32[12,32,256]{2,1,0:T(8,128)}, f32[12,32,256]{2,1,0:T(8,128)S(1)}, u32[]{:S(2)}, u32[]{:S(2)}) %collective-permute-start.13) | collective-permute-done | bytes 393248 | tf_op jit(solution)/shard_map/ppermute | solution.py:78
  184.8 2.8 final.2
  187.6 6.5 %collective-permute-start.23 = (f32[2,1,32,256]{3,2,1,0:T(8,128)}, f32[2,1,32,256]{3,2,1,0:T(8,128)S(1)}, u32[]{:S(2)}, u32[]{:S(2)}) collective-permute-start(f32[2,1,32,256]{3,2,1,0:T(8,128)} %get-tuple-element.66), channel_id=1, source_target_pairs={{0,60},{4,0},{8,4},{12,8},{16,12},{20,16},{24,20},{28,24},{32,28},... | collective-permute-start | bytes 196616 | tf_op jit(solution)/shard_map/ppermute | solution.py:78
  194.2 1.3 collective-permute-start.24
  195.7 1.1 collective-permute-done.24.ylo
  196.8 2.2 collective-permute-done.25.yhi
  199.7 4.7 %forces.3 = (f32[8,32,256]{2,1,0:T(8,128)}, f32[8,32,256]{2,1,0:T(8,128)}, f32[8,32,256]{2,1,0:T(8,128)}, f32[8,32,256]{2,1,0:T(8,128)}, f32[16,32,256]{2,1,0:T(8,128)}, /*index=5*/f32[16,32,256]{2,1,0:T(8,128)}) custom-call(f32[16]{0:T(128)} %get-tuple-element.118.sc.refs_0_, f32[2,16,32,256]{3,2,1,0:T(8,128)} %get-tuple-element.64.x.refs_1_, ...), custom_call_target="tpu_custom_call" | custom-call | flops 8000000 | bytes 6000000 | tf_op jit(solution)/shard_map/forces/pallas_call | solution.py:150
  204.4 1.5 collective-permute-start.34
  206.3 2.2 collective-permute-start.35
  208.5 3.6 %collective-permute-done.26 = f32[8,32,256]{2,1,0:T(8,128)S(1)} collective-permute-done((f32[8,32,256]{2,1,0:T(8,128)}, f32[8,32,256]{2,1,0:T(8,128)S(1)}, u32[]{:S(2)}, u32[]{:S(2)}) %collective-permute-start.26) | collective-permute-done | bytes 262176 | tf_op jit(solution)/shard_map/ppermute | solution.py:372
  212.1 5.6 %collective-permute-done.34 = f32[8,32,256]{2,1,0:T(8,128)S(1)} collective-permute-done((f32[8,32,256]{2,1,0:T(8,128)}, f32[8,32,256]{2,1,0:T(8,128)S(1)}, u32[]{:S(2)}, u32[]{:S(2)}) %collective-permute-start.34) | collective-permute-done | bytes 262176 | tf_op jit(solution)/shard_map/ppermute | solution.py:372
  217.8 3.9 %add_add_fusion.1 = (f32[8,32,256]{2,1,0:T(8,128)S(1)}, f32[8,32,256]{2,1,0:T(8,128)S(1)}, f32[8,32,256]{2,1,0:T(8,128)S(1)}, f32[8,32,256]{2,1,0:T(8,128)S(1)}) fusion(f32[8,32,256]{2,1,0:T(8,128)S(1)} %collective-permute-done.34, f32[8,32,256]{2,1,0:T(8,128)} %get-tuple-element.78, f32[2,8,32,256]{3,2,1,0:T(8,128)S(1)} %get-tuple-element.103, f32[]{:T(128)} %bitcast.8, ...), kind=kLoop, calls=%fused_computation.9 | loop fusion | flops 1179648 | bytes 3145744 | tf_op jit(solution)/shard_map/add | solution.py:374
  221.7 0.9 collective-permute-start.36
  222.7 2.9 add_add_fusion
  225.8 2.1 collective-permute-start.28
  228.4 0.8 pad_maximum_fusion.3.refs_2_
  229.2 0.9 pad_maximum_fusion.2.refs_2_
  230.1 2.5 collective-permute-done.37.refs_4_
  233.3 33.0 %jacobi.7 = (f32[40,32,256]{2,1,0:T(8,128)}, f32[60,8,256]{2,1,0:T(8,128)}, f32[60,8,256]{2,1,0:T(8,128)}) custom-call(f32[16]{0:T(128)} %get-tuple-element.118.sc.refs_0_, f32[2,16,32,256]{3,2,1,0:T(8,128)} %get-tuple-element.64.x.refs_1_, f32[16,32,256]{2,1,0:T(8,128)} %pad_maximum_fusion.3.refs_2_, f32[8,32,256]{2,1,0:T(8,128)} %copy-done.22, ...), custom_call_target="tpu_custom_call" | custom-call | flops 60000000 | bytes 5000000 | tf_op jit(solution)/shard_map/jacobi/pallas_call | solution.py:255
  266.3 2.9 collective-permute-start.38
  271.0 33.1 %jacobi.6 = (f32[40,32,256]{2,1,0:T(8,128)}, f32[60,8,256]{2,1,0:T(8,128)}, f32[60,8,256]{2,1,0:T(8,128)}) custom-call(f32[16]{0:T(128)} %get-tuple-element.118.sc.refs_0_, f32[2,16,32,256]{3,2,1,0:T(8,128)} %get-tuple-element.64.x.refs_1_, f32[16,32,256]{2,1,0:T(8,128)} %pad_maximum_fusion.2.refs_2_, f32[8,32,256]{2,1,0:T(8,128)} %copy-done.24, ...), custom_call_target="tpu_custom_call" | custom-call | flops 60000000 | bytes 5000000 | tf_op jit(solution)/shard_map/jacobi/pallas_call | solution.py:255
  304.1 1.4 collective-permute-start.30
  306.8 2.7 gathered.7
  309.5 5.7 %collective-permute-start.41 = (f32[12,32,256]{2,1,0:T(8,128)}, f32[12,32,256]{2,1,0:T(8,128)S(1)}, u32[]{:S(2)}, u32[]{:S(2)}) collective-permute-start(f32[12,32,256]{2,1,0:T(8,128)} %get-tuple-element.86), channel_id=1, source_target_pairs={{0,60},{4,0},{8,4},{12,8},{16,12},{20,16},{24,20},{28,24},{32,28},... | collective-permute-start | bytes 1179656 | tf_op jit(solution)/shard_map/ppermute | solution.py:78
  315.2 14.4 %collective-permute-done.31.high = f32[60,8,256]{2,1,0:T(8,128)S(1)} collective-permute-done((f32[60,8,256]{2,1,0:T(8,128)}, f32[60,8,256]{2,1,0:T(8,128)S(1)}, u32[]{:S(2)}, u32[]{:S(2)}) %collective-permute-start.31) | collective-permute-done | bytes 491552 | tf_op jit(solution)/shard_map/ppermute | solution.py:78
  329.6 0.8 copy-done.12
  330.4 2.7 gathered.6
  333.1 5.7 %collective-permute-start.33 = (f32[12,32,256]{2,1,0:T(8,128)}, f32[12,32,256]{2,1,0:T(8,128)S(1)}, u32[]{:S(2)}, u32[]{:S(2)}) collective-permute-start(f32[12,32,256]{2,1,0:T(8,128)} %get-tuple-element.77), channel_id=1, source_target_pairs={{0,60},{4,0},{8,4},{12,8},{16,12},{20,16},{24,20},{28,24},{32,28},... | collective-permute-start | bytes 1179656 | tf_op jit(solution)/shard_map/ppermute | solution.py:78
  338.8 15.9 %collective-permute-done.32.lu = f32[12,32,256]{2,1,0:T(8,128)S(1)} collective-permute-done((f32[12,32,256]{2,1,0:T(8,128)}, f32[12,32,256]{2,1,0:T(8,128)S(1)}, u32[]{:S(2)}, u32[]{:S(2)}) %collective-permute-start.32) | collective-permute-done | bytes 393248 | tf_op jit(solution)/shard_map/ppermute | solution.py:78
  354.8 0.8 collective-permute-done.33.hu
  356.3 2.8 final.3
  (134 shorter events, 13.7 us)
Async XLA Ops:
  1.1 24.1 %collective-permute-start.5 = (f32[2,8,32,256]{3,2,1,0:T(8,128)S(1)}, f32[2,8,32,256]{3,2,1,0:T(8,128)S(1)}, u32[]{:S(2)}, u32[]{:S(2)}) collective-permute-start(f32[2,8,32,256]{3,2,1,0:T(8,128)S(1)} %slice.150), channel_id=1, source_target_pairs={{192,128},{193,129},{194,130},{195,131},{196,132},{197,133},{198,1... | collective-permute-start | bytes 1572872 | tf_op jit(solution)/shard_map/ppermute | solution.py:356
  2.7 22.5 %copy-start = (f32[1,2,16,32,256]{4,3,2,1,0:T(8,128)S(1)}, f32[1,2,16,32,256]{4,3,2,1,0:T(8,128)}, u32[]{:S(2)}) copy-start(f32[1,2,16,32,256]{4,3,2,1,0:T(8,128)} %param.4) | copy-start | bytes 3145732
  2.7 15.6 %collective-permute-start = (f32[2,1,32,256]{3,2,1,0:T(8,128)S(1)}, f32[2,1,32,256]{3,2,1,0:T(8,128)S(1)}, u32[]{:S(2)}, u32[]{:S(2)}) collective-permute-start(f32[2,1,32,256]{3,2,1,0:T(8,128)S(1)} %get-tuple-element.108), channel_id=1, source_target_pairs={{0,4},{4,8},{8,12},{12,16},{16,20},{20,24},{24,28},{28,32},{32,36}... | collective-permute-start | bytes 196616 | tf_op jit(solution)/shard_map/ppermute | solution.py:78
  4.9 13.4 %collective-permute-start.1 = (f32[2,1,32,256]{3,2,1,0:T(8,128)S(1)}, f32[2,1,32,256]{3,2,1,0:T(8,128)S(1)}, u32[]{:S(2)}, u32[]{:S(2)}) collective-permute-start(f32[2,1,32,256]{3,2,1,0:T(8,128)S(1)} %get-tuple-element.107), channel_id=1, source_target_pairs={{0,60},{4,0},{8,4},{12,8},{16,12},{20,16},{24,20},{28,24},{32,28},... | collective-permute-start | bytes 196616 | tf_op jit(solution)/shard_map/ppermute | solution.py:78
  13.2 2.9 collective-permute-start.2
  14.9 3.3 collective-permute-start.3
  16.1 2.1 copy-start.39
  23.6 8.5 %collective-permute-start.14 = (f32[8,32,256]{2,1,0:T(8,128)}, f32[8,32,256]{2,1,0:T(8,128)S(1)}, u32[]{:S(2)}, u32[]{:S(2)}) collective-permute-start(f32[8,32,256]{2,1,0:T(8,128)} %get-tuple-element.55), channel_id=1, source_target_pairs={{0,64},{64,0},{128,192},{192,128},{1,65},{65,1},{129,193},{193,129... | collective-permute-start | bytes 786440 | tf_op jit(solution)/shard_map/ppermute | solution.py:372
  24.8 2.6 copy-start.30
  24.8 7.1 %copy-start.29 = (f32[8,32,256]{2,1,0:T(8,128)S(1)}, f32[8,32,256]{2,1,0:T(8,128)}, u32[]{:S(2)}) copy-start(f32[8,32,256]{2,1,0:T(8,128)} %get-tuple-element.48) | copy-start | bytes 786436
  24.8 12.8 %copy-start.1 = (f32[16,32,256]{2,1,0:T(8,128)S(1)}, f32[16,32,256]{2,1,0:T(8,128)}, u32[]{:S(2)}) copy-start(f32[16,32,256]{2,1,0:T(8,128)} %get-tuple-element.47) | copy-start | bytes 1572868
  24.8 12.8 %copy-start.2 = (f32[16,32,256]{2,1,0:T(8,128)S(1)}, f32[16,32,256]{2,1,0:T(8,128)}, u32[]{:S(2)}) copy-start(f32[16,32,256]{2,1,0:T(8,128)} %get-tuple-element.56) | copy-start | bytes 1572868
  24.8 12.8 %copy-start.33 = (f32[8,32,256]{2,1,0:T(8,128)S(1)}, f32[8,32,256]{2,1,0:T(8,128)}, u32[]{:S(2)}) copy-start(f32[8,32,256]{2,1,0:T(8,128)} %get-tuple-element.46) | copy-start | bytes 786436
  24.9 12.8 %copy-start.34 = (f32[8,32,256]{2,1,0:T(8,128)S(1)}, f32[8,32,256]{2,1,0:T(8,128)}, u32[]{:S(2)}) copy-start(f32[8,32,256]{2,1,0:T(8,128)} %get-tuple-element.55) | copy-start | bytes 786436
  24.9 12.8 %collective-permute-start.4 = (f32[8,32,256]{2,1,0:T(8,128)}, f32[8,32,256]{2,1,0:T(8,128)S(1)}, u32[]{:S(2)}, u32[]{:S(2)}) collective-permute-start(f32[8,32,256]{2,1,0:T(8,128)} %get-tuple-element.46), channel_id=1, source_target_pairs={{0,64},{64,0},{128,192},{192,128},{1,65},{65,1},{129,193},{193,129... | collective-permute-start | bytes 786440 | tf_op jit(solution)/shard_map/ppermute | solution.py:372
  25.4 19.6 %collective-permute-start.7 = (f32[2,8,32,256]{3,2,1,0:T(8,128)S(1)}, f32[2,8,32,256]{3,2,1,0:T(8,128)S(1)}, u32[]{:S(2)}, u32[]{:S(2)}) collective-permute-start(f32[2,8,32,256]{3,2,1,0:T(8,128)S(1)} %get-tuple-element.104), channel_id=1, source_target_pairs={{192,0},{193,1},{194,2},{195,3},{196,4},{197,5},{198,6},{199,7},{2... | collective-permute-start | bytes 1572872 | tf_op jit(solution)/shard_map/ppermute | solution.py:357
  27.5 21.7 %collective-permute-start.15 = (f32[8,32,256]{2,1,0:T(8,128)S(1)}, f32[8,32,256]{2,1,0:T(8,128)S(1)}, u32[]{:S(2)}, u32[]{:S(2)}) collective-permute-start(f32[8,32,256]{2,1,0:T(8,128)S(1)} %copy-done.30), channel_id=1, source_target_pairs={{0,192},{192,0},{64,128},{128,64},{1,193},{193,1},{65,129},{129,65... | collective-permute-start | bytes 786440 | tf_op jit(solution)/shard_map/ppermute | solution.py:373
  31.9 22.9 %collective-permute-start.6 = (f32[8,32,256]{2,1,0:T(8,128)S(1)}, f32[8,32,256]{2,1,0:T(8,128)S(1)}, u32[]{:S(2)}, u32[]{:S(2)}) collective-permute-start(f32[8,32,256]{2,1,0:T(8,128)S(1)} %copy-done.29), channel_id=1, source_target_pairs={{0,192},{192,0},{64,128},{128,64},{1,193},{193,1},{65,129},{129,65... | collective-permute-start | bytes 786440 | tf_op jit(solution)/shard_map/ppermute | solution.py:373
  40.3 20.0 %collective-permute-start.16 = (f32[8,32,256]{2,1,0:T(8,128)S(1)}, f32[8,32,256]{2,1,0:T(8,128)S(1)}, u32[]{:S(2)}, u32[]{:S(2)}) collective-permute-start(f32[8,32,256]{2,1,0:T(8,128)S(1)} %get-tuple-element.97), channel_id=1, source_target_pairs={{0,192},{192,0},{64,128},{128,64},{1,193},{193,1},{65,129},{129,65... | collective-permute-start | bytes 786440 | tf_op jit(solution)/shard_map/ppermute | solution.py:374
  57.7 7.3 %collective-permute-start.17 = (f32[8,32,256]{2,1,0:T(8,128)S(1)}, f32[8,32,256]{2,1,0:T(8,128)S(1)}, u32[]{:S(2)}, u32[]{:S(2)}) collective-permute-start(f32[8,32,256]{2,1,0:T(8,128)S(1)} %get-tuple-element.95), channel_id=1, source_target_pairs={{0,64},{64,0},{128,192},{192,128},{1,65},{65,1},{129,193},{193,129... | collective-permute-start | bytes 786440 | tf_op jit(solution)/shard_map/ppermute | solution.py:375
  57.8 44.2 %collective-permute-start.8 = (f32[8,32,256]{2,1,0:T(8,128)S(1)}, f32[8,32,256]{2,1,0:T(8,128)S(1)}, u32[]{:S(2)}, u32[]{:S(2)}) collective-permute-start(f32[8,32,256]{2,1,0:T(8,128)S(1)} %get-tuple-element.116), channel_id=1, source_target_pairs={{0,192},{192,0},{64,128},{128,64},{1,193},{193,1},{65,129},{129,65... | collective-permute-start | bytes 786440 | tf_op jit(solution)/shard_map/ppermute | solution.py:374
  57.9 44.1 %collective-permute-start.9 = (f32[8,32,256]{2,1,0:T(8,128)S(1)}, f32[8,32,256]{2,1,0:T(8,128)S(1)}, u32[]{:S(2)}, u32[]{:S(2)}) collective-permute-start(f32[8,32,256]{2,1,0:T(8,128)S(1)} %get-tuple-element.114), channel_id=1, source_target_pairs={{0,64},{64,0},{128,192},{192,128},{1,65},{65,1},{129,193},{193,129... | collective-permute-start | bytes 786440 | tf_op jit(solution)/shard_map/ppermute | solution.py:375
  60.4 4.6 %copy-start.21 = (f32[8,32,256]{2,1,0:T(8,128)}, f32[8,32,256]{2,1,0:T(8,128)S(1)}, u32[]{:S(2)}) copy-start(f32[8,32,256]{2,1,0:T(8,128)S(1)} %collective-permute-done.16.refs_3_) | copy-start | bytes 786436
  98.8 38.9 %collective-permute-start.18 = (f32[60,8,256]{2,1,0:T(8,128)}, f32[60,8,256]{2,1,0:T(8,128)S(1)}, u32[]{:S(2)}, u32[]{:S(2)}) collective-permute-start(f32[60,8,256]{2,1,0:T(8,128)} %get-tuple-element.59), channel_id=1, source_target_pairs={{0,1},{1,2},{2,3},{3,0},{4,5},{5,6},{6,7},{7,4},{8,9},{9,10},{10,1... | collective-permute-start | bytes 1474568 | tf_op jit(solution)/shard_map/ppermute | solution.py:78
  102.0 35.6 %collective-permute-start.19 = (f32[60,8,256]{2,1,0:T(8,128)}, f32[60,8,256]{2,1,0:T(8,128)S(1)}, u32[]{:S(2)}, u32[]{:S(2)}) collective-permute-start(f32[60,8,256]{2,1,0:T(8,128)} %get-tuple-element.60), channel_id=1, source_target_pairs={{0,3},{1,0},{2,1},{3,2},{4,7},{5,4},{6,5},{7,6},{8,11},{9,8},{10,9... | collective-permute-start | bytes 1474568 | tf_op jit(solution)/shard_map/ppermute | solution.py:78
  135.9 11.8 %collective-permute-start.10 = (f32[60,8,256]{2,1,0:T(8,128)}, f32[60,8,256]{2,1,0:T(8,128)S(1)}, u32[]{:S(2)}, u32[]{:S(2)}) collective-permute-start(f32[60,8,256]{2,1,0:T(8,128)} %get-tuple-element.50), channel_id=1, source_target_pairs={{0,1},{1,2},{2,3},{3,0},{4,5},{5,6},{6,7},{7,4},{8,9},{9,10},{10,1... | collective-permute-start | bytes 1474568 | tf_op jit(solution)/shard_map/ppermute | solution.py:78
  137.6 15.0 %collective-permute-start.11 = (f32[60,8,256]{2,1,0:T(8,128)}, f32[60,8,256]{2,1,0:T(8,128)S(1)}, u32[]{:S(2)}, u32[]{:S(2)}) collective-permute-start(f32[60,8,256]{2,1,0:T(8,128)} %get-tuple-element.51), channel_id=1, source_target_pairs={{0,3},{1,0},{2,1},{3,2},{4,7},{5,4},{6,5},{7,6},{8,11},{9,8},{10,9... | collective-permute-start | bytes 1474568 | tf_op jit(solution)/shard_map/ppermute | solution.py:78
  141.3 26.0 %collective-permute-start.20 = (f32[12,32,256]{2,1,0:T(8,128)}, f32[12,32,256]{2,1,0:T(8,128)S(1)}, u32[]{:S(2)}, u32[]{:S(2)}) collective-permute-start(f32[12,32,256]{2,1,0:T(8,128)} %get-tuple-element.62), channel_id=1, source_target_pairs={{0,4},{4,8},{8,12},{12,16},{16,20},{20,24},{24,28},{28,32},{32,36}... | collective-permute-start | bytes 1179656 | tf_op jit(solution)/shard_map/ppermute | solution.py:78
  141.3 26.0 %collective-permute-start.21 = (f32[12,32,256]{2,1,0:T(8,128)}, f32[12,32,256]{2,1,0:T(8,128)S(1)}, u32[]{:S(2)}, u32[]{:S(2)}) collective-permute-start(f32[12,32,256]{2,1,0:T(8,128)} %get-tuple-element.63), channel_id=1, source_target_pairs={{0,60},{4,0},{8,4},{12,8},{16,12},{20,16},{24,20},{28,24},{32,28},... | collective-permute-start | bytes 1179656 | tf_op jit(solution)/shard_map/ppermute | solution.py:78
  147.7 4.9 %copy-start.7 = (f32[60,8,256]{2,1,0:T(8,128)}, f32[60,8,256]{2,1,0:T(8,128)S(1)}, u32[]{:S(2)}) copy-start(f32[60,8,256]{2,1,0:T(8,128)S(1)} %collective-permute-done.10.low) | copy-start | bytes 1474564
  156.1 23.5 %collective-permute-start.12 = (f32[12,32,256]{2,1,0:T(8,128)}, f32[12,32,256]{2,1,0:T(8,128)S(1)}, u32[]{:S(2)}, u32[]{:S(2)}) collective-permute-start(f32[12,32,256]{2,1,0:T(8,128)} %get-tuple-element.53), channel_id=1, source_target_pairs={{0,4},{4,8},{8,12},{12,16},{16,20},{20,24},{24,28},{28,32},{32,36}... | collective-permute-start | bytes 1179656 | tf_op jit(solution)/shard_map/ppermute | solution.py:78
  156.1 27.9 %collective-permute-start.13 = (f32[12,32,256]{2,1,0:T(8,128)}, f32[12,32,256]{2,1,0:T(8,128)S(1)}, u32[]{:S(2)}, u32[]{:S(2)}) collective-permute-start(f32[12,32,256]{2,1,0:T(8,128)} %get-tuple-element.54), channel_id=1, source_target_pairs={{0,60},{4,0},{8,4},{12,8},{16,12},{20,16},{24,20},{28,24},{32,28},... | collective-permute-start | bytes 1179656 | tf_op jit(solution)/shard_map/ppermute | solution.py:78
  167.3 16.7 %copy-start.13 = (f32[12,32,256]{2,1,0:T(8,128)}, f32[12,32,256]{2,1,0:T(8,128)S(1)}, u32[]{:S(2)}) copy-start(f32[12,32,256]{2,1,0:T(8,128)S(1)} %collective-permute-done.20.lv) | copy-start | bytes 1179652
  167.3 16.7 %copy-start.14 = (f32[12,32,256]{2,1,0:T(8,128)}, f32[12,32,256]{2,1,0:T(8,128)S(1)}, u32[]{:S(2)}) copy-start(f32[12,32,256]{2,1,0:T(8,128)S(1)} %collective-permute-done.21.hv) | copy-start | bytes 1179652
  179.6 4.5 %copy-start.17 = (f32[12,32,256]{2,1,0:T(8,128)}, f32[12,32,256]{2,1,0:T(8,128)S(1)}, u32[]{:S(2)}) copy-start(f32[12,32,256]{2,1,0:T(8,128)S(1)} %collective-permute-done.12.lu) | copy-start | bytes 1179652
  187.6 11.4 %collective-permute-start.22 = (f32[2,1,32,256]{3,2,1,0:T(8,128)}, f32[2,1,32,256]{3,2,1,0:T(8,128)S(1)}, u32[]{:S(2)}, u32[]{:S(2)}) collective-permute-start(f32[2,1,32,256]{3,2,1,0:T(8,128)} %get-tuple-element.65), channel_id=1, source_target_pairs={{0,4},{4,8},{8,12},{12,16},{16,20},{20,24},{24,28},{28,32},{32,36}... | collective-permute-start | bytes 196616 | tf_op jit(solution)/shard_map/ppermute | solution.py:78
  187.6 11.4 %collective-permute-start.23 = (f32[2,1,32,256]{3,2,1,0:T(8,128)}, f32[2,1,32,256]{3,2,1,0:T(8,128)S(1)}, u32[]{:S(2)}, u32[]{:S(2)}) collective-permute-start(f32[2,1,32,256]{3,2,1,0:T(8,128)} %get-tuple-element.66), channel_id=1, source_target_pairs={{0,60},{4,0},{8,4},{12,8},{16,12},{20,16},{24,20},{28,24},{32,28},... | collective-permute-start | bytes 196616 | tf_op jit(solution)/shard_map/ppermute | solution.py:78
  194.2 2.7 collective-permute-start.24
  195.5 3.6 collective-permute-start.25
  196.8 2.2 copy-start.41
  204.4 7.8 %collective-permute-start.26 = (f32[8,32,256]{2,1,0:T(8,128)}, f32[8,32,256]{2,1,0:T(8,128)S(1)}, u32[]{:S(2)}, u32[]{:S(2)}) collective-permute-start(f32[8,32,256]{2,1,0:T(8,128)} %get-tuple-element.69), channel_id=1, source_target_pairs={{0,64},{64,0},{128,192},{192,128},{1,65},{65,1},{129,193},{193,129... | collective-permute-start | bytes 786440 | tf_op jit(solution)/shard_map/ppermute | solution.py:372
  204.4 13.4 %collective-permute-start.34 = (f32[8,32,256]{2,1,0:T(8,128)}, f32[8,32,256]{2,1,0:T(8,128)S(1)}, u32[]{:S(2)}, u32[]{:S(2)}) collective-permute-start(f32[8,32,256]{2,1,0:T(8,128)} %get-tuple-element.78), channel_id=1, source_target_pairs={{0,64},{64,0},{128,192},{192,128},{1,65},{65,1},{129,193},{193,129... | collective-permute-start | bytes 786440 | tf_op jit(solution)/shard_map/ppermute | solution.py:372
  205.8 16.8 %collective-permute-start.27 = (f32[8,32,256]{2,1,0:T(8,128)}, f32[8,32,256]{2,1,0:T(8,128)S(1)}, u32[]{:S(2)}, u32[]{:S(2)}) collective-permute-start(f32[8,32,256]{2,1,0:T(8,128)} %get-tuple-element.71), channel_id=1, source_target_pairs={{0,192},{192,0},{64,128},{128,64},{1,193},{193,1},{65,129},{129,65... | collective-permute-start | bytes 786440 | tf_op jit(solution)/shard_map/ppermute | solution.py:373
  206.3 16.3 %collective-permute-start.35 = (f32[8,32,256]{2,1,0:T(8,128)}, f32[8,32,256]{2,1,0:T(8,128)S(1)}, u32[]{:S(2)}, u32[]{:S(2)}) collective-permute-start(f32[8,32,256]{2,1,0:T(8,128)} %get-tuple-element.80), channel_id=1, source_target_pairs={{0,192},{192,0},{64,128},{128,64},{1,193},{193,1},{65,129},{129,65... | collective-permute-start | bytes 786440 | tf_op jit(solution)/shard_map/ppermute | solution.py:373
  217.8 4.9 %copy-start.3 = (f32[16,32,256]{2,1,0:T(8,128)S(1)}, f32[16,32,256]{2,1,0:T(8,128)}, u32[]{:S(2)}) copy-start(f32[16,32,256]{2,1,0:T(8,128)} %get-tuple-element.70) | copy-start | bytes 1572868
  217.8 4.9 %copy-start.4 = (f32[16,32,256]{2,1,0:T(8,128)S(1)}, f32[16,32,256]{2,1,0:T(8,128)}, u32[]{:S(2)}) copy-start(f32[16,32,256]{2,1,0:T(8,128)} %get-tuple-element.79) | copy-start | bytes 1572868
  217.8 4.9 %copy-start.31 = (f32[8,32,256]{2,1,0:T(8,128)S(1)}, f32[8,32,256]{2,1,0:T(8,128)}, u32[]{:S(2)}) copy-start(f32[8,32,256]{2,1,0:T(8,128)} %get-tuple-element.71) | copy-start | bytes 786436
  217.8 4.9 %copy-start.32 = (f32[8,32,256]{2,1,0:T(8,128)S(1)}, f32[8,32,256]{2,1,0:T(8,128)}, u32[]{:S(2)}) copy-start(f32[8,32,256]{2,1,0:T(8,128)} %get-tuple-element.80) | copy-start | bytes 786436
  221.7 8.4 %collective-permute-start.36 = (f32[8,32,256]{2,1,0:T(8,128)S(1)}, f32[8,32,256]{2,1,0:T(8,128)S(1)}, u32[]{:S(2)}, u32[]{:S(2)}) collective-permute-start(f32[8,32,256]{2,1,0:T(8,128)S(1)} %get-tuple-element.89), channel_id=1, source_target_pairs={{0,192},{192,0},{64,128},{128,64},{1,193},{193,1},{65,129},{129,65... | collective-permute-start | bytes 786440 | tf_op jit(solution)/shard_map/ppermute | solution.py:374
  225.6 7.0 %collective-permute-start.37 = (f32[8,32,256]{2,1,0:T(8,128)S(1)}, f32[8,32,256]{2,1,0:T(8,128)S(1)}, u32[]{:S(2)}, u32[]{:S(2)}) collective-permute-start(f32[8,32,256]{2,1,0:T(8,128)S(1)} %get-tuple-element.87), channel_id=1, source_target_pairs={{0,64},{64,0},{128,192},{192,128},{1,65},{65,1},{129,193},{193,129... | collective-permute-start | bytes 786440 | tf_op jit(solution)/shard_map/ppermute | solution.py:375
  225.8 43.8 %collective-permute-start.28 = (f32[8,32,256]{2,1,0:T(8,128)S(1)}, f32[8,32,256]{2,1,0:T(8,128)S(1)}, u32[]{:S(2)}, u32[]{:S(2)}) collective-permute-start(f32[8,32,256]{2,1,0:T(8,128)S(1)} %get-tuple-element.112), channel_id=1, source_target_pairs={{0,192},{192,0},{64,128},{128,64},{1,193},{193,1},{65,129},{129,65... | collective-permute-start | bytes 786440 | tf_op jit(solution)/shard_map/ppermute | solution.py:374
  227.9 41.7 %collective-permute-start.29 = (f32[8,32,256]{2,1,0:T(8,128)S(1)}, f32[8,32,256]{2,1,0:T(8,128)S(1)}, u32[]{:S(2)}, u32[]{:S(2)}) collective-permute-start(f32[8,32,256]{2,1,0:T(8,128)S(1)} %get-tuple-element.110), channel_id=1, source_target_pairs={{0,64},{64,0},{128,192},{192,128},{1,65},{65,1},{129,193},{193,129... | collective-permute-start | bytes 786440 | tf_op jit(solution)/shard_map/ppermute | solution.py:375
  230.1 2.5 copy-start.22
  266.3 39.5 %collective-permute-start.38 = (f32[60,8,256]{2,1,0:T(8,128)}, f32[60,8,256]{2,1,0:T(8,128)S(1)}, u32[]{:S(2)}, u32[]{:S(2)}) collective-permute-start(f32[60,8,256]{2,1,0:T(8,128)} %get-tuple-element.82), channel_id=1, source_target_pairs={{0,1},{1,2},{2,3},{3,0},{4,5},{5,6},{6,7},{7,4},{8,9},{9,10},{10,1... | collective-permute-start | bytes 1474568 | tf_op jit(solution)/shard_map/ppermute | solution.py:78
  269.2 36.7 %collective-permute-start.39 = (f32[60,8,256]{2,1,0:T(8,128)}, f32[60,8,256]{2,1,0:T(8,128)S(1)}, u32[]{:S(2)}, u32[]{:S(2)}) collective-permute-start(f32[60,8,256]{2,1,0:T(8,128)} %get-tuple-element.83), channel_id=1, source_target_pairs={{0,3},{1,0},{2,1},{3,2},{4,7},{5,4},{6,5},{7,6},{8,11},{9,8},{10,9... | collective-permute-start | bytes 1474568 | tf_op jit(solution)/shard_map/ppermute | solution.py:78
  304.1 11.1 %collective-permute-start.30 = (f32[60,8,256]{2,1,0:T(8,128)}, f32[60,8,256]{2,1,0:T(8,128)S(1)}, u32[]{:S(2)}, u32[]{:S(2)}) collective-permute-start(f32[60,8,256]{2,1,0:T(8,128)} %get-tuple-element.73), channel_id=1, source_target_pairs={{0,1},{1,2},{2,3},{3,0},{4,5},{5,6},{6,7},{7,4},{8,9},{9,10},{10,1... | collective-permute-start | bytes 1474568 | tf_op jit(solution)/shard_map/ppermute | solution.py:78
  305.5 24.1 %collective-permute-start.31 = (f32[60,8,256]{2,1,0:T(8,128)}, f32[60,8,256]{2,1,0:T(8,128)S(1)}, u32[]{:S(2)}, u32[]{:S(2)}) collective-permute-start(f32[60,8,256]{2,1,0:T(8,128)} %get-tuple-element.74), channel_id=1, source_target_pairs={{0,3},{1,0},{2,1},{3,2},{4,7},{5,4},{6,5},{7,6},{8,11},{9,8},{10,9... | collective-permute-start | bytes 1474568 | tf_op jit(solution)/shard_map/ppermute | solution.py:78
  309.5 29.3 %collective-permute-start.40 = (f32[12,32,256]{2,1,0:T(8,128)}, f32[12,32,256]{2,1,0:T(8,128)S(1)}, u32[]{:S(2)}, u32[]{:S(2)}) collective-permute-start(f32[12,32,256]{2,1,0:T(8,128)} %get-tuple-element.85), channel_id=1, source_target_pairs={{0,4},{4,8},{8,12},{12,16},{16,20},{20,24},{24,28},{28,32},{32,36}... | collective-permute-start | bytes 1179656 | tf_op jit(solution)/shard_map/ppermute | solution.py:78
  309.5 29.3 %collective-permute-start.41 = (f32[12,32,256]{2,1,0:T(8,128)}, f32[12,32,256]{2,1,0:T(8,128)S(1)}, u32[]{:S(2)}, u32[]{:S(2)}) collective-permute-start(f32[12,32,256]{2,1,0:T(8,128)} %get-tuple-element.86), channel_id=1, source_target_pairs={{0,60},{4,0},{8,4},{12,8},{16,12},{20,16},{24,20},{28,24},{32,28},... | collective-permute-start | bytes 1179656 | tf_op jit(solution)/shard_map/ppermute | solution.py:78
  315.2 14.4 %copy-start.8 = (f32[60,8,256]{2,1,0:T(8,128)}, f32[60,8,256]{2,1,0:T(8,128)S(1)}, u32[]{:S(2)}) copy-start(f32[60,8,256]{2,1,0:T(8,128)S(1)} %collective-permute-done.30.low) | copy-start | bytes 1474564
  333.1 21.7 %collective-permute-start.32 = (f32[12,32,256]{2,1,0:T(8,128)}, f32[12,32,256]{2,1,0:T(8,128)S(1)}, u32[]{:S(2)}, u32[]{:S(2)}) collective-permute-start(f32[12,32,256]{2,1,0:T(8,128)} %get-tuple-element.76), channel_id=1, source_target_pairs={{0,4},{4,8},{8,12},{12,16},{16,20},{20,24},{24,28},{28,32},{32,36}... | collective-permute-start | bytes 1179656 | tf_op jit(solution)/shard_map/ppermute | solution.py:78
  333.1 22.4 %collective-permute-start.33 = (f32[12,32,256]{2,1,0:T(8,128)}, f32[12,32,256]{2,1,0:T(8,128)S(1)}, u32[]{:S(2)}, u32[]{:S(2)}) collective-permute-start(f32[12,32,256]{2,1,0:T(8,128)} %get-tuple-element.77), channel_id=1, source_target_pairs={{0,60},{4,0},{8,4},{12,8},{16,12},{20,16},{24,20},{28,24},{32,28},... | collective-permute-start | bytes 1179656 | tf_op jit(solution)/shard_map/ppermute | solution.py:78
  338.8 16.8 %copy-start.15 = (f32[12,32,256]{2,1,0:T(8,128)}, f32[12,32,256]{2,1,0:T(8,128)S(1)}, u32[]{:S(2)}) copy-start(f32[12,32,256]{2,1,0:T(8,128)S(1)} %collective-permute-done.40.lv) | copy-start | bytes 1179652
  338.8 16.8 %copy-start.16 = (f32[12,32,256]{2,1,0:T(8,128)}, f32[12,32,256]{2,1,0:T(8,128)S(1)}, u32[]{:S(2)}) copy-start(f32[12,32,256]{2,1,0:T(8,128)S(1)} %collective-permute-done.41.hv) | copy-start | bytes 1179652
  (21 other events, 15.3 us)

commit v2 on v1

--- a/solution.py
+++ b/solution.py
@@ -1,5 +1,6 @@
 import jax
 import jax.numpy as jnp
+import numpy as np
 from jax import lax
 from jax.experimental import pallas as pl
 from jax.experimental.pallas import tpu as pltpu
@@ -68,6 +69,19 @@
             row += [-c, c / (1.0 + 6.0 * c), 1.0 / (1.0 + 6.0 * c), d]
         rows.append(row)
     return rows
+
+
+def fourier():
+    place = np.arange(ZB)[:, None]
+    wave = np.arange(ZB)
+    sine = wave > ZB // 2
+    wave = np.where(sine, wave - ZB // 2, wave)
+    angle = 2.0 * np.pi * ((place * wave) % ZB) / ZB
+    basis = np.where(sine, np.sin(angle), np.cos(angle)) * np.sqrt(2.0 / ZB)
+    basis[:, 0] = np.sqrt(1.0 / ZB)
+    basis[:, ZB // 2] = np.cos(angle[:, ZB // 2]) * np.sqrt(1.0 / ZB)
+    sums = np.broadcast_to(2.0 * np.cos(2.0 * np.pi * wave / ZB), (8, ZB))
+    return basis.astype(np.float32), sums.astype(np.float32)
 
 
 def ring(count, step):
@@ -158,7 +172,7 @@
     )(sc, x, xlo, xhi, ylo, yhi, feed, kill)
 
 
-def jacobi_kernel(species, sc, x, own, ra, rb, core, yhi, ylo, one, two, bs):
+def jacobi_kernel(species, sc, basis, sums, x, own, ra, rb, core, yhi, ylo, one, two, bs):
     spread = sc[8 + 4 * species + 1]
     scale = sc[8 + 4 * species + 2]
     zero = jnp.zeros((ROWS, LANES), jnp.float32)
@@ -167,50 +181,67 @@
         for h in range(2):
             one[p, h] = zero
             two[p, h] = zero
+            bs[p, h] = zero[:YB]
         return carry
 
     lax.fori_loop(0, PLANES, clear, 0)
 
+    def modes(values):
+        flat = values.reshape(-1, ZB)
+        done = jnp.dot(flat, basis[...], precision=lax.Precision.HIGHEST,
+                       preferred_element_type=jnp.float32)
+        return done.reshape(values.shape)
+
     def fill(half, recv):
-        def plane(i, carry):
-            p = half * HALF + i
+        def planes(i, carry):
+            p = half * HALF + i * 4
+            xh = modes(x[0, pl.ds(p, 4)])
+            bh = modes(own[pl.ds(p, 4)] + recv[pl.ds(i * 4, 4)])
             for h in range(2):
                 lanes = slice(h * LANES, (h + 1) * LANES)
-                one[FIRST + p, h, ROW0:ROW0 + YB, :] = x[0, p, :, lanes]
-                bs[p, h] = scale * (own[p, :, lanes] + recv[i, :, lanes])
+                for j in range(4):
+                    one[FIRST + p + j, h, ROW0:ROW0 + YB, :] = xh[j, :, lanes]
+                    bs[FIRST + p + j, h] = scale * bh[j, :, lanes]
             return carry
 
-        lax.fori_loop(0, HALF, plane, 0)
+        lax.fori_loop(0, HALF // 4, planes, 0)
 
     fill(0, ra)
     fill(1, rb)
-    lane = lax.broadcasted_iota(jnp.int32, (8, LANES), 1)
-
-    def plane_of(src, dst, p, tiles, inside):
-        for t in range(-tiles, YB // 8 + tiles):
+    turned = [spread * sums[:, h * LANES:(h + 1) * LANES] for h in range(2)]
+
+    def one_plane(src, dst, p, group, carry):
+        count = 2 * len(group)
+        before, here = carry[:count], carry[count:]
+        after = []
+        for t in group:
             r = ROW0 + 8 * t
-            c = [src[p, h, r:r + 8, :] for h in range(2)]
-            z = z_sum(c[0], c[1], lane)
+            after += [src[p + 1, h, r:r + 8, :] for h in range(2)]
+        for j, t in enumerate(group):
+            r = ROW0 + 8 * t
             for h in range(2):
-                total = src[p - 1, h, r:r + 8, :] + src[p + 1, h, r:r + 8, :]
+                i = 2 * j + h
+                total = before[i] + after[i]
                 total = total + (src[p, h, r - 1:r + 7, :] + src[p, h, r + 1:r + 9, :])
-                new = spread * (total + z[h])
-                if inside and 0 <= t < YB // 8:
-                    new = new + bs[p - FIRST, h, 8 * t:8 * t + 8, :]
+                new = spread * total + turned[h] * here[i]
+                if 0 <= t < YB // 8:
+                    new = new + bs[p, h, 8 * t:8 * t + 8, :]
                 dst[p, h, r:r + 8, :] = new
+        return (*here, *after)
 
     def turn(src, dst, k, tiles):
-        def outside(i, carry):
-            plane_of(src, dst, FIRST - 1 - i, tiles, False)
-            plane_of(src, dst, FIRST + XB + i, tiles, False)
-            return carry
-
-        def inside(i, carry):
-            plane_of(src, dst, FIRST + i, tiles, True)
-            return carry
-
-        lax.fori_loop(0, k, outside, 0)
-        lax.fori_loop(0, XB, inside, 0)
+        wide = (k + 1) // 2
+        first = FIRST - 2 * wide
+        span = list(range(-tiles, YB // 8 + tiles))
+        for group in (span[:len(span) // 2], span[len(span) // 2:]):
+
+            def step(i, carry, group=group):
+                for j in range(4):
+                    carry = one_plane(src, dst, first + 4 * i + j, group, carry)
+                return carry
+
+            carry = (jnp.zeros((8, LANES), jnp.float32),) * (4 * len(group))
+            lax.fori_loop(0, XB // 4 + wide, step, carry)
 
     def pair(tiles):
         def run(i, carry):
@@ -249,7 +280,7 @@
     lax.fori_loop(0, NFAR, far, 0)
 
 
-def jacobi(species, sc, x, own, ra, rb):
+def jacobi(species, sc, basis, sums, x, own, ra, rb):
     vmem = pl.BlockSpec(memory_space=pltpu.VMEM)
     strip = jax.ShapeDtypeStruct((STRIP, 8, ZB), jnp.float32)
     return pl.pallas_call(
@@ -258,6 +289,7 @@
         out_shape=(jax.ShapeDtypeStruct((XB + 2 * JACOBI, YB, ZB), jnp.float32), strip, strip),
         in_specs=[
             pl.BlockSpec(memory_space=pltpu.SMEM),
+            vmem, vmem,
             pl.BlockSpec((1, XB, YB, ZB), lambda i: (species, 0, 0, 0)),
             vmem, vmem, vmem,
         ],
@@ -265,11 +297,11 @@
         scratch_shapes=[
             pltpu.VMEM((PLANES, 2, ROWS, LANES), jnp.float32),
             pltpu.VMEM((PLANES, 2, ROWS, LANES), jnp.float32),
-            pltpu.VMEM((XB, 2, YB, LANES), jnp.float32),
+            pltpu.VMEM((PLANES, 2, YB, LANES), jnp.float32),
         ],
         cost_estimate=pl.CostEstimate(flops=60_000_000, bytes_accessed=5_000_000, transcendentals=0),
         name="jacobi",
-    )(sc, x, own, ra, rb)
+    )(sc, basis, sums, x, own, ra, rb)
 
 
 def gather_kernel(core, low, high, xlo, xhi, center):
@@ -309,27 +341,36 @@
     )(core, low, high)
 
 
-def final_kernel(cu, lu, hu, cv, lv, hv, out, *edges):
+def final_kernel(basis, cu, lu, hu, cv, lv, hv, out, *edges):
     gap = XB - JACOBI
     for s, (c, low, high) in enumerate(((cu, lu, hu), (cv, lv, hv))):
-        for p in range(XB):
-            value = c[p]
-            if p < JACOBI:
-                value = value + low[p]
-            if p >= gap:
-                value = value + high[p - gap]
-            out[s, p] = value
-            if edges:
-                xfirst, xlast, yfirst, ylast = edges
-                if p == 0:
-                    xfirst[s, 0] = value
-                if p == XB - 1:
-                    xlast[s, 0] = value
-                yfirst[s, p:p + 1, :] = value[0:1, :]
-                ylast[s, p:p + 1, :] = value[YB - 1:YB, :]
-
-
-def final(cu, lu, hu, cv, lv, hv, edges):
+        for q in range(0, XB, 4):
+            parts = []
+            for p in range(q, q + 4):
+                value = c[p]
+                if p < JACOBI:
+                    value = value + low[p]
+                if p >= gap:
+                    value = value + high[p - gap]
+                parts.append(value)
+            flat = jnp.concatenate(parts, 0)
+            done = lax.dot_general(flat, basis[...], (((1,), (1,)), ((), ())),
+                                   precision=lax.Precision.HIGHEST,
+                                   preferred_element_type=jnp.float32)
+            for p in range(q, q + 4):
+                value = done[(p - q) * YB:(p - q + 1) * YB]
+                out[s, p] = value
+                if edges:
+                    xfirst, xlast, yfirst, ylast = edges
+                    if p == 0:
+                        xfirst[s, 0] = value
+                    if p == XB - 1:
+                        xlast[s, 0] = value
+                    yfirst[s, p:p + 1, :] = value[0:1, :]
+                    ylast[s, p:p + 1, :] = value[YB - 1:YB, :]
+
+
+def final(basis, cu, lu, hu, cv, lv, hv, edges):
     vmem = pl.BlockSpec(memory_space=pltpu.VMEM)
     shapes = [jax.ShapeDtypeStruct((2, XB, YB, ZB), jnp.float32)]
     if edges:
@@ -338,11 +379,11 @@
     return pl.pallas_call(
         final_kernel,
         out_shape=tuple(shapes),
-        in_specs=[vmem] * 6,
+        in_specs=[vmem] * 7,
         out_specs=(vmem,) * len(shapes),
         cost_estimate=pl.CostEstimate(flops=1_000_000, bytes_accessed=4_000_000, transcendentals=0),
         name="final",
-    )(cu, lu, hu, cv, lv, hv)
+    )(basis, cu, lu, hu, cv, lv, hv)
 
 
 PAIR_A = [(0, 1), (1, 0), (2, 3), (3, 2)]
@@ -352,6 +393,7 @@
 def body(previous, feed_rate, kill_rate):
     node = lax.axis_index("node")
     sc = jnp.asarray(node_table(), jnp.float32)[node]
+    basis, sums = map(jnp.asarray, fourier())
     x = previous[0]
     sent_a = lax.ppermute(x[:, :HALF], "node", [(3, 2)])
     sent_b = lax.ppermute(x[:, HALF:], "node", [(3, 0)])
@@ -380,12 +422,12 @@
                 ],
                 0,
             )
-            core, up, down = jacobi(s, sc, x, own, ra, rb)
+            core, up, down = jacobi(s, sc, basis, sums, x, own, ra, rb)
             low = shifted(up, "sy", 1)
             high = shifted(down, "sy", -1)
             left, right, center = gathered(core, low, high)
             cores += [center, shifted(right, "sx", 1), shifted(left, "sx", -1)]
-        x, *edges = final(*cores, sweep + 1 < SWEEPS)
+        x, *edges = final(basis, *cores, sweep + 1 < SWEEPS)
     return x[None]
 
 

time: 361 us -> 292 us (0.81)
  Pallas kernels: 158 us -> 75.9 us
  starting transfers between devices: 74.2 us -> 86.1 us
    pallas_call x4, Pallas kernels: 132 us -> 45.9 us  [jacobi(): pl.pallas_call(lambda *refs: jacobi_kernel(species, *refs), grid=(1,), ou...]
    ppermute x4, starting transfers between devices: 7.23 us -> 16.5 us  [body(): gb = lax.ppermute(fb, 'node', PAIR_B)]
    ppermute x4, waiting for transfers between devices: 14.8 us -> 5.6 us  [body(): ga = lax.ppermute(fa, 'node', PAIR_A)]
    ppermute x4, waiting for transfers between devices: 9.7 us -> 16.2 us  [body(): gb = lax.ppermute(fb, 'node', PAIR_B)]
    pallas_call x2, Pallas kernels: 5.56 us -> 9.82 us  [final(): pl.pallas_call(final_kernel, out_shape=tuple(shapes), in_specs=[vmem] * 7...]
  transfers between devices with their start and end apart: 42 -> 42, of which waited for: 20 -> 21; matrix products, arithmetic and copies ran while one was open for 5% -> 7% of each run, Pallas kernels for 41% -> 21%
where the time goes in v2:
time: 292 us; the launch traced here: 287 us
  waiting for transfers between devices  94.6 us (32%)
  starting transfers between devices  86.1 us (29%)
  Pallas kernels  75.9 us (26%)
  other arithmetic  15.4 us (5%)
  local copies, waits for them, and re-layouts  14.7 us (5%)
    ppermute x24, waiting for transfers between devices, shifted(): return lax.ppermute(array, axis, ring(lax.axis_size(axis), step))  66.5 us
    ppermute x24, starting transfers between devices, shifted(): return lax.ppermute(array, axis, ring(lax.axis_size(axis), step))  55.4 us
    pallas_call x4, Pallas kernels, jacobi(): pl.pallas_call(lambda *refs: jacobi_kernel(species, *refs), grid=(1,), ou...  45.9 us
    ppermute x4, starting transfers between devices, body(): gb = lax.ppermute(fb, 'node', PAIR_B)  16.5 us
    ppermute x4, waiting for transfers between devices, body(): gb = lax.ppermute(fb, 'node', PAIR_B)  16.2 us
    pallas_call x4, Pallas kernels, gathered(): pl.pallas_call(gather_kernel, out_shape=(side, side, jax.ShapeDtypeStruct...  10.8 us
    pallas_call x2, Pallas kernels, final(): pl.pallas_call(final_kernel, out_shape=tuple(shapes), in_specs=[vmem] * 7...  9.82 us
    unnamed x88, local copies, waits for them, and re-layouts  9.8 us
  transfers between devices with their start and end apart: 42, of which 21 were waited for; matrix products, arithmetic and copies ran while one was open for 7% of the time, Pallas kernels for 21%

profile of v2, /device:TPU:1, one launch (start us, length us, event | category | flops | bytes accessed | tf_op | source)
XLA Modules:
  0.0 287.4 jit_solution(9788306060036391706)
XLA Ops:
  0.0 1.1 slice.150
  1.8 0.9 fusion.2
  2.7 2.2 collective-permute-start
  4.9 7.3 %collective-permute-start.1 = (f32[2,1,32,256]{3,2,1,0:T(8,128)S(1)}, f32[2,1,32,256]{3,2,1,0:T(8,128)S(1)}, u32[]{:S(2)}, u32[]{:S(2)}) collective-permute-start(f32[2,1,32,256]{3,2,1,0:T(8,128)S(1)} %get-tuple-element.107), channel_id=1, source_target_pairs={{0,60},{4,0},{8,4},{12,8},{16,12},{20,16},{24,20},{28,24},{32,28},... | collective-permute-start | bytes 196616 | tf_op jit(solution)/shard_map/ppermute | solution.py:92
  12.1 1.1 fusion.1
  13.2 1.7 collective-permute-start.2
  14.9 1.2 constant_dynamic-slice_fusion
  16.1 2.1 collective-permute-done.3.yhi
  18.9 4.7 %forces.2 = (f32[8,32,256]{2,1,0:T(8,128)}, f32[8,32,256]{2,1,0:T(8,128)}, f32[8,32,256]{2,1,0:T(8,128)}, f32[8,32,256]{2,1,0:T(8,128)}, f32[16,32,256]{2,1,0:T(8,128)}, /*index=5*/f32[16,32,256]{2,1,0:T(8,128)}) custom-call(f32[16]{0:T(128)} %get-tuple-element.118.sc.refs_0_, f32[2,16,32,256]{3,2,1,0:T(8,128)} %bitcast.60, f32[2,1,32,256]{3,2,1,0:T(8,128)} %copy-done.35, ...), custom_call_target="tpu_custom_call" | custom-call | flops 8000000 | bytes 6000000 | tf_op jit(solution)/shard_map/forces/pallas_call | solution.py:164
  23.6 1.2 collective-permute-start.14
  25.4 1.4 collective-permute-start.7
  27.5 4.5 %collective-permute-start.15 = (f32[8,32,256]{2,1,0:T(8,128)S(1)}, f32[8,32,256]{2,1,0:T(8,128)S(1)}, u32[]{:S(2)}, u32[]{:S(2)}) collective-permute-start(f32[8,32,256]{2,1,0:T(8,128)S(1)} %copy-done.22), channel_id=1, source_target_pairs={{0,192},{192,0},{64,128},{128,64},{1,193},{193,1},{65,129},{129,65... | collective-permute-start | bytes 786440 | tf_op jit(solution)/shard_map/ppermute | solution.py:415
  32.1 5.5 %collective-permute-done.4 = f32[8,32,256]{2,1,0:T(8,128)S(1)} collective-permute-done((f32[8,32,256]{2,1,0:T(8,128)}, f32[8,32,256]{2,1,0:T(8,128)S(1)}, u32[]{:S(2)}, u32[]{:S(2)}) %collective-permute-start.4) | collective-permute-done | bytes 262176 | tf_op jit(solution)/shard_map/ppermute | solution.py:414
  37.6 2.7 add_add_fusion.5
  40.3 4.6 %collective-permute-start.16 = (f32[8,32,256]{2,1,0:T(8,128)S(1)}, f32[8,32,256]{2,1,0:T(8,128)S(1)}, u32[]{:S(2)}, u32[]{:S(2)}) collective-permute-start(f32[8,32,256]{2,1,0:T(8,128)S(1)} %get-tuple-element.97), channel_id=1, source_target_pairs={{0,192},{192,0},{64,128},{128,64},{1,193},{193,1},{65,129},{129,65... | collective-permute-start | bytes 786440 | tf_op jit(solution)/shard_map/ppermute | solution.py:416
  45.1 4.1 %collective-permute-done.15 = f32[8,32,256]{2,1,0:T(8,128)S(1)} collective-permute-done((f32[8,32,256]{2,1,0:T(8,128)S(1)}, f32[8,32,256]{2,1,0:T(8,128)S(1)}, u32[]{:S(2)}, u32[]{:S(2)}) %collective-permute-start.15) | collective-permute-done | bytes 262176 | tf_op jit(solution)/shard_map/ppermute | solution.py:415
  49.2 5.6 %collective-permute-done.6 = f32[8,32,256]{2,1,0:T(8,128)S(1)} collective-permute-done((f32[8,32,256]{2,1,0:T(8,128)S(1)}, f32[8,32,256]{2,1,0:T(8,128)S(1)}, u32[]{:S(2)}, u32[]{:S(2)}) %collective-permute-start.6) | collective-permute-done | bytes 262176 | tf_op jit(solution)/shard_map/ppermute | solution.py:415
  54.8 2.9 %add_add_fusion.4 = (f32[8,32,256]{2,1,0:T(8,128)S(1)}, f32[8,32,256]{2,1,0:T(8,128)S(1)}, f32[8,32,256]{2,1,0:T(8,128)S(1)}, f32[8,32,256]{2,1,0:T(8,128)S(1)}) fusion(f32[8,32,256]{2,1,0:T(8,128)S(1)} %collective-permute-done.15, f32[8,32,256]{2,1,0:T(8,128)S(1)} %copy-done.22, f32[2,8,32,256]{3,2,1,0:T(8,128)S(1)} %broadcast_select_fusion, f32[]{:T(128)} %bitcast.10, ...), kind=kLoop, calls=%fused_computation.16 | loop fusion | flops 1179648 | bytes 3145744 | tf_op jit(solution)/shard_map/add | solution.py:417
  57.9 1.4 collective-permute-start.9
  59.3 1.0 pad_maximum_fusion
  60.4 4.6 %collective-permute-done.17.refs_6_ = f32[8,32,256]{2,1,0:T(8,128)S(1)} collective-permute-done((f32[8,32,256]{2,1,0:T(8,128)S(1)}, f32[8,32,256]{2,1,0:T(8,128)S(1)}, u32[]{:S(2)}, u32[]{:S(2)}) %collective-permute-start.17) | collective-permute-done | bytes 262176 | tf_op jit(solution)/shard_map/ppermute | solution.py:417
  65.7 11.5 %jacobi.5 = (f32[40,32,256]{2,1,0:T(8,128)}, f32[60,8,256]{2,1,0:T(8,128)}, f32[60,8,256]{2,1,0:T(8,128)}) custom-call(f32[16]{0:T(128)} %get-tuple-element.118.sc.refs_0_, f32[256,256]{1,0:T(8,128)} %constant.19.clone.refs_1_.basis, f32[8,256]{1,0:T(8,128)} %constant.20.clone.refs_2_, f32[2,16,32,256]{3,2,1,0:T(8,128)} %bitcast.61, ...), custom_call_target="tpu_custom_call" | custom-call | flops 60000000 | bytes 5000000 | tf_op jit(solution)/shard_map/jacobi/pallas_call | solution.py:286
  77.2 3.2 %collective-permute-start.18 = (f32[60,8,256]{2,1,0:T(8,128)}, f32[60,8,256]{2,1,0:T(8,128)S(1)}, u32[]{:S(2)}, u32[]{:S(2)}) collective-permute-start(f32[60,8,256]{2,1,0:T(8,128)} %get-tuple-element.59), channel_id=1, source_target_pairs={{0,1},{1,2},{2,3},{3,0},{4,5},{5,6},{6,7},{7,4},{8,9},{9,10},{10,1... | collective-permute-start | bytes 1474568 | tf_op jit(solution)/shard_map/ppermute | solution.py:92
  81.5 11.5 %jacobi.4 = (f32[40,32,256]{2,1,0:T(8,128)}, f32[60,8,256]{2,1,0:T(8,128)}, f32[60,8,256]{2,1,0:T(8,128)}) custom-call(f32[16]{0:T(128)} %get-tuple-element.118.sc.refs_0_, f32[256,256]{1,0:T(8,128)} %constant.19.clone.refs_1_.basis, f32[8,256]{1,0:T(8,128)} %constant.20.clone.refs_2_, f32[2,16,32,256]{3,2,1,0:T(8,128)} %bitcast.62, ...), custom_call_target="tpu_custom_call" | custom-call | flops 60000000 | bytes 5000000 | tf_op jit(solution)/shard_map/jacobi/pallas_call | solution.py:286
  92.9 1.7 collective-permute-start.10
  95.6 2.7 gathered.5
  98.3 5.7 %collective-permute-start.21 = (f32[12,32,256]{2,1,0:T(8,128)}, f32[12,32,256]{2,1,0:T(8,128)S(1)}, u32[]{:S(2)}, u32[]{:S(2)}) collective-permute-start(f32[12,32,256]{2,1,0:T(8,128)} %get-tuple-element.63), channel_id=1, source_target_pairs={{0,60},{4,0},{8,4},{12,8},{16,12},{20,16},{24,20},{28,24},{32,28},... | collective-permute-start | bytes 1179656 | tf_op jit(solution)/shard_map/ppermute | solution.py:92
  104.7 4.9 %collective-permute-done.11.high = f32[60,8,256]{2,1,0:T(8,128)S(1)} collective-permute-done((f32[60,8,256]{2,1,0:T(8,128)}, f32[60,8,256]{2,1,0:T(8,128)S(1)}, u32[]{:S(2)}, u32[]{:S(2)}) %collective-permute-start.11) | collective-permute-done | bytes 491552 | tf_op jit(solution)/shard_map/ppermute | solution.py:92
  109.7 0.8 copy-done.11
  110.4 2.7 gathered.4
  113.2 5.7 %collective-permute-start.13 = (f32[12,32,256]{2,1,0:T(8,128)}, f32[12,32,256]{2,1,0:T(8,128)S(1)}, u32[]{:S(2)}, u32[]{:S(2)}) collective-permute-start(f32[12,32,256]{2,1,0:T(8,128)} %get-tuple-element.54), channel_id=1, source_target_pairs={{0,60},{4,0},{8,4},{12,8},{16,12},{20,16},{24,20},{28,24},{32,28},... | collective-permute-start | bytes 1179656 | tf_op jit(solution)/shard_map/ppermute | solution.py:92
  118.8 5.5 %collective-permute-done.20.lv = f32[12,32,256]{2,1,0:T(8,128)S(1)} collective-permute-done((f32[12,32,256]{2,1,0:T(8,128)}, f32[12,32,256]{2,1,0:T(8,128)S(1)}, u32[]{:S(2)}, u32[]{:S(2)}) %collective-permute-start.20) | collective-permute-done | bytes 393248 | tf_op jit(solution)/shard_map/ppermute | solution.py:92
  124.4 12.2 %collective-permute-done.12.lu = f32[12,32,256]{2,1,0:T(8,128)S(1)} collective-permute-done((f32[12,32,256]{2,1,0:T(8,128)}, f32[12,32,256]{2,1,0:T(8,128)S(1)}, u32[]{:S(2)}, u32[]{:S(2)}) %collective-permute-start.12) | collective-permute-done | bytes 393248 | tf_op jit(solution)/shard_map/ppermute | solution.py:92
  136.6 4.5 %collective-permute-done.13.hu = f32[12,32,256]{2,1,0:T(8,128)S(1)} collective-permute-done((f32[12,32,256]{2,1,0:T(8,128)}, f32[12,32,256]{2,1,0:T(8,128)S(1)}, u32[]{:S(2)}, u32[]{:S(2)}) %collective-permute-start.13) | collective-permute-done | bytes 393248 | tf_op jit(solution)/shard_map/ppermute | solution.py:92
  141.8 4.9 %final.2 = (f32[2,16,32,256]{3,2,1,0:T(8,128)}, f32[2,1,32,256]{3,2,1,0:T(8,128)}, f32[2,1,32,256]{3,2,1,0:T(8,128)}, f32[2,16,256]{2,1,0:T(8,128)}, f32[2,16,256]{2,1,0:T(8,128)}) custom-call(f32[256,256]{1,0:T(8,128)} %constant.19.clone.refs_1_.basis, f32[16,32,256]{2,1,0:T(8,128)} %get-tuple-element.52.cu, f32[12,32,256]{2,1,0:T(8,128)} %copy-done.15, ...), custom_call_target="tpu_custom_call" | custom-call | flops 1000000 | bytes 4000000 | tf_op jit(solution)/shard_map/final/pallas_call | solution.py:379
  146.8 6.5 %collective-permute-start.23 = (f32[2,1,32,256]{3,2,1,0:T(8,128)}, f32[2,1,32,256]{3,2,1,0:T(8,128)S(1)}, u32[]{:S(2)}, u32[]{:S(2)}) collective-permute-start(f32[2,1,32,256]{3,2,1,0:T(8,128)} %get-tuple-element.66), channel_id=1, source_target_pairs={{0,60},{4,0},{8,4},{12,8},{16,12},{20,16},{24,20},{28,24},{32,28},... | collective-permute-start | bytes 196616 | tf_op jit(solution)/shard_map/ppermute | solution.py:92
  153.3 1.3 collective-permute-start.24
  154.8 1.1 collective-permute-done.24.ylo
  156.0 2.2 collective-permute-done.25.yhi
  158.8 4.7 %forces.3 = (f32[8,32,256]{2,1,0:T(8,128)}, f32[8,32,256]{2,1,0:T(8,128)}, f32[8,32,256]{2,1,0:T(8,128)}, f32[8,32,256]{2,1,0:T(8,128)}, f32[16,32,256]{2,1,0:T(8,128)}, /*index=5*/f32[16,32,256]{2,1,0:T(8,128)}) custom-call(f32[16]{0:T(128)} %get-tuple-element.118.sc.refs_0_, f32[2,16,32,256]{3,2,1,0:T(8,128)} %get-tuple-element.64.x.refs_3_, ...), custom_call_target="tpu_custom_call" | custom-call | flops 8000000 | bytes 6000000 | tf_op jit(solution)/shard_map/forces/pallas_call | solution.py:164
  163.5 1.5 collective-permute-start.34
  165.0 9.7 %collective-permute-start.27 = (f32[8,32,256]{2,1,0:T(8,128)}, f32[8,32,256]{2,1,0:T(8,128)S(1)}, u32[]{:S(2)}, u32[]{:S(2)}) collective-permute-start(f32[8,32,256]{2,1,0:T(8,128)} %get-tuple-element.71), channel_id=1, source_target_pairs={{0,192},{192,0},{64,128},{128,64},{1,193},{193,1},{65,129},{129,65... | collective-permute-start | bytes 786440 | tf_op jit(solution)/shard_map/ppermute | solution.py:415
  174.7 2.2 collective-permute-start.35
  177.0 3.9 %add_add_fusion.1 = (f32[8,32,256]{2,1,0:T(8,128)S(1)}, f32[8,32,256]{2,1,0:T(8,128)S(1)}, f32[8,32,256]{2,1,0:T(8,128)S(1)}, f32[8,32,256]{2,1,0:T(8,128)S(1)}) fusion(f32[8,32,256]{2,1,0:T(8,128)S(1)} %collective-permute-done.34, f32[8,32,256]{2,1,0:T(8,128)} %get-tuple-element.78, f32[2,8,32,256]{3,2,1,0:T(8,128)S(1)} %get-tuple-element.103, f32[]{:T(128)} %bitcast.8, ...), kind=kLoop, calls=%fused_computation.9 | loop fusion | flops 1179648 | bytes 3145744 | tf_op jit(solution)/shard_map/add | solution.py:416
  180.9 0.9 collective-permute-start.36
  181.8 0.9 collective-permute-done.27
  182.7 5.6 %collective-permute-done.35 = f32[8,32,256]{2,1,0:T(8,128)S(1)} collective-permute-done((f32[8,32,256]{2,1,0:T(8,128)}, f32[8,32,256]{2,1,0:T(8,128)S(1)}, u32[]{:S(2)}, u32[]{:S(2)}) %collective-permute-start.35) | collective-permute-done | bytes 262176 | tf_op jit(solution)/shard_map/ppermute | solution.py:415
  188.3 2.9 %add_add_fusion = (f32[8,32,256]{2,1,0:T(8,128)S(1)}, f32[8,32,256]{2,1,0:T(8,128)S(1)}, f32[8,32,256]{2,1,0:T(8,128)S(1)}, f32[8,32,256]{2,1,0:T(8,128)S(1)}) fusion(f32[8,32,256]{2,1,0:T(8,128)S(1)} %collective-permute-done.35, f32[8,32,256]{2,1,0:T(8,128)S(1)} %copy-done.24, f32[2,8,32,256]{3,2,1,0:T(8,128)S(1)} %broadcast_select_fusion, f32[]{:T(128)} %bitcast.10, ...), kind=kLoop, calls=%fused_computation.8 | loop fusion | flops 1179648 | bytes 3145744 | tf_op jit(solution)/shard_map/add | solution.py:417
  191.3 1.9 collective-permute-start.28
  193.3 0.8 pad_maximum_fusion.3.refs_4_
  194.1 0.9 pad_maximum_fusion.2.refs_4_
  195.0 1.6 collective-permute-done.37.refs_6_
  197.2 11.4 %jacobi.7 = (f32[40,32,256]{2,1,0:T(8,128)}, f32[60,8,256]{2,1,0:T(8,128)}, f32[60,8,256]{2,1,0:T(8,128)}) custom-call(f32[16]{0:T(128)} %get-tuple-element.118.sc.refs_0_, f32[256,256]{1,0:T(8,128)} %constant.19.clone.refs_1_.basis, f32[8,256]{1,0:T(8,128)} %constant.20.clone.refs_2_, f32[2,16,32,256]{3,2,1,0:T(8,128)} %get-tuple-element.64.x.refs_3_, ...), custom_call_target="tpu_custom_call" | custom-call | flops 60000000 | bytes 5000000 | tf_op jit(solution)/shard_map/jacobi/pallas_call | solution.py:286
  208.7 6.5 %collective-permute-start.38 = (f32[60,8,256]{2,1,0:T(8,128)}, f32[60,8,256]{2,1,0:T(8,128)S(1)}, u32[]{:S(2)}, u32[]{:S(2)}) collective-permute-start(f32[60,8,256]{2,1,0:T(8,128)} %get-tuple-element.82), channel_id=1, source_target_pairs={{0,1},{1,2},{2,3},{3,0},{4,5},{5,6},{6,7},{7,4},{8,9},{9,10},{10,1... | collective-permute-start | bytes 1474568 | tf_op jit(solution)/shard_map/ppermute | solution.py:92
  216.6 11.5 %jacobi.6 = (f32[40,32,256]{2,1,0:T(8,128)}, f32[60,8,256]{2,1,0:T(8,128)}, f32[60,8,256]{2,1,0:T(8,128)}) custom-call(f32[16]{0:T(128)} %get-tuple-element.118.sc.refs_0_, f32[256,256]{1,0:T(8,128)} %constant.19.clone.refs_1_.basis, f32[8,256]{1,0:T(8,128)} %constant.20.clone.refs_2_, f32[2,16,32,256]{3,2,1,0:T(8,128)} %get-tuple-element.64.x.refs_3_, ...), custom_call_target="tpu_custom_call" | custom-call | flops 60000000 | bytes 5000000 | tf_op jit(solution)/shard_map/jacobi/pallas_call | solution.py:286
  228.1 1.7 collective-permute-start.30
  230.8 2.7 gathered.7
  233.5 5.7 %collective-permute-start.41 = (f32[12,32,256]{2,1,0:T(8,128)}, f32[12,32,256]{2,1,0:T(8,128)S(1)}, u32[]{:S(2)}, u32[]{:S(2)}) collective-permute-start(f32[12,32,256]{2,1,0:T(8,128)} %get-tuple-element.86), channel_id=1, source_target_pairs={{0,60},{4,0},{8,4},{12,8},{16,12},{20,16},{24,20},{28,24},{32,28},... | collective-permute-start | bytes 1179656 | tf_op jit(solution)/shard_map/ppermute | solution.py:92
  239.5 15.4 %collective-permute-done.31.high = f32[60,8,256]{2,1,0:T(8,128)S(1)} collective-permute-done((f32[60,8,256]{2,1,0:T(8,128)}, f32[60,8,256]{2,1,0:T(8,128)S(1)}, u32[]{:S(2)}, u32[]{:S(2)}) %collective-permute-start.31) | collective-permute-done | bytes 491552 | tf_op jit(solution)/shard_map/ppermute | solution.py:92
  255.7 2.7 gathered.6
  258.4 5.7 %collective-permute-start.33 = (f32[12,32,256]{2,1,0:T(8,128)}, f32[12,32,256]{2,1,0:T(8,128)S(1)}, u32[]{:S(2)}, u32[]{:S(2)}) collective-permute-start(f32[12,32,256]{2,1,0:T(8,128)} %get-tuple-element.77), channel_id=1, source_target_pairs={{0,60},{4,0},{8,4},{12,8},{16,12},{20,16},{24,20},{28,24},{32,28},... | collective-permute-start | bytes 1179656 | tf_op jit(solution)/shard_map/ppermute | solution.py:92
  264.1 14.3 %collective-permute-done.32.lu = f32[12,32,256]{2,1,0:T(8,128)S(1)} collective-permute-done((f32[12,32,256]{2,1,0:T(8,128)}, f32[12,32,256]{2,1,0:T(8,128)S(1)}, u32[]{:S(2)}, u32[]{:S(2)}) %collective-permute-start.32) | collective-permute-done | bytes 393248 | tf_op jit(solution)/shard_map/ppermute | solution.py:92
  278.4 3.1 %collective-permute-done.33.hu = f32[12,32,256]{2,1,0:T(8,128)S(1)} collective-permute-done((f32[12,32,256]{2,1,0:T(8,128)}, f32[12,32,256]{2,1,0:T(8,128)S(1)}, u32[]{:S(2)}, u32[]{:S(2)}) %collective-permute-start.33) | collective-permute-done | bytes 393248 | tf_op jit(solution)/shard_map/ppermute | solution.py:92
  282.3 4.9 %final.3 = f32[2,16,32,256]{3,2,1,0:T(8,128)} custom-call(f32[256,256]{1,0:T(8,128)} %constant.19.clone.refs_1_.basis, f32[16,32,256]{2,1,0:T(8,128)} %get-tuple-element.75.cu, f32[12,32,256]{2,1,0:T(8,128)} %copy-done.19, f32[12,32,256]{2,1,0:T(8,128)} %copy-done.20, f32[16,32,256]{2,1,0:T(8,128)} %get-tuple-element.84.cv, f32[12,32,256]{2,1,0:T(8,128)} %copy-done.17, ...), custom_call_target="tpu_custom_call" | custom-call | flops 1000000 | bytes 4000000 | tf_op jit(solution)/shard_map/final/pallas_call | solution.py:379
  (134 shorter events, 13.1 us)
Async XLA Ops:
  1.1 24.1 %collective-permute-start.5 = (f32[2,8,32,256]{3,2,1,0:T(8,128)S(1)}, f32[2,8,32,256]{3,2,1,0:T(8,128)S(1)}, u32[]{:S(2)}, u32[]{:S(2)}) collective-permute-start(f32[2,8,32,256]{3,2,1,0:T(8,128)S(1)} %slice.150), channel_id=1, source_target_pairs={{192,128},{193,129},{194,130},{195,131},{196,132},{197,133},{198,1... | collective-permute-start | bytes 1572872 | tf_op jit(solution)/shard_map/ppermute | solution.py:398
  2.7 22.5 %copy-start = (f32[1,2,16,32,256]{4,3,2,1,0:T(8,128)S(1)}, f32[1,2,16,32,256]{4,3,2,1,0:T(8,128)}, u32[]{:S(2)}) copy-start(f32[1,2,16,32,256]{4,3,2,1,0:T(8,128)} %param.6) | copy-start | bytes 3145732
  2.7 15.6 %collective-permute-start = (f32[2,1,32,256]{3,2,1,0:T(8,128)S(1)}, f32[2,1,32,256]{3,2,1,0:T(8,128)S(1)}, u32[]{:S(2)}, u32[]{:S(2)}) collective-permute-start(f32[2,1,32,256]{3,2,1,0:T(8,128)S(1)} %get-tuple-element.108), channel_id=1, source_target_pairs={{0,4},{4,8},{8,12},{12,16},{16,20},{20,24},{24,28},{28,32},{32,36}... | collective-permute-start | bytes 196616 | tf_op jit(solution)/shard_map/ppermute | solution.py:92
  4.9 13.4 %collective-permute-start.1 = (f32[2,1,32,256]{3,2,1,0:T(8,128)S(1)}, f32[2,1,32,256]{3,2,1,0:T(8,128)S(1)}, u32[]{:S(2)}, u32[]{:S(2)}) collective-permute-start(f32[2,1,32,256]{3,2,1,0:T(8,128)S(1)} %get-tuple-element.107), channel_id=1, source_target_pairs={{0,60},{4,0},{8,4},{12,8},{16,12},{20,16},{24,20},{28,24},{32,28},... | collective-permute-start | bytes 196616 | tf_op jit(solution)/shard_map/ppermute | solution.py:92
  13.2 2.9 %collective-permute-start.2 = (f32[2,16,256]{2,1,0:T(8,128)S(1)}, f32[2,16,256]{2,1,0:T(8,128)S(1)}, u32[]{:S(2)}, u32[]{:S(2)}) collective-permute-start(f32[2,16,256]{2,1,0:T(8,128)S(1)} %bitcast.65), channel_id=1, source_target_pairs={{0,1},{1,2},{2,3},{3,0},{4,5},{5,6},{6,7},{7,4},{8,9},{9,10},{10,1... | collective-permute-start | bytes 98312 | tf_op jit(solution)/shard_map/ppermute | solution.py:92
  14.9 3.3 %collective-permute-start.3 = (f32[2,16,256]{2,1,0:T(8,128)S(1)}, f32[2,16,256]{2,1,0:T(8,128)S(1)}, u32[]{:S(2)}, u32[]{:S(2)}) collective-permute-start(f32[2,16,256]{2,1,0:T(8,128)S(1)} %bitcast.66), channel_id=1, source_target_pairs={{0,3},{1,0},{2,1},{3,2},{4,7},{5,4},{6,5},{7,6},{8,11},{9,8},{10,9... | collective-permute-start | bytes 98312 | tf_op jit(solution)/shard_map/ppermute | solution.py:92
  16.1 2.1 copy-start.39
  23.6 8.5 %collective-permute-start.14 = (f32[8,32,256]{2,1,0:T(8,128)}, f32[8,32,256]{2,1,0:T(8,128)S(1)}, u32[]{:S(2)}, u32[]{:S(2)}) collective-permute-start(f32[8,32,256]{2,1,0:T(8,128)} %get-tuple-element.55), channel_id=1, source_target_pairs={{0,64},{64,0},{128,192},{192,128},{1,65},{65,1},{129,193},{193,129... | collective-permute-start | bytes 786440 | tf_op jit(solution)/shard_map/ppermute | solution.py:414
  24.8 2.6 copy-start.22
  24.8 7.1 %copy-start.21 = (f32[8,32,256]{2,1,0:T(8,128)S(1)}, f32[8,32,256]{2,1,0:T(8,128)}, u32[]{:S(2)}) copy-start(f32[8,32,256]{2,1,0:T(8,128)} %get-tuple-element.48) | copy-start | bytes 786436
  24.8 12.8 %copy-start.1 = (f32[16,32,256]{2,1,0:T(8,128)S(1)}, f32[16,32,256]{2,1,0:T(8,128)}, u32[]{:S(2)}) copy-start(f32[16,32,256]{2,1,0:T(8,128)} %get-tuple-element.47) | copy-start | bytes 1572868
  24.8 12.8 %copy-start.2 = (f32[16,32,256]{2,1,0:T(8,128)S(1)}, f32[16,32,256]{2,1,0:T(8,128)}, u32[]{:S(2)}) copy-start(f32[16,32,256]{2,1,0:T(8,128)} %get-tuple-element.56) | copy-start | bytes 1572868
  24.8 12.8 %copy-start.25 = (f32[8,32,256]{2,1,0:T(8,128)S(1)}, f32[8,32,256]{2,1,0:T(8,128)}, u32[]{:S(2)}) copy-start(f32[8,32,256]{2,1,0:T(8,128)} %get-tuple-element.46) | copy-start | bytes 786436
  24.9 12.8 %copy-start.26 = (f32[8,32,256]{2,1,0:T(8,128)S(1)}, f32[8,32,256]{2,1,0:T(8,128)}, u32[]{:S(2)}) copy-start(f32[8,32,256]{2,1,0:T(8,128)} %get-tuple-element.55) | copy-start | bytes 786436
  24.9 12.8 %collective-permute-start.4 = (f32[8,32,256]{2,1,0:T(8,128)}, f32[8,32,256]{2,1,0:T(8,128)S(1)}, u32[]{:S(2)}, u32[]{:S(2)}) collective-permute-start(f32[8,32,256]{2,1,0:T(8,128)} %get-tuple-element.46), channel_id=1, source_target_pairs={{0,64},{64,0},{128,192},{192,128},{1,65},{65,1},{129,193},{193,129... | collective-permute-start | bytes 786440 | tf_op jit(solution)/shard_map/ppermute | solution.py:414
  25.4 19.6 %collective-permute-start.7 = (f32[2,8,32,256]{3,2,1,0:T(8,128)S(1)}, f32[2,8,32,256]{3,2,1,0:T(8,128)S(1)}, u32[]{:S(2)}, u32[]{:S(2)}) collective-permute-start(f32[2,8,32,256]{3,2,1,0:T(8,128)S(1)} %get-tuple-element.104), channel_id=1, source_target_pairs={{192,0},{193,1},{194,2},{195,3},{196,4},{197,5},{198,6},{199,7},{2... | collective-permute-start | bytes 1572872 | tf_op jit(solution)/shard_map/ppermute | solution.py:399
  27.5 21.7 %collective-permute-start.15 = (f32[8,32,256]{2,1,0:T(8,128)S(1)}, f32[8,32,256]{2,1,0:T(8,128)S(1)}, u32[]{:S(2)}, u32[]{:S(2)}) collective-permute-start(f32[8,32,256]{2,1,0:T(8,128)S(1)} %copy-done.22), channel_id=1, source_target_pairs={{0,192},{192,0},{64,128},{128,64},{1,193},{193,1},{65,129},{129,65... | collective-permute-start | bytes 786440 | tf_op jit(solution)/shard_map/ppermute | solution.py:415
  31.9 22.9 %collective-permute-start.6 = (f32[8,32,256]{2,1,0:T(8,128)S(1)}, f32[8,32,256]{2,1,0:T(8,128)S(1)}, u32[]{:S(2)}, u32[]{:S(2)}) collective-permute-start(f32[8,32,256]{2,1,0:T(8,128)S(1)} %copy-done.21), channel_id=1, source_target_pairs={{0,192},{192,0},{64,128},{128,64},{1,193},{193,1},{65,129},{129,65... | collective-permute-start | bytes 786440 | tf_op jit(solution)/shard_map/ppermute | solution.py:415
  40.3 20.0 %collective-permute-start.16 = (f32[8,32,256]{2,1,0:T(8,128)S(1)}, f32[8,32,256]{2,1,0:T(8,128)S(1)}, u32[]{:S(2)}, u32[]{:S(2)}) collective-permute-start(f32[8,32,256]{2,1,0:T(8,128)S(1)} %get-tuple-element.97), channel_id=1, source_target_pairs={{0,192},{192,0},{64,128},{128,64},{1,193},{193,1},{65,129},{129,65... | collective-permute-start | bytes 786440 | tf_op jit(solution)/shard_map/ppermute | solution.py:416
  57.7 7.3 %collective-permute-start.17 = (f32[8,32,256]{2,1,0:T(8,128)S(1)}, f32[8,32,256]{2,1,0:T(8,128)S(1)}, u32[]{:S(2)}, u32[]{:S(2)}) collective-permute-start(f32[8,32,256]{2,1,0:T(8,128)S(1)} %get-tuple-element.95), channel_id=1, source_target_pairs={{0,64},{64,0},{128,192},{192,128},{1,65},{65,1},{129,193},{193,129... | collective-permute-start | bytes 786440 | tf_op jit(solution)/shard_map/ppermute | solution.py:417
  57.8 22.9 %collective-permute-start.8 = (f32[8,32,256]{2,1,0:T(8,128)S(1)}, f32[8,32,256]{2,1,0:T(8,128)S(1)}, u32[]{:S(2)}, u32[]{:S(2)}) collective-permute-start(f32[8,32,256]{2,1,0:T(8,128)S(1)} %get-tuple-element.116), channel_id=1, source_target_pairs={{0,192},{192,0},{64,128},{128,64},{1,193},{193,1},{65,129},{129,65... | collective-permute-start | bytes 786440 | tf_op jit(solution)/shard_map/ppermute | solution.py:416
  57.9 22.8 %collective-permute-start.9 = (f32[8,32,256]{2,1,0:T(8,128)S(1)}, f32[8,32,256]{2,1,0:T(8,128)S(1)}, u32[]{:S(2)}, u32[]{:S(2)}) collective-permute-start(f32[8,32,256]{2,1,0:T(8,128)S(1)} %get-tuple-element.114), channel_id=1, source_target_pairs={{0,64},{64,0},{128,192},{192,128},{1,65},{65,1},{129,193},{193,129... | collective-permute-start | bytes 786440 | tf_op jit(solution)/shard_map/ppermute | solution.py:417
  60.4 4.6 %copy-start.27 = (f32[8,32,256]{2,1,0:T(8,128)}, f32[8,32,256]{2,1,0:T(8,128)S(1)}, u32[]{:S(2)}) copy-start(f32[8,32,256]{2,1,0:T(8,128)S(1)} %collective-permute-done.16.refs_5_) | copy-start | bytes 786436
  77.2 17.5 %collective-permute-start.18 = (f32[60,8,256]{2,1,0:T(8,128)}, f32[60,8,256]{2,1,0:T(8,128)S(1)}, u32[]{:S(2)}, u32[]{:S(2)}) collective-permute-start(f32[60,8,256]{2,1,0:T(8,128)} %get-tuple-element.59), channel_id=1, source_target_pairs={{0,1},{1,2},{2,3},{3,0},{4,5},{5,6},{6,7},{7,4},{8,9},{9,10},{10,1... | collective-permute-start | bytes 1474568 | tf_op jit(solution)/shard_map/ppermute | solution.py:92
  80.4 14.3 %collective-permute-start.19 = (f32[60,8,256]{2,1,0:T(8,128)}, f32[60,8,256]{2,1,0:T(8,128)S(1)}, u32[]{:S(2)}, u32[]{:S(2)}) collective-permute-start(f32[60,8,256]{2,1,0:T(8,128)} %get-tuple-element.60), channel_id=1, source_target_pairs={{0,3},{1,0},{2,1},{3,2},{4,7},{5,4},{6,5},{7,6},{8,11},{9,8},{10,9... | collective-permute-start | bytes 1474568 | tf_op jit(solution)/shard_map/ppermute | solution.py:92
  92.9 11.8 %collective-permute-start.10 = (f32[60,8,256]{2,1,0:T(8,128)}, f32[60,8,256]{2,1,0:T(8,128)S(1)}, u32[]{:S(2)}, u32[]{:S(2)}) collective-permute-start(f32[60,8,256]{2,1,0:T(8,128)} %get-tuple-element.50), channel_id=1, source_target_pairs={{0,1},{1,2},{2,3},{3,0},{4,5},{5,6},{6,7},{7,4},{8,9},{9,10},{10,1... | collective-permute-start | bytes 1474568 | tf_op jit(solution)/shard_map/ppermute | solution.py:92
  94.7 15.0 %collective-permute-start.11 = (f32[60,8,256]{2,1,0:T(8,128)}, f32[60,8,256]{2,1,0:T(8,128)S(1)}, u32[]{:S(2)}, u32[]{:S(2)}) collective-permute-start(f32[60,8,256]{2,1,0:T(8,128)} %get-tuple-element.51), channel_id=1, source_target_pairs={{0,3},{1,0},{2,1},{3,2},{4,7},{5,4},{6,5},{7,6},{8,11},{9,8},{10,9... | collective-permute-start | bytes 1474568 | tf_op jit(solution)/shard_map/ppermute | solution.py:92
  98.3 26.0 %collective-permute-start.20 = (f32[12,32,256]{2,1,0:T(8,128)}, f32[12,32,256]{2,1,0:T(8,128)S(1)}, u32[]{:S(2)}, u32[]{:S(2)}) collective-permute-start(f32[12,32,256]{2,1,0:T(8,128)} %get-tuple-element.62), channel_id=1, source_target_pairs={{0,4},{4,8},{8,12},{12,16},{16,20},{20,24},{24,28},{28,32},{32,36}... | collective-permute-start | bytes 1179656 | tf_op jit(solution)/shard_map/ppermute | solution.py:92
  98.3 26.0 %collective-permute-start.21 = (f32[12,32,256]{2,1,0:T(8,128)}, f32[12,32,256]{2,1,0:T(8,128)S(1)}, u32[]{:S(2)}, u32[]{:S(2)}) collective-permute-start(f32[12,32,256]{2,1,0:T(8,128)} %get-tuple-element.63), channel_id=1, source_target_pairs={{0,60},{4,0},{8,4},{12,8},{16,12},{20,16},{24,20},{28,24},{32,28},... | collective-permute-start | bytes 1179656 | tf_op jit(solution)/shard_map/ppermute | solution.py:92
  104.7 4.9 %copy-start.7 = (f32[60,8,256]{2,1,0:T(8,128)}, f32[60,8,256]{2,1,0:T(8,128)S(1)}, u32[]{:S(2)}) copy-start(f32[60,8,256]{2,1,0:T(8,128)S(1)} %collective-permute-done.10.low) | copy-start | bytes 1474564
  113.2 23.4 %collective-permute-start.12 = (f32[12,32,256]{2,1,0:T(8,128)}, f32[12,32,256]{2,1,0:T(8,128)S(1)}, u32[]{:S(2)}, u32[]{:S(2)}) collective-permute-start(f32[12,32,256]{2,1,0:T(8,128)} %get-tuple-element.53), channel_id=1, source_target_pairs={{0,4},{4,8},{8,12},{12,16},{16,20},{20,24},{24,28},{28,32},{32,36}... | collective-permute-start | bytes 1179656 | tf_op jit(solution)/shard_map/ppermute | solution.py:92
  113.2 27.9 %collective-permute-start.13 = (f32[12,32,256]{2,1,0:T(8,128)}, f32[12,32,256]{2,1,0:T(8,128)S(1)}, u32[]{:S(2)}, u32[]{:S(2)}) collective-permute-start(f32[12,32,256]{2,1,0:T(8,128)} %get-tuple-element.54), channel_id=1, source_target_pairs={{0,60},{4,0},{8,4},{12,8},{16,12},{20,16},{24,20},{28,24},{32,28},... | collective-permute-start | bytes 1179656 | tf_op jit(solution)/shard_map/ppermute | solution.py:92
  124.4 16.7 %copy-start.13 = (f32[12,32,256]{2,1,0:T(8,128)}, f32[12,32,256]{2,1,0:T(8,128)S(1)}, u32[]{:S(2)}) copy-start(f32[12,32,256]{2,1,0:T(8,128)S(1)} %collective-permute-done.20.lv) | copy-start | bytes 1179652
  124.4 16.7 %copy-start.14 = (f32[12,32,256]{2,1,0:T(8,128)}, f32[12,32,256]{2,1,0:T(8,128)S(1)}, u32[]{:S(2)}) copy-start(f32[12,32,256]{2,1,0:T(8,128)S(1)} %collective-permute-done.21.hv) | copy-start | bytes 1179652
  136.6 4.5 %copy-start.15 = (f32[12,32,256]{2,1,0:T(8,128)}, f32[12,32,256]{2,1,0:T(8,128)S(1)}, u32[]{:S(2)}) copy-start(f32[12,32,256]{2,1,0:T(8,128)S(1)} %collective-permute-done.12.lu) | copy-start | bytes 1179652
  146.8 11.4 %collective-permute-start.22 = (f32[2,1,32,256]{3,2,1,0:T(8,128)}, f32[2,1,32,256]{3,2,1,0:T(8,128)S(1)}, u32[]{:S(2)}, u32[]{:S(2)}) collective-permute-start(f32[2,1,32,256]{3,2,1,0:T(8,128)} %get-tuple-element.65), channel_id=1, source_target_pairs={{0,4},{4,8},{8,12},{12,16},{16,20},{20,24},{24,28},{28,32},{32,36}... | collective-permute-start | bytes 196616 | tf_op jit(solution)/shard_map/ppermute | solution.py:92
  146.8 11.4 %collective-permute-start.23 = (f32[2,1,32,256]{3,2,1,0:T(8,128)}, f32[2,1,32,256]{3,2,1,0:T(8,128)S(1)}, u32[]{:S(2)}, u32[]{:S(2)}) collective-permute-start(f32[2,1,32,256]{3,2,1,0:T(8,128)} %get-tuple-element.66), channel_id=1, source_target_pairs={{0,60},{4,0},{8,4},{12,8},{16,12},{20,16},{24,20},{28,24},{32,28},... | collective-permute-start | bytes 196616 | tf_op jit(solution)/shard_map/ppermute | solution.py:92
  153.3 2.7 collective-permute-start.24
  154.6 3.6 %collective-permute-start.25 = (f32[2,16,256]{2,1,0:T(8,128)}, f32[2,16,256]{2,1,0:T(8,128)S(1)}, u32[]{:S(2)}, u32[]{:S(2)}) collective-permute-start(f32[2,16,256]{2,1,0:T(8,128)} %get-tuple-element.68), channel_id=1, source_target_pairs={{0,3},{1,0},{2,1},{3,2},{4,7},{5,4},{6,5},{7,6},{8,11},{9,8},{10,9... | collective-permute-start | bytes 98312 | tf_op jit(solution)/shard_map/ppermute | solution.py:92
  156.0 2.2 copy-start.41
  163.5 13.4 %collective-permute-start.26 = (f32[8,32,256]{2,1,0:T(8,128)}, f32[8,32,256]{2,1,0:T(8,128)S(1)}, u32[]{:S(2)}, u32[]{:S(2)}) collective-permute-start(f32[8,32,256]{2,1,0:T(8,128)} %get-tuple-element.69), channel_id=1, source_target_pairs={{0,64},{64,0},{128,192},{192,128},{1,65},{65,1},{129,193},{193,129... | collective-permute-start | bytes 786440 | tf_op jit(solution)/shard_map/ppermute | solution.py:414
  163.5 13.4 %collective-permute-start.34 = (f32[8,32,256]{2,1,0:T(8,128)}, f32[8,32,256]{2,1,0:T(8,128)S(1)}, u32[]{:S(2)}, u32[]{:S(2)}) collective-permute-start(f32[8,32,256]{2,1,0:T(8,128)} %get-tuple-element.78), channel_id=1, source_target_pairs={{0,64},{64,0},{128,192},{192,128},{1,65},{65,1},{129,193},{193,129... | collective-permute-start | bytes 786440 | tf_op jit(solution)/shard_map/ppermute | solution.py:414
  165.0 17.7 %collective-permute-start.27 = (f32[8,32,256]{2,1,0:T(8,128)}, f32[8,32,256]{2,1,0:T(8,128)S(1)}, u32[]{:S(2)}, u32[]{:S(2)}) collective-permute-start(f32[8,32,256]{2,1,0:T(8,128)} %get-tuple-element.71), channel_id=1, source_target_pairs={{0,192},{192,0},{64,128},{128,64},{1,193},{193,1},{65,129},{129,65... | collective-permute-start | bytes 786440 | tf_op jit(solution)/shard_map/ppermute | solution.py:415
  174.7 13.6 %collective-permute-start.35 = (f32[8,32,256]{2,1,0:T(8,128)}, f32[8,32,256]{2,1,0:T(8,128)S(1)}, u32[]{:S(2)}, u32[]{:S(2)}) collective-permute-start(f32[8,32,256]{2,1,0:T(8,128)} %get-tuple-element.80), channel_id=1, source_target_pairs={{0,192},{192,0},{64,128},{128,64},{1,193},{193,1},{65,129},{129,65... | collective-permute-start | bytes 786440 | tf_op jit(solution)/shard_map/ppermute | solution.py:415
  176.9 11.3 %copy-start.3 = (f32[16,32,256]{2,1,0:T(8,128)S(1)}, f32[16,32,256]{2,1,0:T(8,128)}, u32[]{:S(2)}) copy-start(f32[16,32,256]{2,1,0:T(8,128)} %get-tuple-element.70) | copy-start | bytes 1572868
  176.9 11.3 %copy-start.4 = (f32[16,32,256]{2,1,0:T(8,128)S(1)}, f32[16,32,256]{2,1,0:T(8,128)}, u32[]{:S(2)}) copy-start(f32[16,32,256]{2,1,0:T(8,128)} %get-tuple-element.79) | copy-start | bytes 1572868
  176.9 11.3 %copy-start.23 = (f32[8,32,256]{2,1,0:T(8,128)S(1)}, f32[8,32,256]{2,1,0:T(8,128)}, u32[]{:S(2)}) copy-start(f32[8,32,256]{2,1,0:T(8,128)} %get-tuple-element.71) | copy-start | bytes 786436
  177.0 11.3 %copy-start.24 = (f32[8,32,256]{2,1,0:T(8,128)S(1)}, f32[8,32,256]{2,1,0:T(8,128)}, u32[]{:S(2)}) copy-start(f32[8,32,256]{2,1,0:T(8,128)} %get-tuple-element.80) | copy-start | bytes 786436
  180.9 14.0 %collective-permute-start.36 = (f32[8,32,256]{2,1,0:T(8,128)S(1)}, f32[8,32,256]{2,1,0:T(8,128)S(1)}, u32[]{:S(2)}, u32[]{:S(2)}) collective-permute-start(f32[8,32,256]{2,1,0:T(8,128)S(1)} %get-tuple-element.89), channel_id=1, source_target_pairs={{0,192},{192,0},{64,128},{128,64},{1,193},{193,1},{65,129},{129,65... | collective-permute-start | bytes 786440 | tf_op jit(solution)/shard_map/ppermute | solution.py:416
  191.2 5.3 %collective-permute-start.37 = (f32[8,32,256]{2,1,0:T(8,128)S(1)}, f32[8,32,256]{2,1,0:T(8,128)S(1)}, u32[]{:S(2)}, u32[]{:S(2)}) collective-permute-start(f32[8,32,256]{2,1,0:T(8,128)S(1)} %get-tuple-element.87), channel_id=1, source_target_pairs={{0,64},{64,0},{128,192},{192,128},{1,65},{65,1},{129,193},{193,129... | collective-permute-start | bytes 786440 | tf_op jit(solution)/shard_map/ppermute | solution.py:417
  191.3 23.9 %collective-permute-start.28 = (f32[8,32,256]{2,1,0:T(8,128)S(1)}, f32[8,32,256]{2,1,0:T(8,128)S(1)}, u32[]{:S(2)}, u32[]{:S(2)}) collective-permute-start(f32[8,32,256]{2,1,0:T(8,128)S(1)} %get-tuple-element.112), channel_id=1, source_target_pairs={{0,192},{192,0},{64,128},{128,64},{1,193},{193,1},{65,129},{129,65... | collective-permute-start | bytes 786440 | tf_op jit(solution)/shard_map/ppermute | solution.py:416
  193.3 21.9 %collective-permute-start.29 = (f32[8,32,256]{2,1,0:T(8,128)S(1)}, f32[8,32,256]{2,1,0:T(8,128)S(1)}, u32[]{:S(2)}, u32[]{:S(2)}) collective-permute-start(f32[8,32,256]{2,1,0:T(8,128)S(1)} %get-tuple-element.110), channel_id=1, source_target_pairs={{0,64},{64,0},{128,192},{192,128},{1,65},{65,1},{129,193},{193,129... | collective-permute-start | bytes 786440 | tf_op jit(solution)/shard_map/ppermute | solution.py:417
  208.7 21.2 %collective-permute-start.38 = (f32[60,8,256]{2,1,0:T(8,128)}, f32[60,8,256]{2,1,0:T(8,128)S(1)}, u32[]{:S(2)}, u32[]{:S(2)}) collective-permute-start(f32[60,8,256]{2,1,0:T(8,128)} %get-tuple-element.82), channel_id=1, source_target_pairs={{0,1},{1,2},{2,3},{3,0},{4,5},{5,6},{6,7},{7,4},{8,9},{9,10},{10,1... | collective-permute-start | bytes 1474568 | tf_op jit(solution)/shard_map/ppermute | solution.py:92
  215.2 14.7 %collective-permute-start.39 = (f32[60,8,256]{2,1,0:T(8,128)}, f32[60,8,256]{2,1,0:T(8,128)S(1)}, u32[]{:S(2)}, u32[]{:S(2)}) collective-permute-start(f32[60,8,256]{2,1,0:T(8,128)} %get-tuple-element.83), channel_id=1, source_target_pairs={{0,3},{1,0},{2,1},{3,2},{4,7},{5,4},{6,5},{7,6},{8,11},{9,8},{10,9... | collective-permute-start | bytes 1474568 | tf_op jit(solution)/shard_map/ppermute | solution.py:92
  228.1 11.4 %collective-permute-start.30 = (f32[60,8,256]{2,1,0:T(8,128)}, f32[60,8,256]{2,1,0:T(8,128)S(1)}, u32[]{:S(2)}, u32[]{:S(2)}) collective-permute-start(f32[60,8,256]{2,1,0:T(8,128)} %get-tuple-element.73), channel_id=1, source_target_pairs={{0,1},{1,2},{2,3},{3,0},{4,5},{5,6},{6,7},{7,4},{8,9},{9,10},{10,1... | collective-permute-start | bytes 1474568 | tf_op jit(solution)/shard_map/ppermute | solution.py:92
  229.8 25.0 %collective-permute-start.31 = (f32[60,8,256]{2,1,0:T(8,128)}, f32[60,8,256]{2,1,0:T(8,128)S(1)}, u32[]{:S(2)}, u32[]{:S(2)}) collective-permute-start(f32[60,8,256]{2,1,0:T(8,128)} %get-tuple-element.74), channel_id=1, source_target_pairs={{0,3},{1,0},{2,1},{3,2},{4,7},{5,4},{6,5},{7,6},{8,11},{9,8},{10,9... | collective-permute-start | bytes 1474568 | tf_op jit(solution)/shard_map/ppermute | solution.py:92
  233.5 30.6 %collective-permute-start.40 = (f32[12,32,256]{2,1,0:T(8,128)}, f32[12,32,256]{2,1,0:T(8,128)S(1)}, u32[]{:S(2)}, u32[]{:S(2)}) collective-permute-start(f32[12,32,256]{2,1,0:T(8,128)} %get-tuple-element.85), channel_id=1, source_target_pairs={{0,4},{4,8},{8,12},{12,16},{16,20},{20,24},{24,28},{28,32},{32,36}... | collective-permute-start | bytes 1179656 | tf_op jit(solution)/shard_map/ppermute | solution.py:92
  233.5 30.6 %collective-permute-start.41 = (f32[12,32,256]{2,1,0:T(8,128)}, f32[12,32,256]{2,1,0:T(8,128)S(1)}, u32[]{:S(2)}, u32[]{:S(2)}) collective-permute-start(f32[12,32,256]{2,1,0:T(8,128)} %get-tuple-element.86), channel_id=1, source_target_pairs={{0,60},{4,0},{8,4},{12,8},{16,12},{20,16},{24,20},{28,24},{32,28},... | collective-permute-start | bytes 1179656 | tf_op jit(solution)/shard_map/ppermute | solution.py:92
  239.5 15.4 %copy-start.8 = (f32[60,8,256]{2,1,0:T(8,128)}, f32[60,8,256]{2,1,0:T(8,128)S(1)}, u32[]{:S(2)}) copy-start(f32[60,8,256]{2,1,0:T(8,128)S(1)} %collective-permute-done.30.low) | copy-start | bytes 1474564
  258.4 20.0 %collective-permute-start.32 = (f32[12,32,256]{2,1,0:T(8,128)}, f32[12,32,256]{2,1,0:T(8,128)S(1)}, u32[]{:S(2)}, u32[]{:S(2)}) collective-permute-start(f32[12,32,256]{2,1,0:T(8,128)} %get-tuple-element.76), channel_id=1, source_target_pairs={{0,4},{4,8},{8,12},{12,16},{16,20},{20,24},{24,28},{28,32},{32,36}... | collective-permute-start | bytes 1179656 | tf_op jit(solution)/shard_map/ppermute | solution.py:92
  258.4 23.2 %collective-permute-start.33 = (f32[12,32,256]{2,1,0:T(8,128)}, f32[12,32,256]{2,1,0:T(8,128)S(1)}, u32[]{:S(2)}, u32[]{:S(2)}) collective-permute-start(f32[12,32,256]{2,1,0:T(8,128)} %get-tuple-element.77), channel_id=1, source_target_pairs={{0,60},{4,0},{8,4},{12,8},{16,12},{20,16},{24,20},{28,24},{32,28},... | collective-permute-start | bytes 1179656 | tf_op jit(solution)/shard_map/ppermute | solution.py:92
  264.1 17.5 %copy-start.17 = (f32[12,32,256]{2,1,0:T(8,128)}, f32[12,32,256]{2,1,0:T(8,128)S(1)}, u32[]{:S(2)}) copy-start(f32[12,32,256]{2,1,0:T(8,128)S(1)} %collective-permute-done.40.lv) | copy-start | bytes 1179652
  264.1 17.5 %copy-start.18 = (f32[12,32,256]{2,1,0:T(8,128)}, f32[12,32,256]{2,1,0:T(8,128)S(1)}, u32[]{:S(2)}) copy-start(f32[12,32,256]{2,1,0:T(8,128)S(1)} %collective-permute-done.41.hv) | copy-start | bytes 1179652
  278.4 3.1 %copy-start.19 = (f32[12,32,256]{2,1,0:T(8,128)}, f32[12,32,256]{2,1,0:T(8,128)S(1)}, u32[]{:S(2)}) copy-start(f32[12,32,256]{2,1,0:T(8,128)S(1)} %collective-permute-done.32.lu) | copy-start | bytes 1179652
  (21 other events, 16.1 us)

commit v3 on v2

--- a/solution.py
+++ b/solution.py
@@ -62,7 +62,7 @@
             time_step * q[n][n], time_step * q[n][a], time_step * q[n][b],
             time_step * q[b][n], time_step * q[b][a],
             time_step * q[a][n], time_step * q[a][b],
-            0.0,
+            1.0 if n == 3 else 0.0,
         ]
         for d in diffusion_values:
             c = time_step * radau_points[n] * d
@@ -92,6 +92,25 @@
     return lax.ppermute(array, axis, ring(lax.axis_size(axis), step))
 
 
+def call(kernel, outs, args, scratch=(), flops=1_000_000, name=None):
+    vmem = pl.BlockSpec(memory_space=pltpu.VMEM)
+    smem = pl.BlockSpec(memory_space=pltpu.SMEM)
+    return pl.pallas_call(
+        kernel,
+        out_shape=tuple(outs),
+        in_specs=[smem] + [vmem] * (len(args) - 1),
+        out_specs=(vmem,) * len(outs),
+        scratch_shapes=list(scratch),
+        compiler_params=pltpu.CompilerParams(vmem_limit_bytes=24 * 2**20),
+        cost_estimate=pl.CostEstimate(flops=flops, bytes_accessed=1_000_000, transcendentals=0),
+        name=name,
+    )(args[0], *(pltpu.with_memory_space_constraint(a, pltpu.VMEM) for a in args[1:]))
+
+
+def local(*shape):
+    return pltpu.VMEM(shape, jnp.float32)
+
+
 def z_sum(c0, c1, lane):
     first, last = lane == 0, lane == LANES - 1
     up0, up1 = pltpu.roll(c0, 1, 1), pltpu.roll(c1, 1, 1)
@@ -101,27 +120,27 @@
     return low, high
 
 
-def force_kernel(sc, x, xlo, xhi, ylo, yhi, feed, kill,
-                 fua, fub, fva, fvb, du, dv, work):
+def force_kernel(sc, xu, xv, xlo, xhi, ylo, yhi, feed, kill,
+                 fua, fub, fva, fvb, dua, dub, dva, dvb, work):
     def fill(p, carry):
-        for s in range(2):
+        for s, x in enumerate((xu, xv)):
             for h in range(2):
                 lanes = slice(h * LANES, (h + 1) * LANES)
-                work[s, p + 1, h, 8:8 + YB, :] = x[s, p, :, lanes]
+                work[s, p + 1, h, 8:8 + YB, :] = x[p, :, lanes]
         return carry
 
     lax.fori_loop(0, XB, fill, 0)
     for s in range(2):
         for h in range(2):
             lanes = slice(h * LANES, (h + 1) * LANES)
-            work[s, 0, h, 8:8 + YB, :] = xlo[s, 0, :, lanes]
-            work[s, XB + 1, h, 8:8 + YB, :] = xhi[s, 0, :, lanes]
+            work[s, 0, h, 8:8 + YB, :] = xlo[s, :, lanes]
+            work[s, XB + 1, h, 8:8 + YB, :] = xhi[s, :, lanes]
             for p in range(XB):
                 work[s, p + 1, h, 7:8, :] = ylo[s, p:p + 1, lanes]
                 work[s, p + 1, h, 8 + YB:9 + YB, :] = yhi[s, p:p + 1, lanes]
     lane = lax.broadcasted_iota(jnp.int32, (8, LANES), 1)
 
-    def run(base, fu, fv):
+    def run(base, fu, fv, du, dv):
         def plane(i, carry):
             p = base + i
             for t in range(YB // 8):
@@ -147,32 +166,49 @@
                     uvv = u * v * v
                     fu[i, out, lanes] = sc[11] * lap[0][h] + (fr * (1.0 - u) - uvv)
                     fv[i, out, lanes] = sc[15] * lap[1][h] + (uvv - (fr + kr) * v)
-                    du[p, out, lanes] = sc[8] * lap[0][h]
-                    dv[p, out, lanes] = sc[12] * lap[1][h]
+                    du[i, out, lanes] = sc[8] * lap[0][h]
+                    dv[i, out, lanes] = sc[12] * lap[1][h]
             return carry
 
         lax.fori_loop(0, HALF, plane, 0)
 
-    run(0, fua, fva)
-    run(HALF, fub, fvb)
-
-
-def forces(sc, x, xlo, xhi, ylo, yhi, feed, kill):
-    half = jax.ShapeDtypeStruct((HALF, YB, ZB), jnp.float32)
-    full = jax.ShapeDtypeStruct((XB, YB, ZB), jnp.float32)
-    vmem = pl.BlockSpec(memory_space=pltpu.VMEM)
-    return pl.pallas_call(
+    run(0, fua, fva, dua, dva)
+    run(HALF, fub, fvb, dub, dvb)
+
+
+def forces(*args):
+    return call(
         force_kernel,
-        out_shape=(half, half, half, half, full, full),
-        in_specs=[pl.BlockSpec(memory_space=pltpu.SMEM)] + [vmem] * 7,
-        out_specs=(vmem,) * 6,
-        scratch_shapes=[pltpu.VMEM((2, XB + 2, 2, YB + 16, LANES), jnp.float32)],
-        cost_estimate=pl.CostEstimate(flops=8_000_000, bytes_accessed=6_000_000, transcendentals=0),
+        [local(HALF, YB, ZB)] * 8,
+        args,
+        [pltpu.VMEM((2, XB + 2, 2, YB + 16, LANES), jnp.float32)],
+        flops=8_000_000,
         name="forces",
-    )(sc, x, xlo, xhi, ylo, yhi, feed, kill)
-
-
-def jacobi_kernel(species, sc, basis, sums, x, own, ra, rb, core, yhi, ylo, one, two, bs):
+    )
+
+
+def partial_kernel(species, sc, fa, fb, ga, gb, na, nb, x0, sa, sb):
+    def plane(p, carry):
+        low = na[species, p] + sc[7] * x0[p]
+        high = nb[species, p] + sc[7] * x0[HALF + p]
+        sa[p] = sc[3] * fa[p] + sc[4] * ga[p] + low
+        sb[p] = sc[5] * fb[p] + sc[6] * gb[p] + high
+        return carry
+
+    lax.fori_loop(0, HALF, plane, 0)
+
+
+def partial(species, *args):
+    return call(
+        lambda *refs: partial_kernel(species, *refs),
+        [local(HALF, YB, ZB)] * 2,
+        args,
+        name="partial",
+    )
+
+
+def jacobi_kernel(species, sc, basis, sums, x, x0, na, nb, fa, fb, ga, gb, da, db, ra, rb,
+                  core, yhi, ylo, one, two, bs):
     spread = sc[8 + 4 * species + 1]
     scale = sc[8 + 4 * species + 2]
     zero = jnp.zeros((ROWS, LANES), jnp.float32)
@@ -192,11 +228,14 @@
                        preferred_element_type=jnp.float32)
         return done.reshape(values.shape)
 
-    def fill(half, recv):
+    def fill(half, f, g, d, n, recv, weight):
         def planes(i, carry):
             p = half * HALF + i * 4
-            xh = modes(x[0, pl.ds(p, 4)])
-            bh = modes(own[pl.ds(p, 4)] + recv[pl.ds(i * 4, 4)])
+            part = pl.ds(i * 4, 4)
+            xh = modes(x[pl.ds(p, 4)])
+            own = sc[0] * f[part] + sc[weight] * g[part] + d[part]
+            own = own + (n[species, part] + sc[7] * x0[pl.ds(p, 4)])
+            bh = modes(own + recv[part])
             for h in range(2):
                 lanes = slice(h * LANES, (h + 1) * LANES)
                 for j in range(4):
@@ -206,8 +245,8 @@
 
         lax.fori_loop(0, HALF // 4, planes, 0)
 
-    fill(0, ra)
-    fill(1, rb)
+    fill(0, fa, ga, da, na, ra, 1)
+    fill(1, fb, gb, db, nb, rb, 2)
     turned = [spread * sums[:, h * LANES:(h + 1) * LANES] for h in range(2)]
 
     def one_plane(src, dst, p, group, carry):
@@ -280,31 +319,22 @@
     lax.fori_loop(0, NFAR, far, 0)
 
 
-def jacobi(species, sc, basis, sums, x, own, ra, rb):
-    vmem = pl.BlockSpec(memory_space=pltpu.VMEM)
-    strip = jax.ShapeDtypeStruct((STRIP, 8, ZB), jnp.float32)
-    return pl.pallas_call(
+def jacobi(species, *args):
+    return call(
         lambda *refs: jacobi_kernel(species, *refs),
-        grid=(1,),
-        out_shape=(jax.ShapeDtypeStruct((XB + 2 * JACOBI, YB, ZB), jnp.float32), strip, strip),
-        in_specs=[
-            pl.BlockSpec(memory_space=pltpu.SMEM),
-            vmem, vmem,
-            pl.BlockSpec((1, XB, YB, ZB), lambda i: (species, 0, 0, 0)),
-            vmem, vmem, vmem,
-        ],
-        out_specs=(vmem,) * 3,
-        scratch_shapes=[
+        [local(XB + 2 * JACOBI, YB, ZB)] + [local(STRIP, 8, ZB)] * 2,
+        args,
+        [
             pltpu.VMEM((PLANES, 2, ROWS, LANES), jnp.float32),
             pltpu.VMEM((PLANES, 2, ROWS, LANES), jnp.float32),
             pltpu.VMEM((PLANES, 2, YB, LANES), jnp.float32),
         ],
-        cost_estimate=pl.CostEstimate(flops=60_000_000, bytes_accessed=5_000_000, transcendentals=0),
+        flops=60_000_000,
         name="jacobi",
-    )(sc, basis, sums, x, own, ra, rb)
-
-
-def gather_kernel(core, low, high, xlo, xhi, center):
+    )
+
+
+def gather_kernel(sc, core, low, high, xlo, xhi, center):
     wide = XB + 2 * JACOBI
     for p in range(wide):
         if p < JACOBI:
@@ -328,62 +358,92 @@
             dst[q, 8 * t:8 * t + 8, :] = parts[t]
 
 
-def gathered(core, low, high):
-    vmem = pl.BlockSpec(memory_space=pltpu.VMEM)
-    side = jax.ShapeDtypeStruct((JACOBI, YB, ZB), jnp.float32)
-    return pl.pallas_call(
+def gathered(*args):
+    return call(
         gather_kernel,
-        out_shape=(side, side, jax.ShapeDtypeStruct((XB, YB, ZB), jnp.float32)),
-        in_specs=[vmem] * 3,
-        out_specs=(vmem,) * 3,
-        cost_estimate=pl.CostEstimate(flops=1_000_000, bytes_accessed=4_000_000, transcendentals=0),
+        [local(JACOBI, YB, ZB)] * 2 + [local(XB, YB, ZB)],
+        args,
         name="gathered",
-    )(core, low, high)
-
-
-def final_kernel(basis, cu, lu, hu, cv, lv, hv, out, *edges):
+    )
+
+
+def back(basis, c, low, high, total, give):
     gap = XB - JACOBI
-    for s, (c, low, high) in enumerate(((cu, lu, hu), (cv, lv, hv))):
-        for q in range(0, XB, 4):
-            parts = []
-            for p in range(q, q + 4):
-                value = c[p]
-                if p < JACOBI:
-                    value = value + low[p]
-                if p >= gap:
-                    value = value + high[p - gap]
-                parts.append(value)
-            flat = jnp.concatenate(parts, 0)
-            done = lax.dot_general(flat, basis[...], (((1,), (1,)), ((), ())),
-                                   precision=lax.Precision.HIGHEST,
-                                   preferred_element_type=jnp.float32)
-            for p in range(q, q + 4):
-                value = done[(p - q) * YB:(p - q + 1) * YB]
-                out[s, p] = value
-                if edges:
-                    xfirst, xlast, yfirst, ylast = edges
-                    if p == 0:
-                        xfirst[s, 0] = value
-                    if p == XB - 1:
-                        xlast[s, 0] = value
-                    yfirst[s, p:p + 1, :] = value[0:1, :]
-                    ylast[s, p:p + 1, :] = value[YB - 1:YB, :]
-
-
-def final(basis, cu, lu, hu, cv, lv, hv, edges):
-    vmem = pl.BlockSpec(memory_space=pltpu.VMEM)
-    shapes = [jax.ShapeDtypeStruct((2, XB, YB, ZB), jnp.float32)]
-    if edges:
-        shapes += [jax.ShapeDtypeStruct((2, 1, YB, ZB), jnp.float32)] * 2
-        shapes += [jax.ShapeDtypeStruct((2, XB, ZB), jnp.float32)] * 2
-    return pl.pallas_call(
-        final_kernel,
-        out_shape=tuple(shapes),
-        in_specs=[vmem] * 7,
-        out_specs=(vmem,) * len(shapes),
-        cost_estimate=pl.CostEstimate(flops=1_000_000, bytes_accessed=4_000_000, transcendentals=0),
-        name="final",
-    )(basis, cu, lu, hu, cv, lv, hv)
+
+    def add(p, carry):
+        total[p] = c[p]
+        return carry
+
+    def add_low(p, carry):
+        total[p] += low[p]
+        return carry
+
+    def add_high(p, carry):
+        total[gap + p] += high[p]
+        return carry
+
+    lax.fori_loop(0, XB, add, 0)
+    lax.fori_loop(0, JACOBI, add_low, 0)
+    lax.fori_loop(0, JACOBI, add_high, 0)
+
+    def turn(i, carry):
+        flat = total[pl.ds(8 * i, 8)].reshape(8 * YB, ZB)
+        done = lax.dot_general(flat, basis[...], (((1,), (1,)), ((), ())),
+                               precision=lax.Precision.HIGHEST,
+                               preferred_element_type=jnp.float32)
+        give(8 * i, done.reshape(8, YB, ZB))
+        return carry
+
+    lax.fori_loop(0, XB // 8, turn, 0)
+
+
+def first_kernel(sc, basis, c, low, high, out, total):
+    def give(p, value):
+        out[pl.ds(p, 8)] = value
+
+    back(basis, c, low, high, total, give)
+
+
+def middle_kernel(sc, basis, c, low, high, xu, out, xfirst, xlast, yfirst, ylast, total):
+    def give(p, value):
+        out[pl.ds(p, 8)] = value
+
+    back(basis, c, low, high, total, give)
+    for s, x in enumerate((xu, out)):
+        xfirst[s] = x[0]
+        xlast[s] = x[XB - 1]
+        for p in range(XB):
+            yfirst[s, p:p + 1, :] = x[p, 0:1, :]
+            ylast[s, p:p + 1, :] = x[p, YB - 1:YB, :]
+
+
+def last_kernel(sc, basis, c, low, high, xu, out, total):
+    def give(p, value):
+        out[1, pl.ds(p, 8)] = value
+
+    def copy(p, carry):
+        out[0, p] = xu[p]
+        return carry
+
+    lax.fori_loop(0, XB, copy, 0)
+    back(basis, c, low, high, total, give)
+
+
+TOTAL = [pltpu.VMEM((XB, YB, ZB), jnp.float32)]
+
+
+def first(*args):
+    return call(first_kernel, [local(XB, YB, ZB)], args, TOTAL, name="first")[0]
+
+
+def middle(*args):
+    outs = [local(XB, YB, ZB)] + [local(2, YB, ZB)] * 2 + [local(2, XB, ZB)] * 2
+    return call(middle_kernel, outs, args, TOTAL, name="middle")
+
+
+def last(*args):
+    outs = [jax.ShapeDtypeStruct((2, XB, YB, ZB), jnp.float32)]
+    return call(last_kernel, outs, args, TOTAL, name="last")[0]
 
 
 PAIR_A = [(0, 1), (1, 0), (2, 3), (3, 2)]
@@ -391,14 +451,12 @@
 
 
 def body(previous, feed_rate, kill_rate):
-    node = lax.axis_index("node")
-    sc = jnp.asarray(node_table(), jnp.float32)[node]
+    sc = jnp.asarray(node_table(), jnp.float32)[lax.axis_index("node")]
     basis, sums = map(jnp.asarray, fourier())
+    hold = lax.optimization_barrier
     x = previous[0]
-    sent_a = lax.ppermute(x[:, :HALF], "node", [(3, 2)])
-    sent_b = lax.ppermute(x[:, HALF:], "node", [(3, 0)])
-    last = node == 3
-    edges = (x[:, :1], x[:, XB - 1:], x[:, :, 0], x[:, :, YB - 1])
+    x0 = xs = (x[0], x[1])
+    edges = (x[:, 0], x[:, XB - 1], x[:, :, 0], x[:, :, YB - 1])
     for sweep in range(SWEEPS):
         xfirst, xlast, yfirst, ylast = edges
         xlo = shifted(xlast, "sx", 1)
@@ -406,29 +464,37 @@
         ylo = shifted(ylast, "sy", 1)
         yhi = shifted(yfirst, "sy", -1)
         if sweep == 0:
-            start_a = jnp.where(last, x[:, :HALF], sent_a)
-            start_b = jnp.where(last, x[:, HALF:], sent_b)
-        fua, fub, fva, fvb, du, dv = forces(sc, x, xlo, xhi, ylo, yhi, feed_rate, kill_rate)
-        cores = []
-        for s, (fa, fb, d) in enumerate(((fua, fub, du), (fva, fvb, dv))):
-            ga = lax.ppermute(fa, "node", PAIR_A)
-            gb = lax.ppermute(fb, "node", PAIR_B)
-            ra = lax.ppermute(sc[3] * fa + sc[4] * ga + start_a[s], "node", PAIR_B)
-            rb = lax.ppermute(sc[5] * fb + sc[6] * gb + start_b[s], "node", PAIR_A)
-            own = jnp.concatenate(
-                [
-                    sc[0] * fa + sc[1] * ga + start_a[s] + d[:HALF],
-                    sc[0] * fb + sc[2] * gb + start_b[s] + d[HALF:],
-                ],
-                0,
+            na = lax.ppermute(x[:, :HALF], "node", [(3, 2)])
+            nb = lax.ppermute(x[:, HALF:], "node", [(3, 0)])
+        fua, fub, fva, fvb, dua, dub, dva, dvb = forces(
+            sc, *xs, xlo, xhi, ylo, yhi, feed_rate, kill_rate
+        )
+        fua, fub, na, nb = hold((fua, fub, na, nb))
+        gua = lax.ppermute(fua, "node", PAIR_A)
+        gub = lax.ppermute(fub, "node", PAIR_B)
+        fva, fvb, gua, gub = hold((fva, fvb, gua, gub))
+        gva = lax.ppermute(fva, "node", PAIR_A)
+        gvb = lax.ppermute(fvb, "node", PAIR_B)
+        done = []
+        for s, (fa, fb, ga, gb, da, db) in enumerate(
+            ((fua, fub, gua, gub, dua, dub), (fva, fvb, gva, gvb, dva, dvb))
+        ):
+            pa, pb = partial(s, sc, fa, fb, ga, gb, na, nb, x0[s])
+            ra = lax.ppermute(pa, "node", PAIR_B)
+            rb = lax.ppermute(pb, "node", PAIR_A)
+            core, up, down = jacobi(
+                s, sc, basis, sums, xs[s], x0[s], na, nb, fa, fb, ga, gb, da, db, ra, rb
             )
-            core, up, down = jacobi(s, sc, basis, sums, x, own, ra, rb)
             low = shifted(up, "sy", 1)
             high = shifted(down, "sy", -1)
-            left, right, center = gathered(core, low, high)
-            cores += [center, shifted(right, "sx", 1), shifted(left, "sx", -1)]
-        x, *edges = final(basis, *cores, sweep + 1 < SWEEPS)
-    return x[None]
+            left, right, center = gathered(sc, core, low, high)
+            parts = (sc, basis, center, shifted(right, "sx", 1), shifted(left, "sx", -1))
+            if s == 0:
+                xu = first(*parts)
+        if sweep + 1 < SWEEPS:
+            xv, *edges = middle(*parts, xu)
+            xs = (xu, xv)
+    return last(*parts, xu)[None]
 
 
 def solution(mesh):

time: 292 us -> 237 us (0.81); the launches traced: 287 us -> 236 us
  Pallas kernels: 75.9 us -> 55.5 us
  other arithmetic: 15.4 us -> 0 us
  starting transfers between devices: 86.1 us -> 71.2 us
  local copies, waits for them, and re-layouts: 14.7 us -> 4.1 us
  waiting for transfers between devices: 94.6 us -> 105 us
    pallas_call x12 -> x18, Pallas kernels: 75.9 us -> 55.5 us  [call(): pl.pallas_call(kernel, out_shape=tuple(outs), in_specs=[smem] + [vmem] *...]
    ppermute x18, starting transfers between devices: 30.7 us -> 11.5 us  [the longest x4 5.92 us: body(): ra = lax.ppermute(pa, 'node', PAIR_B)]
    add x4 -> x0, other arithmetic: 12.5 us -> none  [the longest x2 6.63 us: body(): ra = lax.ppermute(sc[3] * fa + sc[4] * ga + start_a[s], 'node', PAIR_B)]
    unnamed x88 -> x12, local copies, waits for them, and re-layouts: 9.8 us -> 0.03 us
    ppermute x18, waiting for transfers between devices: 28.1 us -> 36.4 us  [the longest x2 12.1 us: body(): gua = lax.ppermute(fua, 'node', PAIR_A)]
    ppermute x24, starting transfers between devices: 55.4 us -> 59.6 us  [shifted(): return lax.ppermute(array, axis, ring(lax.axis_size(axis), step))]
  transfers between devices with their start and end apart: 42 -> 42, of which waited for: 21 -> 26; matrix products, arithmetic and copies ran while one was open for 7% -> 1% of each run, Pallas kernels for 21% -> 21%
where the time goes in v3:
time: 237 us; the launch traced here: 236 us
  waiting for transfers between devices  105 us (44%)
  starting transfers between devices  71.2 us (30%)
  Pallas kernels  55.5 us (23%)
  local copies, waits for them, and re-layouts  4.1 us (2%)
    ppermute x24, waiting for transfers between devices, shifted(): return lax.ppermute(array, axis, ring(lax.axis_size(axis), step))  68.9 us
    ppermute x24, starting transfers between devices, shifted(): return lax.ppermute(array, axis, ring(lax.axis_size(axis), step))  59.6 us
    pallas_call x18, Pallas kernels, call(): pl.pallas_call(kernel, out_shape=tuple(outs), in_specs=[smem] + [vmem] *...  55.5 us
    ppermute x2, waiting for transfers between devices, body(): gua = lax.ppermute(fua, 'node', PAIR_A)  12.1 us
    ppermute x4, waiting for transfers between devices, body(): ra = lax.ppermute(pa, 'node', PAIR_B)  7.09 us
    ppermute x1, waiting for transfers between devices, body(): nb = lax.ppermute(x[:, HALF:], 'node', [(3, 0)])  6.38 us
    ppermute x4, starting transfers between devices, body(): ra = lax.ppermute(pa, 'node', PAIR_B)  5.92 us
    ppermute x2, waiting for transfers between devices, body(): gva = lax.ppermute(fva, 'node', PAIR_A)  5.72 us
  transfers between devices with their start and end apart: 42, of which 26 were waited for; matrix products, arithmetic and copies ran while one was open for 1% of the time, Pallas kernels for 21%

profile of v3, /device:TPU:1, one launch (start us, length us, event | category | flops | bytes accessed | tf_op | source)
XLA Modules:
  0.0 236.4 jit_solution(3462820368059604703)
XLA Ops:
  0.0 1.0 slice_bitcast_fusion.2
  1.0 2.2 collective-permute-start
  3.2 7.3 %collective-permute-start.1 = (f32[2,32,256]{2,1,0:T(8,128)S(1)}, f32[2,32,256]{2,1,0:T(8,128)S(1)}, u32[]{:S(2)}, u32[]{:S(2)}) collective-permute-start(f32[2,32,256]{2,1,0:T(8,128)S(1)} %get-tuple-element.147), channel_id=1, source_target_pairs={{0,60},{4,0},{8,4},{12,8},{16,12},{20,16},{24,20},{28,24},{32,28},... | collective-permute-start | bytes 196616 | tf_op jit(solution)/shard_map/ppermute | solution.py:92
  10.4 2.3 fusion
  12.7 0.8 collective-permute-start.4
  13.6 1.3 collective-permute-start.5
  14.9 1.7 collective-permute-start.2
  16.7 0.9 collective-permute-done.2.ylo
  17.6 1.7 collective-permute-start.3
  20.0 1.5 collective-permute-done.3.yhi
  21.5 2.4 %forces.2 = (f32[8,32,256]{2,1,0:T(8,128)S(1)}, f32[8,32,256]{2,1,0:T(8,128)S(1)}, f32[8,32,256]{2,1,0:T(8,128)S(1)}, f32[8,32,256]{2,1,0:T(8,128)S(1)}, f32[8,3...) custom-call(f32[16]{0:T(128)S(1)} %dynamic-slice_bitcast_fusion.sc.refs_0, ...), custom_call_target="tpu_custom_call" | custom-call | flops 8000000 | bytes 1000000 | tf_op jit(solution)/shard_map/forces/pallas_call | solution.py:98
  24.0 6.4 %collective-permute-done.5.refs_6_ = f32[2,8,32,256]{3,2,1,0:T(8,128)S(1)} collective-permute-done((f32[2,8,32,256]{3,2,1,0:T(8,128)}, f32[2,8,32,256]{3,2,1,0:T(8,128)S(1)}, u32[]{:S(2)}, u32[]{:S(2)}) %collective-permute-start.5) | collective-permute-done | bytes 524320 | tf_op jit(solution)/shard_map/ppermute | solution.py:468
  30.5 5.9 %collective-permute-done.6.refs_3_.refs_9_ = f32[8,32,256]{2,1,0:T(8,128)S(1)} collective-permute-done((f32[8,32,256]{2,1,0:T(8,128)S(1)}, f32[8,32,256]{2,1,0:T(8,128)S(1)}, u32[]{:S(2)}, u32[]{:S(2)}) %collective-permute-start.6) | collective-permute-done | bytes 262176 | tf_op jit(solution)/shard_map/ppermute | solution.py:473
  36.4 1.2 collective-permute-done.7.refs_4_.refs_10_
  37.6 0.9 collective-permute-start.9
  38.5 0.7 partial.5
  39.2 1.9 collective-permute-start.16
  41.4 1.5 collective-permute-done.8.refs_3_.refs_9_
  42.9 1.2 collective-permute-done.9.refs_4_.refs_10_
  44.1 0.7 partial.4
  44.8 0.9 collective-permute-start.10
  45.8 3.4 %collective-permute-done.16.refs_13_ = f32[8,32,256]{2,1,0:T(8,128)S(1)} collective-permute-done((f32[8,32,256]{2,1,0:T(8,128)S(1)}, f32[8,32,256]{2,1,0:T(8,128)S(1)}, u32[]{:S(2)}, u32[]{:S(2)}) %collective-permute-start.16) | collective-permute-done | bytes 262176 | tf_op jit(solution)/shard_map/ppermute | solution.py:483
  49.5 9.4 %jacobi.5 = (f32[40,32,256]{2,1,0:T(8,128)S(1)}, f32[60,8,256]{2,1,0:T(8,128)S(1)}, f32[60,8,256]{2,1,0:T(8,128)S(1)}) custom-call(f32[16]{0:T(128)S(1)} %dynamic-slice_bitcast_fusion.sc.refs_0_, f32[256,256]{1,0:T(8,128)S(1)} %copy-done, f32[8,256]{1,0:T(8,128)S(1)} %copy-done.3, f32[16,32,256]{2,1,0:T(8,128)S(1)} %get-tuple-element.149.xu.refs_7_.refs_3_.refs_4_, ...), custom_call_target="tpu_custom_call" | custom-call | flops 60000000 | bytes 1000000 | tf_op jit(solution)/shard_map/jacobi/pallas_call | solution.py:98
  58.8 7.2 %collective-permute-start.18 = (f32[60,8,256]{2,1,0:T(8,128)S(1)}, f32[60,8,256]{2,1,0:T(8,128)S(1)}, u32[]{:S(2)}, u32[]{:S(2)}) collective-permute-start(f32[60,8,256]{2,1,0:T(8,128)S(1)} %get-tuple-element.101), channel_id=1, source_target_pairs={{0,1},{1,2},{2,3},{3,0},{4,5},{5,6},{6,7},{7,4},{8,9},{9,10},{10,1... | collective-permute-start | bytes 1474568 | tf_op jit(solution)/shard_map/ppermute | solution.py:92
  66.1 9.4 %jacobi.4 = (f32[40,32,256]{2,1,0:T(8,128)S(1)}, f32[60,8,256]{2,1,0:T(8,128)S(1)}, f32[60,8,256]{2,1,0:T(8,128)S(1)}) custom-call(f32[16]{0:T(128)S(1)} %dynamic-slice_bitcast_fusion.sc.refs_0_, f32[256,256]{1,0:T(8,128)S(1)} %copy-done, f32[8,256]{1,0:T(8,128)S(1)} %copy-done.3, f32[16,32,256]{2,1,0:T(8,128)S(1)} %get-tuple-element.150.xv.refs_7_.refs_3_.refs_4_, ...), custom_call_target="tpu_custom_call" | custom-call | flops 60000000 | bytes 1000000 | tf_op jit(solution)/shard_map/jacobi/pallas_call | solution.py:98
  75.5 2.0 collective-permute-start.12
  77.5 0.8 collective-permute-done.19.high
  79.1 5.7 %collective-permute-start.21 = (f32[12,32,256]{2,1,0:T(8,128)S(1)}, f32[12,32,256]{2,1,0:T(8,128)S(1)}, u32[]{:S(2)}, u32[]{:S(2)}) collective-permute-start(f32[12,32,256]{2,1,0:T(8,128)S(1)} %get-tuple-element.105), channel_id=1, source_target_pairs={{0,60},{4,0},{8,4},{12,8},{16,12},{20,16},{24,20},{28,24},{32,28},... | collective-permute-start | bytes 1179656 | tf_op jit(solution)/shard_map/ppermute | solution.py:92
  84.7 2.5 %collective-permute-done.12.low = f32[60,8,256]{2,1,0:T(8,128)S(1)} collective-permute-done((f32[60,8,256]{2,1,0:T(8,128)S(1)}, f32[60,8,256]{2,1,0:T(8,128)S(1)}, u32[]{:S(2)}, u32[]{:S(2)}) %collective-permute-start.12) | collective-permute-done | bytes 491552 | tf_op jit(solution)/shard_map/ppermute | solution.py:92
  87.2 12.2 %collective-permute-done.13.high = f32[60,8,256]{2,1,0:T(8,128)S(1)} collective-permute-done((f32[60,8,256]{2,1,0:T(8,128)S(1)}, f32[60,8,256]{2,1,0:T(8,128)S(1)}, u32[]{:S(2)}, u32[]{:S(2)}) %collective-permute-start.13) | collective-permute-done | bytes 491552 | tf_op jit(solution)/shard_map/ppermute | solution.py:92
  99.4 0.7 gathered.4
  100.2 5.7 %collective-permute-start.15 = (f32[12,32,256]{2,1,0:T(8,128)S(1)}, f32[12,32,256]{2,1,0:T(8,128)S(1)}, u32[]{:S(2)}, u32[]{:S(2)}) collective-permute-start(f32[12,32,256]{2,1,0:T(8,128)S(1)} %get-tuple-element.93), channel_id=1, source_target_pairs={{0,60},{4,0},{8,4},{12,8},{16,12},{20,16},{24,20},{28,24},{32,28},... | collective-permute-start | bytes 1179656 | tf_op jit(solution)/shard_map/ppermute | solution.py:92
  105.9 1.6 first.2.xu.refs_3_
  107.5 7.9 %collective-permute-done.14.low = f32[12,32,256]{2,1,0:T(8,128)S(1)} collective-permute-done((f32[12,32,256]{2,1,0:T(8,128)S(1)}, f32[12,32,256]{2,1,0:T(8,128)S(1)}, u32[]{:S(2)}, u32[]{:S(2)}) %collective-permute-start.14) | collective-permute-done | bytes 393248 | tf_op jit(solution)/shard_map/ppermute | solution.py:92
  115.4 5.6 %collective-permute-done.15.high = f32[12,32,256]{2,1,0:T(8,128)S(1)} collective-permute-done((f32[12,32,256]{2,1,0:T(8,128)S(1)}, f32[12,32,256]{2,1,0:T(8,128)S(1)}, u32[]{:S(2)}, u32[]{:S(2)}) %collective-permute-start.15) | collective-permute-done | bytes 393248 | tf_op jit(solution)/shard_map/ppermute | solution.py:92
  121.0 1.6 middle.1
  122.7 6.3 %collective-permute-start.23 = (f32[2,32,256]{2,1,0:T(8,128)S(1)}, f32[2,32,256]{2,1,0:T(8,128)S(1)}, u32[]{:S(2)}, u32[]{:S(2)}) collective-permute-start(f32[2,32,256]{2,1,0:T(8,128)S(1)} %get-tuple-element.108), channel_id=1, source_target_pairs={{0,60},{4,0},{8,4},{12,8},{16,12},{20,16},{24,20},{28,24},{32,28},... | collective-permute-start | bytes 196616 | tf_op jit(solution)/shard_map/ppermute | solution.py:92
  129.0 4.2 %collective-permute-start.24 = (f32[2,16,256]{2,1,0:T(8,128)S(1)}, f32[2,16,256]{2,1,0:T(8,128)S(1)}, u32[]{:S(2)}, u32[]{:S(2)}) collective-permute-start(f32[2,16,256]{2,1,0:T(8,128)S(1)} %get-tuple-element.109), channel_id=1, source_target_pairs={{0,1},{1,2},{2,3},{3,0},{4,5},{5,6},{6,7},{7,4},{8,9},{9,10},{10,1... | collective-permute-start | bytes 98312 | tf_op jit(solution)/shard_map/ppermute | solution.py:92
  133.2 1.0 collective-permute-done.24.ylo
  134.2 2.3 collective-permute-done.25.yhi
  136.6 2.4 %forces.3 = (f32[8,32,256]{2,1,0:T(8,128)S(1)}, f32[8,32,256]{2,1,0:T(8,128)S(1)}, f32[8,32,256]{2,1,0:T(8,128)S(1)}, f32[8,32,256]{2,1,0:T(8,128)S(1)}, f32[8,3...) custom-call(f32[16]{0:T(128)S(1)} %dynamic-slice_bitcast_fusion.sc.refs_0, ...), custom_call_target="tpu_custom_call" | custom-call | flops 8000000 | bytes 1000000 | tf_op jit(solution)/shard_map/forces/pallas_call | solution.py:98
  139.3 0.8 collective-permute-start.27
  140.1 6.1 %collective-permute-done.26.refs_3_.refs_9_ = f32[8,32,256]{2,1,0:T(8,128)S(1)} collective-permute-done((f32[8,32,256]{2,1,0:T(8,128)S(1)}, f32[8,32,256]{2,1,0:T(8,128)S(1)}, u32[]{:S(2)}, u32[]{:S(2)}) %collective-permute-start.26) | collective-permute-done | bytes 262176 | tf_op jit(solution)/shard_map/ppermute | solution.py:473
  146.3 1.5 collective-permute-done.27.refs_4_.refs_10_
  147.7 0.9 collective-permute-start.29
  148.6 0.7 partial.7
  149.3 1.9 collective-permute-start.36
  151.5 4.3 %collective-permute-done.28.refs_3_.refs_9_ = f32[8,32,256]{2,1,0:T(8,128)S(1)} collective-permute-done((f32[8,32,256]{2,1,0:T(8,128)S(1)}, f32[8,32,256]{2,1,0:T(8,128)S(1)}, u32[]{:S(2)}, u32[]{:S(2)}) %collective-permute-start.28) | collective-permute-done | bytes 262176 | tf_op jit(solution)/shard_map/ppermute | solution.py:476
  155.8 0.9 collective-permute-done.29.refs_4_.refs_10_
  156.7 0.7 partial.6
  157.4 1.2 collective-permute-start.30
  158.6 3.7 %collective-permute-done.36.refs_13_ = f32[8,32,256]{2,1,0:T(8,128)S(1)} collective-permute-done((f32[8,32,256]{2,1,0:T(8,128)S(1)}, f32[8,32,256]{2,1,0:T(8,128)S(1)}, u32[]{:S(2)}, u32[]{:S(2)}) %collective-permute-start.36) | collective-permute-done | bytes 262176 | tf_op jit(solution)/shard_map/ppermute | solution.py:483
  162.3 9.3 %jacobi.7 = (f32[40,32,256]{2,1,0:T(8,128)S(1)}, f32[60,8,256]{2,1,0:T(8,128)S(1)}, f32[60,8,256]{2,1,0:T(8,128)S(1)}) custom-call(f32[16]{0:T(128)S(1)} %dynamic-slice_bitcast_fusion.sc.refs_0_, f32[256,256]{1,0:T(8,128)S(1)} %copy-done, f32[8,256]{1,0:T(8,128)S(1)} %copy-done.3, f32[16,32,256]{2,1,0:T(8,128)S(1)} %first.2.xu.refs_3_, ...), custom_call_target="tpu_custom_call" | custom-call | flops 60000000 | bytes 1000000 | tf_op jit(solution)/shard_map/jacobi/pallas_call | solution.py:98
  171.7 2.1 collective-permute-start.38
  173.8 9.4 %jacobi.6 = (f32[40,32,256]{2,1,0:T(8,128)S(1)}, f32[60,8,256]{2,1,0:T(8,128)S(1)}, f32[60,8,256]{2,1,0:T(8,128)S(1)}) custom-call(f32[16]{0:T(128)S(1)} %dynamic-slice_bitcast_fusion.sc.refs_0_, f32[256,256]{1,0:T(8,128)S(1)} %copy-done, f32[8,256]{1,0:T(8,128)S(1)} %copy-done.3, f32[16,32,256]{2,1,0:T(8,128)S(1)} %get-tuple-element.106.xv.refs_3_, ...), custom_call_target="tpu_custom_call" | custom-call | flops 60000000 | bytes 1000000 | tf_op jit(solution)/shard_map/jacobi/pallas_call | solution.py:98
  183.2 1.8 collective-permute-start.32
  185.0 1.1 collective-permute-done.39.high
  186.9 5.7 %collective-permute-start.41 = (f32[12,32,256]{2,1,0:T(8,128)S(1)}, f32[12,32,256]{2,1,0:T(8,128)S(1)}, u32[]{:S(2)}, u32[]{:S(2)}) collective-permute-start(f32[12,32,256]{2,1,0:T(8,128)S(1)} %get-tuple-element.142), channel_id=1, source_target_pairs={{0,60},{4,0},{8,4},{12,8},{16,12},{20,16},{24,20},{28,24},{32,28},... | collective-permute-start | bytes 1179656 | tf_op jit(solution)/shard_map/ppermute | solution.py:92
  192.6 2.1 collective-permute-done.32.low
  194.6 15.8 %collective-permute-done.33.high = f32[60,8,256]{2,1,0:T(8,128)S(1)} collective-permute-done((f32[60,8,256]{2,1,0:T(8,128)S(1)}, f32[60,8,256]{2,1,0:T(8,128)S(1)}, u32[]{:S(2)}, u32[]{:S(2)}) %collective-permute-start.33) | collective-permute-done | bytes 491552 | tf_op jit(solution)/shard_map/ppermute | solution.py:92
  211.2 5.7 %collective-permute-start.35 = (f32[12,32,256]{2,1,0:T(8,128)S(1)}, f32[12,32,256]{2,1,0:T(8,128)S(1)}, u32[]{:S(2)}, u32[]{:S(2)}) collective-permute-start(f32[12,32,256]{2,1,0:T(8,128)S(1)} %get-tuple-element.130), channel_id=1, source_target_pairs={{0,60},{4,0},{8,4},{12,8},{16,12},{20,16},{24,20},{28,24},{32,28},... | collective-permute-start | bytes 1179656 | tf_op jit(solution)/shard_map/ppermute | solution.py:92
  216.9 1.6 first.3.xu
  218.5 14.9 %collective-permute-done.34.low = f32[12,32,256]{2,1,0:T(8,128)S(1)} collective-permute-done((f32[12,32,256]{2,1,0:T(8,128)S(1)}, f32[12,32,256]{2,1,0:T(8,128)S(1)}, u32[]{:S(2)}, u32[]{:S(2)}) %collective-permute-start.34) | collective-permute-done | bytes 393248 | tf_op jit(solution)/shard_map/ppermute | solution.py:92
  233.7 2.7 %last.1 = f32[2,16,32,256]{3,2,1,0:T(8,128)} custom-call(f32[16]{0:T(128)S(1)} %dynamic-slice_bitcast_fusion.sc.refs_0_, f32[256,256]{1,0:T(8,128)S(1)} %copy-done, f32[16,32,256]{2,1,0:T(8,128)S(1)} %get-tuple-element.128.c, f32[12,32,256]{2,1,0:T(8,128)S(1)} %collective-permute-done.34.low, f32[12,32,256]{2,1,0:T(8,128)S(1)} %collective-permute-done.35.high, ...), custom_call_target="tpu_custom_call" | custom-call | flops 1000000 | bytes 1000000 | tf_op jit(solution)/shard_map/last/pallas_call | solution.py:98
  (55 shorter events, 4.8 us)
Async XLA Ops:
  0.0 14.9 %copy-start.4 = (f32[1,2,16,32,256]{4,3,2,1,0:T(8,128)S(1)}, f32[1,2,16,32,256]{4,3,2,1,0:T(8,128)}, u32[]{:S(2)}) copy-start(f32[1,2,16,32,256]{4,3,2,1,0:T(8,128)} %param.6) | copy-start | bytes 3145732
  1.0 20.6 %collective-permute-start = (f32[2,32,256]{2,1,0:T(8,128)S(1)}, f32[2,32,256]{2,1,0:T(8,128)S(1)}, u32[]{:S(2)}, u32[]{:S(2)}) collective-permute-start(f32[2,32,256]{2,1,0:T(8,128)S(1)} %get-tuple-element.148), channel_id=1, source_target_pairs={{0,4},{4,8},{8,12},{12,16},{16,20},{20,24},{24,28},{28,32},{32,36}... | collective-permute-start | bytes 196616 | tf_op jit(solution)/shard_map/ppermute | solution.py:92
  3.2 18.4 %collective-permute-start.1 = (f32[2,32,256]{2,1,0:T(8,128)S(1)}, f32[2,32,256]{2,1,0:T(8,128)S(1)}, u32[]{:S(2)}, u32[]{:S(2)}) collective-permute-start(f32[2,32,256]{2,1,0:T(8,128)S(1)} %get-tuple-element.147), channel_id=1, source_target_pairs={{0,60},{4,0},{8,4},{12,8},{16,12},{20,16},{24,20},{28,24},{32,28},... | collective-permute-start | bytes 196616 | tf_op jit(solution)/shard_map/ppermute | solution.py:92
  12.7 8.8 %copy-start.1 = (f32[16,32,256]{2,1,0:T(8,128)S(1)}, f32[16,32,256]{2,1,0:T(8,128)}, u32[]{:S(2)}) copy-start(f32[16,32,256]{2,1,0:T(8,128)} %feed.3) | copy-start | bytes 1572868
  12.7 8.8 %copy-start.2 = (f32[16,32,256]{2,1,0:T(8,128)S(1)}, f32[16,32,256]{2,1,0:T(8,128)}, u32[]{:S(2)}) copy-start(f32[16,32,256]{2,1,0:T(8,128)} %kill.3) | copy-start | bytes 1572868
  12.7 11.3 %collective-permute-start.4 = (f32[2,8,32,256]{3,2,1,0:T(8,128)}, f32[2,8,32,256]{3,2,1,0:T(8,128)S(1)}, u32[]{:S(2)}, u32[]{:S(2)}) collective-permute-start(f32[2,8,32,256]{3,2,1,0:T(8,128)} %get-tuple-element.144), channel_id=1, source_target_pairs={{192,128},{193,129},{194,130},{195,131},{196,132},{197,133},{198,1... | collective-permute-start | bytes 1572872 | tf_op jit(solution)/shard_map/ppermute | solution.py:467
  13.6 16.8 %collective-permute-start.5 = (f32[2,8,32,256]{3,2,1,0:T(8,128)}, f32[2,8,32,256]{3,2,1,0:T(8,128)S(1)}, u32[]{:S(2)}, u32[]{:S(2)}) collective-permute-start(f32[2,8,32,256]{3,2,1,0:T(8,128)} %get-tuple-element.143), channel_id=1, source_target_pairs={{192,0},{193,1},{194,2},{195,3},{196,4},{197,5},{198,6},{199,7},{2... | collective-permute-start | bytes 1572872 | tf_op jit(solution)/shard_map/ppermute | solution.py:468
  14.9 2.7 %collective-permute-start.2 = (f32[2,16,256]{2,1,0:T(8,128)S(1)}, f32[2,16,256]{2,1,0:T(8,128)S(1)}, u32[]{:S(2)}, u32[]{:S(2)}) collective-permute-start(f32[2,16,256]{2,1,0:T(8,128)S(1)} %bitcast.21), channel_id=1, source_target_pairs={{0,1},{1,2},{2,3},{3,0},{4,5},{5,6},{6,7},{7,4},{8,9},{9,10},{10,1... | collective-permute-start | bytes 98312 | tf_op jit(solution)/shard_map/ppermute | solution.py:92
  17.6 3.9 %collective-permute-start.3 = (f32[2,16,256]{2,1,0:T(8,128)S(1)}, f32[2,16,256]{2,1,0:T(8,128)S(1)}, u32[]{:S(2)}, u32[]{:S(2)}) collective-permute-start(f32[2,16,256]{2,1,0:T(8,128)S(1)} %bitcast.22), channel_id=1, source_target_pairs={{0,3},{1,0},{2,1},{3,2},{4,7},{5,4},{6,5},{7,6},{8,11},{9,8},{10,9... | collective-permute-start | bytes 98312 | tf_op jit(solution)/shard_map/ppermute | solution.py:92
  30.4 6.1 %collective-permute-start.6 = (f32[8,32,256]{2,1,0:T(8,128)S(1)}, f32[8,32,256]{2,1,0:T(8,128)S(1)}, u32[]{:S(2)}, u32[]{:S(2)}) collective-permute-start(f32[8,32,256]{2,1,0:T(8,128)S(1)} %get-tuple-element.80.refs_1_.refs_7_), channel_id=1, source_target_pairs={{0,64},{64,0},{128,192},{192,128},{1,65},{65,1},{129,193},{193,129... | collective-permute-start | bytes 786440 | tf_op jit(solution)/shard_map/ppermute | solution.py:473
  30.4 7.3 %collective-permute-start.7 = (f32[8,32,256]{2,1,0:T(8,128)S(1)}, f32[8,32,256]{2,1,0:T(8,128)S(1)}, u32[]{:S(2)}, u32[]{:S(2)}) collective-permute-start(f32[8,32,256]{2,1,0:T(8,128)S(1)} %get-tuple-element.81.refs_2_.refs_8_), channel_id=1, source_target_pairs={{0,192},{192,0},{64,128},{128,64},{1,193},{193,1},{65,129},{129,65... | collective-permute-start | bytes 786440 | tf_op jit(solution)/shard_map/ppermute | solution.py:474
  37.6 5.2 %collective-permute-start.8 = (f32[8,32,256]{2,1,0:T(8,128)S(1)}, f32[8,32,256]{2,1,0:T(8,128)S(1)}, u32[]{:S(2)}, u32[]{:S(2)}) collective-permute-start(f32[8,32,256]{2,1,0:T(8,128)S(1)} %get-tuple-element.82.refs_1_.refs_7_), channel_id=1, source_target_pairs={{0,64},{64,0},{128,192},{192,128},{1,65},{65,1},{129,193},{193,129... | collective-permute-start | bytes 786440 | tf_op jit(solution)/shard_map/ppermute | solution.py:476
  37.6 6.4 %collective-permute-start.9 = (f32[8,32,256]{2,1,0:T(8,128)S(1)}, f32[8,32,256]{2,1,0:T(8,128)S(1)}, u32[]{:S(2)}, u32[]{:S(2)}) collective-permute-start(f32[8,32,256]{2,1,0:T(8,128)S(1)} %get-tuple-element.83.refs_2_.refs_8_), channel_id=1, source_target_pairs={{0,192},{192,0},{64,128},{128,64},{1,193},{193,1},{65,129},{129,65... | collective-permute-start | bytes 786440 | tf_op jit(solution)/shard_map/ppermute | solution.py:477
  39.2 9.9 %collective-permute-start.16 = (f32[8,32,256]{2,1,0:T(8,128)S(1)}, f32[8,32,256]{2,1,0:T(8,128)S(1)}, u32[]{:S(2)}, u32[]{:S(2)}) collective-permute-start(f32[8,32,256]{2,1,0:T(8,128)S(1)} %get-tuple-element.98), channel_id=1, source_target_pairs={{0,192},{192,0},{64,128},{128,64},{1,193},{193,1},{65,129},{129,65... | collective-permute-start | bytes 786440 | tf_op jit(solution)/shard_map/ppermute | solution.py:483
  41.2 8.3 %copy-start = (f32[256,256]{1,0:T(8,128)S(1)}, f32[256,256]{1,0:T(8,128)}, u32[]{:S(2)}) copy-start(f32[256,256]{1,0:T(8,128)} %constant.17.clone.refs_1_.basis) | copy-start | bytes 786436
  41.2 8.3 %copy-start.3 = (f32[8,256]{1,0:T(8,128)S(1)}, f32[8,256]{1,0:T(8,128)}, u32[]{:S(2)}) copy-start(f32[8,256]{1,0:T(8,128)} %constant.18.clone.refs_2_) | copy-start | bytes 24580
  41.2 8.3 %collective-permute-start.17 = (f32[8,32,256]{2,1,0:T(8,128)S(1)}, f32[8,32,256]{2,1,0:T(8,128)S(1)}, u32[]{:S(2)}, u32[]{:S(2)}) collective-permute-start(f32[8,32,256]{2,1,0:T(8,128)S(1)} %get-tuple-element.99), channel_id=1, source_target_pairs={{0,64},{64,0},{128,192},{192,128},{1,65},{65,1},{129,193},{193,129... | collective-permute-start | bytes 786440 | tf_op jit(solution)/shard_map/ppermute | solution.py:484
  44.8 21.3 %collective-permute-start.10 = (f32[8,32,256]{2,1,0:T(8,128)S(1)}, f32[8,32,256]{2,1,0:T(8,128)S(1)}, u32[]{:S(2)}, u32[]{:S(2)}) collective-permute-start(f32[8,32,256]{2,1,0:T(8,128)S(1)} %get-tuple-element.86), channel_id=1, source_target_pairs={{0,192},{192,0},{64,128},{128,64},{1,193},{193,1},{65,129},{129,65... | collective-permute-start | bytes 786440 | tf_op jit(solution)/shard_map/ppermute | solution.py:483
  45.8 20.3 %collective-permute-start.11 = (f32[8,32,256]{2,1,0:T(8,128)S(1)}, f32[8,32,256]{2,1,0:T(8,128)S(1)}, u32[]{:S(2)}, u32[]{:S(2)}) collective-permute-start(f32[8,32,256]{2,1,0:T(8,128)S(1)} %get-tuple-element.87), channel_id=1, source_target_pairs={{0,64},{64,0},{128,192},{192,128},{1,65},{65,1},{129,193},{193,129... | collective-permute-start | bytes 786440 | tf_op jit(solution)/shard_map/ppermute | solution.py:484
  58.8 18.6 %collective-permute-start.18 = (f32[60,8,256]{2,1,0:T(8,128)S(1)}, f32[60,8,256]{2,1,0:T(8,128)S(1)}, u32[]{:S(2)}, u32[]{:S(2)}) collective-permute-start(f32[60,8,256]{2,1,0:T(8,128)S(1)} %get-tuple-element.101), channel_id=1, source_target_pairs={{0,1},{1,2},{2,3},{3,0},{4,5},{5,6},{6,7},{7,4},{8,9},{9,10},{10,1... | collective-permute-start | bytes 1474568 | tf_op jit(solution)/shard_map/ppermute | solution.py:92
  66.1 12.2 %collective-permute-start.19 = (f32[60,8,256]{2,1,0:T(8,128)S(1)}, f32[60,8,256]{2,1,0:T(8,128)S(1)}, u32[]{:S(2)}, u32[]{:S(2)}) collective-permute-start(f32[60,8,256]{2,1,0:T(8,128)S(1)} %get-tuple-element.102), channel_id=1, source_target_pairs={{0,3},{1,0},{2,1},{3,2},{4,7},{5,4},{6,5},{7,6},{8,11},{9,8},{10,9... | collective-permute-start | bytes 1474568 | tf_op jit(solution)/shard_map/ppermute | solution.py:92
  75.5 11.7 %collective-permute-start.12 = (f32[60,8,256]{2,1,0:T(8,128)S(1)}, f32[60,8,256]{2,1,0:T(8,128)S(1)}, u32[]{:S(2)}, u32[]{:S(2)}) collective-permute-start(f32[60,8,256]{2,1,0:T(8,128)S(1)} %get-tuple-element.89), channel_id=1, source_target_pairs={{0,1},{1,2},{2,3},{3,0},{4,5},{5,6},{6,7},{7,4},{8,9},{9,10},{10,1... | collective-permute-start | bytes 1474568 | tf_op jit(solution)/shard_map/ppermute | solution.py:92
  77.5 21.9 %collective-permute-start.13 = (f32[60,8,256]{2,1,0:T(8,128)S(1)}, f32[60,8,256]{2,1,0:T(8,128)S(1)}, u32[]{:S(2)}, u32[]{:S(2)}) collective-permute-start(f32[60,8,256]{2,1,0:T(8,128)S(1)} %get-tuple-element.90), channel_id=1, source_target_pairs={{0,3},{1,0},{2,1},{3,2},{4,7},{5,4},{6,5},{7,6},{8,11},{9,8},{10,9... | collective-permute-start | bytes 1474568 | tf_op jit(solution)/shard_map/ppermute | solution.py:92
  79.0 26.9 %collective-permute-start.20 = (f32[12,32,256]{2,1,0:T(8,128)S(1)}, f32[12,32,256]{2,1,0:T(8,128)S(1)}, u32[]{:S(2)}, u32[]{:S(2)}) collective-permute-start(f32[12,32,256]{2,1,0:T(8,128)S(1)} %get-tuple-element.104), channel_id=1, source_target_pairs={{0,4},{4,8},{8,12},{12,16},{16,20},{20,24},{24,28},{28,32},{32,36}... | collective-permute-start | bytes 1179656 | tf_op jit(solution)/shard_map/ppermute | solution.py:92
  79.1 26.8 %collective-permute-start.21 = (f32[12,32,256]{2,1,0:T(8,128)S(1)}, f32[12,32,256]{2,1,0:T(8,128)S(1)}, u32[]{:S(2)}, u32[]{:S(2)}) collective-permute-start(f32[12,32,256]{2,1,0:T(8,128)S(1)} %get-tuple-element.105), channel_id=1, source_target_pairs={{0,60},{4,0},{8,4},{12,8},{16,12},{20,16},{24,20},{28,24},{32,28},... | collective-permute-start | bytes 1179656 | tf_op jit(solution)/shard_map/ppermute | solution.py:92
  100.1 15.3 %collective-permute-start.14 = (f32[12,32,256]{2,1,0:T(8,128)S(1)}, f32[12,32,256]{2,1,0:T(8,128)S(1)}, u32[]{:S(2)}, u32[]{:S(2)}) collective-permute-start(f32[12,32,256]{2,1,0:T(8,128)S(1)} %get-tuple-element.92), channel_id=1, source_target_pairs={{0,4},{4,8},{8,12},{12,16},{16,20},{20,24},{24,28},{28,32},{32,36}... | collective-permute-start | bytes 1179656 | tf_op jit(solution)/shard_map/ppermute | solution.py:92
  100.2 20.7 %collective-permute-start.15 = (f32[12,32,256]{2,1,0:T(8,128)S(1)}, f32[12,32,256]{2,1,0:T(8,128)S(1)}, u32[]{:S(2)}, u32[]{:S(2)}) collective-permute-start(f32[12,32,256]{2,1,0:T(8,128)S(1)} %get-tuple-element.93), channel_id=1, source_target_pairs={{0,60},{4,0},{8,4},{12,8},{16,12},{20,16},{24,20},{28,24},{32,28},... | collective-permute-start | bytes 1179656 | tf_op jit(solution)/shard_map/ppermute | solution.py:92
  122.6 13.9 %collective-permute-start.22 = (f32[2,32,256]{2,1,0:T(8,128)S(1)}, f32[2,32,256]{2,1,0:T(8,128)S(1)}, u32[]{:S(2)}, u32[]{:S(2)}) collective-permute-start(f32[2,32,256]{2,1,0:T(8,128)S(1)} %get-tuple-element.107), channel_id=1, source_target_pairs={{0,4},{4,8},{8,12},{12,16},{16,20},{20,24},{24,28},{28,32},{32,36}... | collective-permute-start | bytes 196616 | tf_op jit(solution)/shard_map/ppermute | solution.py:92
  122.7 13.9 %collective-permute-start.23 = (f32[2,32,256]{2,1,0:T(8,128)S(1)}, f32[2,32,256]{2,1,0:T(8,128)S(1)}, u32[]{:S(2)}, u32[]{:S(2)}) collective-permute-start(f32[2,32,256]{2,1,0:T(8,128)S(1)} %get-tuple-element.108), channel_id=1, source_target_pairs={{0,60},{4,0},{8,4},{12,8},{16,12},{20,16},{24,20},{28,24},{32,28},... | collective-permute-start | bytes 196616 | tf_op jit(solution)/shard_map/ppermute | solution.py:92
  129.0 5.2 %collective-permute-start.24 = (f32[2,16,256]{2,1,0:T(8,128)S(1)}, f32[2,16,256]{2,1,0:T(8,128)S(1)}, u32[]{:S(2)}, u32[]{:S(2)}) collective-permute-start(f32[2,16,256]{2,1,0:T(8,128)S(1)} %get-tuple-element.109), channel_id=1, source_target_pairs={{0,1},{1,2},{2,3},{3,0},{4,5},{5,6},{6,7},{7,4},{8,9},{9,10},{10,1... | collective-permute-start | bytes 98312 | tf_op jit(solution)/shard_map/ppermute | solution.py:92
  133.2 3.3 %collective-permute-start.25 = (f32[2,16,256]{2,1,0:T(8,128)S(1)}, f32[2,16,256]{2,1,0:T(8,128)S(1)}, u32[]{:S(2)}, u32[]{:S(2)}) collective-permute-start(f32[2,16,256]{2,1,0:T(8,128)S(1)} %get-tuple-element.110), channel_id=1, source_target_pairs={{0,3},{1,0},{2,1},{3,2},{4,7},{5,4},{6,5},{7,6},{8,11},{9,8},{10,9... | collective-permute-start | bytes 98312 | tf_op jit(solution)/shard_map/ppermute | solution.py:92
  139.0 7.3 %collective-permute-start.26 = (f32[8,32,256]{2,1,0:T(8,128)S(1)}, f32[8,32,256]{2,1,0:T(8,128)S(1)}, u32[]{:S(2)}, u32[]{:S(2)}) collective-permute-start(f32[8,32,256]{2,1,0:T(8,128)S(1)} %get-tuple-element.117.refs_1_.refs_7_), channel_id=1, source_target_pairs={{0,64},{64,0},{128,192},{192,128},{1,65},{65,1},{129,193},{193,129... | collective-permute-start | bytes 786440 | tf_op jit(solution)/shard_map/ppermute | solution.py:473
  139.3 8.4 %collective-permute-start.27 = (f32[8,32,256]{2,1,0:T(8,128)S(1)}, f32[8,32,256]{2,1,0:T(8,128)S(1)}, u32[]{:S(2)}, u32[]{:S(2)}) collective-permute-start(f32[8,32,256]{2,1,0:T(8,128)S(1)} %get-tuple-element.118.refs_2_.refs_8_), channel_id=1, source_target_pairs={{0,192},{192,0},{64,128},{128,64},{1,193},{193,1},{65,129},{129,65... | collective-permute-start | bytes 786440 | tf_op jit(solution)/shard_map/ppermute | solution.py:474
  147.7 8.0 %collective-permute-start.28 = (f32[8,32,256]{2,1,0:T(8,128)S(1)}, f32[8,32,256]{2,1,0:T(8,128)S(1)}, u32[]{:S(2)}, u32[]{:S(2)}) collective-permute-start(f32[8,32,256]{2,1,0:T(8,128)S(1)} %get-tuple-element.119.refs_1_.refs_7_), channel_id=1, source_target_pairs={{0,64},{64,0},{128,192},{192,128},{1,65},{65,1},{129,193},{193,129... | collective-permute-start | bytes 786440 | tf_op jit(solution)/shard_map/ppermute | solution.py:476
  147.7 8.9 %collective-permute-start.29 = (f32[8,32,256]{2,1,0:T(8,128)S(1)}, f32[8,32,256]{2,1,0:T(8,128)S(1)}, u32[]{:S(2)}, u32[]{:S(2)}) collective-permute-start(f32[8,32,256]{2,1,0:T(8,128)S(1)} %get-tuple-element.120.refs_2_.refs_8_), channel_id=1, source_target_pairs={{0,192},{192,0},{64,128},{128,64},{1,193},{193,1},{65,129},{129,65... | collective-permute-start | bytes 786440 | tf_op jit(solution)/shard_map/ppermute | solution.py:477
  149.3 13.0 %collective-permute-start.36 = (f32[8,32,256]{2,1,0:T(8,128)S(1)}, f32[8,32,256]{2,1,0:T(8,128)S(1)}, u32[]{:S(2)}, u32[]{:S(2)}) collective-permute-start(f32[8,32,256]{2,1,0:T(8,128)S(1)} %get-tuple-element.135), channel_id=1, source_target_pairs={{0,192},{192,0},{64,128},{128,64},{1,193},{193,1},{65,129},{129,65... | collective-permute-start | bytes 786440 | tf_op jit(solution)/shard_map/ppermute | solution.py:483
  151.2 11.1 %collective-permute-start.37 = (f32[8,32,256]{2,1,0:T(8,128)S(1)}, f32[8,32,256]{2,1,0:T(8,128)S(1)}, u32[]{:S(2)}, u32[]{:S(2)}) collective-permute-start(f32[8,32,256]{2,1,0:T(8,128)S(1)} %get-tuple-element.136), channel_id=1, source_target_pairs={{0,64},{64,0},{128,192},{192,128},{1,65},{65,1},{129,193},{193,129... | collective-permute-start | bytes 786440 | tf_op jit(solution)/shard_map/ppermute | solution.py:484
  157.4 16.4 %collective-permute-start.30 = (f32[8,32,256]{2,1,0:T(8,128)S(1)}, f32[8,32,256]{2,1,0:T(8,128)S(1)}, u32[]{:S(2)}, u32[]{:S(2)}) collective-permute-start(f32[8,32,256]{2,1,0:T(8,128)S(1)} %get-tuple-element.123), channel_id=1, source_target_pairs={{0,192},{192,0},{64,128},{128,64},{1,193},{193,1},{65,129},{129,65... | collective-permute-start | bytes 786440 | tf_op jit(solution)/shard_map/ppermute | solution.py:483
  158.6 15.2 %collective-permute-start.31 = (f32[8,32,256]{2,1,0:T(8,128)S(1)}, f32[8,32,256]{2,1,0:T(8,128)S(1)}, u32[]{:S(2)}, u32[]{:S(2)}) collective-permute-start(f32[8,32,256]{2,1,0:T(8,128)S(1)} %get-tuple-element.124), channel_id=1, source_target_pairs={{0,64},{64,0},{128,192},{192,128},{1,65},{65,1},{129,193},{193,129... | collective-permute-start | bytes 786440 | tf_op jit(solution)/shard_map/ppermute | solution.py:484
  171.7 13.4 %collective-permute-start.38 = (f32[60,8,256]{2,1,0:T(8,128)S(1)}, f32[60,8,256]{2,1,0:T(8,128)S(1)}, u32[]{:S(2)}, u32[]{:S(2)}) collective-permute-start(f32[60,8,256]{2,1,0:T(8,128)S(1)} %get-tuple-element.138), channel_id=1, source_target_pairs={{0,1},{1,2},{2,3},{3,0},{4,5},{5,6},{6,7},{7,4},{8,9},{9,10},{10,1... | collective-permute-start | bytes 1474568 | tf_op jit(solution)/shard_map/ppermute | solution.py:92
  173.8 12.3 %collective-permute-start.39 = (f32[60,8,256]{2,1,0:T(8,128)S(1)}, f32[60,8,256]{2,1,0:T(8,128)S(1)}, u32[]{:S(2)}, u32[]{:S(2)}) collective-permute-start(f32[60,8,256]{2,1,0:T(8,128)S(1)} %get-tuple-element.139), channel_id=1, source_target_pairs={{0,3},{1,0},{2,1},{3,2},{4,7},{5,4},{6,5},{7,6},{8,11},{9,8},{10,9... | collective-permute-start | bytes 1474568 | tf_op jit(solution)/shard_map/ppermute | solution.py:92
  183.2 11.4 %collective-permute-start.32 = (f32[60,8,256]{2,1,0:T(8,128)S(1)}, f32[60,8,256]{2,1,0:T(8,128)S(1)}, u32[]{:S(2)}, u32[]{:S(2)}) collective-permute-start(f32[60,8,256]{2,1,0:T(8,128)S(1)} %get-tuple-element.126), channel_id=1, source_target_pairs={{0,1},{1,2},{2,3},{3,0},{4,5},{5,6},{6,7},{7,4},{8,9},{9,10},{10,1... | collective-permute-start | bytes 1474568 | tf_op jit(solution)/shard_map/ppermute | solution.py:92
  185.0 25.4 %collective-permute-start.33 = (f32[60,8,256]{2,1,0:T(8,128)S(1)}, f32[60,8,256]{2,1,0:T(8,128)S(1)}, u32[]{:S(2)}, u32[]{:S(2)}) collective-permute-start(f32[60,8,256]{2,1,0:T(8,128)S(1)} %get-tuple-element.127), channel_id=1, source_target_pairs={{0,3},{1,0},{2,1},{3,2},{4,7},{5,4},{6,5},{7,6},{8,11},{9,8},{10,9... | collective-permute-start | bytes 1474568 | tf_op jit(solution)/shard_map/ppermute | solution.py:92
  186.8 30.0 %collective-permute-start.40 = (f32[12,32,256]{2,1,0:T(8,128)S(1)}, f32[12,32,256]{2,1,0:T(8,128)S(1)}, u32[]{:S(2)}, u32[]{:S(2)}) collective-permute-start(f32[12,32,256]{2,1,0:T(8,128)S(1)} %get-tuple-element.141), channel_id=1, source_target_pairs={{0,4},{4,8},{8,12},{12,16},{16,20},{20,24},{24,28},{28,32},{32,36}... | collective-permute-start | bytes 1179656 | tf_op jit(solution)/shard_map/ppermute | solution.py:92
  186.9 30.0 %collective-permute-start.41 = (f32[12,32,256]{2,1,0:T(8,128)S(1)}, f32[12,32,256]{2,1,0:T(8,128)S(1)}, u32[]{:S(2)}, u32[]{:S(2)}) collective-permute-start(f32[12,32,256]{2,1,0:T(8,128)S(1)} %get-tuple-element.142), channel_id=1, source_target_pairs={{0,60},{4,0},{8,4},{12,8},{16,12},{20,16},{24,20},{28,24},{32,28},... | collective-permute-start | bytes 1179656 | tf_op jit(solution)/shard_map/ppermute | solution.py:92
  211.1 22.3 %collective-permute-start.34 = (f32[12,32,256]{2,1,0:T(8,128)S(1)}, f32[12,32,256]{2,1,0:T(8,128)S(1)}, u32[]{:S(2)}, u32[]{:S(2)}) collective-permute-start(f32[12,32,256]{2,1,0:T(8,128)S(1)} %get-tuple-element.129), channel_id=1, source_target_pairs={{0,4},{4,8},{8,12},{12,16},{16,20},{20,24},{24,28},{28,32},{32,36}... | collective-permute-start | bytes 1179656 | tf_op jit(solution)/shard_map/ppermute | solution.py:92
  211.2 22.5 %collective-permute-start.35 = (f32[12,32,256]{2,1,0:T(8,128)S(1)}, f32[12,32,256]{2,1,0:T(8,128)S(1)}, u32[]{:S(2)}, u32[]{:S(2)}) collective-permute-start(f32[12,32,256]{2,1,0:T(8,128)S(1)} %get-tuple-element.130), channel_id=1, source_target_pairs={{0,60},{4,0},{8,4},{12,8},{16,12},{20,16},{24,20},{28,24},{32,28},... | collective-permute-start | bytes 1179656 | tf_op jit(solution)/shard_map/ppermute | solution.py:92

commit v4 on v3

v4 whole, which is shorter than its diff:
```python
import jax
import jax.numpy as jnp
import numpy as np
from jax import lax
from jax.experimental import pallas as pl
from jax.experimental.pallas import tpu as pltpu
from jax.sharding import PartitionSpec as P


SWEEPS = 2
JACOBI = 12


radau_points = [0.088587959512704, 0.409466864440735, 0.787659461760847, 1.0]
time_step = 4.0
diffusion_values = [1.0, 0.5]

XB, YB, ZB = 16, 32, 256
HALF = XB // 2
LANES = 128
PLANES = XB + 2 * (JACOBI + 1)
FIRST = JACOBI + 1
ROW0 = 24
ROWS = YB + 2 * ROW0
WHOLE = (FIRST - 4, XB + 8)


def shared_rows():
    pieces = []
    tile = WHOLE[1]
    for out in range(5, 12):
        pieces.append((tile, 0, FIRST - out, 1, JACOBI - out))
        pieces.append((tile, JACOBI - out, FIRST + XB - 1 + 16 - out, 1, out - 4))
        tile += 1
    thick = [FIRST + p for p in range(XB)]
    for left, right in zip(thick[::2], thick[1::2]):
        pieces.append((tile, 0, left, 9, 4))
        pieces.append((tile, 4, right, 9, 4))
        tile += 1
    for side in (lambda d: FIRST - d, lambda d: FIRST + XB - 1 + d):
        place = 0
        for out in range(1, 4):
            pieces.append((tile, place, side(out), 9, 4 - out))
            place += 4 - out
        tile += 1
    return pieces, tile


PIECES, STRIP = shared_rows()


def collocation():
    count = len(radau_points)
    table = []
    for _ in range(count):
        table.append([0.0] * count)
    for column in range(count):
        poly = [1.0]
        denom = 1.0
        for other in range(count):
            if other != column:
                longer = [0.0] * (len(poly) + 1)
                for place in range(len(poly)):
                    longer[place + 1] = longer[place + 1] + poly[place]
                    longer[place] = longer[place] - radau_points[other] * poly[place]
                poly = longer
                denom = denom * (radau_points[column] - radau_points[other])
        for row in range(count):
            point = radau_points[row]
            total = 0.0
            for place in range(len(poly)):
                total = total + poly[place] * point ** (place + 1) / (place + 1)
            table[row][column] = total / denom
    return table


def node_table():
    q = collocation()
    rows = []
    for n in range(4):
        a, b = n ^ 1, 3 - n
        common = [
            time_step * q[n][n], time_step * q[n][a], time_step * q[n][b],
            time_step * q[b][n], time_step * q[b][a],
            time_step * q[a][n], time_step * q[a][b],
            1.0 if n == 3 else 0.0,
        ]
        row = []
        for s, d in enumerate(diffusion_values):
            c = time_step * radau_points[n] * d
            row.append(common + [-c, c / (1.0 + 6.0 * c), 1.0 / (1.0 + 6.0 * c), d, float(s)])
        rows.append(row)
    return rows


def fourier():
    wave = np.arange(ZB)
    sine = wave > ZB // 2
    wave = np.where(sine, wave - ZB // 2, wave)
    norm = np.sqrt(np.where((wave == 0) | (wave == ZB // 2), 1.0, 2.0) / ZB)
    angle = 2.0 * np.pi * ((np.arange(0, ZB, 8)[:, None] * wave) % ZB) / ZB
    wide = norm * np.stack(
        [
            np.where(sine, np.sin(angle), np.cos(angle)),
            np.where(sine, np.cos(angle), -np.sin(angle)),
        ]
    )
    angle = 2.0 * np.pi * (np.arange(8)[:, None] * wave) / ZB
    near = np.stack([np.cos(angle), np.sin(angle)])
    sums = np.broadcast_to(2.0 * np.cos(2.0 * np.pi * wave / ZB), (8, ZB))
    return [v.astype(np.float32) for v in (wide, near, sums)]


def ring(count, step):
    return [(i, (i + step) % count) for i in range(count)]


def shifted(array, axis, step):
    return lax.ppermute(array, axis, ring(lax.axis_size(axis), step))


def call(kernel, outs, args, scratch=(), flops=1_000_000):
    vmem = pl.BlockSpec(memory_space=pltpu.VMEM)
    smem = pl.BlockSpec(memory_space=pltpu.SMEM)
    return pl.pallas_call(
        kernel,
        out_shape=tuple(outs),
        in_specs=[smem] + [vmem] * (len(args) - 1),
        out_specs=(vmem,) * len(outs),
        scratch_shapes=list(scratch),
        compiler_params=pltpu.CompilerParams(vmem_limit_bytes=24 * 2**20),
        cost_estimate=pl.CostEstimate(flops=flops, bytes_accessed=1_000_000, transcendentals=0),
    )(args[0], *(pltpu.with_memory_space_constraint(a, pltpu.VMEM) for a in args[1:]))


def local(*shape):
    return pltpu.VMEM(shape, jnp.float32)


def z_sum(c0, c1, lane):
    first, last = lane == 0, lane == LANES - 1
    up0, up1 = pltpu.roll(c0, 1, 1), pltpu.roll(c1, 1, 1)
    dn0, dn1 = pltpu.roll(c0, LANES - 1, 1), pltpu.roll(c1, LANES - 1, 1)
    low = jnp.where(first, up1, up0) + jnp.where(last, dn1, dn0)
    high = jnp.where(first, up0, up1) + jnp.where(last, dn0, dn1)
    return low, high


def force_kernel(species, sc, xu, xv, xlo, xhi, ylo, yhi, feed, kill, fa, fb, da, db, work):
    own = (xu, xv)[species]
    if len(xlo.shape) == 3:
        xlo, xhi, ylo, yhi = (edge.at[species] for edge in (xlo, xhi, ylo, yhi))

    def fill(p, carry):
        for h in range(2):
            lanes = slice(h * LANES, (h + 1) * LANES)
            work[p + 1, h, 8:8 + YB, :] = own[p, :, lanes]
        return carry

    lax.fori_loop(0, XB, fill, 0)
    for h in range(2):
        lanes = slice(h * LANES, (h + 1) * LANES)
        work[0, h, 8:8 + YB, :] = xlo[:, lanes]
        work[XB + 1, h, 8:8 + YB, :] = xhi[:, lanes]
        for p in range(XB):
            work[p + 1, h, 7:8, :] = ylo[p:p + 1, lanes]
            work[p + 1, h, 8 + YB:9 + YB, :] = yhi[p:p + 1, lanes]
    lane = lax.broadcasted_iota(jnp.int32, (8, LANES), 1)

    def run(base, f, d):
        def plane(i, carry):
            p = base + i
            for t in range(YB // 8):
                r = 8 + 8 * t
                out = slice(8 * t, 8 * t + 8)
                c = [work[p + 1, h, r:r + 8, :] for h in range(2)]
                z = z_sum(c[0], c[1], lane)
                for h in range(2):
                    lanes = slice(h * LANES, (h + 1) * LANES)
                    total = work[p, h, r:r + 8, :] + work[p + 2, h, r:r + 8, :]
                    total = total + work[p + 1, h, r - 1:r + 7, :]
                    total = total + work[p + 1, h, r + 1:r + 9, :]
                    lap = total + z[h] - 6.0 * c[h]
                    fr = feed[p, out, lanes]
                    u, v = xu[p, out, lanes], xv[p, out, lanes]
                    uvv = u * v * v
                    if species == 0:
                        react = fr * (1.0 - u) - uvv
                    else:
                        react = uvv - (fr + kill[p, out, lanes]) * v
                    f[i, out, lanes] = sc[11] * lap + react
                    d[i, out, lanes] = sc[8] * lap
            return carry

        lax.fori_loop(0, HALF, plane, 0)

    run(0, fa, da)
    run(HALF, fb, db)


def edges_of(x, xfirst, xlast, yfirst, ylast):
    xfirst[...] = x[0]
    xlast[...] = x[XB - 1]
    for p in range(XB):
        yfirst[p:p + 1, :] = x[p, 0:1, :]
        ylast[p:p + 1, :] = x[p, YB - 1:YB, :]


def prepare_kernel(sc, x, wide, near, xu, xv, ha, hb, basis, *edges):
    for a in range(ZB // 8):
        rows = wide[0, a:a + 1, :] * near[0] + wide[1, a:a + 1, :] * near[1]
        basis[8 * a:8 * a + 8, :] = rows
    for s, dst in enumerate((xu, xv)):
        edges_of(x.at[s], *(edge.at[s] for edge in edges))

        def plane(p, carry, s=s, dst=dst):
            dst[p] = x[s, p]
            dst[HALF + p] = x[s, HALF + p]
            ha[s, p] = x[s, p]
            hb[s, p] = x[s, HALF + p]
            return carry

        lax.fori_loop(0, HALF, plane, 0)


EDGES = [(YB, ZB)] * 2 + [(XB, ZB)] * 2


def prepare(*args):
    outs = [(XB, YB, ZB)] * 2 + [(2, HALF, YB, ZB)] * 2 + [(ZB, ZB)]
    outs += [(2, *e) for e in EDGES]
    return call(prepare_kernel, [local(*o) for o in outs], args)


def forces(species, *args):
    return call(
        lambda *refs: force_kernel(species, *refs),
        [local(HALF, YB, ZB)] * 4,
        args,
        [pltpu.VMEM((XB + 2, 2, YB + 16, LANES), jnp.float32)],
        flops=4_000_000,
    )


def partial_kernel(sc, fa, fb, ga, gb, na, nb, x0, sa, sb):
    species = sc[12].astype(jnp.int32)

    def plane(p, carry):
        low = na[species, p] + sc[7] * x0[p]
        high = nb[species, p] + sc[7] * x0[HALF + p]
        sa[p] = sc[3] * fa[p] + sc[4] * ga[p] + low
        sb[p] = sc[5] * fb[p] + sc[6] * gb[p] + high
        return carry

    lax.fori_loop(0, HALF, plane, 0)


def partial(*args):
    return call(partial_kernel, [local(HALF, YB, ZB)] * 2, args)


def jacobi_kernel(sc, basis, sums, x, x0, na, nb, fa, fb, ga, gb, da, db, ra, rb,
                  core, yhi, ylo, one, two, bs, right):
    spread, scale = sc[9], sc[10]
    species = sc[12].astype(jnp.int32)
    zero = jnp.zeros((ROWS, LANES), jnp.float32)

    def clear(p, carry):
        for h in range(2):
            one[p, h] = zero
            two[p, h] = zero
            bs[p, h] = zero[:YB]
        return carry

    lax.fori_loop(0, PLANES, clear, 0)

    def modes(values):
        flat = values.reshape(-1, ZB)
        done = jnp.dot(flat, basis[...], precision=lax.Precision.HIGHEST,
                       preferred_element_type=jnp.float32)
        return done.reshape(values.shape)

    def gather(half, f, g, d, n, recv, weight):
        def plane(i, carry):
            own = sc[0] * f[i] + sc[weight] * g[i] + d[i]
            own = own + (n[species, i] + sc[7] * x0[half * HALF + i])
            right[half * HALF + i] = own + recv[i]
            return carry

        lax.fori_loop(0, HALF, plane, 0)

    gather(0, fa, ga, da, na, ra, 1)
    gather(1, fb, gb, db, nb, rb, 2)

    def fill(i, carry):
        p = i * 4
        xh = modes(x[pl.ds(p, 4)])
        bh = modes(right[pl.ds(p, 4)])
        for h in range(2):
            lanes = slice(h * LANES, (h + 1) * LANES)
            one[pl.ds(FIRST + p, 4), h, ROW0:ROW0 + YB, :] = xh[:, :, lanes]
            bs[pl.ds(FIRST + p, 4), h] = scale * bh[:, :, lanes]
        return carry

    lax.fori_loop(0, XB // 4, fill, 0)
    turned = [spread * sums[:, h * LANES:(h + 1) * LANES] for h in range(2)]

    def one_plane(src, dst, p, group, carry):
        count = 2 * len(group)
        before, here = carry[:count], carry[count:]
        after = []
        for t in group:
            r = ROW0 + 8 * t
            after += [src[p + 1, h, r:r + 8, :] for h in range(2)]
        for j, t in enumerate(group):
            r = ROW0 + 8 * t
            for h in range(2):
                i = 2 * j + h
                total = before[i] + after[i]
                total = total + (src[p, h, r - 1:r + 7, :] + src[p, h, r + 1:r + 9, :])
                new = spread * total + turned[h] * here[i]
                if 0 <= t < YB // 8:
                    new = new + bs[p, h, 8 * t:8 * t + 8, :]
                dst[p, h, r:r + 8, :] = new
        return (*here, *after)

    def turn(src, dst, k, tiles):
        wide = (k + 1) // 2
        first = FIRST - 2 * wide
        span = list(range(-tiles, YB // 8 + tiles))
        for group in (span[:len(span) // 2], span[len(span) // 2:]):

            def step(i, carry, group=group):
                for j in range(4):
                    carry = one_plane(src, dst, first + 4 * i + j, group, carry)
                return carry

            carry = (jnp.zeros((8, LANES), jnp.float32),) * (4 * len(group))
            lax.fori_loop(0, XB // 4 + wide, step, carry)

    def pair(tiles):
        def run(i, carry):
            turn(one, two, 2 * i + 1, tiles)
            turn(two, one, 2 * i + 2, tiles)
            return carry

        return run

    lax.fori_loop(0, 4, pair(1), 0)
    lax.fori_loop(4, JACOBI // 2, pair(2), 0)

    def give(p, carry):
        for h in range(2):
            lanes = slice(h * LANES, (h + 1) * LANES)
            core[p, :, lanes] = one[p + 1, h, ROW0:ROW0 + YB, :]
        return carry

    lax.fori_loop(0, XB + 2 * JACOBI, give, 0)

    def whole(i, carry):
        for h in range(2):
            lanes = slice(h * LANES, (h + 1) * LANES)
            yhi[i, :, lanes] = one[WHOLE[0] + i, h, ROW0 + YB:ROW0 + YB + 8, :]
            ylo[i, :, lanes] = one[WHOLE[0] + i, h, ROW0 - 8:ROW0, :]
        return carry

    lax.fori_loop(0, WHOLE[1], whole, 0)
    for tile, place, p, row, count in PIECES:
        top, low = ROW0 + YB - 1 + row, ROW0 - row - count + 1
        for h in range(2):
            lanes = slice(h * LANES, (h + 1) * LANES)
            yhi[tile, place:place + count, lanes] = one[p, h, top:top + count, :]
            ylo[tile, place:place + count, lanes] = one[p, h, low:low + count, :]


def jacobi(*args):
    return call(
        jacobi_kernel,
        [local(XB + 2 * JACOBI, YB, ZB)] + [local(STRIP, 8, ZB)] * 2,
        args,
        [
            pltpu.VMEM((PLANES, 2, ROWS, LANES), jnp.float32),
            pltpu.VMEM((PLANES, 2, ROWS, LANES), jnp.float32),
            pltpu.VMEM((PLANES, 2, YB, LANES), jnp.float32),
            pltpu.VMEM((XB, YB, ZB), jnp.float32),
        ],
        flops=60_000_000,
    )


def gather_kernel(sc, core, low, high, xlo, xhi, center):
    def part(p):
        if p < JACOBI:
            return xlo, p
        if p < JACOBI + XB:
            return center, p - JACOBI
        return xhi, p - JACOBI - XB

    for p in range(XB + 2 * JACOBI):
        dst, q = part(p)
        whole = p + 1 - WHOLE[0]
        if 0 <= whole < WHOLE[1]:
            dst[q, :8, :] = core[p, :8, :] + low[whole]
            dst[q, 8:YB - 8, :] = core[p, 8:YB - 8, :]
            dst[q, YB - 8:, :] = core[p, YB - 8:, :] + high[whole]
        else:
            dst[q] = core[p]
    for tile, place, p, row, count in PIECES:
        dst, q = part(p - 1)
        end = YB - row + 1
        dst[q, row - 1:row - 1 + count, :] += low[tile, place:place + count, :]
        dst[q, end - count:end, :] += high[tile, place:place + count, :]


def gathered(*args):
    return call(gather_kernel, [local(JACOBI, YB, ZB)] * 2 + [local(XB, YB, ZB)], args)


def back(basis, c, low, high, total, give):
    gap = XB - JACOBI

    def add(p, carry):
        total[p] = c[p]
        return carry

    def add_low(p, carry):
        total[p] += low[p]
        return carry

    def add_high(p, carry):
        total[gap + p] += high[p]
        return carry

    lax.fori_loop(0, XB, add, 0)
    lax.fori_loop(0, JACOBI, add_low, 0)
    lax.fori_loop(0, JACOBI, add_high, 0)

    def turn(i, carry):
        flat = total[pl.ds(4 * i, 4)].reshape(4 * YB, ZB)
        done = lax.dot_general(flat, basis[...], (((1,), (1,)), ((), ())),
                               precision=lax.Precision.HIGHEST,
                               preferred_element_type=jnp.float32)
        give(4 * i, done.reshape(4, YB, ZB))
        return carry

    lax.fori_loop(0, XB // 4, turn, 0)


def middle_kernel(sc, basis, c, low, high, out, xfirst, xlast, yfirst, ylast, total):

    def give(p, value):
        out[pl.ds(p, 4)] = value

    back(basis, c, low, high, total, give)
    edges_of(out, xfirst, xlast, yfirst, ylast)


def last_kernel(sc, basis, c, low, high, xu, out, total):
    def give(p, value):
        out[1, pl.ds(p, 4)] = value

    def copy(p, carry):
        out[0, p] = xu[p]
        return carry

    lax.fori_loop(0, XB, copy, 0)
    back(basis, c, low, high, total, give)


TOTAL = [pltpu.VMEM((XB, YB, ZB), jnp.float32)]


def middle(*args):
    outs = [local(*o) for o in [(XB, YB, ZB)] + EDGES]
    return call(middle_kernel, outs, args, TOTAL)


def last(*args):
    outs = [jax.ShapeDtypeStruct((2, XB, YB, ZB), jnp.float32)]
    return call(last_kernel, outs, args, TOTAL)[0]


PAIR_A = [(0, 1), (1, 0), (2, 3), (3, 2)]
PAIR_B = [(0, 3), (3, 0), (1, 2), (2, 1)]


def body(previous, feed_rate, kill_rate):
    sc = jnp.asarray(node_table(), jnp.float32)[lax.axis_index("node")]
    wide, near, sums = map(jnp.asarray, fourier())
    hold = lax.optimization_barrier
    xu, xv, ha, hb, basis, *edges = prepare(sc[0], previous[0], wide, near)
    x0 = (xu, xv)
    na = lax.ppermute(ha, "node", [(3, 2)])
    nb = lax.ppermute(hb, "node", [(3, 0)])

    def halos_of(xfirst, xlast, yfirst, ylast):
        return (
            shifted(xlast, "sx", 1),
            shifted(xfirst, "sx", -1),
            shifted(ylast, "sy", 1),
            shifted(yfirst, "sy", -1),
        )

    for sweep in range(SWEEPS):
        more = sweep + 1 < SWEEPS
        xs = (xu, xv)
        if sweep == 0:
            halos = halos_of(*edges)
            fs = [forces(s, sc[s], *xs, *halos, feed_rate, kill_rate) for s in range(2)]
        else:
            fs = [forces(0, sc[0], *xs, *halos_of(*edges[0]), feed_rate, kill_rate)]
            *late, _, _ = hold((*edges[1], *fs[0][:2]))
            halos = halos_of(*late)
            fs.append(forces(1, sc[1], *xs, *halos, feed_rate, kill_rate))
        edges = []
        for s in range(2):
            fa, fb, da, db = fs[s]
            ga = lax.ppermute(fa, "node", PAIR_A)
            gb = lax.ppermute(fb, "node", PAIR_B)
            pa, pb = partial(sc[s], fa, fb, ga, gb, na, nb, x0[s])
            if s == 0:
                va, vb, _, _ = hold((*fs[1][:2], pa, pb))
                fs[1] = (va, vb, *fs[1][2:])
            ra = lax.ppermute(pa, "node", PAIR_B)
            rb = lax.ppermute(pb, "node", PAIR_A)
            if s == 1:
                ra, rb, _, _ = hold((ra, rb, left, right))
            core, up, down = jacobi(
                sc[s], basis, sums, xs[s], x0[s], na, nb, fa, fb, ga, gb, da, db, ra, rb
            )
            low = shifted(up, "sy", 1)
            high = shifted(down, "sy", -1)
            left, right, center = gathered(sc[0], core, low, high)
            low = shifted(right, "sx", 1)
            high = shifted(left, "sx", -1)
            parts = (sc[0], basis, center, low, high)
            if s == 0:
                xu, *rest = middle(*parts)
            elif more:
                xv, *rest = middle(*parts)
            edges.append(rest)
    return last(*parts, xu)[None]


def solution(mesh):
    return jax.shard_map(
        body,
        mesh=mesh,
        in_specs=(P("node", None, "sx", "sy", None), P("sx", "sy", None), P("sx", "sy", None)),
        out_specs=P("node", None, "sx", "sy", None),
        check_vma=False,
    )
```

time: 237 us -> 247 us (1.042)
  the two profiles are of different devices: /device:TPU:1 before, /device:TPU:89 now
where the time goes in v4:
time: 247 us
  waiting for transfers between devices  98.2 us (40%)
  starting transfers between devices  80.8 us (33%)
  Pallas kernels  63.8 us (26%)
  local copies, waits for them, and re-layouts  3.57 us (1%)
    ppermute x28, waiting for transfers between devices, shifted(): return lax.ppermute(array, axis, ring(lax.axis_size(axis), step))  82.5 us
    pallas_call x21, Pallas kernels, call(): pl.pallas_call(kernel, out_shape=tuple(outs), in_specs=[smem] + [vmem] *...  63.8 us
    ppermute x28, starting transfers between devices, shifted(): return lax.ppermute(array, axis, ring(lax.axis_size(axis), step))  60.3 us
    ppermute x4, waiting for transfers between devices, body(): ga = lax.ppermute(fa, 'node', PAIR_A)  8.25 us
    ppermute x4, starting transfers between devices, body(): gb = lax.ppermute(fb, 'node', PAIR_B)  7.23 us
    ppermute x4, starting transfers between devices, body(): ra = lax.ppermute(pa, 'node', PAIR_B)  7.13 us
  transfers between devices with their start and end apart: 46, of which 24 were waited for; matrix products, arithmetic and copies ran while one was open for 0% of the time, Pallas kernels for 15%

profile of v4, /device:TPU:89, one launch (start us, length us, event | category | flops | bytes accessed | tf_op | source)
XLA Modules:
  0.0 246.6 jit_solution(9133715508499643577)
XLA Ops:
  0.0 0.8 constant_dynamic-slice_fusion
  0.8 1.2 copy-done.2
  2.0 0.8 copy-done.4
  3.6 0.8 shard_map.73
  5.0 1.3 collective-permute-start.1
  6.3 2.3 collective-permute-start.4
  8.6 3.0 %collective-permute-start.2 = (f32[2,32,256]{2,1,0:T(8,128)S(1)}, f32[2,32,256]{2,1,0:T(8,128)S(1)}, u32[]{:S(2)}, u32[]{:S(2)}) collective-permute-start(f32[2,32,256]{2,1,0:T(8,128)S(1)} %get-tuple-element.90), channel_id=1, source_target_pairs={{0,4},{4,8},{8,12},{12,16},{16,20},{20,24},{24,28},{28,32},{32,36}... | collective-permute-start | bytes 196616 | tf_op jit(solution)/shard_map/ppermute | solution.py:119
  11.6 3.6 %collective-permute-done.5.refs_6_ = f32[2,16,256]{2,1,0:T(8,128)S(1)} collective-permute-done((f32[2,16,256]{2,1,0:T(8,128)S(1)}, f32[2,16,256]{2,1,0:T(8,128)S(1)}, u32[]{:S(2)}, u32[]{:S(2)}) %collective-permute-start.5) | collective-permute-done | bytes 32800 | tf_op jit(solution)/shard_map/ppermute | solution.py:119
  15.2 5.7 %collective-permute-done.3.refs_4_ = f32[2,32,256]{2,1,0:T(8,128)S(1)} collective-permute-done((f32[2,32,256]{2,1,0:T(8,128)S(1)}, f32[2,32,256]{2,1,0:T(8,128)S(1)}, u32[]{:S(2)}, u32[]{:S(2)}) %collective-permute-start.3) | collective-permute-done | bytes 65568 | tf_op jit(solution)/shard_map/ppermute | solution.py:119
  20.9 2.2 shard_map.75
  23.8 4.1 %collective-permute-start.7 = (f32[8,32,256]{2,1,0:T(8,128)S(1)}, f32[8,32,256]{2,1,0:T(8,128)S(1)}, u32[]{:S(2)}, u32[]{:S(2)}) collective-permute-start(f32[8,32,256]{2,1,0:T(8,128)S(1)} %get-tuple-element.97.fb), channel_id=1, source_target_pairs={{0,192},{192,0},{64,128},{128,64},{1,193},{193,1},{65,129},{129,65... | collective-permute-start | bytes 786440 | tf_op jit(solution)/shard_map/ppermute | solution.py:519
  27.9 2.4 collective-permute-done.6.ga
  30.3 3.5 %collective-permute-done.7.gb = f32[8,32,256]{2,1,0:T(8,128)S(1)} collective-permute-done((f32[8,32,256]{2,1,0:T(8,128)S(1)}, f32[8,32,256]{2,1,0:T(8,128)S(1)}, u32[]{:S(2)}, u32[]{:S(2)}) %collective-permute-start.7) | collective-permute-done | bytes 262176 | tf_op jit(solution)/shard_map/ppermute | solution.py:519
  33.8 0.7 shard_map.76
  34.5 2.5 %collective-permute-start.12 = (f32[8,32,256]{2,1,0:T(8,128)S(1)}, f32[8,32,256]{2,1,0:T(8,128)S(1)}, u32[]{:S(2)}, u32[]{:S(2)}) collective-permute-start(f32[8,32,256]{2,1,0:T(8,128)S(1)} %get-tuple-element.98), channel_id=1, source_target_pairs={{0,192},{192,0},{64,128},{128,64},{1,193},{193,1},{65,129},{129,65... | collective-permute-start | bytes 786440 | tf_op jit(solution)/shard_map/ppermute | solution.py:524
  37.0 2.2 shard_map.74
  39.1 1.5 collective-permute-start.8
  41.0 1.3 collective-permute-done.12.ra
  42.9 9.3 %shard_map.78 = (f32[40,32,256]{2,1,0:T(8,128)S(1)}, f32[41,8,256]{2,1,0:T(8,128)S(1)}, f32[41,8,256]{2,1,0:T(8,128)S(1)}) custom-call(f32[13]{0:T(128)S(1)} %get-tuple-element.166.sc.refs_0_, f32[256,256]{1,0:T(8,128)S(1)} %get-tuple-element.85.basis, f32[8,256]{1,0:T(8,128)S(1)} %copy-done.3, f32[16,32,256]{2,1,0:T(8,128)S(1)} %get-tuple-element.89.refs_1_.x0.x, ...), custom_call_target="tpu_custom_call" | custom-call | flops 60000000 | bytes 1000000 | tf_op jit(solution)/shard_map/pallas_call | solution.py:125
  52.2 5.2 %collective-permute-start.14 = (f32[41,8,256]{2,1,0:T(8,128)S(1)}, f32[41,8,256]{2,1,0:T(8,128)S(1)}, u32[]{:S(2)}, u32[]{:S(2)}) collective-permute-start(f32[41,8,256]{2,1,0:T(8,128)S(1)} %get-tuple-element.109), channel_id=1, source_target_pairs={{0,1},{1,2},{2,3},{3,0},{4,5},{5,6},{6,7},{7,4},{8,9},{9,10},{10,1... | collective-permute-start | bytes 1007624 | tf_op jit(solution)/shard_map/ppermute | solution.py:119
  58.8 4.3 %collective-permute-done.14.low = f32[41,8,256]{2,1,0:T(8,128)S(1)} collective-permute-done((f32[41,8,256]{2,1,0:T(8,128)S(1)}, f32[41,8,256]{2,1,0:T(8,128)S(1)}, u32[]{:S(2)}, u32[]{:S(2)}) %collective-permute-start.14) | collective-permute-done | bytes 335904 | tf_op jit(solution)/shard_map/ppermute | solution.py:119
  63.1 4.1 %collective-permute-done.15.high = f32[41,8,256]{2,1,0:T(8,128)S(1)} collective-permute-done((f32[41,8,256]{2,1,0:T(8,128)S(1)}, f32[41,8,256]{2,1,0:T(8,128)S(1)}, u32[]{:S(2)}, u32[]{:S(2)}) %collective-permute-start.15) | collective-permute-done | bytes 335904 | tf_op jit(solution)/shard_map/ppermute | solution.py:119
  68.0 9.3 %shard_map.80 = (f32[40,32,256]{2,1,0:T(8,128)S(1)}, f32[41,8,256]{2,1,0:T(8,128)S(1)}, f32[41,8,256]{2,1,0:T(8,128)S(1)}) custom-call(f32[13]{0:T(128)S(1)} %get-tuple-element.165.refs_0_.sc, f32[256,256]{1,0:T(8,128)S(1)} %get-tuple-element.85.basis, f32[8,256]{1,0:T(8,128)S(1)} %copy-done.3, f32[16,32,256]{2,1,0:T(8,128)S(1)} %get-tuple-element.86.refs_2_.x0.x, ...), custom_call_target="tpu_custom_call" | custom-call | flops 60000000 | bytes 1000000 | tf_op jit(solution)/shard_map/pallas_call | solution.py:125
  77.3 1.7 collective-permute-start.16
  79.0 5.7 %collective-permute-start.20 = (f32[12,32,256]{2,1,0:T(8,128)S(1)}, f32[12,32,256]{2,1,0:T(8,128)S(1)}, u32[]{:S(2)}, u32[]{:S(2)}) collective-permute-start(f32[12,32,256]{2,1,0:T(8,128)S(1)} %get-tuple-element.112), channel_id=1, source_target_pairs={{0,4},{4,8},{8,12},{12,16},{16,20},{20,24},{24,28},{28,32},{32,36}... | collective-permute-start | bytes 1179656 | tf_op jit(solution)/shard_map/ppermute | solution.py:119
  84.7 11.2 %collective-permute-done.16.low = f32[41,8,256]{2,1,0:T(8,128)S(1)} collective-permute-done((f32[41,8,256]{2,1,0:T(8,128)S(1)}, f32[41,8,256]{2,1,0:T(8,128)S(1)}, u32[]{:S(2)}, u32[]{:S(2)}) %collective-permute-start.16) | collective-permute-done | bytes 335904 | tf_op jit(solution)/shard_map/ppermute | solution.py:119
  95.9 0.7 shard_map.81
  96.7 3.7 %collective-permute-start.18 = (f32[12,32,256]{2,1,0:T(8,128)S(1)}, f32[12,32,256]{2,1,0:T(8,128)S(1)}, u32[]{:S(2)}, u32[]{:S(2)}) collective-permute-start(f32[12,32,256]{2,1,0:T(8,128)S(1)} %get-tuple-element.119), channel_id=1, source_target_pairs={{0,4},{4,8},{8,12},{12,16},{16,20},{20,24},{24,28},{28,32},{32,36}... | collective-permute-start | bytes 1179656 | tf_op jit(solution)/shard_map/ppermute | solution.py:119
  100.4 4.0 %collective-permute-done.20.low = f32[12,32,256]{2,1,0:T(8,128)S(1)} collective-permute-done((f32[12,32,256]{2,1,0:T(8,128)S(1)}, f32[12,32,256]{2,1,0:T(8,128)S(1)}, u32[]{:S(2)}, u32[]{:S(2)}) %collective-permute-start.20) | collective-permute-done | bytes 393248 | tf_op jit(solution)/shard_map/ppermute | solution.py:119
  104.4 2.4 shard_map.83
  106.8 6.5 %collective-permute-start.22 = (f32[32,256]{1,0:T(8,128)S(1)}, f32[32,256]{1,0:T(8,128)S(1)}, u32[]{:S(2)}, u32[]{:S(2)}) collective-permute-start(f32[32,256]{1,0:T(8,128)S(1)} %get-tuple-element.128), channel_id=1, source_target_pairs={{0,4},{4,8},{8,12},{12,16},{16,20},{20,24},{24,28},{28,32},{32,36}... | collective-permute-start | bytes 98312 | tf_op jit(solution)/shard_map/ppermute | solution.py:119
  113.3 7.2 %collective-permute-done.18.low = f32[12,32,256]{2,1,0:T(8,128)S(1)} collective-permute-done((f32[12,32,256]{2,1,0:T(8,128)S(1)}, f32[12,32,256]{2,1,0:T(8,128)S(1)}, u32[]{:S(2)}, u32[]{:S(2)}) %collective-permute-start.18) | collective-permute-done | bytes 393248 | tf_op jit(solution)/shard_map/ppermute | solution.py:119
  120.5 1.6 collective-permute-start.25
  122.1 2.4 collective-permute-done.19.high
  124.6 2.4 shard_map.82
  127.0 2.2 shard_map.84
  129.3 1.8 collective-permute-start.31
  131.1 5.9 %collective-permute-done.30.ga = f32[8,32,256]{2,1,0:T(8,128)S(1)} collective-permute-done((f32[8,32,256]{2,1,0:T(8,128)S(1)}, f32[8,32,256]{2,1,0:T(8,128)S(1)}, u32[]{:S(2)}, u32[]{:S(2)}) %collective-permute-start.30) | collective-permute-done | bytes 262176 | tf_op jit(solution)/shard_map/ppermute | solution.py:518
  136.9 1.2 collective-permute-done.31.gb
  138.9 1.9 collective-permute-start.36
  140.8 1.4 collective-permute-start.28
  142.2 6.4 %collective-permute-start.26 = (f32[32,256]{1,0:T(8,128)S(1)}, f32[32,256]{1,0:T(8,128)S(1)}, u32[]{:S(2)}, u32[]{:S(2)}) collective-permute-start(f32[32,256]{1,0:T(8,128)S(1)} %get-tuple-element.134), channel_id=1, source_target_pairs={{0,4},{4,8},{8,12},{12,16},{16,20},{20,24},{24,28},{28,32},{32,36}... | collective-permute-start | bytes 98312 | tf_op jit(solution)/shard_map/ppermute | solution.py:119
  148.7 3.2 %collective-permute-done.29.refs_6_ = f32[16,256]{1,0:T(8,128)S(1)} collective-permute-done((f32[16,256]{1,0:T(8,128)S(1)}, f32[16,256]{1,0:T(8,128)S(1)}, u32[]{:S(2)}, u32[]{:S(2)}) %collective-permute-start.29) | collective-permute-done | bytes 16416 | tf_op jit(solution)/shard_map/ppermute | solution.py:119
  151.8 3.9 %collective-permute-done.27.refs_4_ = f32[32,256]{1,0:T(8,128)S(1)} collective-permute-done((f32[32,256]{1,0:T(8,128)S(1)}, f32[32,256]{1,0:T(8,128)S(1)}, u32[]{:S(2)}, u32[]{:S(2)}) %collective-permute-start.27) | collective-permute-done | bytes 32800 | tf_op jit(solution)/shard_map/ppermute | solution.py:119
  155.7 2.2 shard_map.85
  157.9 1.8 collective-permute-start.32
  159.7 1.1 collective-permute-start.33
  160.8 9.3 %shard_map.88 = (f32[40,32,256]{2,1,0:T(8,128)S(1)}, f32[41,8,256]{2,1,0:T(8,128)S(1)}, f32[41,8,256]{2,1,0:T(8,128)S(1)}) custom-call(f32[13]{0:T(128)S(1)} %get-tuple-element.166.sc.refs_0_, f32[256,256]{1,0:T(8,128)S(1)} %get-tuple-element.85.basis, f32[8,256]{1,0:T(8,128)S(1)} %copy-done.3, f32[16,32,256]{2,1,0:T(8,128)S(1)} %get-tuple-element.123.refs_1_.x, ...), custom_call_target="tpu_custom_call" | custom-call | flops 60000000 | bytes 1000000 | tf_op jit(solution)/shard_map/pallas_call | solution.py:125
  170.1 1.5 collective-permute-start.38
  172.3 2.2 collective-permute-start.34
  174.5 4.0 %collective-permute-done.38.low = f32[41,8,256]{2,1,0:T(8,128)S(1)} collective-permute-done((f32[41,8,256]{2,1,0:T(8,128)S(1)}, f32[41,8,256]{2,1,0:T(8,128)S(1)}, u32[]{:S(2)}, u32[]{:S(2)}) %collective-permute-start.38) | collective-permute-done | bytes 335904 | tf_op jit(solution)/shard_map/ppermute | solution.py:119
  178.5 1.6 collective-permute-done.39.high
  180.9 0.8 collective-permute-done.35.rb
  181.7 9.3 %shard_map.90 = (f32[40,32,256]{2,1,0:T(8,128)S(1)}, f32[41,8,256]{2,1,0:T(8,128)S(1)}, f32[41,8,256]{2,1,0:T(8,128)S(1)}) custom-call(f32[13]{0:T(128)S(1)} %get-tuple-element.165.refs_0_.sc, f32[256,256]{1,0:T(8,128)S(1)} %get-tuple-element.85.basis, f32[8,256]{1,0:T(8,128)S(1)} %copy-done.3, f32[16,32,256]{2,1,0:T(8,128)S(1)} %get-tuple-element.121.refs_2_.x, ...), custom_call_target="tpu_custom_call" | custom-call | flops 60000000 | bytes 1000000 | tf_op jit(solution)/shard_map/pallas_call | solution.py:125
  191.0 1.7 collective-permute-start.40
  192.7 5.7 %collective-permute-start.44 = (f32[12,32,256]{2,1,0:T(8,128)S(1)}, f32[12,32,256]{2,1,0:T(8,128)S(1)}, u32[]{:S(2)}, u32[]{:S(2)}) collective-permute-start(f32[12,32,256]{2,1,0:T(8,128)S(1)} %get-tuple-element.154), channel_id=1, source_target_pairs={{0,4},{4,8},{8,12},{12,16},{16,20},{20,24},{24,28},{28,32},{32,36}... | collective-permute-start | bytes 1179656 | tf_op jit(solution)/shard_map/ppermute | solution.py:119
  198.5 3.9 %collective-permute-done.41.high = f32[41,8,256]{2,1,0:T(8,128)S(1)} collective-permute-done((f32[41,8,256]{2,1,0:T(8,128)S(1)}, f32[41,8,256]{2,1,0:T(8,128)S(1)}, u32[]{:S(2)}, u32[]{:S(2)}) %collective-permute-start.41) | collective-permute-done | bytes 335904 | tf_op jit(solution)/shard_map/ppermute | solution.py:119
  202.4 0.7 shard_map.91
  203.1 13.9 %collective-permute-start.42 = (f32[12,32,256]{2,1,0:T(8,128)S(1)}, f32[12,32,256]{2,1,0:T(8,128)S(1)}, u32[]{:S(2)}, u32[]{:S(2)}) collective-permute-start(f32[12,32,256]{2,1,0:T(8,128)S(1)} %get-tuple-element.161), channel_id=1, source_target_pairs={{0,4},{4,8},{8,12},{12,16},{16,20},{20,24},{24,28},{28,32},{32,36}... | collective-permute-start | bytes 1179656 | tf_op jit(solution)/shard_map/ppermute | solution.py:119
  217.0 2.5 %collective-permute-done.44.low = f32[12,32,256]{2,1,0:T(8,128)S(1)} collective-permute-done((f32[12,32,256]{2,1,0:T(8,128)S(1)}, f32[12,32,256]{2,1,0:T(8,128)S(1)}, u32[]{:S(2)}, u32[]{:S(2)}) %collective-permute-start.44) | collective-permute-done | bytes 393248 | tf_op jit(solution)/shard_map/ppermute | solution.py:119
  219.5 3.1 %shard_map.92 = (f32[16,32,256]{2,1,0:T(8,128)S(1)}, f32[32,256]{1,0:T(8,128)}, f32[32,256]{1,0:T(8,128)}, f32[16,256]{1,0:T(8,128)}, f32[16,256]{1,0:T(8,128)}) custom-call(f32[13]{0:T(128)S(1)} %get-tuple-element.166.sc.refs_0_, f32[256,256]{1,0:T(8,128)S(1)} %get-tuple-element.85.basis, f32[16,32,256]{2,1,0:T(8,128)S(1)} %get-tuple-element.163.c, ...), custom_call_target="tpu_custom_call" | custom-call | flops 1000000 | bytes 1000000 | tf_op jit(solution)/shard_map/pallas_call | solution.py:125
  222.5 6.0 %collective-permute-done.42.low = f32[12,32,256]{2,1,0:T(8,128)S(1)} collective-permute-done((f32[12,32,256]{2,1,0:T(8,128)S(1)}, f32[12,32,256]{2,1,0:T(8,128)S(1)}, u32[]{:S(2)}, u32[]{:S(2)}) %collective-permute-start.42) | collective-permute-done | bytes 393248 | tf_op jit(solution)/shard_map/ppermute | solution.py:119
  228.5 14.7 %collective-permute-done.43.high = f32[12,32,256]{2,1,0:T(8,128)S(1)} collective-permute-done((f32[12,32,256]{2,1,0:T(8,128)S(1)}, f32[12,32,256]{2,1,0:T(8,128)S(1)}, u32[]{:S(2)}, u32[]{:S(2)}) %collective-permute-start.43) | collective-permute-done | bytes 393248 | tf_op jit(solution)/shard_map/ppermute | solution.py:119
  243.2 3.5 %shard_map.93 = f32[2,16,32,256]{3,2,1,0:T(8,128)} custom-call(f32[13]{0:T(128)S(1)} %get-tuple-element.166.sc.refs_0_, f32[256,256]{1,0:T(8,128)S(1)} %get-tuple-element.85.basis, f32[16,32,256]{2,1,0:T(8,128)S(1)} %get-tuple-element.160.c, f32[12,32,256]{2,1,0:T(8,128)S(1)} %collective-permute-done.42.low, ...), custom_call_target="tpu_custom_call" | custom-call | flops 1000000 | bytes 1000000 | tf_op jit(solution)/shard_map/pallas_call | solution.py:125
  (63 shorter events, 7.7 us)
Async XLA Ops:
  0.0 20.9 %copy-start.1 = (f32[16,32,256]{2,1,0:T(8,128)S(1)}, f32[16,32,256]{2,1,0:T(8,128)}, u32[]{:S(2)}) copy-start(f32[16,32,256]{2,1,0:T(8,128)} %refs_8_.7) | copy-start | bytes 1572868
  0.0 20.9 %copy-start = (f32[16,32,256]{2,1,0:T(8,128)S(1)}, f32[16,32,256]{2,1,0:T(8,128)}, u32[]{:S(2)}) copy-start(f32[16,32,256]{2,1,0:T(8,128)} %refs_7_.7) | copy-start | bytes 1572868
  0.8 1.2 copy-start.2
  2.0 0.8 copy-start.4
  2.8 0.7 copy-start.5
  4.3 29.4 %collective-permute-start = (f32[2,8,32,256]{3,2,1,0:T(8,128)S(1)}, f32[2,8,32,256]{3,2,1,0:T(8,128)S(1)}, u32[]{:S(2)}, u32[]{:S(2)}) collective-permute-start(f32[2,8,32,256]{3,2,1,0:T(8,128)S(1)} %get-tuple-element.87), channel_id=1, source_target_pairs={{192,128},{193,129},{194,130},{195,131},{196,132},{197,133},{198,1... | collective-permute-start | bytes 1572872 | tf_op jit(solution)/shard_map/ppermute | solution.py:493
  5.0 28.7 %collective-permute-start.1 = (f32[2,8,32,256]{3,2,1,0:T(8,128)S(1)}, f32[2,8,32,256]{3,2,1,0:T(8,128)S(1)}, u32[]{:S(2)}, u32[]{:S(2)}) collective-permute-start(f32[2,8,32,256]{3,2,1,0:T(8,128)S(1)} %get-tuple-element.88), channel_id=1, source_target_pairs={{192,0},{193,1},{194,2},{195,3},{196,4},{197,5},{198,6},{199,7},{2... | collective-permute-start | bytes 1572872 | tf_op jit(solution)/shard_map/ppermute | solution.py:494
  6.3 5.2 %collective-permute-start.4 = (f32[2,16,256]{2,1,0:T(8,128)S(1)}, f32[2,16,256]{2,1,0:T(8,128)S(1)}, u32[]{:S(2)}, u32[]{:S(2)}) collective-permute-start(f32[2,16,256]{2,1,0:T(8,128)S(1)} %get-tuple-element.92), channel_id=1, source_target_pairs={{0,1},{1,2},{2,3},{3,0},{4,5},{5,6},{6,7},{7,4},{8,9},{9,10},{10,1... | collective-permute-start | bytes 98312 | tf_op jit(solution)/shard_map/ppermute | solution.py:119
  8.6 6.6 %collective-permute-start.2 = (f32[2,32,256]{2,1,0:T(8,128)S(1)}, f32[2,32,256]{2,1,0:T(8,128)S(1)}, u32[]{:S(2)}, u32[]{:S(2)}) collective-permute-start(f32[2,32,256]{2,1,0:T(8,128)S(1)} %get-tuple-element.90), channel_id=1, source_target_pairs={{0,4},{4,8},{8,12},{12,16},{16,20},{20,24},{24,28},{28,32},{32,36}... | collective-permute-start | bytes 196616 | tf_op jit(solution)/shard_map/ppermute | solution.py:119
  11.6 9.3 %collective-permute-start.3 = (f32[2,32,256]{2,1,0:T(8,128)S(1)}, f32[2,32,256]{2,1,0:T(8,128)S(1)}, u32[]{:S(2)}, u32[]{:S(2)}) collective-permute-start(f32[2,32,256]{2,1,0:T(8,128)S(1)} %get-tuple-element.91), channel_id=1, source_target_pairs={{0,60},{4,0},{8,4},{12,8},{16,12},{20,16},{24,20},{28,24},{32,28},... | collective-permute-start | bytes 196616 | tf_op jit(solution)/shard_map/ppermute | solution.py:119
  11.6 3.6 %collective-permute-start.5 = (f32[2,16,256]{2,1,0:T(8,128)S(1)}, f32[2,16,256]{2,1,0:T(8,128)S(1)}, u32[]{:S(2)}, u32[]{:S(2)}) collective-permute-start(f32[2,16,256]{2,1,0:T(8,128)S(1)} %get-tuple-element.93), channel_id=1, source_target_pairs={{0,3},{1,0},{2,1},{3,2},{4,7},{5,4},{6,5},{7,6},{8,11},{9,8},{10,9... | collective-permute-start | bytes 98312 | tf_op jit(solution)/shard_map/ppermute | solution.py:119
  23.1 7.2 %collective-permute-start.6 = (f32[8,32,256]{2,1,0:T(8,128)S(1)}, f32[8,32,256]{2,1,0:T(8,128)S(1)}, u32[]{:S(2)}, u32[]{:S(2)}) collective-permute-start(f32[8,32,256]{2,1,0:T(8,128)S(1)} %get-tuple-element.96.fa), channel_id=1, source_target_pairs={{0,64},{64,0},{128,192},{192,128},{1,65},{65,1},{129,193},{193,129... | collective-permute-start | bytes 786440 | tf_op jit(solution)/shard_map/ppermute | solution.py:518
  23.8 10.0 %collective-permute-start.7 = (f32[8,32,256]{2,1,0:T(8,128)S(1)}, f32[8,32,256]{2,1,0:T(8,128)S(1)}, u32[]{:S(2)}, u32[]{:S(2)}) collective-permute-start(f32[8,32,256]{2,1,0:T(8,128)S(1)} %get-tuple-element.97.fb), channel_id=1, source_target_pairs={{0,192},{192,0},{64,128},{128,64},{1,193},{193,1},{65,129},{129,65... | collective-permute-start | bytes 786440 | tf_op jit(solution)/shard_map/ppermute | solution.py:519
  34.5 8.4 %copy-start.3 = (f32[8,256]{1,0:T(8,128)S(1)}, f32[8,256]{1,0:T(8,128)}, u32[]{:S(2)}) copy-start(f32[8,256]{1,0:T(8,128)} %constant.21.clone.sums) | copy-start | bytes 24580
  34.5 7.8 %collective-permute-start.12 = (f32[8,32,256]{2,1,0:T(8,128)S(1)}, f32[8,32,256]{2,1,0:T(8,128)S(1)}, u32[]{:S(2)}, u32[]{:S(2)}) collective-permute-start(f32[8,32,256]{2,1,0:T(8,128)S(1)} %get-tuple-element.98), channel_id=1, source_target_pairs={{0,192},{192,0},{64,128},{128,64},{1,193},{193,1},{65,129},{129,65... | collective-permute-start | bytes 786440 | tf_op jit(solution)/shard_map/ppermute | solution.py:524
  37.0 5.9 %collective-permute-start.13 = (f32[8,32,256]{2,1,0:T(8,128)S(1)}, f32[8,32,256]{2,1,0:T(8,128)S(1)}, u32[]{:S(2)}, u32[]{:S(2)}) collective-permute-start(f32[8,32,256]{2,1,0:T(8,128)S(1)} %get-tuple-element.99), channel_id=1, source_target_pairs={{0,64},{64,0},{128,192},{192,128},{1,65},{65,1},{129,193},{193,129... | collective-permute-start | bytes 786440 | tf_op jit(solution)/shard_map/ppermute | solution.py:525
  39.1 18.4 %collective-permute-start.8 = (f32[8,32,256]{2,1,0:T(8,128)S(1)}, f32[8,32,256]{2,1,0:T(8,128)S(1)}, u32[]{:S(2)}, u32[]{:S(2)}) collective-permute-start(f32[8,32,256]{2,1,0:T(8,128)S(1)} %get-tuple-element.100.fa), channel_id=1, source_target_pairs={{0,64},{64,0},{128,192},{192,128},{1,65},{65,1},{129,193},{193,129... | collective-permute-start | bytes 786440 | tf_op jit(solution)/shard_map/ppermute | solution.py:518
  40.7 16.9 %collective-permute-start.9 = (f32[8,32,256]{2,1,0:T(8,128)S(1)}, f32[8,32,256]{2,1,0:T(8,128)S(1)}, u32[]{:S(2)}, u32[]{:S(2)}) collective-permute-start(f32[8,32,256]{2,1,0:T(8,128)S(1)} %get-tuple-element.101.fb), channel_id=1, source_target_pairs={{0,192},{192,0},{64,128},{128,64},{1,193},{193,1},{65,129},{129,65... | collective-permute-start | bytes 786440 | tf_op jit(solution)/shard_map/ppermute | solution.py:519
  52.2 10.9 %collective-permute-start.14 = (f32[41,8,256]{2,1,0:T(8,128)S(1)}, f32[41,8,256]{2,1,0:T(8,128)S(1)}, u32[]{:S(2)}, u32[]{:S(2)}) collective-permute-start(f32[41,8,256]{2,1,0:T(8,128)S(1)} %get-tuple-element.109), channel_id=1, source_target_pairs={{0,1},{1,2},{2,3},{3,0},{4,5},{5,6},{6,7},{7,4},{8,9},{9,10},{10,1... | collective-permute-start | bytes 1007624 | tf_op jit(solution)/shard_map/ppermute | solution.py:119
  57.4 9.9 %collective-permute-start.15 = (f32[41,8,256]{2,1,0:T(8,128)S(1)}, f32[41,8,256]{2,1,0:T(8,128)S(1)}, u32[]{:S(2)}, u32[]{:S(2)}) collective-permute-start(f32[41,8,256]{2,1,0:T(8,128)S(1)} %get-tuple-element.110), channel_id=1, source_target_pairs={{0,3},{1,0},{2,1},{3,2},{4,7},{5,4},{6,5},{7,6},{8,11},{9,8},{10,9... | collective-permute-start | bytes 1007624 | tf_op jit(solution)/shard_map/ppermute | solution.py:119
  58.3 9.7 %collective-permute-start.10 = (f32[8,32,256]{2,1,0:T(8,128)S(1)}, f32[8,32,256]{2,1,0:T(8,128)S(1)}, u32[]{:S(2)}, u32[]{:S(2)}) collective-permute-start(f32[8,32,256]{2,1,0:T(8,128)S(1)} %get-tuple-element.104), channel_id=1, source_target_pairs={{0,192},{192,0},{64,128},{128,64},{1,193},{193,1},{65,129},{129,65... | collective-permute-start | bytes 786440 | tf_op jit(solution)/shard_map/ppermute | solution.py:524
  58.8 9.2 %collective-permute-start.11 = (f32[8,32,256]{2,1,0:T(8,128)S(1)}, f32[8,32,256]{2,1,0:T(8,128)S(1)}, u32[]{:S(2)}, u32[]{:S(2)}) collective-permute-start(f32[8,32,256]{2,1,0:T(8,128)S(1)} %get-tuple-element.105), channel_id=1, source_target_pairs={{0,64},{64,0},{128,192},{192,128},{1,65},{65,1},{129,193},{193,129... | collective-permute-start | bytes 786440 | tf_op jit(solution)/shard_map/ppermute | solution.py:525
  77.3 18.6 %collective-permute-start.16 = (f32[41,8,256]{2,1,0:T(8,128)S(1)}, f32[41,8,256]{2,1,0:T(8,128)S(1)}, u32[]{:S(2)}, u32[]{:S(2)}) collective-permute-start(f32[41,8,256]{2,1,0:T(8,128)S(1)} %get-tuple-element.116), channel_id=1, source_target_pairs={{0,1},{1,2},{2,3},{3,0},{4,5},{5,6},{6,7},{7,4},{8,9},{9,10},{10,1... | collective-permute-start | bytes 1007624 | tf_op jit(solution)/shard_map/ppermute | solution.py:119
  79.0 16.9 %collective-permute-start.17 = (f32[41,8,256]{2,1,0:T(8,128)S(1)}, f32[41,8,256]{2,1,0:T(8,128)S(1)}, u32[]{:S(2)}, u32[]{:S(2)}) collective-permute-start(f32[41,8,256]{2,1,0:T(8,128)S(1)} %get-tuple-element.117), channel_id=1, source_target_pairs={{0,3},{1,0},{2,1},{3,2},{4,7},{5,4},{6,5},{7,6},{8,11},{9,8},{10,9... | collective-permute-start | bytes 1007624 | tf_op jit(solution)/shard_map/ppermute | solution.py:119
  79.0 21.3 %collective-permute-start.21 = (f32[12,32,256]{2,1,0:T(8,128)S(1)}, f32[12,32,256]{2,1,0:T(8,128)S(1)}, u32[]{:S(2)}, u32[]{:S(2)}) collective-permute-start(f32[12,32,256]{2,1,0:T(8,128)S(1)} %get-tuple-element.111), channel_id=1, source_target_pairs={{0,60},{4,0},{8,4},{12,8},{16,12},{20,16},{24,20},{28,24},{32,28},... | collective-permute-start | bytes 1179656 | tf_op jit(solution)/shard_map/ppermute | solution.py:119
  79.0 25.4 %collective-permute-start.20 = (f32[12,32,256]{2,1,0:T(8,128)S(1)}, f32[12,32,256]{2,1,0:T(8,128)S(1)}, u32[]{:S(2)}, u32[]{:S(2)}) collective-permute-start(f32[12,32,256]{2,1,0:T(8,128)S(1)} %get-tuple-element.112), channel_id=1, source_target_pairs={{0,4},{4,8},{8,12},{12,16},{16,20},{20,24},{24,28},{28,32},{32,36}... | collective-permute-start | bytes 1179656 | tf_op jit(solution)/shard_map/ppermute | solution.py:119
  96.7 23.9 %collective-permute-start.18 = (f32[12,32,256]{2,1,0:T(8,128)S(1)}, f32[12,32,256]{2,1,0:T(8,128)S(1)}, u32[]{:S(2)}, u32[]{:S(2)}) collective-permute-start(f32[12,32,256]{2,1,0:T(8,128)S(1)} %get-tuple-element.119), channel_id=1, source_target_pairs={{0,4},{4,8},{8,12},{12,16},{16,20},{20,24},{24,28},{28,32},{32,36}... | collective-permute-start | bytes 1179656 | tf_op jit(solution)/shard_map/ppermute | solution.py:119
  100.4 24.2 %collective-permute-start.19 = (f32[12,32,256]{2,1,0:T(8,128)S(1)}, f32[12,32,256]{2,1,0:T(8,128)S(1)}, u32[]{:S(2)}, u32[]{:S(2)}) collective-permute-start(f32[12,32,256]{2,1,0:T(8,128)S(1)} %get-tuple-element.120), channel_id=1, source_target_pairs={{0,60},{4,0},{8,4},{12,8},{16,12},{20,16},{24,20},{28,24},{32,28},... | collective-permute-start | bytes 1179656 | tf_op jit(solution)/shard_map/ppermute | solution.py:119
  106.8 20.2 %collective-permute-start.22 = (f32[32,256]{1,0:T(8,128)S(1)}, f32[32,256]{1,0:T(8,128)S(1)}, u32[]{:S(2)}, u32[]{:S(2)}) collective-permute-start(f32[32,256]{1,0:T(8,128)S(1)} %get-tuple-element.128), channel_id=1, source_target_pairs={{0,4},{4,8},{8,12},{12,16},{16,20},{20,24},{24,28},{28,32},{32,36}... | collective-permute-start | bytes 98312 | tf_op jit(solution)/shard_map/ppermute | solution.py:119
  113.3 13.7 %collective-permute-start.23 = (f32[32,256]{1,0:T(8,128)S(1)}, f32[32,256]{1,0:T(8,128)S(1)}, u32[]{:S(2)}, u32[]{:S(2)}) collective-permute-start(f32[32,256]{1,0:T(8,128)S(1)} %get-tuple-element.129), channel_id=1, source_target_pairs={{0,60},{4,0},{8,4},{12,8},{16,12},{20,16},{24,20},{28,24},{32,28},... | collective-permute-start | bytes 98312 | tf_op jit(solution)/shard_map/ppermute | solution.py:119
  113.3 13.7 %collective-permute-start.24 = (f32[16,256]{1,0:T(8,128)S(1)}, f32[16,256]{1,0:T(8,128)S(1)}, u32[]{:S(2)}, u32[]{:S(2)}) collective-permute-start(f32[16,256]{1,0:T(8,128)S(1)} %get-tuple-element.130), channel_id=1, source_target_pairs={{0,1},{1,2},{2,3},{3,0},{4,5},{5,6},{6,7},{7,4},{8,9},{9,10},{10,1... | collective-permute-start | bytes 49160 | tf_op jit(solution)/shard_map/ppermute | solution.py:119
  120.5 6.5 %collective-permute-start.25 = (f32[16,256]{1,0:T(8,128)S(1)}, f32[16,256]{1,0:T(8,128)S(1)}, u32[]{:S(2)}, u32[]{:S(2)}) collective-permute-start(f32[16,256]{1,0:T(8,128)S(1)} %get-tuple-element.131), channel_id=1, source_target_pairs={{0,3},{1,0},{2,1},{3,2},{4,7},{5,4},{6,5},{7,6},{8,11},{9,8},{10,9... | collective-permute-start | bytes 49160 | tf_op jit(solution)/shard_map/ppermute | solution.py:119
  129.2 7.7 %collective-permute-start.30 = (f32[8,32,256]{2,1,0:T(8,128)S(1)}, f32[8,32,256]{2,1,0:T(8,128)S(1)}, u32[]{:S(2)}, u32[]{:S(2)}) collective-permute-start(f32[8,32,256]{2,1,0:T(8,128)S(1)} %get-tuple-element.132.fa), channel_id=1, source_target_pairs={{0,64},{64,0},{128,192},{192,128},{1,65},{65,1},{129,193},{193,129... | collective-permute-start | bytes 786440 | tf_op jit(solution)/shard_map/ppermute | solution.py:518
  129.3 8.8 %collective-permute-start.31 = (f32[8,32,256]{2,1,0:T(8,128)S(1)}, f32[8,32,256]{2,1,0:T(8,128)S(1)}, u32[]{:S(2)}, u32[]{:S(2)}) collective-permute-start(f32[8,32,256]{2,1,0:T(8,128)S(1)} %get-tuple-element.133.fb), channel_id=1, source_target_pairs={{0,192},{192,0},{64,128},{128,64},{1,193},{193,1},{65,129},{129,65... | collective-permute-start | bytes 786440 | tf_op jit(solution)/shard_map/ppermute | solution.py:519
  138.9 21.9 %collective-permute-start.36 = (f32[8,32,256]{2,1,0:T(8,128)S(1)}, f32[8,32,256]{2,1,0:T(8,128)S(1)}, u32[]{:S(2)}, u32[]{:S(2)}) collective-permute-start(f32[8,32,256]{2,1,0:T(8,128)S(1)} %get-tuple-element.140), channel_id=1, source_target_pairs={{0,192},{192,0},{64,128},{128,64},{1,193},{193,1},{65,129},{129,65... | collective-permute-start | bytes 786440 | tf_op jit(solution)/shard_map/ppermute | solution.py:524
  140.8 20.0 %collective-permute-start.37 = (f32[8,32,256]{2,1,0:T(8,128)S(1)}, f32[8,32,256]{2,1,0:T(8,128)S(1)}, u32[]{:S(2)}, u32[]{:S(2)}) collective-permute-start(f32[8,32,256]{2,1,0:T(8,128)S(1)} %get-tuple-element.141), channel_id=1, source_target_pairs={{0,64},{64,0},{128,192},{192,128},{1,65},{65,1},{129,193},{193,129... | collective-permute-start | bytes 786440 | tf_op jit(solution)/shard_map/ppermute | solution.py:525
  140.8 7.8 %collective-permute-start.28 = (f32[16,256]{1,0:T(8,128)S(1)}, f32[16,256]{1,0:T(8,128)S(1)}, u32[]{:S(2)}, u32[]{:S(2)}) collective-permute-start(f32[16,256]{1,0:T(8,128)S(1)} %get-tuple-element.136), channel_id=1, source_target_pairs={{0,1},{1,2},{2,3},{3,0},{4,5},{5,6},{6,7},{7,4},{8,9},{9,10},{10,1... | collective-permute-start | bytes 49160 | tf_op jit(solution)/shard_map/ppermute | solution.py:119
  142.2 9.6 %collective-permute-start.26 = (f32[32,256]{1,0:T(8,128)S(1)}, f32[32,256]{1,0:T(8,128)S(1)}, u32[]{:S(2)}, u32[]{:S(2)}) collective-permute-start(f32[32,256]{1,0:T(8,128)S(1)} %get-tuple-element.134), channel_id=1, source_target_pairs={{0,4},{4,8},{8,12},{12,16},{16,20},{20,24},{24,28},{28,32},{32,36}... | collective-permute-start | bytes 98312 | tf_op jit(solution)/shard_map/ppermute | solution.py:119
  148.6 7.1 %collective-permute-start.27 = (f32[32,256]{1,0:T(8,128)S(1)}, f32[32,256]{1,0:T(8,128)S(1)}, u32[]{:S(2)}, u32[]{:S(2)}) collective-permute-start(f32[32,256]{1,0:T(8,128)S(1)} %get-tuple-element.135), channel_id=1, source_target_pairs={{0,60},{4,0},{8,4},{12,8},{16,12},{20,16},{24,20},{28,24},{32,28},... | collective-permute-start | bytes 98312 | tf_op jit(solution)/shard_map/ppermute | solution.py:119
  148.6 3.2 %collective-permute-start.29 = (f32[16,256]{1,0:T(8,128)S(1)}, f32[16,256]{1,0:T(8,128)S(1)}, u32[]{:S(2)}, u32[]{:S(2)}) collective-permute-start(f32[16,256]{1,0:T(8,128)S(1)} %get-tuple-element.137), channel_id=1, source_target_pairs={{0,3},{1,0},{2,1},{3,2},{4,7},{5,4},{6,5},{7,6},{8,11},{9,8},{10,9... | collective-permute-start | bytes 49160 | tf_op jit(solution)/shard_map/ppermute | solution.py:119
  157.9 13.7 %collective-permute-start.32 = (f32[8,32,256]{2,1,0:T(8,128)S(1)}, f32[8,32,256]{2,1,0:T(8,128)S(1)}, u32[]{:S(2)}, u32[]{:S(2)}) collective-permute-start(f32[8,32,256]{2,1,0:T(8,128)S(1)} %get-tuple-element.142.fa), channel_id=1, source_target_pairs={{0,64},{64,0},{128,192},{192,128},{1,65},{65,1},{129,193},{193,129... | collective-permute-start | bytes 786440 | tf_op jit(solution)/shard_map/ppermute | solution.py:518
  159.7 11.9 %collective-permute-start.33 = (f32[8,32,256]{2,1,0:T(8,128)S(1)}, f32[8,32,256]{2,1,0:T(8,128)S(1)}, u32[]{:S(2)}, u32[]{:S(2)}) collective-permute-start(f32[8,32,256]{2,1,0:T(8,128)S(1)} %get-tuple-element.143.fb), channel_id=1, source_target_pairs={{0,192},{192,0},{64,128},{128,64},{1,193},{193,1},{65,129},{129,65... | collective-permute-start | bytes 786440 | tf_op jit(solution)/shard_map/ppermute | solution.py:519
  170.1 8.4 %collective-permute-start.38 = (f32[41,8,256]{2,1,0:T(8,128)S(1)}, f32[41,8,256]{2,1,0:T(8,128)S(1)}, u32[]{:S(2)}, u32[]{:S(2)}) collective-permute-start(f32[41,8,256]{2,1,0:T(8,128)S(1)} %get-tuple-element.151), channel_id=1, source_target_pairs={{0,1},{1,2},{2,3},{3,0},{4,5},{5,6},{6,7},{7,4},{8,9},{9,10},{10,1... | collective-permute-start | bytes 1007624 | tf_op jit(solution)/shard_map/ppermute | solution.py:119
  171.6 8.6 %collective-permute-start.39 = (f32[41,8,256]{2,1,0:T(8,128)S(1)}, f32[41,8,256]{2,1,0:T(8,128)S(1)}, u32[]{:S(2)}, u32[]{:S(2)}) collective-permute-start(f32[41,8,256]{2,1,0:T(8,128)S(1)} %get-tuple-element.152), channel_id=1, source_target_pairs={{0,3},{1,0},{2,1},{3,2},{4,7},{5,4},{6,5},{7,6},{8,11},{9,8},{10,9... | collective-permute-start | bytes 1007624 | tf_op jit(solution)/shard_map/ppermute | solution.py:119
  172.3 8.6 %collective-permute-start.34 = (f32[8,32,256]{2,1,0:T(8,128)S(1)}, f32[8,32,256]{2,1,0:T(8,128)S(1)}, u32[]{:S(2)}, u32[]{:S(2)}) collective-permute-start(f32[8,32,256]{2,1,0:T(8,128)S(1)} %get-tuple-element.146), channel_id=1, source_target_pairs={{0,192},{192,0},{64,128},{128,64},{1,193},{193,1},{65,129},{129,65... | collective-permute-start | bytes 786440 | tf_op jit(solution)/shard_map/ppermute | solution.py:524
  174.5 7.2 %collective-permute-start.35 = (f32[8,32,256]{2,1,0:T(8,128)S(1)}, f32[8,32,256]{2,1,0:T(8,128)S(1)}, u32[]{:S(2)}, u32[]{:S(2)}) collective-permute-start(f32[8,32,256]{2,1,0:T(8,128)S(1)} %get-tuple-element.147), channel_id=1, source_target_pairs={{0,64},{64,0},{128,192},{192,128},{1,65},{65,1},{129,193},{193,129... | collective-permute-start | bytes 786440 | tf_op jit(solution)/shard_map/ppermute | solution.py:525
  191.0 7.5 %collective-permute-start.40 = (f32[41,8,256]{2,1,0:T(8,128)S(1)}, f32[41,8,256]{2,1,0:T(8,128)S(1)}, u32[]{:S(2)}, u32[]{:S(2)}) collective-permute-start(f32[41,8,256]{2,1,0:T(8,128)S(1)} %get-tuple-element.158), channel_id=1, source_target_pairs={{0,1},{1,2},{2,3},{3,0},{4,5},{5,6},{6,7},{7,4},{8,9},{9,10},{10,1... | collective-permute-start | bytes 1007624 | tf_op jit(solution)/shard_map/ppermute | solution.py:119
  192.7 9.7 %collective-permute-start.41 = (f32[41,8,256]{2,1,0:T(8,128)S(1)}, f32[41,8,256]{2,1,0:T(8,128)S(1)}, u32[]{:S(2)}, u32[]{:S(2)}) collective-permute-start(f32[41,8,256]{2,1,0:T(8,128)S(1)} %get-tuple-element.159), channel_id=1, source_target_pairs={{0,3},{1,0},{2,1},{3,2},{4,7},{5,4},{6,5},{7,6},{8,11},{9,8},{10,9... | collective-permute-start | bytes 1007624 | tf_op jit(solution)/shard_map/ppermute | solution.py:119
  192.7 24.3 %collective-permute-start.45 = (f32[12,32,256]{2,1,0:T(8,128)S(1)}, f32[12,32,256]{2,1,0:T(8,128)S(1)}, u32[]{:S(2)}, u32[]{:S(2)}) collective-permute-start(f32[12,32,256]{2,1,0:T(8,128)S(1)} %get-tuple-element.153), channel_id=1, source_target_pairs={{0,60},{4,0},{8,4},{12,8},{16,12},{20,16},{24,20},{28,24},{32,28},... | collective-permute-start | bytes 1179656 | tf_op jit(solution)/shard_map/ppermute | solution.py:119
  192.7 26.8 %collective-permute-start.44 = (f32[12,32,256]{2,1,0:T(8,128)S(1)}, f32[12,32,256]{2,1,0:T(8,128)S(1)}, u32[]{:S(2)}, u32[]{:S(2)}) collective-permute-start(f32[12,32,256]{2,1,0:T(8,128)S(1)} %get-tuple-element.154), channel_id=1, source_target_pairs={{0,4},{4,8},{8,12},{12,16},{16,20},{20,24},{24,28},{28,32},{32,36}... | collective-permute-start | bytes 1179656 | tf_op jit(solution)/shard_map/ppermute | solution.py:119
  203.1 25.4 %collective-permute-start.42 = (f32[12,32,256]{2,1,0:T(8,128)S(1)}, f32[12,32,256]{2,1,0:T(8,128)S(1)}, u32[]{:S(2)}, u32[]{:S(2)}) collective-permute-start(f32[12,32,256]{2,1,0:T(8,128)S(1)} %get-tuple-element.161), channel_id=1, source_target_pairs={{0,4},{4,8},{8,12},{12,16},{16,20},{20,24},{24,28},{28,32},{32,36}... | collective-permute-start | bytes 1179656 | tf_op jit(solution)/shard_map/ppermute | solution.py:119
  217.0 26.2 %collective-permute-start.43 = (f32[12,32,256]{2,1,0:T(8,128)S(1)}, f32[12,32,256]{2,1,0:T(8,128)S(1)}, u32[]{:S(2)}, u32[]{:S(2)}) collective-permute-start(f32[12,32,256]{2,1,0:T(8,128)S(1)} %get-tuple-element.162), channel_id=1, source_target_pairs={{0,60},{4,0},{8,4},{12,8},{16,12},{20,16},{24,20},{28,24},{32,28},... | collective-permute-start | bytes 1179656 | tf_op jit(solution)/shard_map/ppermute | solution.py:119

commit v5 on v4

--- a/solution.py
+++ b/solution.py
@@ -119,6 +119,21 @@
     return lax.ppermute(array, axis, ring(lax.axis_size(axis), step))
 
 
+def halves(values):
+    high = values.astype(jnp.bfloat16)
+    return high, (values - high.astype(jnp.float32)).astype(jnp.bfloat16)
+
+
+def product(values, high, low, side):
+    a, b = halves(values)
+
+    def dot(x, y):
+        return lax.dot_general(x, y[...], (((1,), (side,)), ((), ())),
+                               preferred_element_type=jnp.float32)
+
+    return dot(a, high) + (dot(a, low) + dot(b, high))
+
+
 def call(kernel, outs, args, scratch=(), flops=1_000_000):
     vmem = pl.BlockSpec(memory_space=pltpu.VMEM)
     smem = pl.BlockSpec(memory_space=pltpu.SMEM)
@@ -168,7 +183,7 @@
     lane = lax.broadcasted_iota(jnp.int32, (8, LANES), 1)
 
     def run(base, f, d):
-        def plane(i, carry):
+        def plane(i):
             p = base + i
             for t in range(YB // 8):
                 r = 8 + 8 * t
@@ -190,9 +205,13 @@
                         react = uvv - (fr + kill[p, out, lanes]) * v
                     f[i, out, lanes] = sc[11] * lap + react
                     d[i, out, lanes] = sc[8] * lap
+
+        def planes(i, carry):
+            plane(2 * i)
+            plane(2 * i + 1)
             return carry
 
-        lax.fori_loop(0, HALF, plane, 0)
+        lax.fori_loop(0, HALF // 2, planes, 0)
 
     run(0, fa, da)
     run(HALF, fb, db)
@@ -206,10 +225,12 @@
         ylast[p:p + 1, :] = x[p, YB - 1:YB, :]
 
 
-def prepare_kernel(sc, x, wide, near, xu, xv, ha, hb, basis, *edges):
-    for a in range(ZB // 8):
-        rows = wide[0, a:a + 1, :] * near[0] + wide[1, a:a + 1, :] * near[1]
-        basis[8 * a:8 * a + 8, :] = rows
+def prepare_kernel(sc, x, wide, near, xu, xv, ha, hb, bhi, blo, *edges):
+    for a in range(0, ZB // 8, 2):
+        rows = jnp.concatenate(
+            [wide[0, b:b + 1, :] * near[0] + wide[1, b:b + 1, :] * near[1] for b in (a, a + 1)], 0
+        )
+        bhi[8 * a:8 * a + 16, :], blo[8 * a:8 * a + 16, :] = halves(rows)
     for s, dst in enumerate((xu, xv)):
         edges_of(x.at[s], *(edge.at[s] for edge in edges))
 
@@ -227,9 +248,9 @@
 
 
 def prepare(*args):
-    outs = [(XB, YB, ZB)] * 2 + [(2, HALF, YB, ZB)] * 2 + [(ZB, ZB)]
-    outs += [(2, *e) for e in EDGES]
-    return call(prepare_kernel, [local(*o) for o in outs], args)
+    outs = [local(*o) for o in [(XB, YB, ZB)] * 2 + [(2, HALF, YB, ZB)] * 2]
+    outs += [pltpu.VMEM((ZB, ZB), jnp.bfloat16)] * 2 + [local(2, *e) for e in EDGES]
+    return call(prepare_kernel, outs, args)
 
 
 def forces(species, *args):
@@ -259,7 +280,7 @@
     return call(partial_kernel, [local(HALF, YB, ZB)] * 2, args)
 
 
-def jacobi_kernel(sc, basis, sums, x, x0, na, nb, fa, fb, ga, gb, da, db, ra, rb,
+def jacobi_kernel(sc, bhi, blo, sums, x, x0, na, nb, fa, fb, ga, gb, da, db, ra, rb,
                   core, yhi, ylo, one, two, bs, right):
     spread, scale = sc[9], sc[10]
     species = sc[12].astype(jnp.int32)
@@ -275,10 +296,7 @@
     lax.fori_loop(0, PLANES, clear, 0)
 
     def modes(values):
-        flat = values.reshape(-1, ZB)
-        done = jnp.dot(flat, basis[...], precision=lax.Precision.HIGHEST,
-                       preferred_element_type=jnp.float32)
-        return done.reshape(values.shape)
+        return product(values.reshape(-1, ZB), bhi, blo, 0).reshape(values.shape)
 
     def gather(half, f, g, d, n, recv, weight):
         def plane(i, carry):
@@ -416,7 +434,7 @@
     return call(gather_kernel, [local(JACOBI, YB, ZB)] * 2 + [local(XB, YB, ZB)], args)
 
 
-def back(basis, c, low, high, total, give):
+def back(bhi, blo, c, low, high, total, give):
     gap = XB - JACOBI
 
     def add(p, carry):
@@ -436,35 +454,33 @@
     lax.fori_loop(0, JACOBI, add_high, 0)
 
     def turn(i, carry):
-        flat = total[pl.ds(4 * i, 4)].reshape(4 * YB, ZB)
-        done = lax.dot_general(flat, basis[...], (((1,), (1,)), ((), ())),
-                               precision=lax.Precision.HIGHEST,
-                               preferred_element_type=jnp.float32)
-        give(4 * i, done.reshape(4, YB, ZB))
-        return carry
-
-    lax.fori_loop(0, XB // 4, turn, 0)
-
-
-def middle_kernel(sc, basis, c, low, high, out, xfirst, xlast, yfirst, ylast, total):
+        flat = total[pl.ds(8 * i, 8)].reshape(8 * YB, ZB)
+        done = product(flat, bhi, blo, 1)
+        give(8 * i, done.reshape(8, YB, ZB))
+        return carry
+
+    lax.fori_loop(0, XB // 8, turn, 0)
+
+
+def middle_kernel(sc, bhi, blo, c, low, high, out, xfirst, xlast, yfirst, ylast, total):
 
     def give(p, value):
-        out[pl.ds(p, 4)] = value
-
-    back(basis, c, low, high, total, give)
+        out[pl.ds(p, 8)] = value
+
+    back(bhi, blo, c, low, high, total, give)
     edges_of(out, xfirst, xlast, yfirst, ylast)
 
 
-def last_kernel(sc, basis, c, low, high, xu, out, total):
+def last_kernel(sc, bhi, blo, c, low, high, xu, out, total):
     def give(p, value):
-        out[1, pl.ds(p, 4)] = value
+        out[1, pl.ds(p, 8)] = value
 
     def copy(p, carry):
         out[0, p] = xu[p]
         return carry
 
     lax.fori_loop(0, XB, copy, 0)
-    back(basis, c, low, high, total, give)
+    back(bhi, blo, c, low, high, total, give)
 
 
 TOTAL = [pltpu.VMEM((XB, YB, ZB), jnp.float32)]
@@ -488,7 +504,7 @@
     sc = jnp.asarray(node_table(), jnp.float32)[lax.axis_index("node")]
     wide, near, sums = map(jnp.asarray, fourier())
     hold = lax.optimization_barrier
-    xu, xv, ha, hb, basis, *edges = prepare(sc[0], previous[0], wide, near)
+    xu, xv, ha, hb, bhi, blo, *edges = prepare(sc[0], previous[0], wide, near)
     x0 = (xu, xv)
     na = lax.ppermute(ha, "node", [(3, 2)])
     nb = lax.ppermute(hb, "node", [(3, 0)])
@@ -526,14 +542,14 @@
             if s == 1:
                 ra, rb, _, _ = hold((ra, rb, left, right))
             core, up, down = jacobi(
-                sc[s], basis, sums, xs[s], x0[s], na, nb, fa, fb, ga, gb, da, db, ra, rb
+                sc[s], bhi, blo, sums, xs[s], x0[s], na, nb, fa, fb, ga, gb, da, db, ra, rb
             )
             low = shifted(up, "sy", 1)
             high = shifted(down, "sy", -1)
             left, right, center = gathered(sc[0], core, low, high)
             low = shifted(right, "sx", 1)
             high = shifted(left, "sx", -1)
-            parts = (sc[0], basis, center, low, high)
+            parts = (sc[0], bhi, blo, center, low, high)
             if s == 0:
                 xu, *rest = middle(*parts)
             elif more:

time: 247 us -> 242 us (0.980)
  the two profiles are of different devices: /device:TPU:89 before, /device:TPU:1 now
where the time goes in v5:
time: 242 us; the launch traced here: 237 us
  waiting for transfers between devices  103 us (43%)
  starting transfers between devices  75.5 us (31%)
  Pallas kernels  55.2 us (23%)
  local copies, waits for them, and re-layouts  3.57 us (1%)
    ppermute x28, waiting for transfers between devices, shifted(): return lax.ppermute(array, axis, ring(lax.axis_size(axis), step))  84.8 us
    ppermute x28, starting transfers between devices, shifted(): return lax.ppermute(array, axis, ring(lax.axis_size(axis), step))  55.8 us
    pallas_call x21, Pallas kernels, call(): pl.pallas_call(kernel, out_shape=tuple(outs), in_specs=[smem] + [vmem] *...  55.2 us
    ppermute x4, waiting for transfers between devices, body(): ga = lax.ppermute(fa, 'node', PAIR_A)  9.88 us
    ppermute x4, starting transfers between devices, body(): ra = lax.ppermute(pa, 'node', PAIR_B)  7.31 us
    ppermute x4, starting transfers between devices, body(): gb = lax.ppermute(fb, 'node', PAIR_B)  6.56 us
  transfers between devices with their start and end apart: 46, of which 21 were waited for; matrix products, arithmetic and copies ran while one was open for 0% of the time, Pallas kernels for 13%

profile of v5, /device:TPU:1, one launch (start us, length us, event | category | flops | bytes accessed | tf_op | source)
XLA Modules:
  0.0 237.2 jit_solution(9944957237719859158)
XLA Ops:
  0.0 0.8 constant_dynamic-slice_fusion
  0.8 1.2 copy-done.2
  2.0 0.8 copy-done.4
  3.6 0.8 shard_map.73
  5.1 1.3 collective-permute-start.1
  6.4 3.1 %collective-permute-start.4 = (f32[2,16,256]{2,1,0:T(8,128)S(1)}, f32[2,16,256]{2,1,0:T(8,128)S(1)}, u32[]{:S(2)}, u32[]{:S(2)}) collective-permute-start(f32[2,16,256]{2,1,0:T(8,128)S(1)} %get-tuple-element.94), channel_id=1, source_target_pairs={{0,1},{1,2},{2,3},{3,0},{4,5},{5,6},{6,7},{7,4},{8,9},{9,10},{10,1... | collective-permute-start | bytes 98312 | tf_op jit(solution)/shard_map/ppermute | solution.py:119
  9.5 1.3 collective-permute-start.2
  10.8 6.3 %collective-permute-start.3 = (f32[2,32,256]{2,1,0:T(8,128)S(1)}, f32[2,32,256]{2,1,0:T(8,128)S(1)}, u32[]{:S(2)}, u32[]{:S(2)}) collective-permute-start(f32[2,32,256]{2,1,0:T(8,128)S(1)} %get-tuple-element.93), channel_id=1, source_target_pairs={{0,60},{4,0},{8,4},{12,8},{16,12},{20,16},{24,20},{28,24},{32,28},... | collective-permute-start | bytes 196616 | tf_op jit(solution)/shard_map/ppermute | solution.py:119
  17.0 4.5 %collective-permute-done.5.refs_6_ = f32[2,16,256]{2,1,0:T(8,128)S(1)} collective-permute-done((f32[2,16,256]{2,1,0:T(8,128)S(1)}, f32[2,16,256]{2,1,0:T(8,128)S(1)}, u32[]{:S(2)}, u32[]{:S(2)}) %collective-permute-start.5) | collective-permute-done | bytes 32800 | tf_op jit(solution)/shard_map/ppermute | solution.py:119
  21.5 1.5 shard_map.75
  23.5 4.1 %collective-permute-start.7 = (f32[8,32,256]{2,1,0:T(8,128)S(1)}, f32[8,32,256]{2,1,0:T(8,128)S(1)}, u32[]{:S(2)}, u32[]{:S(2)}) collective-permute-start(f32[8,32,256]{2,1,0:T(8,128)S(1)} %get-tuple-element.99.fb), channel_id=1, source_target_pairs={{0,192},{192,0},{64,128},{128,64},{1,193},{193,1},{65,129},{129,65... | collective-permute-start | bytes 786440 | tf_op jit(solution)/shard_map/ppermute | solution.py:535
  27.5 3.6 %collective-permute-done.6.ga = f32[8,32,256]{2,1,0:T(8,128)S(1)} collective-permute-done((f32[8,32,256]{2,1,0:T(8,128)S(1)}, f32[8,32,256]{2,1,0:T(8,128)S(1)}, u32[]{:S(2)}, u32[]{:S(2)}) %collective-permute-start.6) | collective-permute-done | bytes 262176 | tf_op jit(solution)/shard_map/ppermute | solution.py:534
  31.2 2.7 %collective-permute-done.7.gb = f32[8,32,256]{2,1,0:T(8,128)S(1)} collective-permute-done((f32[8,32,256]{2,1,0:T(8,128)S(1)}, f32[8,32,256]{2,1,0:T(8,128)S(1)}, u32[]{:S(2)}, u32[]{:S(2)}) %collective-permute-start.7) | collective-permute-done | bytes 262176 | tf_op jit(solution)/shard_map/ppermute | solution.py:535
  33.9 0.7 shard_map.76
  34.6 3.3 %collective-permute-start.12 = (f32[8,32,256]{2,1,0:T(8,128)S(1)}, f32[8,32,256]{2,1,0:T(8,128)S(1)}, u32[]{:S(2)}, u32[]{:S(2)}) collective-permute-start(f32[8,32,256]{2,1,0:T(8,128)S(1)} %get-tuple-element.100), channel_id=1, source_target_pairs={{0,192},{192,0},{64,128},{128,64},{1,193},{193,1},{65,129},{129,65... | collective-permute-start | bytes 786440 | tf_op jit(solution)/shard_map/ppermute | solution.py:540
  37.9 1.5 shard_map.74
  39.5 1.5 collective-permute-start.8
  41.1 3.1 %collective-permute-done.12.ra = f32[8,32,256]{2,1,0:T(8,128)S(1)} collective-permute-done((f32[8,32,256]{2,1,0:T(8,128)S(1)}, f32[8,32,256]{2,1,0:T(8,128)S(1)}, u32[]{:S(2)}, u32[]{:S(2)}) %collective-permute-start.12) | collective-permute-done | bytes 262176 | tf_op jit(solution)/shard_map/ppermute | solution.py:540
  44.2 0.9 collective-permute-done.13.rb
  45.1 8.8 %shard_map.78 = (f32[40,32,256]{2,1,0:T(8,128)S(1)}, f32[41,8,256]{2,1,0:T(8,128)S(1)}, f32[41,8,256]{2,1,0:T(8,128)S(1)}) custom-call(f32[13]{0:T(128)S(1)} %get-tuple-element.168.sc.refs_0_, bf16[256,256]{1,0:T(8,128)(2,1)S(1)} %get-tuple-element.86.bhi, bf16[256,256]{1,0:T(8,128)(2,1)S(1)} %get-tuple-element.87.blo, f32[8,256]{1,0:T(8,128)S(1)} %copy-done.3, ...), custom_call_target="tpu_custom_call" | custom-call | flops 60000000 | bytes 1000000 | tf_op jit(solution)/shard_map/pallas_call | solution.py:140
  53.9 2.6 %collective-permute-start.14 = (f32[41,8,256]{2,1,0:T(8,128)S(1)}, f32[41,8,256]{2,1,0:T(8,128)S(1)}, u32[]{:S(2)}, u32[]{:S(2)}) collective-permute-start(f32[41,8,256]{2,1,0:T(8,128)S(1)} %get-tuple-element.111), channel_id=1, source_target_pairs={{0,1},{1,2},{2,3},{3,0},{4,5},{5,6},{6,7},{7,4},{8,9},{9,10},{10,1... | collective-permute-start | bytes 1007624 | tf_op jit(solution)/shard_map/ppermute | solution.py:119
  57.4 1.0 collective-permute-start.10
  58.5 3.6 %collective-permute-done.14.low = f32[41,8,256]{2,1,0:T(8,128)S(1)} collective-permute-done((f32[41,8,256]{2,1,0:T(8,128)S(1)}, f32[41,8,256]{2,1,0:T(8,128)S(1)}, u32[]{:S(2)}, u32[]{:S(2)}) %collective-permute-start.14) | collective-permute-done | bytes 335904 | tf_op jit(solution)/shard_map/ppermute | solution.py:119
  62.1 4.3 %collective-permute-done.15.high = f32[41,8,256]{2,1,0:T(8,128)S(1)} collective-permute-done((f32[41,8,256]{2,1,0:T(8,128)S(1)}, f32[41,8,256]{2,1,0:T(8,128)S(1)}, u32[]{:S(2)}, u32[]{:S(2)}) %collective-permute-start.15) | collective-permute-done | bytes 335904 | tf_op jit(solution)/shard_map/ppermute | solution.py:119
  67.2 8.8 %shard_map.80 = (f32[40,32,256]{2,1,0:T(8,128)S(1)}, f32[41,8,256]{2,1,0:T(8,128)S(1)}, f32[41,8,256]{2,1,0:T(8,128)S(1)}) custom-call(f32[13]{0:T(128)S(1)} %get-tuple-element.167.refs_0_.sc, bf16[256,256]{1,0:T(8,128)(2,1)S(1)} %get-tuple-element.86.bhi, bf16[256,256]{1,0:T(8,128)(2,1)S(1)} %get-tuple-element.87.blo, f32[8,256]{1,0:T(8,128)S(1)} %copy-done.3, ...), custom_call_target="tpu_custom_call" | custom-call | flops 60000000 | bytes 1000000 | tf_op jit(solution)/shard_map/pallas_call | solution.py:140
  75.9 1.5 collective-permute-start.16
  77.5 5.5 %collective-permute-start.21 = (f32[12,32,256]{2,1,0:T(8,128)S(1)}, f32[12,32,256]{2,1,0:T(8,128)S(1)}, u32[]{:S(2)}, u32[]{:S(2)}) collective-permute-start(f32[12,32,256]{2,1,0:T(8,128)S(1)} %get-tuple-element.113), channel_id=1, source_target_pairs={{0,60},{4,0},{8,4},{12,8},{16,12},{20,16},{24,20},{28,24},{32,28},... | collective-permute-start | bytes 1179656 | tf_op jit(solution)/shard_map/ppermute | solution.py:119
  83.0 1.4 collective-permute-done.16.low
  84.4 15.4 %collective-permute-done.17.high = f32[41,8,256]{2,1,0:T(8,128)S(1)} collective-permute-done((f32[41,8,256]{2,1,0:T(8,128)S(1)}, f32[41,8,256]{2,1,0:T(8,128)S(1)}, u32[]{:S(2)}, u32[]{:S(2)}) %collective-permute-start.17) | collective-permute-done | bytes 335904 | tf_op jit(solution)/shard_map/ppermute | solution.py:119
  99.8 0.7 shard_map.81
  100.6 5.7 %collective-permute-start.19 = (f32[12,32,256]{2,1,0:T(8,128)S(1)}, f32[12,32,256]{2,1,0:T(8,128)S(1)}, u32[]{:S(2)}, u32[]{:S(2)}) collective-permute-start(f32[12,32,256]{2,1,0:T(8,128)S(1)} %get-tuple-element.122), channel_id=1, source_target_pairs={{0,60},{4,0},{8,4},{12,8},{16,12},{20,16},{24,20},{28,24},{32,28},... | collective-permute-start | bytes 1179656 | tf_op jit(solution)/shard_map/ppermute | solution.py:119
  106.3 4.9 %collective-permute-done.20.low = f32[12,32,256]{2,1,0:T(8,128)S(1)} collective-permute-done((f32[12,32,256]{2,1,0:T(8,128)S(1)}, f32[12,32,256]{2,1,0:T(8,128)S(1)}, u32[]{:S(2)}, u32[]{:S(2)}) %collective-permute-start.20) | collective-permute-done | bytes 393248 | tf_op jit(solution)/shard_map/ppermute | solution.py:119
  111.2 1.4 shard_map.83
  112.7 5.7 %collective-permute-start.23 = (f32[32,256]{1,0:T(8,128)S(1)}, f32[32,256]{1,0:T(8,128)S(1)}, u32[]{:S(2)}, u32[]{:S(2)}) collective-permute-start(f32[32,256]{1,0:T(8,128)S(1)} %get-tuple-element.131), channel_id=1, source_target_pairs={{0,60},{4,0},{8,4},{12,8},{16,12},{20,16},{24,20},{28,24},{32,28},... | collective-permute-start | bytes 98312 | tf_op jit(solution)/shard_map/ppermute | solution.py:119
  118.4 6.8 %collective-permute-done.18.low = f32[12,32,256]{2,1,0:T(8,128)S(1)} collective-permute-done((f32[12,32,256]{2,1,0:T(8,128)S(1)}, f32[12,32,256]{2,1,0:T(8,128)S(1)}, u32[]{:S(2)}, u32[]{:S(2)}) %collective-permute-start.18) | collective-permute-done | bytes 393248 | tf_op jit(solution)/shard_map/ppermute | solution.py:119
  125.1 1.7 collective-permute-start.25
  126.8 1.4 shard_map.82
  128.3 4.0 %collective-permute-done.25.refs_6_ = f32[16,256]{1,0:T(8,128)S(1)} collective-permute-done((f32[16,256]{1,0:T(8,128)S(1)}, f32[16,256]{1,0:T(8,128)S(1)}, u32[]{:S(2)}, u32[]{:S(2)}) %collective-permute-start.25) | collective-permute-done | bytes 16416 | tf_op jit(solution)/shard_map/ppermute | solution.py:119
  132.3 1.5 shard_map.84
  134.0 1.5 collective-permute-start.31
  135.5 6.2 %collective-permute-done.30.ga = f32[8,32,256]{2,1,0:T(8,128)S(1)} collective-permute-done((f32[8,32,256]{2,1,0:T(8,128)S(1)}, f32[8,32,256]{2,1,0:T(8,128)S(1)}, u32[]{:S(2)}, u32[]{:S(2)}) %collective-permute-start.30) | collective-permute-done | bytes 262176 | tf_op jit(solution)/shard_map/ppermute | solution.py:534
  141.7 1.3 collective-permute-done.31.gb
  143.8 1.4 collective-permute-start.36
  145.1 1.6 collective-permute-start.28
  146.7 5.7 %collective-permute-start.27 = (f32[32,256]{1,0:T(8,128)S(1)}, f32[32,256]{1,0:T(8,128)S(1)}, u32[]{:S(2)}, u32[]{:S(2)}) collective-permute-start(f32[32,256]{1,0:T(8,128)S(1)} %get-tuple-element.137), channel_id=1, source_target_pairs={{0,60},{4,0},{8,4},{12,8},{16,12},{20,16},{24,20},{28,24},{32,28},... | collective-permute-start | bytes 98312 | tf_op jit(solution)/shard_map/ppermute | solution.py:119
  152.8 2.8 %collective-permute-done.29.refs_6_ = f32[16,256]{1,0:T(8,128)S(1)} collective-permute-done((f32[16,256]{1,0:T(8,128)S(1)}, f32[16,256]{1,0:T(8,128)S(1)}, u32[]{:S(2)}, u32[]{:S(2)}) %collective-permute-start.29) | collective-permute-done | bytes 16416 | tf_op jit(solution)/shard_map/ppermute | solution.py:119
  155.6 1.5 shard_map.85
  157.1 1.8 collective-permute-start.32
  158.9 0.9 collective-permute-start.33
  159.8 8.7 %shard_map.88 = (f32[40,32,256]{2,1,0:T(8,128)S(1)}, f32[41,8,256]{2,1,0:T(8,128)S(1)}, f32[41,8,256]{2,1,0:T(8,128)S(1)}) custom-call(f32[13]{0:T(128)S(1)} %get-tuple-element.168.sc.refs_0_, bf16[256,256]{1,0:T(8,128)(2,1)S(1)} %get-tuple-element.86.bhi, bf16[256,256]{1,0:T(8,128)(2,1)S(1)} %get-tuple-element.87.blo, f32[8,256]{1,0:T(8,128)S(1)} %copy-done.3, ...), custom_call_target="tpu_custom_call" | custom-call | flops 60000000 | bytes 1000000 | tf_op jit(solution)/shard_map/pallas_call | solution.py:140
  170.2 1.6 collective-permute-start.34
  171.8 2.9 %collective-permute-done.38.low = f32[41,8,256]{2,1,0:T(8,128)S(1)} collective-permute-done((f32[41,8,256]{2,1,0:T(8,128)S(1)}, f32[41,8,256]{2,1,0:T(8,128)S(1)}, u32[]{:S(2)}, u32[]{:S(2)}) %collective-permute-start.38) | collective-permute-done | bytes 335904 | tf_op jit(solution)/shard_map/ppermute | solution.py:119
  174.8 4.4 %collective-permute-done.39.high = f32[41,8,256]{2,1,0:T(8,128)S(1)} collective-permute-done((f32[41,8,256]{2,1,0:T(8,128)S(1)}, f32[41,8,256]{2,1,0:T(8,128)S(1)}, u32[]{:S(2)}, u32[]{:S(2)}) %collective-permute-start.39) | collective-permute-done | bytes 335904 | tf_op jit(solution)/shard_map/ppermute | solution.py:119
  179.9 8.8 %shard_map.90 = (f32[40,32,256]{2,1,0:T(8,128)S(1)}, f32[41,8,256]{2,1,0:T(8,128)S(1)}, f32[41,8,256]{2,1,0:T(8,128)S(1)}) custom-call(f32[13]{0:T(128)S(1)} %get-tuple-element.167.refs_0_.sc, bf16[256,256]{1,0:T(8,128)(2,1)S(1)} %get-tuple-element.86.bhi, bf16[256,256]{1,0:T(8,128)(2,1)S(1)} %get-tuple-element.87.blo, f32[8,256]{1,0:T(8,128)S(1)} %copy-done.3, ...), custom_call_target="tpu_custom_call" | custom-call | flops 60000000 | bytes 1000000 | tf_op jit(solution)/shard_map/pallas_call | solution.py:140
  188.7 1.8 collective-permute-start.40
  190.5 5.9 %collective-permute-start.45 = (f32[12,32,256]{2,1,0:T(8,128)S(1)}, f32[12,32,256]{2,1,0:T(8,128)S(1)}, u32[]{:S(2)}, u32[]{:S(2)}) collective-permute-start(f32[12,32,256]{2,1,0:T(8,128)S(1)} %get-tuple-element.155), channel_id=1, source_target_pairs={{0,60},{4,0},{8,4},{12,8},{16,12},{20,16},{24,20},{28,24},{32,28},... | collective-permute-start | bytes 1179656 | tf_op jit(solution)/shard_map/ppermute | solution.py:119
  196.4 0.9 collective-permute-done.40.low
  197.3 11.4 %collective-permute-done.41.high = f32[41,8,256]{2,1,0:T(8,128)S(1)} collective-permute-done((f32[41,8,256]{2,1,0:T(8,128)S(1)}, f32[41,8,256]{2,1,0:T(8,128)S(1)}, u32[]{:S(2)}, u32[]{:S(2)}) %collective-permute-start.41) | collective-permute-done | bytes 335904 | tf_op jit(solution)/shard_map/ppermute | solution.py:119
  208.7 0.7 shard_map.91
  209.5 5.7 %collective-permute-start.43 = (f32[12,32,256]{2,1,0:T(8,128)S(1)}, f32[12,32,256]{2,1,0:T(8,128)S(1)}, u32[]{:S(2)}, u32[]{:S(2)}) collective-permute-start(f32[12,32,256]{2,1,0:T(8,128)S(1)} %get-tuple-element.164), channel_id=1, source_target_pairs={{0,60},{4,0},{8,4},{12,8},{16,12},{20,16},{24,20},{28,24},{32,28},... | collective-permute-start | bytes 1179656 | tf_op jit(solution)/shard_map/ppermute | solution.py:119
  215.2 11.1 %collective-permute-done.44.low = f32[12,32,256]{2,1,0:T(8,128)S(1)} collective-permute-done((f32[12,32,256]{2,1,0:T(8,128)S(1)}, f32[12,32,256]{2,1,0:T(8,128)S(1)}, u32[]{:S(2)}, u32[]{:S(2)}) %collective-permute-start.44) | collective-permute-done | bytes 393248 | tf_op jit(solution)/shard_map/ppermute | solution.py:119
  226.3 2.1 shard_map.92
  228.3 6.4 %collective-permute-done.42.low = f32[12,32,256]{2,1,0:T(8,128)S(1)} collective-permute-done((f32[12,32,256]{2,1,0:T(8,128)S(1)}, f32[12,32,256]{2,1,0:T(8,128)S(1)}, u32[]{:S(2)}, u32[]{:S(2)}) %collective-permute-start.42) | collective-permute-done | bytes 393248 | tf_op jit(solution)/shard_map/ppermute | solution.py:119
  234.7 2.5 %shard_map.93 = f32[2,16,32,256]{3,2,1,0:T(8,128)} custom-call(f32[13]{0:T(128)S(1)} %get-tuple-element.168.sc.refs_0_, bf16[256,256]{1,0:T(8,128)(2,1)S(1)} %get-tuple-element.86.bhi, bf16[256,256]{1,0:T(8,128)(2,1)S(1)} %get-tuple-element.87.blo, f32[16,32,256]{2,1,0:T(8,128)S(1)} %get-tuple-element.162.c, f32[12,32,256]{2,1,0:T(8,128)S(1)} %collective-permute-done.42.low, ...), custom_call_target="tpu_custom_call" | custom-call | flops 1000000 | bytes 1000000 | tf_op jit(solution)/shard_map/pallas_call | solution.py:140
  (63 shorter events, 7.6 us)
Async XLA Ops:
  0.0 21.5 %copy-start.1 = (f32[16,32,256]{2,1,0:T(8,128)S(1)}, f32[16,32,256]{2,1,0:T(8,128)}, u32[]{:S(2)}) copy-start(f32[16,32,256]{2,1,0:T(8,128)} %refs_8_.7) | copy-start | bytes 1572868
  0.0 21.5 %copy-start = (f32[16,32,256]{2,1,0:T(8,128)S(1)}, f32[16,32,256]{2,1,0:T(8,128)}, u32[]{:S(2)}) copy-start(f32[16,32,256]{2,1,0:T(8,128)} %refs_7_.7) | copy-start | bytes 1572868
  0.8 1.2 copy-start.2
  2.0 0.8 copy-start.4
  2.8 0.7 copy-start.5
  4.4 29.5 %collective-permute-start = (f32[2,8,32,256]{3,2,1,0:T(8,128)S(1)}, f32[2,8,32,256]{3,2,1,0:T(8,128)S(1)}, u32[]{:S(2)}, u32[]{:S(2)}) collective-permute-start(f32[2,8,32,256]{3,2,1,0:T(8,128)S(1)} %get-tuple-element.89), channel_id=1, source_target_pairs={{192,128},{193,129},{194,130},{195,131},{196,132},{197,133},{198,1... | collective-permute-start | bytes 1572872 | tf_op jit(solution)/shard_map/ppermute | solution.py:509
  5.1 28.8 %collective-permute-start.1 = (f32[2,8,32,256]{3,2,1,0:T(8,128)S(1)}, f32[2,8,32,256]{3,2,1,0:T(8,128)S(1)}, u32[]{:S(2)}, u32[]{:S(2)}) collective-permute-start(f32[2,8,32,256]{3,2,1,0:T(8,128)S(1)} %get-tuple-element.90), channel_id=1, source_target_pairs={{192,0},{193,1},{194,2},{195,3},{196,4},{197,5},{198,6},{199,7},{2... | collective-permute-start | bytes 1572872 | tf_op jit(solution)/shard_map/ppermute | solution.py:510
  6.4 10.7 %collective-permute-start.4 = (f32[2,16,256]{2,1,0:T(8,128)S(1)}, f32[2,16,256]{2,1,0:T(8,128)S(1)}, u32[]{:S(2)}, u32[]{:S(2)}) collective-permute-start(f32[2,16,256]{2,1,0:T(8,128)S(1)} %get-tuple-element.94), channel_id=1, source_target_pairs={{0,1},{1,2},{2,3},{3,0},{4,5},{5,6},{6,7},{7,4},{8,9},{9,10},{10,1... | collective-permute-start | bytes 98312 | tf_op jit(solution)/shard_map/ppermute | solution.py:119
  9.5 12.1 %collective-permute-start.2 = (f32[2,32,256]{2,1,0:T(8,128)S(1)}, f32[2,32,256]{2,1,0:T(8,128)S(1)}, u32[]{:S(2)}, u32[]{:S(2)}) collective-permute-start(f32[2,32,256]{2,1,0:T(8,128)S(1)} %get-tuple-element.92), channel_id=1, source_target_pairs={{0,4},{4,8},{8,12},{12,16},{16,20},{20,24},{24,28},{28,32},{32,36}... | collective-permute-start | bytes 196616 | tf_op jit(solution)/shard_map/ppermute | solution.py:119
  10.8 10.8 %collective-permute-start.3 = (f32[2,32,256]{2,1,0:T(8,128)S(1)}, f32[2,32,256]{2,1,0:T(8,128)S(1)}, u32[]{:S(2)}, u32[]{:S(2)}) collective-permute-start(f32[2,32,256]{2,1,0:T(8,128)S(1)} %get-tuple-element.93), channel_id=1, source_target_pairs={{0,60},{4,0},{8,4},{12,8},{16,12},{20,16},{24,20},{28,24},{32,28},... | collective-permute-start | bytes 196616 | tf_op jit(solution)/shard_map/ppermute | solution.py:119
  17.0 4.5 %collective-permute-start.5 = (f32[2,16,256]{2,1,0:T(8,128)S(1)}, f32[2,16,256]{2,1,0:T(8,128)S(1)}, u32[]{:S(2)}, u32[]{:S(2)}) collective-permute-start(f32[2,16,256]{2,1,0:T(8,128)S(1)} %get-tuple-element.95), channel_id=1, source_target_pairs={{0,3},{1,0},{2,1},{3,2},{4,7},{5,4},{6,5},{7,6},{8,11},{9,8},{10,9... | collective-permute-start | bytes 98312 | tf_op jit(solution)/shard_map/ppermute | solution.py:119
  23.1 8.1 %collective-permute-start.6 = (f32[8,32,256]{2,1,0:T(8,128)S(1)}, f32[8,32,256]{2,1,0:T(8,128)S(1)}, u32[]{:S(2)}, u32[]{:S(2)}) collective-permute-start(f32[8,32,256]{2,1,0:T(8,128)S(1)} %get-tuple-element.98.fa), channel_id=1, source_target_pairs={{0,64},{64,0},{128,192},{192,128},{1,65},{65,1},{129,193},{193,129... | collective-permute-start | bytes 786440 | tf_op jit(solution)/shard_map/ppermute | solution.py:534
  23.5 10.4 %collective-permute-start.7 = (f32[8,32,256]{2,1,0:T(8,128)S(1)}, f32[8,32,256]{2,1,0:T(8,128)S(1)}, u32[]{:S(2)}, u32[]{:S(2)}) collective-permute-start(f32[8,32,256]{2,1,0:T(8,128)S(1)} %get-tuple-element.99.fb), channel_id=1, source_target_pairs={{0,192},{192,0},{64,128},{128,64},{1,193},{193,1},{65,129},{129,65... | collective-permute-start | bytes 786440 | tf_op jit(solution)/shard_map/ppermute | solution.py:535
  34.6 10.5 %copy-start.3 = (f32[8,256]{1,0:T(8,128)S(1)}, f32[8,256]{1,0:T(8,128)}, u32[]{:S(2)}) copy-start(f32[8,256]{1,0:T(8,128)} %constant.21.clone.sums) | copy-start | bytes 24580
  34.6 9.6 %collective-permute-start.12 = (f32[8,32,256]{2,1,0:T(8,128)S(1)}, f32[8,32,256]{2,1,0:T(8,128)S(1)}, u32[]{:S(2)}, u32[]{:S(2)}) collective-permute-start(f32[8,32,256]{2,1,0:T(8,128)S(1)} %get-tuple-element.100), channel_id=1, source_target_pairs={{0,192},{192,0},{64,128},{128,64},{1,193},{193,1},{65,129},{129,65... | collective-permute-start | bytes 786440 | tf_op jit(solution)/shard_map/ppermute | solution.py:540
  37.9 7.2 %collective-permute-start.13 = (f32[8,32,256]{2,1,0:T(8,128)S(1)}, f32[8,32,256]{2,1,0:T(8,128)S(1)}, u32[]{:S(2)}, u32[]{:S(2)}) collective-permute-start(f32[8,32,256]{2,1,0:T(8,128)S(1)} %get-tuple-element.101), channel_id=1, source_target_pairs={{0,64},{64,0},{128,192},{192,128},{1,65},{65,1},{129,193},{193,129... | collective-permute-start | bytes 786440 | tf_op jit(solution)/shard_map/ppermute | solution.py:541
  39.5 17.3 %collective-permute-start.8 = (f32[8,32,256]{2,1,0:T(8,128)S(1)}, f32[8,32,256]{2,1,0:T(8,128)S(1)}, u32[]{:S(2)}, u32[]{:S(2)}) collective-permute-start(f32[8,32,256]{2,1,0:T(8,128)S(1)} %get-tuple-element.102.fa), channel_id=1, source_target_pairs={{0,64},{64,0},{128,192},{192,128},{1,65},{65,1},{129,193},{193,129... | collective-permute-start | bytes 786440 | tf_op jit(solution)/shard_map/ppermute | solution.py:534
  41.0 15.7 %collective-permute-start.9 = (f32[8,32,256]{2,1,0:T(8,128)S(1)}, f32[8,32,256]{2,1,0:T(8,128)S(1)}, u32[]{:S(2)}, u32[]{:S(2)}) collective-permute-start(f32[8,32,256]{2,1,0:T(8,128)S(1)} %get-tuple-element.103.fb), channel_id=1, source_target_pairs={{0,192},{192,0},{64,128},{128,64},{1,193},{193,1},{65,129},{129,65... | collective-permute-start | bytes 786440 | tf_op jit(solution)/shard_map/ppermute | solution.py:535
  53.9 8.2 %collective-permute-start.14 = (f32[41,8,256]{2,1,0:T(8,128)S(1)}, f32[41,8,256]{2,1,0:T(8,128)S(1)}, u32[]{:S(2)}, u32[]{:S(2)}) collective-permute-start(f32[41,8,256]{2,1,0:T(8,128)S(1)} %get-tuple-element.111), channel_id=1, source_target_pairs={{0,1},{1,2},{2,3},{3,0},{4,5},{5,6},{6,7},{7,4},{8,9},{9,10},{10,1... | collective-permute-start | bytes 1007624 | tf_op jit(solution)/shard_map/ppermute | solution.py:119
  56.5 10.0 %collective-permute-start.15 = (f32[41,8,256]{2,1,0:T(8,128)S(1)}, f32[41,8,256]{2,1,0:T(8,128)S(1)}, u32[]{:S(2)}, u32[]{:S(2)}) collective-permute-start(f32[41,8,256]{2,1,0:T(8,128)S(1)} %get-tuple-element.112), channel_id=1, source_target_pairs={{0,3},{1,0},{2,1},{3,2},{4,7},{5,4},{6,5},{7,6},{8,11},{9,8},{10,9... | collective-permute-start | bytes 1007624 | tf_op jit(solution)/shard_map/ppermute | solution.py:119
  57.4 9.7 %collective-permute-start.10 = (f32[8,32,256]{2,1,0:T(8,128)S(1)}, f32[8,32,256]{2,1,0:T(8,128)S(1)}, u32[]{:S(2)}, u32[]{:S(2)}) collective-permute-start(f32[8,32,256]{2,1,0:T(8,128)S(1)} %get-tuple-element.106), channel_id=1, source_target_pairs={{0,192},{192,0},{64,128},{128,64},{1,193},{193,1},{65,129},{129,65... | collective-permute-start | bytes 786440 | tf_op jit(solution)/shard_map/ppermute | solution.py:540
  58.5 8.7 %collective-permute-start.11 = (f32[8,32,256]{2,1,0:T(8,128)S(1)}, f32[8,32,256]{2,1,0:T(8,128)S(1)}, u32[]{:S(2)}, u32[]{:S(2)}) collective-permute-start(f32[8,32,256]{2,1,0:T(8,128)S(1)} %get-tuple-element.107), channel_id=1, source_target_pairs={{0,64},{64,0},{128,192},{192,128},{1,65},{65,1},{129,193},{193,129... | collective-permute-start | bytes 786440 | tf_op jit(solution)/shard_map/ppermute | solution.py:541
  75.9 8.4 %collective-permute-start.16 = (f32[41,8,256]{2,1,0:T(8,128)S(1)}, f32[41,8,256]{2,1,0:T(8,128)S(1)}, u32[]{:S(2)}, u32[]{:S(2)}) collective-permute-start(f32[41,8,256]{2,1,0:T(8,128)S(1)} %get-tuple-element.118), channel_id=1, source_target_pairs={{0,1},{1,2},{2,3},{3,0},{4,5},{5,6},{6,7},{7,4},{8,9},{9,10},{10,1... | collective-permute-start | bytes 1007624 | tf_op jit(solution)/shard_map/ppermute | solution.py:119
  77.5 22.3 %collective-permute-start.17 = (f32[41,8,256]{2,1,0:T(8,128)S(1)}, f32[41,8,256]{2,1,0:T(8,128)S(1)}, u32[]{:S(2)}, u32[]{:S(2)}) collective-permute-start(f32[41,8,256]{2,1,0:T(8,128)S(1)} %get-tuple-element.119), channel_id=1, source_target_pairs={{0,3},{1,0},{2,1},{3,2},{4,7},{5,4},{6,5},{7,6},{8,11},{9,8},{10,9... | collective-permute-start | bytes 1007624 | tf_op jit(solution)/shard_map/ppermute | solution.py:119
  77.5 28.8 %collective-permute-start.21 = (f32[12,32,256]{2,1,0:T(8,128)S(1)}, f32[12,32,256]{2,1,0:T(8,128)S(1)}, u32[]{:S(2)}, u32[]{:S(2)}) collective-permute-start(f32[12,32,256]{2,1,0:T(8,128)S(1)} %get-tuple-element.113), channel_id=1, source_target_pairs={{0,60},{4,0},{8,4},{12,8},{16,12},{20,16},{24,20},{28,24},{32,28},... | collective-permute-start | bytes 1179656 | tf_op jit(solution)/shard_map/ppermute | solution.py:119
  83.0 28.2 %collective-permute-start.20 = (f32[12,32,256]{2,1,0:T(8,128)S(1)}, f32[12,32,256]{2,1,0:T(8,128)S(1)}, u32[]{:S(2)}, u32[]{:S(2)}) collective-permute-start(f32[12,32,256]{2,1,0:T(8,128)S(1)} %get-tuple-element.114), channel_id=1, source_target_pairs={{0,4},{4,8},{8,12},{12,16},{16,20},{20,24},{24,28},{28,32},{32,36}... | collective-permute-start | bytes 1179656 | tf_op jit(solution)/shard_map/ppermute | solution.py:119
  100.5 24.6 %collective-permute-start.18 = (f32[12,32,256]{2,1,0:T(8,128)S(1)}, f32[12,32,256]{2,1,0:T(8,128)S(1)}, u32[]{:S(2)}, u32[]{:S(2)}) collective-permute-start(f32[12,32,256]{2,1,0:T(8,128)S(1)} %get-tuple-element.121), channel_id=1, source_target_pairs={{0,4},{4,8},{8,12},{12,16},{16,20},{20,24},{24,28},{28,32},{32,36}... | collective-permute-start | bytes 1179656 | tf_op jit(solution)/shard_map/ppermute | solution.py:119
  100.6 26.2 %collective-permute-start.19 = (f32[12,32,256]{2,1,0:T(8,128)S(1)}, f32[12,32,256]{2,1,0:T(8,128)S(1)}, u32[]{:S(2)}, u32[]{:S(2)}) collective-permute-start(f32[12,32,256]{2,1,0:T(8,128)S(1)} %get-tuple-element.122), channel_id=1, source_target_pairs={{0,60},{4,0},{8,4},{12,8},{16,12},{20,16},{24,20},{28,24},{32,28},... | collective-permute-start | bytes 1179656 | tf_op jit(solution)/shard_map/ppermute | solution.py:119
  112.6 19.7 %collective-permute-start.22 = (f32[32,256]{1,0:T(8,128)S(1)}, f32[32,256]{1,0:T(8,128)S(1)}, u32[]{:S(2)}, u32[]{:S(2)}) collective-permute-start(f32[32,256]{1,0:T(8,128)S(1)} %get-tuple-element.130), channel_id=1, source_target_pairs={{0,4},{4,8},{8,12},{12,16},{16,20},{20,24},{24,28},{28,32},{32,36}... | collective-permute-start | bytes 98312 | tf_op jit(solution)/shard_map/ppermute | solution.py:119
  112.7 19.6 %collective-permute-start.23 = (f32[32,256]{1,0:T(8,128)S(1)}, f32[32,256]{1,0:T(8,128)S(1)}, u32[]{:S(2)}, u32[]{:S(2)}) collective-permute-start(f32[32,256]{1,0:T(8,128)S(1)} %get-tuple-element.131), channel_id=1, source_target_pairs={{0,60},{4,0},{8,4},{12,8},{16,12},{20,16},{24,20},{28,24},{32,28},... | collective-permute-start | bytes 98312 | tf_op jit(solution)/shard_map/ppermute | solution.py:119
  118.4 9.9 %collective-permute-start.24 = (f32[16,256]{1,0:T(8,128)S(1)}, f32[16,256]{1,0:T(8,128)S(1)}, u32[]{:S(2)}, u32[]{:S(2)}) collective-permute-start(f32[16,256]{1,0:T(8,128)S(1)} %get-tuple-element.132), channel_id=1, source_target_pairs={{0,1},{1,2},{2,3},{3,0},{4,5},{5,6},{6,7},{7,4},{8,9},{9,10},{10,1... | collective-permute-start | bytes 49160 | tf_op jit(solution)/shard_map/ppermute | solution.py:119
  125.1 7.2 %collective-permute-start.25 = (f32[16,256]{1,0:T(8,128)S(1)}, f32[16,256]{1,0:T(8,128)S(1)}, u32[]{:S(2)}, u32[]{:S(2)}) collective-permute-start(f32[16,256]{1,0:T(8,128)S(1)} %get-tuple-element.133), channel_id=1, source_target_pairs={{0,3},{1,0},{2,1},{3,2},{4,7},{5,4},{6,5},{7,6},{8,11},{9,8},{10,9... | collective-permute-start | bytes 49160 | tf_op jit(solution)/shard_map/ppermute | solution.py:119
  133.9 7.9 %collective-permute-start.30 = (f32[8,32,256]{2,1,0:T(8,128)S(1)}, f32[8,32,256]{2,1,0:T(8,128)S(1)}, u32[]{:S(2)}, u32[]{:S(2)}) collective-permute-start(f32[8,32,256]{2,1,0:T(8,128)S(1)} %get-tuple-element.134.fa), channel_id=1, source_target_pairs={{0,64},{64,0},{128,192},{192,128},{1,65},{65,1},{129,193},{193,129... | collective-permute-start | bytes 786440 | tf_op jit(solution)/shard_map/ppermute | solution.py:534
  134.0 9.1 %collective-permute-start.31 = (f32[8,32,256]{2,1,0:T(8,128)S(1)}, f32[8,32,256]{2,1,0:T(8,128)S(1)}, u32[]{:S(2)}, u32[]{:S(2)}) collective-permute-start(f32[8,32,256]{2,1,0:T(8,128)S(1)} %get-tuple-element.135.fb), channel_id=1, source_target_pairs={{0,192},{192,0},{64,128},{128,64},{1,193},{193,1},{65,129},{129,65... | collective-permute-start | bytes 786440 | tf_op jit(solution)/shard_map/ppermute | solution.py:535
  143.8 16.0 %collective-permute-start.36 = (f32[8,32,256]{2,1,0:T(8,128)S(1)}, f32[8,32,256]{2,1,0:T(8,128)S(1)}, u32[]{:S(2)}, u32[]{:S(2)}) collective-permute-start(f32[8,32,256]{2,1,0:T(8,128)S(1)} %get-tuple-element.142), channel_id=1, source_target_pairs={{0,192},{192,0},{64,128},{128,64},{1,193},{193,1},{65,129},{129,65... | collective-permute-start | bytes 786440 | tf_op jit(solution)/shard_map/ppermute | solution.py:540
  145.1 14.7 %collective-permute-start.37 = (f32[8,32,256]{2,1,0:T(8,128)S(1)}, f32[8,32,256]{2,1,0:T(8,128)S(1)}, u32[]{:S(2)}, u32[]{:S(2)}) collective-permute-start(f32[8,32,256]{2,1,0:T(8,128)S(1)} %get-tuple-element.143), channel_id=1, source_target_pairs={{0,64},{64,0},{128,192},{192,128},{1,65},{65,1},{129,193},{193,129... | collective-permute-start | bytes 786440 | tf_op jit(solution)/shard_map/ppermute | solution.py:541
  145.1 7.3 %collective-permute-start.28 = (f32[16,256]{1,0:T(8,128)S(1)}, f32[16,256]{1,0:T(8,128)S(1)}, u32[]{:S(2)}, u32[]{:S(2)}) collective-permute-start(f32[16,256]{1,0:T(8,128)S(1)} %get-tuple-element.138), channel_id=1, source_target_pairs={{0,1},{1,2},{2,3},{3,0},{4,5},{5,6},{6,7},{7,4},{8,9},{9,10},{10,1... | collective-permute-start | bytes 49160 | tf_op jit(solution)/shard_map/ppermute | solution.py:119
  146.7 8.9 %collective-permute-start.26 = (f32[32,256]{1,0:T(8,128)S(1)}, f32[32,256]{1,0:T(8,128)S(1)}, u32[]{:S(2)}, u32[]{:S(2)}) collective-permute-start(f32[32,256]{1,0:T(8,128)S(1)} %get-tuple-element.136), channel_id=1, source_target_pairs={{0,4},{4,8},{8,12},{12,16},{16,20},{20,24},{24,28},{28,32},{32,36}... | collective-permute-start | bytes 98312 | tf_op jit(solution)/shard_map/ppermute | solution.py:119
  146.7 8.9 %collective-permute-start.27 = (f32[32,256]{1,0:T(8,128)S(1)}, f32[32,256]{1,0:T(8,128)S(1)}, u32[]{:S(2)}, u32[]{:S(2)}) collective-permute-start(f32[32,256]{1,0:T(8,128)S(1)} %get-tuple-element.137), channel_id=1, source_target_pairs={{0,60},{4,0},{8,4},{12,8},{16,12},{20,16},{24,20},{28,24},{32,28},... | collective-permute-start | bytes 98312 | tf_op jit(solution)/shard_map/ppermute | solution.py:119
  152.4 3.2 %collective-permute-start.29 = (f32[16,256]{1,0:T(8,128)S(1)}, f32[16,256]{1,0:T(8,128)S(1)}, u32[]{:S(2)}, u32[]{:S(2)}) collective-permute-start(f32[16,256]{1,0:T(8,128)S(1)} %get-tuple-element.139), channel_id=1, source_target_pairs={{0,3},{1,0},{2,1},{3,2},{4,7},{5,4},{6,5},{7,6},{8,11},{9,8},{10,9... | collective-permute-start | bytes 49160 | tf_op jit(solution)/shard_map/ppermute | solution.py:119
  157.1 12.4 %collective-permute-start.32 = (f32[8,32,256]{2,1,0:T(8,128)S(1)}, f32[8,32,256]{2,1,0:T(8,128)S(1)}, u32[]{:S(2)}, u32[]{:S(2)}) collective-permute-start(f32[8,32,256]{2,1,0:T(8,128)S(1)} %get-tuple-element.144.fa), channel_id=1, source_target_pairs={{0,64},{64,0},{128,192},{192,128},{1,65},{65,1},{129,193},{193,129... | collective-permute-start | bytes 786440 | tf_op jit(solution)/shard_map/ppermute | solution.py:534
  158.9 10.6 %collective-permute-start.33 = (f32[8,32,256]{2,1,0:T(8,128)S(1)}, f32[8,32,256]{2,1,0:T(8,128)S(1)}, u32[]{:S(2)}, u32[]{:S(2)}) collective-permute-start(f32[8,32,256]{2,1,0:T(8,128)S(1)} %get-tuple-element.145.fb), channel_id=1, source_target_pairs={{0,192},{192,0},{64,128},{128,64},{1,193},{193,1},{65,129},{129,65... | collective-permute-start | bytes 786440 | tf_op jit(solution)/shard_map/ppermute | solution.py:535
  168.5 6.2 %collective-permute-start.38 = (f32[41,8,256]{2,1,0:T(8,128)S(1)}, f32[41,8,256]{2,1,0:T(8,128)S(1)}, u32[]{:S(2)}, u32[]{:S(2)}) collective-permute-start(f32[41,8,256]{2,1,0:T(8,128)S(1)} %get-tuple-element.153), channel_id=1, source_target_pairs={{0,1},{1,2},{2,3},{3,0},{4,5},{5,6},{6,7},{7,4},{8,9},{9,10},{10,1... | collective-permute-start | bytes 1007624 | tf_op jit(solution)/shard_map/ppermute | solution.py:119
  169.2 10.0 %collective-permute-start.39 = (f32[41,8,256]{2,1,0:T(8,128)S(1)}, f32[41,8,256]{2,1,0:T(8,128)S(1)}, u32[]{:S(2)}, u32[]{:S(2)}) collective-permute-start(f32[41,8,256]{2,1,0:T(8,128)S(1)} %get-tuple-element.154), channel_id=1, source_target_pairs={{0,3},{1,0},{2,1},{3,2},{4,7},{5,4},{6,5},{7,6},{8,11},{9,8},{10,9... | collective-permute-start | bytes 1007624 | tf_op jit(solution)/shard_map/ppermute | solution.py:119
  170.2 9.7 %collective-permute-start.34 = (f32[8,32,256]{2,1,0:T(8,128)S(1)}, f32[8,32,256]{2,1,0:T(8,128)S(1)}, u32[]{:S(2)}, u32[]{:S(2)}) collective-permute-start(f32[8,32,256]{2,1,0:T(8,128)S(1)} %get-tuple-element.148), channel_id=1, source_target_pairs={{0,192},{192,0},{64,128},{128,64},{1,193},{193,1},{65,129},{129,65... | collective-permute-start | bytes 786440 | tf_op jit(solution)/shard_map/ppermute | solution.py:540
  171.8 8.1 %collective-permute-start.35 = (f32[8,32,256]{2,1,0:T(8,128)S(1)}, f32[8,32,256]{2,1,0:T(8,128)S(1)}, u32[]{:S(2)}, u32[]{:S(2)}) collective-permute-start(f32[8,32,256]{2,1,0:T(8,128)S(1)} %get-tuple-element.149), channel_id=1, source_target_pairs={{0,64},{64,0},{128,192},{192,128},{1,65},{65,1},{129,193},{193,129... | collective-permute-start | bytes 786440 | tf_op jit(solution)/shard_map/ppermute | solution.py:541
  188.7 8.6 %collective-permute-start.40 = (f32[41,8,256]{2,1,0:T(8,128)S(1)}, f32[41,8,256]{2,1,0:T(8,128)S(1)}, u32[]{:S(2)}, u32[]{:S(2)}) collective-permute-start(f32[41,8,256]{2,1,0:T(8,128)S(1)} %get-tuple-element.160), channel_id=1, source_target_pairs={{0,1},{1,2},{2,3},{3,0},{4,5},{5,6},{6,7},{7,4},{8,9},{9,10},{10,1... | collective-permute-start | bytes 1007624 | tf_op jit(solution)/shard_map/ppermute | solution.py:119
  190.5 18.2 %collective-permute-start.41 = (f32[41,8,256]{2,1,0:T(8,128)S(1)}, f32[41,8,256]{2,1,0:T(8,128)S(1)}, u32[]{:S(2)}, u32[]{:S(2)}) collective-permute-start(f32[41,8,256]{2,1,0:T(8,128)S(1)} %get-tuple-element.161), channel_id=1, source_target_pairs={{0,3},{1,0},{2,1},{3,2},{4,7},{5,4},{6,5},{7,6},{8,11},{9,8},{10,9... | collective-permute-start | bytes 1007624 | tf_op jit(solution)/shard_map/ppermute | solution.py:119
  190.5 24.7 %collective-permute-start.45 = (f32[12,32,256]{2,1,0:T(8,128)S(1)}, f32[12,32,256]{2,1,0:T(8,128)S(1)}, u32[]{:S(2)}, u32[]{:S(2)}) collective-permute-start(f32[12,32,256]{2,1,0:T(8,128)S(1)} %get-tuple-element.155), channel_id=1, source_target_pairs={{0,60},{4,0},{8,4},{12,8},{16,12},{20,16},{24,20},{28,24},{32,28},... | collective-permute-start | bytes 1179656 | tf_op jit(solution)/shard_map/ppermute | solution.py:119
  196.4 29.9 %collective-permute-start.44 = (f32[12,32,256]{2,1,0:T(8,128)S(1)}, f32[12,32,256]{2,1,0:T(8,128)S(1)}, u32[]{:S(2)}, u32[]{:S(2)}) collective-permute-start(f32[12,32,256]{2,1,0:T(8,128)S(1)} %get-tuple-element.156), channel_id=1, source_target_pairs={{0,4},{4,8},{8,12},{12,16},{16,20},{20,24},{24,28},{28,32},{32,36}... | collective-permute-start | bytes 1179656 | tf_op jit(solution)/shard_map/ppermute | solution.py:119
  209.4 25.3 %collective-permute-start.42 = (f32[12,32,256]{2,1,0:T(8,128)S(1)}, f32[12,32,256]{2,1,0:T(8,128)S(1)}, u32[]{:S(2)}, u32[]{:S(2)}) collective-permute-start(f32[12,32,256]{2,1,0:T(8,128)S(1)} %get-tuple-element.163), channel_id=1, source_target_pairs={{0,4},{4,8},{8,12},{12,16},{16,20},{20,24},{24,28},{28,32},{32,36}... | collective-permute-start | bytes 1179656 | tf_op jit(solution)/shard_map/ppermute | solution.py:119
  209.5 25.2 %collective-permute-start.43 = (f32[12,32,256]{2,1,0:T(8,128)S(1)}, f32[12,32,256]{2,1,0:T(8,128)S(1)}, u32[]{:S(2)}, u32[]{:S(2)}) collective-permute-start(f32[12,32,256]{2,1,0:T(8,128)S(1)} %get-tuple-element.164), channel_id=1, source_target_pairs={{0,60},{4,0},{8,4},{12,8},{16,12},{20,16},{24,20},{28,24},{32,28},... | collective-permute-start | bytes 1179656 | tf_op jit(solution)/shard_map/ppermute | solution.py:119

commit v6 on v5

--- a/solution.py
+++ b/solution.py
@@ -225,20 +225,20 @@
         ylast[p:p + 1, :] = x[p, YB - 1:YB, :]
 
 
-def prepare_kernel(sc, x, wide, near, xu, xv, ha, hb, bhi, blo, *edges):
+def prepare_kernel(sc, x, wide, near, xu, xv, hua, hub, hva, hvb, bhi, blo, *edges):
     for a in range(0, ZB // 8, 2):
         rows = jnp.concatenate(
             [wide[0, b:b + 1, :] * near[0] + wide[1, b:b + 1, :] * near[1] for b in (a, a + 1)], 0
         )
         bhi[8 * a:8 * a + 16, :], blo[8 * a:8 * a + 16, :] = halves(rows)
-    for s, dst in enumerate((xu, xv)):
+    for s, (dst, ha, hb) in enumerate(((xu, hua, hub), (xv, hva, hvb))):
         edges_of(x.at[s], *(edge.at[s] for edge in edges))
 
-        def plane(p, carry, s=s, dst=dst):
+        def plane(p, carry, s=s, dst=dst, ha=ha, hb=hb):
             dst[p] = x[s, p]
             dst[HALF + p] = x[s, HALF + p]
-            ha[s, p] = x[s, p]
-            hb[s, p] = x[s, HALF + p]
+            ha[p] = x[s, p]
+            hb[p] = x[s, HALF + p]
             return carry
 
         lax.fori_loop(0, HALF, plane, 0)
@@ -248,7 +248,7 @@
 
 
 def prepare(*args):
-    outs = [local(*o) for o in [(XB, YB, ZB)] * 2 + [(2, HALF, YB, ZB)] * 2]
+    outs = [local(*o) for o in [(XB, YB, ZB)] * 2 + [(HALF, YB, ZB)] * 4]
     outs += [pltpu.VMEM((ZB, ZB), jnp.bfloat16)] * 2 + [local(2, *e) for e in EDGES]
     return call(prepare_kernel, outs, args)
 
@@ -264,11 +264,9 @@
 
 
 def partial_kernel(sc, fa, fb, ga, gb, na, nb, x0, sa, sb):
-    species = sc[12].astype(jnp.int32)
-
     def plane(p, carry):
-        low = na[species, p] + sc[7] * x0[p]
-        high = nb[species, p] + sc[7] * x0[HALF + p]
+        low = na[p] + sc[7] * x0[p]
+        high = nb[p] + sc[7] * x0[HALF + p]
         sa[p] = sc[3] * fa[p] + sc[4] * ga[p] + low
         sb[p] = sc[5] * fb[p] + sc[6] * gb[p] + high
         return carry
@@ -283,7 +281,6 @@
 def jacobi_kernel(sc, bhi, blo, sums, x, x0, na, nb, fa, fb, ga, gb, da, db, ra, rb,
                   core, yhi, ylo, one, two, bs, right):
     spread, scale = sc[9], sc[10]
-    species = sc[12].astype(jnp.int32)
     zero = jnp.zeros((ROWS, LANES), jnp.float32)
 
     def clear(p, carry):
@@ -301,7 +298,7 @@
     def gather(half, f, g, d, n, recv, weight):
         def plane(i, carry):
             own = sc[0] * f[i] + sc[weight] * g[i] + d[i]
-            own = own + (n[species, i] + sc[7] * x0[half * HALF + i])
+            own = own + (n[i] + sc[7] * x0[half * HALF + i])
             right[half * HALF + i] = own + recv[i]
             return carry
 
@@ -504,10 +501,13 @@
     sc = jnp.asarray(node_table(), jnp.float32)[lax.axis_index("node")]
     wide, near, sums = map(jnp.asarray, fourier())
     hold = lax.optimization_barrier
-    xu, xv, ha, hb, bhi, blo, *edges = prepare(sc[0], previous[0], wide, near)
+    xu, xv, hua, hub, hva, hvb, bhi, blo, *edges = prepare(sc[0], previous[0], wide, near)
     x0 = (xu, xv)
-    na = lax.ppermute(ha, "node", [(3, 2)])
-    nb = lax.ppermute(hb, "node", [(3, 0)])
+
+    def start(a, b):
+        return lax.ppermute(a, "node", [(3, 2)]), lax.ppermute(b, "node", [(3, 0)])
+
+    starts = [start(hua, hub)]
 
     def halos_of(xfirst, xlast, yfirst, ylast):
         return (
@@ -533,6 +533,10 @@
             fa, fb, da, db = fs[s]
             ga = lax.ppermute(fa, "node", PAIR_A)
             gb = lax.ppermute(fb, "node", PAIR_B)
+            if s == len(starts):
+                hva, hvb, _, _ = hold((hva, hvb, pa, pb))
+                starts.append(start(hva, hvb))
+            na, nb = starts[s]
             pa, pb = partial(sc[s], fa, fb, ga, gb, na, nb, x0[s])
             if s == 0:
                 va, vb, _, _ = hold((*fs[1][:2], pa, pb))

time: 242 us -> 235 us (0.971)
  waiting for transfers between devices: 103 us -> 96.9 us
    ppermute x28, waiting for transfers between devices: 84.8 us -> 78.6 us  [shifted(): return lax.ppermute(array, axis, ring(lax.axis_size(axis), step))]
    ppermute x4, waiting for transfers between devices: 9.88 us -> 6.67 us  [body(): ga = lax.ppermute(fa, 'node', PAIR_A)]
    ppermute x2 -> x4, waiting for transfers between devices: 0.01 us -> 3.17 us  [the longest x2 3.16 us: start(): lax.ppermute(b, 'node', [(3, 0)])]
    ppermute x4, starting transfers between devices: 7.31 us -> 4.75 us  [body(): ra = lax.ppermute(pa, 'node', PAIR_B)]
  transfers between devices with their start and end apart: 46 -> 48, of which waited for: 21 -> 23; matrix products, arithmetic and copies ran while one was open for 0% -> 0% of each run, Pallas kernels for 13% -> 14%
where the time goes in v6:
time: 235 us; the launch traced here: 231 us
  waiting for transfers between devices  96.9 us (41%)
  starting transfers between devices  75.3 us (32%)
  Pallas kernels  55.1 us (23%)
  local copies, waits for them, and re-layouts  3.57 us (2%)
    ppermute x28, waiting for transfers between devices, shifted(): return lax.ppermute(array, axis, ring(lax.axis_size(axis), step))  78.6 us
    ppermute x28, starting transfers between devices, shifted(): return lax.ppermute(array, axis, ring(lax.axis_size(axis), step))  55.3 us
    pallas_call x21, Pallas kernels, call(): pl.pallas_call(kernel, out_shape=tuple(outs), in_specs=[smem] + [vmem] *...  55.1 us
    ppermute x4, waiting for transfers between devices, body(): ga = lax.ppermute(fa, 'node', PAIR_A)  6.67 us
    ppermute x4, starting transfers between devices, body(): gb = lax.ppermute(fb, 'node', PAIR_B)  6.61 us
    ppermute x4, waiting for transfers between devices, body(): gb = lax.ppermute(fb, 'node', PAIR_B)  6.25 us
    ppermute x4, starting transfers between devices, body(): ra = lax.ppermute(pa, 'node', PAIR_B)  4.75 us
  transfers between devices with their start and end apart: 48, of which 23 were waited for; matrix products, arithmetic and copies ran while one was open for 0% of the time, Pallas kernels for 14%

profile of v6, /device:TPU:1, one launch (start us, length us, event | category | flops | bytes accessed | tf_op | source)
XLA Modules:
  0.0 231.2 jit_solution(9710809313386813678)
XLA Ops:
  0.0 0.8 constant_dynamic-slice_fusion
  0.8 1.2 copy-done.2
  2.0 0.8 copy-done.4
  3.6 0.8 shard_map.73
  4.4 2.2 collective-permute-start
  6.6 7.3 %collective-permute-start.1 = (f32[2,32,256]{2,1,0:T(8,128)S(1)}, f32[2,32,256]{2,1,0:T(8,128)S(1)}, u32[]{:S(2)}, u32[]{:S(2)}) collective-permute-start(f32[2,32,256]{2,1,0:T(8,128)S(1)} %get-tuple-element.97), channel_id=1, source_target_pairs={{0,60},{4,0},{8,4},{12,8},{16,12},{20,16},{24,20},{28,24},{32,28},... | collective-permute-start | bytes 196616 | tf_op jit(solution)/shard_map/ppermute | solution.py:119
  13.8 1.6 collective-permute-start.2
  16.4 1.3 collective-permute-start.7
  17.7 1.0 collective-permute-done.3.refs_6_
  18.8 1.5 shard_map.74
  20.3 1.3 collective-permute-start.4
  21.6 1.8 collective-permute-start.5
  23.5 3.2 %collective-permute-done.7.nb = f32[8,32,256]{2,1,0:T(8,128)S(1)} collective-permute-done((f32[8,32,256]{2,1,0:T(8,128)S(1)}, f32[8,32,256]{2,1,0:T(8,128)S(1)}, u32[]{:S(2)}, u32[]{:S(2)}) %collective-permute-start.7) | collective-permute-done | bytes 262176 | tf_op jit(solution)/shard_map/ppermute | solution.py:508
  27.2 5.0 %collective-permute-done.5.gb = f32[8,32,256]{2,1,0:T(8,128)S(1)} collective-permute-done((f32[8,32,256]{2,1,0:T(8,128)S(1)}, f32[8,32,256]{2,1,0:T(8,128)S(1)}, u32[]{:S(2)}, u32[]{:S(2)}) %collective-permute-start.5) | collective-permute-done | bytes 262176 | tf_op jit(solution)/shard_map/ppermute | solution.py:535
  33.9 1.5 shard_map.76
  35.4 1.3 collective-permute-start.9
  36.7 0.9 collective-permute-start.10
  37.6 2.2 collective-permute-done.14.ra
  39.9 2.3 collective-permute-start.11
  42.2 8.7 %shard_map.78 = (f32[40,32,256]{2,1,0:T(8,128)S(1)}, f32[41,8,256]{2,1,0:T(8,128)S(1)}, f32[41,8,256]{2,1,0:T(8,128)S(1)}) custom-call(f32[13]{0:T(128)S(1)} %get-tuple-element.176.sc.refs_0_, bf16[256,256]{1,0:T(8,128)(2,1)S(1)} %get-tuple-element.90.bhi, bf16[256,256]{1,0:T(8,128)(2,1)S(1)} %get-tuple-element.91.blo, f32[8,256]{1,0:T(8,128)S(1)} %copy-done.3, ...), custom_call_target="tpu_custom_call" | custom-call | flops 60000000 | bytes 1000000 | tf_op jit(solution)/shard_map/pallas_call | solution.py:140
  50.9 4.1 %collective-permute-start.16 = (f32[41,8,256]{2,1,0:T(8,128)S(1)}, f32[41,8,256]{2,1,0:T(8,128)S(1)}, u32[]{:S(2)}, u32[]{:S(2)}) collective-permute-start(f32[41,8,256]{2,1,0:T(8,128)S(1)} %get-tuple-element.119), channel_id=1, source_target_pairs={{0,1},{1,2},{2,3},{3,0},{4,5},{5,6},{6,7},{7,4},{8,9},{9,10},{10,1... | collective-permute-start | bytes 1007624 | tf_op jit(solution)/shard_map/ppermute | solution.py:119
  55.7 0.8 collective-permute-start.12
  57.0 4.4 %collective-permute-done.16.low = f32[41,8,256]{2,1,0:T(8,128)S(1)} collective-permute-done((f32[41,8,256]{2,1,0:T(8,128)S(1)}, f32[41,8,256]{2,1,0:T(8,128)S(1)}, u32[]{:S(2)}, u32[]{:S(2)}) %collective-permute-start.16) | collective-permute-done | bytes 335904 | tf_op jit(solution)/shard_map/ppermute | solution.py:119
  61.4 2.8 %collective-permute-done.17.high = f32[41,8,256]{2,1,0:T(8,128)S(1)} collective-permute-done((f32[41,8,256]{2,1,0:T(8,128)S(1)}, f32[41,8,256]{2,1,0:T(8,128)S(1)}, u32[]{:S(2)}, u32[]{:S(2)}) %collective-permute-start.17) | collective-permute-done | bytes 335904 | tf_op jit(solution)/shard_map/ppermute | solution.py:119
  64.2 0.7 shard_map.79
  64.9 8.7 %shard_map.80 = (f32[40,32,256]{2,1,0:T(8,128)S(1)}, f32[41,8,256]{2,1,0:T(8,128)S(1)}, f32[41,8,256]{2,1,0:T(8,128)S(1)}) custom-call(f32[13]{0:T(128)S(1)} %get-tuple-element.175.refs_0_.sc, bf16[256,256]{1,0:T(8,128)(2,1)S(1)} %get-tuple-element.90.bhi, bf16[256,256]{1,0:T(8,128)(2,1)S(1)} %get-tuple-element.91.blo, f32[8,256]{1,0:T(8,128)S(1)} %copy-done.3, ...), custom_call_target="tpu_custom_call" | custom-call | flops 60000000 | bytes 1000000 | tf_op jit(solution)/shard_map/pallas_call | solution.py:140
  73.7 1.7 collective-permute-start.18
  75.4 1.7 collective-permute-start.23
  77.0 4.7 %collective-permute-done.18.low = f32[41,8,256]{2,1,0:T(8,128)S(1)} collective-permute-done((f32[41,8,256]{2,1,0:T(8,128)S(1)}, f32[41,8,256]{2,1,0:T(8,128)S(1)}, u32[]{:S(2)}, u32[]{:S(2)}) %collective-permute-start.18) | collective-permute-done | bytes 335904 | tf_op jit(solution)/shard_map/ppermute | solution.py:119
  81.8 10.8 %collective-permute-done.19.high = f32[41,8,256]{2,1,0:T(8,128)S(1)} collective-permute-done((f32[41,8,256]{2,1,0:T(8,128)S(1)}, f32[41,8,256]{2,1,0:T(8,128)S(1)}, u32[]{:S(2)}, u32[]{:S(2)}) %collective-permute-start.19) | collective-permute-done | bytes 335904 | tf_op jit(solution)/shard_map/ppermute | solution.py:119
  93.4 5.7 %collective-permute-start.21 = (f32[12,32,256]{2,1,0:T(8,128)S(1)}, f32[12,32,256]{2,1,0:T(8,128)S(1)}, u32[]{:S(2)}, u32[]{:S(2)}) collective-permute-start(f32[12,32,256]{2,1,0:T(8,128)S(1)} %get-tuple-element.130), channel_id=1, source_target_pairs={{0,60},{4,0},{8,4},{12,8},{16,12},{20,16},{24,20},{28,24},{32,28},... | collective-permute-start | bytes 1179656 | tf_op jit(solution)/shard_map/ppermute | solution.py:119
  99.0 2.1 collective-permute-done.22.low
  101.1 1.4 shard_map.83
  102.6 5.7 %collective-permute-start.25 = (f32[32,256]{1,0:T(8,128)S(1)}, f32[32,256]{1,0:T(8,128)S(1)}, u32[]{:S(2)}, u32[]{:S(2)}) collective-permute-start(f32[32,256]{1,0:T(8,128)S(1)} %get-tuple-element.139), channel_id=1, source_target_pairs={{0,60},{4,0},{8,4},{12,8},{16,12},{20,16},{24,20},{28,24},{32,28},... | collective-permute-start | bytes 98312 | tf_op jit(solution)/shard_map/ppermute | solution.py:119
  108.3 0.9 collective-permute-start.26
  109.6 2.4 %collective-permute-start.27 = (f32[16,256]{1,0:T(8,128)S(1)}, f32[16,256]{1,0:T(8,128)S(1)}, u32[]{:S(2)}, u32[]{:S(2)}) collective-permute-start(f32[16,256]{1,0:T(8,128)S(1)} %get-tuple-element.141), channel_id=1, source_target_pairs={{0,3},{1,0},{2,1},{3,2},{4,7},{5,4},{6,5},{7,6},{8,11},{9,8},{10,9... | collective-permute-start | bytes 49160 | tf_op jit(solution)/shard_map/ppermute | solution.py:119
  112.0 5.6 %collective-permute-done.21.high = f32[12,32,256]{2,1,0:T(8,128)S(1)} collective-permute-done((f32[12,32,256]{2,1,0:T(8,128)S(1)}, f32[12,32,256]{2,1,0:T(8,128)S(1)}, u32[]{:S(2)}, u32[]{:S(2)}) %collective-permute-start.21) | collective-permute-done | bytes 393248 | tf_op jit(solution)/shard_map/ppermute | solution.py:119
  117.5 1.4 shard_map.82
  119.0 3.7 %collective-permute-done.27.refs_6_ = f32[16,256]{1,0:T(8,128)S(1)} collective-permute-done((f32[16,256]{1,0:T(8,128)S(1)}, f32[16,256]{1,0:T(8,128)S(1)}, u32[]{:S(2)}, u32[]{:S(2)}) %collective-permute-start.27) | collective-permute-done | bytes 16416 | tf_op jit(solution)/shard_map/ppermute | solution.py:119
  122.7 1.5 shard_map.84
  124.4 1.9 collective-permute-start.33
  126.2 6.1 %collective-permute-done.32.ga = f32[8,32,256]{2,1,0:T(8,128)S(1)} collective-permute-done((f32[8,32,256]{2,1,0:T(8,128)S(1)}, f32[8,32,256]{2,1,0:T(8,128)S(1)}, u32[]{:S(2)}, u32[]{:S(2)}) %collective-permute-start.32) | collective-permute-done | bytes 262176 | tf_op jit(solution)/shard_map/ppermute | solution.py:534
  132.3 1.2 collective-permute-done.33.gb
  134.3 1.7 collective-permute-start.38
  136.0 1.8 collective-permute-start.30
  137.8 5.7 %collective-permute-start.29 = (f32[32,256]{1,0:T(8,128)S(1)}, f32[32,256]{1,0:T(8,128)S(1)}, u32[]{:S(2)}, u32[]{:S(2)}) collective-permute-start(f32[32,256]{1,0:T(8,128)S(1)} %get-tuple-element.145), channel_id=1, source_target_pairs={{0,60},{4,0},{8,4},{12,8},{16,12},{20,16},{24,20},{28,24},{32,28},... | collective-permute-start | bytes 98312 | tf_op jit(solution)/shard_map/ppermute | solution.py:119
  143.5 3.1 %collective-permute-done.31.refs_6_ = f32[16,256]{1,0:T(8,128)S(1)} collective-permute-done((f32[16,256]{1,0:T(8,128)S(1)}, f32[16,256]{1,0:T(8,128)S(1)}, u32[]{:S(2)}, u32[]{:S(2)}) %collective-permute-start.31) | collective-permute-done | bytes 16416 | tf_op jit(solution)/shard_map/ppermute | solution.py:119
  146.7 1.5 shard_map.85
  148.2 1.8 collective-permute-start.34
  150.6 8.7 %shard_map.88 = (f32[40,32,256]{2,1,0:T(8,128)S(1)}, f32[41,8,256]{2,1,0:T(8,128)S(1)}, f32[41,8,256]{2,1,0:T(8,128)S(1)}) custom-call(f32[13]{0:T(128)S(1)} %get-tuple-element.176.sc.refs_0_, bf16[256,256]{1,0:T(8,128)(2,1)S(1)} %get-tuple-element.90.bhi, bf16[256,256]{1,0:T(8,128)(2,1)S(1)} %get-tuple-element.91.blo, f32[8,256]{1,0:T(8,128)S(1)} %copy-done.3, ...), custom_call_target="tpu_custom_call" | custom-call | flops 60000000 | bytes 1000000 | tf_op jit(solution)/shard_map/pallas_call | solution.py:140
  160.7 2.2 collective-permute-start.36
  162.9 3.1 %collective-permute-done.40.low = f32[41,8,256]{2,1,0:T(8,128)S(1)} collective-permute-done((f32[41,8,256]{2,1,0:T(8,128)S(1)}, f32[41,8,256]{2,1,0:T(8,128)S(1)}, u32[]{:S(2)}, u32[]{:S(2)}) %collective-permute-start.40) | collective-permute-done | bytes 335904 | tf_op jit(solution)/shard_map/ppermute | solution.py:119
  166.0 3.6 %collective-permute-done.41.high = f32[41,8,256]{2,1,0:T(8,128)S(1)} collective-permute-done((f32[41,8,256]{2,1,0:T(8,128)S(1)}, f32[41,8,256]{2,1,0:T(8,128)S(1)}, u32[]{:S(2)}, u32[]{:S(2)}) %collective-permute-start.41) | collective-permute-done | bytes 335904 | tf_op jit(solution)/shard_map/ppermute | solution.py:119
  169.6 0.7 shard_map.89
  170.3 8.7 %shard_map.90 = (f32[40,32,256]{2,1,0:T(8,128)S(1)}, f32[41,8,256]{2,1,0:T(8,128)S(1)}, f32[41,8,256]{2,1,0:T(8,128)S(1)}) custom-call(f32[13]{0:T(128)S(1)} %get-tuple-element.175.refs_0_.sc, bf16[256,256]{1,0:T(8,128)(2,1)S(1)} %get-tuple-element.90.bhi, bf16[256,256]{1,0:T(8,128)(2,1)S(1)} %get-tuple-element.91.blo, f32[8,256]{1,0:T(8,128)S(1)} %copy-done.3, ...), custom_call_target="tpu_custom_call" | custom-call | flops 60000000 | bytes 1000000 | tf_op jit(solution)/shard_map/pallas_call | solution.py:140
  179.1 2.1 collective-permute-start.42
  181.2 6.1 %collective-permute-start.47 = (f32[12,32,256]{2,1,0:T(8,128)S(1)}, f32[12,32,256]{2,1,0:T(8,128)S(1)}, u32[]{:S(2)}, u32[]{:S(2)}) collective-permute-start(f32[12,32,256]{2,1,0:T(8,128)S(1)} %get-tuple-element.163), channel_id=1, source_target_pairs={{0,60},{4,0},{8,4},{12,8},{16,12},{20,16},{24,20},{28,24},{32,28},... | collective-permute-start | bytes 1179656 | tf_op jit(solution)/shard_map/ppermute | solution.py:119
  187.6 15.0 %collective-permute-done.43.high = f32[41,8,256]{2,1,0:T(8,128)S(1)} collective-permute-done((f32[41,8,256]{2,1,0:T(8,128)S(1)}, f32[41,8,256]{2,1,0:T(8,128)S(1)}, u32[]{:S(2)}, u32[]{:S(2)}) %collective-permute-start.43) | collective-permute-done | bytes 335904 | tf_op jit(solution)/shard_map/ppermute | solution.py:119
  202.7 0.7 shard_map.91
  203.5 5.7 %collective-permute-start.45 = (f32[12,32,256]{2,1,0:T(8,128)S(1)}, f32[12,32,256]{2,1,0:T(8,128)S(1)}, u32[]{:S(2)}, u32[]{:S(2)}) collective-permute-start(f32[12,32,256]{2,1,0:T(8,128)S(1)} %get-tuple-element.172), channel_id=1, source_target_pairs={{0,60},{4,0},{8,4},{12,8},{16,12},{20,16},{24,20},{28,24},{32,28},... | collective-permute-start | bytes 1179656 | tf_op jit(solution)/shard_map/ppermute | solution.py:119
  209.2 6.4 %collective-permute-done.46.low = f32[12,32,256]{2,1,0:T(8,128)S(1)} collective-permute-done((f32[12,32,256]{2,1,0:T(8,128)S(1)}, f32[12,32,256]{2,1,0:T(8,128)S(1)}, u32[]{:S(2)}, u32[]{:S(2)}) %collective-permute-start.46) | collective-permute-done | bytes 393248 | tf_op jit(solution)/shard_map/ppermute | solution.py:119
  215.5 2.1 shard_map.92
  217.6 11.1 %collective-permute-done.44.low = f32[12,32,256]{2,1,0:T(8,128)S(1)} collective-permute-done((f32[12,32,256]{2,1,0:T(8,128)S(1)}, f32[12,32,256]{2,1,0:T(8,128)S(1)}, u32[]{:S(2)}, u32[]{:S(2)}) %collective-permute-start.44) | collective-permute-done | bytes 393248 | tf_op jit(solution)/shard_map/ppermute | solution.py:119
  228.7 2.5 %shard_map.93 = f32[2,16,32,256]{3,2,1,0:T(8,128)} custom-call(f32[13]{0:T(128)S(1)} %get-tuple-element.176.sc.refs_0_, bf16[256,256]{1,0:T(8,128)(2,1)S(1)} %get-tuple-element.90.bhi, bf16[256,256]{1,0:T(8,128)(2,1)S(1)} %get-tuple-element.91.blo, f32[16,32,256]{2,1,0:T(8,128)S(1)} %get-tuple-element.170.c, f32[12,32,256]{2,1,0:T(8,128)S(1)} %collective-permute-done.44.low, ...), custom_call_target="tpu_custom_call" | custom-call | flops 1000000 | bytes 1000000 | tf_op jit(solution)/shard_map/pallas_call | solution.py:140
  (67 shorter events, 9.7 us)
Async XLA Ops:
  0.0 18.7 %copy-start.1 = (f32[16,32,256]{2,1,0:T(8,128)S(1)}, f32[16,32,256]{2,1,0:T(8,128)}, u32[]{:S(2)}) copy-start(f32[16,32,256]{2,1,0:T(8,128)} %refs_8_.7) | copy-start | bytes 1572868
  0.0 18.7 %copy-start = (f32[16,32,256]{2,1,0:T(8,128)S(1)}, f32[16,32,256]{2,1,0:T(8,128)}, u32[]{:S(2)}) copy-start(f32[16,32,256]{2,1,0:T(8,128)} %refs_7_.7) | copy-start | bytes 1572868
  0.8 1.2 copy-start.2
  2.0 0.8 copy-start.4
  2.8 0.7 copy-start.5
  4.4 14.4 %collective-permute-start = (f32[2,32,256]{2,1,0:T(8,128)S(1)}, f32[2,32,256]{2,1,0:T(8,128)S(1)}, u32[]{:S(2)}, u32[]{:S(2)}) collective-permute-start(f32[2,32,256]{2,1,0:T(8,128)S(1)} %get-tuple-element.96), channel_id=1, source_target_pairs={{0,4},{4,8},{8,12},{12,16},{16,20},{20,24},{24,28},{28,32},{32,36}... | collective-permute-start | bytes 196616 | tf_op jit(solution)/shard_map/ppermute | solution.py:119
  6.6 12.2 %collective-permute-start.1 = (f32[2,32,256]{2,1,0:T(8,128)S(1)}, f32[2,32,256]{2,1,0:T(8,128)S(1)}, u32[]{:S(2)}, u32[]{:S(2)}) collective-permute-start(f32[2,32,256]{2,1,0:T(8,128)S(1)} %get-tuple-element.97), channel_id=1, source_target_pairs={{0,60},{4,0},{8,4},{12,8},{16,12},{20,16},{24,20},{28,24},{32,28},... | collective-permute-start | bytes 196616 | tf_op jit(solution)/shard_map/ppermute | solution.py:119
  13.8 2.6 %collective-permute-start.2 = (f32[2,16,256]{2,1,0:T(8,128)S(1)}, f32[2,16,256]{2,1,0:T(8,128)S(1)}, u32[]{:S(2)}, u32[]{:S(2)}) collective-permute-start(f32[2,16,256]{2,1,0:T(8,128)S(1)} %get-tuple-element.98), channel_id=1, source_target_pairs={{0,1},{1,2},{2,3},{3,0},{4,5},{5,6},{6,7},{7,4},{8,9},{9,10},{10,1... | collective-permute-start | bytes 98312 | tf_op jit(solution)/shard_map/ppermute | solution.py:119
  15.4 3.3 %collective-permute-start.3 = (f32[2,16,256]{2,1,0:T(8,128)S(1)}, f32[2,16,256]{2,1,0:T(8,128)S(1)}, u32[]{:S(2)}, u32[]{:S(2)}) collective-permute-start(f32[2,16,256]{2,1,0:T(8,128)S(1)} %get-tuple-element.99), channel_id=1, source_target_pairs={{0,3},{1,0},{2,1},{3,2},{4,7},{5,4},{6,5},{7,6},{8,11},{9,8},{10,9... | collective-permute-start | bytes 98312 | tf_op jit(solution)/shard_map/ppermute | solution.py:119
  15.4 8.1 %collective-permute-start.6 = (f32[8,32,256]{2,1,0:T(8,128)S(1)}, f32[8,32,256]{2,1,0:T(8,128)S(1)}, u32[]{:S(2)}, u32[]{:S(2)}) collective-permute-start(f32[8,32,256]{2,1,0:T(8,128)S(1)} %get-tuple-element.102), channel_id=1, source_target_pairs={{192,128},{193,129},{194,130},{195,131},{196,132},{197,133},{198,1... | collective-permute-start | bytes 786440 | tf_op jit(solution)/shard_map/ppermute | solution.py:508
  16.4 10.2 %collective-permute-start.7 = (f32[8,32,256]{2,1,0:T(8,128)S(1)}, f32[8,32,256]{2,1,0:T(8,128)S(1)}, u32[]{:S(2)}, u32[]{:S(2)}) collective-permute-start(f32[8,32,256]{2,1,0:T(8,128)S(1)} %get-tuple-element.103), channel_id=1, source_target_pairs={{192,0},{193,1},{194,2},{195,3},{196,4},{197,5},{198,6},{199,7},{2... | collective-permute-start | bytes 786440 | tf_op jit(solution)/shard_map/ppermute | solution.py:508
  20.3 6.9 %collective-permute-start.4 = (f32[8,32,256]{2,1,0:T(8,128)S(1)}, f32[8,32,256]{2,1,0:T(8,128)S(1)}, u32[]{:S(2)}, u32[]{:S(2)}) collective-permute-start(f32[8,32,256]{2,1,0:T(8,128)S(1)} %get-tuple-element.100.fa), channel_id=1, source_target_pairs={{0,64},{64,0},{128,192},{192,128},{1,65},{65,1},{129,193},{193,129... | collective-permute-start | bytes 786440 | tf_op jit(solution)/shard_map/ppermute | solution.py:534
  21.6 10.6 %collective-permute-start.5 = (f32[8,32,256]{2,1,0:T(8,128)S(1)}, f32[8,32,256]{2,1,0:T(8,128)S(1)}, u32[]{:S(2)}, u32[]{:S(2)}) collective-permute-start(f32[8,32,256]{2,1,0:T(8,128)S(1)} %get-tuple-element.101.fb), channel_id=1, source_target_pairs={{0,192},{192,0},{64,128},{128,64},{1,193},{193,1},{65,129},{129,65... | collective-permute-start | bytes 786440 | tf_op jit(solution)/shard_map/ppermute | solution.py:535
  33.0 9.2 %copy-start.3 = (f32[8,256]{1,0:T(8,128)S(1)}, f32[8,256]{1,0:T(8,128)}, u32[]{:S(2)}) copy-start(f32[8,256]{1,0:T(8,128)} %constant.21.clone.sums) | copy-start | bytes 24580
  33.0 6.9 %collective-permute-start.14 = (f32[8,32,256]{2,1,0:T(8,128)S(1)}, f32[8,32,256]{2,1,0:T(8,128)S(1)}, u32[]{:S(2)}, u32[]{:S(2)}) collective-permute-start(f32[8,32,256]{2,1,0:T(8,128)S(1)} %get-tuple-element.104), channel_id=1, source_target_pairs={{0,192},{192,0},{64,128},{128,64},{1,193},{193,1},{65,129},{129,65... | collective-permute-start | bytes 786440 | tf_op jit(solution)/shard_map/ppermute | solution.py:544
  33.1 9.1 %collective-permute-start.15 = (f32[8,32,256]{2,1,0:T(8,128)S(1)}, f32[8,32,256]{2,1,0:T(8,128)S(1)}, u32[]{:S(2)}, u32[]{:S(2)}) collective-permute-start(f32[8,32,256]{2,1,0:T(8,128)S(1)} %get-tuple-element.105), channel_id=1, source_target_pairs={{0,64},{64,0},{128,192},{192,128},{1,65},{65,1},{129,193},{193,129... | collective-permute-start | bytes 786440 | tf_op jit(solution)/shard_map/ppermute | solution.py:545
  33.2 21.8 %collective-permute-start.8 = (f32[8,32,256]{2,1,0:T(8,128)S(1)}, f32[8,32,256]{2,1,0:T(8,128)S(1)}, u32[]{:S(2)}, u32[]{:S(2)}) collective-permute-start(f32[8,32,256]{2,1,0:T(8,128)S(1)} %get-tuple-element.106), channel_id=1, source_target_pairs={{192,128},{193,129},{194,130},{195,131},{196,132},{197,133},{198,1... | collective-permute-start | bytes 786440 | tf_op jit(solution)/shard_map/ppermute | solution.py:508
  35.4 19.6 %collective-permute-start.9 = (f32[8,32,256]{2,1,0:T(8,128)S(1)}, f32[8,32,256]{2,1,0:T(8,128)S(1)}, u32[]{:S(2)}, u32[]{:S(2)}) collective-permute-start(f32[8,32,256]{2,1,0:T(8,128)S(1)} %get-tuple-element.107), channel_id=1, source_target_pairs={{192,0},{193,1},{194,2},{195,3},{196,4},{197,5},{198,6},{199,7},{2... | collective-permute-start | bytes 786440 | tf_op jit(solution)/shard_map/ppermute | solution.py:508
  36.7 18.3 %collective-permute-start.10 = (f32[8,32,256]{2,1,0:T(8,128)S(1)}, f32[8,32,256]{2,1,0:T(8,128)S(1)}, u32[]{:S(2)}, u32[]{:S(2)}) collective-permute-start(f32[8,32,256]{2,1,0:T(8,128)S(1)} %get-tuple-element.110.fa), channel_id=1, source_target_pairs={{0,64},{64,0},{128,192},{192,128},{1,65},{65,1},{129,193},{193,129... | collective-permute-start | bytes 786440 | tf_op jit(solution)/shard_map/ppermute | solution.py:534
  39.9 15.2 %collective-permute-start.11 = (f32[8,32,256]{2,1,0:T(8,128)S(1)}, f32[8,32,256]{2,1,0:T(8,128)S(1)}, u32[]{:S(2)}, u32[]{:S(2)}) collective-permute-start(f32[8,32,256]{2,1,0:T(8,128)S(1)} %get-tuple-element.111.fb), channel_id=1, source_target_pairs={{0,192},{192,0},{64,128},{128,64},{1,193},{193,1},{65,129},{129,65... | collective-permute-start | bytes 786440 | tf_op jit(solution)/shard_map/ppermute | solution.py:535
  50.9 10.5 %collective-permute-start.16 = (f32[41,8,256]{2,1,0:T(8,128)S(1)}, f32[41,8,256]{2,1,0:T(8,128)S(1)}, u32[]{:S(2)}, u32[]{:S(2)}) collective-permute-start(f32[41,8,256]{2,1,0:T(8,128)S(1)} %get-tuple-element.119), channel_id=1, source_target_pairs={{0,1},{1,2},{2,3},{3,0},{4,5},{5,6},{6,7},{7,4},{8,9},{9,10},{10,1... | collective-permute-start | bytes 1007624 | tf_op jit(solution)/shard_map/ppermute | solution.py:119
  55.0 9.2 %collective-permute-start.17 = (f32[41,8,256]{2,1,0:T(8,128)S(1)}, f32[41,8,256]{2,1,0:T(8,128)S(1)}, u32[]{:S(2)}, u32[]{:S(2)}) collective-permute-start(f32[41,8,256]{2,1,0:T(8,128)S(1)} %get-tuple-element.120), channel_id=1, source_target_pairs={{0,3},{1,0},{2,1},{3,2},{4,7},{5,4},{6,5},{7,6},{8,11},{9,8},{10,9... | collective-permute-start | bytes 1007624 | tf_op jit(solution)/shard_map/ppermute | solution.py:119
  55.7 9.2 %collective-permute-start.12 = (f32[8,32,256]{2,1,0:T(8,128)S(1)}, f32[8,32,256]{2,1,0:T(8,128)S(1)}, u32[]{:S(2)}, u32[]{:S(2)}) collective-permute-start(f32[8,32,256]{2,1,0:T(8,128)S(1)} %get-tuple-element.114), channel_id=1, source_target_pairs={{0,192},{192,0},{64,128},{128,64},{1,193},{193,1},{65,129},{129,65... | collective-permute-start | bytes 786440 | tf_op jit(solution)/shard_map/ppermute | solution.py:544
  56.5 8.4 %collective-permute-start.13 = (f32[8,32,256]{2,1,0:T(8,128)S(1)}, f32[8,32,256]{2,1,0:T(8,128)S(1)}, u32[]{:S(2)}, u32[]{:S(2)}) collective-permute-start(f32[8,32,256]{2,1,0:T(8,128)S(1)} %get-tuple-element.115), channel_id=1, source_target_pairs={{0,64},{64,0},{128,192},{192,128},{1,65},{65,1},{129,193},{193,129... | collective-permute-start | bytes 786440 | tf_op jit(solution)/shard_map/ppermute | solution.py:545
  73.7 8.1 %collective-permute-start.18 = (f32[41,8,256]{2,1,0:T(8,128)S(1)}, f32[41,8,256]{2,1,0:T(8,128)S(1)}, u32[]{:S(2)}, u32[]{:S(2)}) collective-permute-start(f32[41,8,256]{2,1,0:T(8,128)S(1)} %get-tuple-element.126), channel_id=1, source_target_pairs={{0,1},{1,2},{2,3},{3,0},{4,5},{5,6},{6,7},{7,4},{8,9},{9,10},{10,1... | collective-permute-start | bytes 1007624 | tf_op jit(solution)/shard_map/ppermute | solution.py:119
  75.4 17.1 %collective-permute-start.19 = (f32[41,8,256]{2,1,0:T(8,128)S(1)}, f32[41,8,256]{2,1,0:T(8,128)S(1)}, u32[]{:S(2)}, u32[]{:S(2)}) collective-permute-start(f32[41,8,256]{2,1,0:T(8,128)S(1)} %get-tuple-element.127), channel_id=1, source_target_pairs={{0,3},{1,0},{2,1},{3,2},{4,7},{5,4},{6,5},{7,6},{8,11},{9,8},{10,9... | collective-permute-start | bytes 1007624 | tf_op jit(solution)/shard_map/ppermute | solution.py:119
  75.4 23.6 %collective-permute-start.23 = (f32[12,32,256]{2,1,0:T(8,128)S(1)}, f32[12,32,256]{2,1,0:T(8,128)S(1)}, u32[]{:S(2)}, u32[]{:S(2)}) collective-permute-start(f32[12,32,256]{2,1,0:T(8,128)S(1)} %get-tuple-element.121), channel_id=1, source_target_pairs={{0,60},{4,0},{8,4},{12,8},{16,12},{20,16},{24,20},{28,24},{32,28},... | collective-permute-start | bytes 1179656 | tf_op jit(solution)/shard_map/ppermute | solution.py:119
  77.0 24.1 %collective-permute-start.22 = (f32[12,32,256]{2,1,0:T(8,128)S(1)}, f32[12,32,256]{2,1,0:T(8,128)S(1)}, u32[]{:S(2)}, u32[]{:S(2)}) collective-permute-start(f32[12,32,256]{2,1,0:T(8,128)S(1)} %get-tuple-element.122), channel_id=1, source_target_pairs={{0,4},{4,8},{8,12},{12,16},{16,20},{20,24},{24,28},{28,32},{32,36}... | collective-permute-start | bytes 1179656 | tf_op jit(solution)/shard_map/ppermute | solution.py:119
  93.3 16.3 %collective-permute-start.20 = (f32[12,32,256]{2,1,0:T(8,128)S(1)}, f32[12,32,256]{2,1,0:T(8,128)S(1)}, u32[]{:S(2)}, u32[]{:S(2)}) collective-permute-start(f32[12,32,256]{2,1,0:T(8,128)S(1)} %get-tuple-element.129), channel_id=1, source_target_pairs={{0,4},{4,8},{8,12},{12,16},{16,20},{20,24},{24,28},{28,32},{32,36}... | collective-permute-start | bytes 1179656 | tf_op jit(solution)/shard_map/ppermute | solution.py:119
  93.4 24.2 %collective-permute-start.21 = (f32[12,32,256]{2,1,0:T(8,128)S(1)}, f32[12,32,256]{2,1,0:T(8,128)S(1)}, u32[]{:S(2)}, u32[]{:S(2)}) collective-permute-start(f32[12,32,256]{2,1,0:T(8,128)S(1)} %get-tuple-element.130), channel_id=1, source_target_pairs={{0,60},{4,0},{8,4},{12,8},{16,12},{20,16},{24,20},{28,24},{32,28},... | collective-permute-start | bytes 1179656 | tf_op jit(solution)/shard_map/ppermute | solution.py:119
  102.6 20.2 %collective-permute-start.24 = (f32[32,256]{1,0:T(8,128)S(1)}, f32[32,256]{1,0:T(8,128)S(1)}, u32[]{:S(2)}, u32[]{:S(2)}) collective-permute-start(f32[32,256]{1,0:T(8,128)S(1)} %get-tuple-element.138), channel_id=1, source_target_pairs={{0,4},{4,8},{8,12},{12,16},{16,20},{20,24},{24,28},{28,32},{32,36}... | collective-permute-start | bytes 98312 | tf_op jit(solution)/shard_map/ppermute | solution.py:119
  102.6 20.1 %collective-permute-start.25 = (f32[32,256]{1,0:T(8,128)S(1)}, f32[32,256]{1,0:T(8,128)S(1)}, u32[]{:S(2)}, u32[]{:S(2)}) collective-permute-start(f32[32,256]{1,0:T(8,128)S(1)} %get-tuple-element.139), channel_id=1, source_target_pairs={{0,60},{4,0},{8,4},{12,8},{16,12},{20,16},{24,20},{28,24},{32,28},... | collective-permute-start | bytes 98312 | tf_op jit(solution)/shard_map/ppermute | solution.py:119
  108.3 10.7 %collective-permute-start.26 = (f32[16,256]{1,0:T(8,128)S(1)}, f32[16,256]{1,0:T(8,128)S(1)}, u32[]{:S(2)}, u32[]{:S(2)}) collective-permute-start(f32[16,256]{1,0:T(8,128)S(1)} %get-tuple-element.140), channel_id=1, source_target_pairs={{0,1},{1,2},{2,3},{3,0},{4,5},{5,6},{6,7},{7,4},{8,9},{9,10},{10,1... | collective-permute-start | bytes 49160 | tf_op jit(solution)/shard_map/ppermute | solution.py:119
  109.6 13.1 %collective-permute-start.27 = (f32[16,256]{1,0:T(8,128)S(1)}, f32[16,256]{1,0:T(8,128)S(1)}, u32[]{:S(2)}, u32[]{:S(2)}) collective-permute-start(f32[16,256]{1,0:T(8,128)S(1)} %get-tuple-element.141), channel_id=1, source_target_pairs={{0,3},{1,0},{2,1},{3,2},{4,7},{5,4},{6,5},{7,6},{8,11},{9,8},{10,9... | collective-permute-start | bytes 49160 | tf_op jit(solution)/shard_map/ppermute | solution.py:119
  124.3 8.1 %collective-permute-start.32 = (f32[8,32,256]{2,1,0:T(8,128)S(1)}, f32[8,32,256]{2,1,0:T(8,128)S(1)}, u32[]{:S(2)}, u32[]{:S(2)}) collective-permute-start(f32[8,32,256]{2,1,0:T(8,128)S(1)} %get-tuple-element.142.fa), channel_id=1, source_target_pairs={{0,64},{64,0},{128,192},{192,128},{1,65},{65,1},{129,193},{193,129... | collective-permute-start | bytes 786440 | tf_op jit(solution)/shard_map/ppermute | solution.py:534
  124.4 9.2 %collective-permute-start.33 = (f32[8,32,256]{2,1,0:T(8,128)S(1)}, f32[8,32,256]{2,1,0:T(8,128)S(1)}, u32[]{:S(2)}, u32[]{:S(2)}) collective-permute-start(f32[8,32,256]{2,1,0:T(8,128)S(1)} %get-tuple-element.143.fb), channel_id=1, source_target_pairs={{0,192},{192,0},{64,128},{128,64},{1,193},{193,1},{65,129},{129,65... | collective-permute-start | bytes 786440 | tf_op jit(solution)/shard_map/ppermute | solution.py:535
  134.3 16.4 %collective-permute-start.38 = (f32[8,32,256]{2,1,0:T(8,128)S(1)}, f32[8,32,256]{2,1,0:T(8,128)S(1)}, u32[]{:S(2)}, u32[]{:S(2)}) collective-permute-start(f32[8,32,256]{2,1,0:T(8,128)S(1)} %get-tuple-element.150), channel_id=1, source_target_pairs={{0,192},{192,0},{64,128},{128,64},{1,193},{193,1},{65,129},{129,65... | collective-permute-start | bytes 786440 | tf_op jit(solution)/shard_map/ppermute | solution.py:544
  136.0 14.7 %collective-permute-start.39 = (f32[8,32,256]{2,1,0:T(8,128)S(1)}, f32[8,32,256]{2,1,0:T(8,128)S(1)}, u32[]{:S(2)}, u32[]{:S(2)}) collective-permute-start(f32[8,32,256]{2,1,0:T(8,128)S(1)} %get-tuple-element.151), channel_id=1, source_target_pairs={{0,64},{64,0},{128,192},{192,128},{1,65},{65,1},{129,193},{193,129... | collective-permute-start | bytes 786440 | tf_op jit(solution)/shard_map/ppermute | solution.py:545
  136.0 7.5 %collective-permute-start.30 = (f32[16,256]{1,0:T(8,128)S(1)}, f32[16,256]{1,0:T(8,128)S(1)}, u32[]{:S(2)}, u32[]{:S(2)}) collective-permute-start(f32[16,256]{1,0:T(8,128)S(1)} %get-tuple-element.146), channel_id=1, source_target_pairs={{0,1},{1,2},{2,3},{3,0},{4,5},{5,6},{6,7},{7,4},{8,9},{9,10},{10,1... | collective-permute-start | bytes 49160 | tf_op jit(solution)/shard_map/ppermute | solution.py:119
  137.8 8.9 %collective-permute-start.28 = (f32[32,256]{1,0:T(8,128)S(1)}, f32[32,256]{1,0:T(8,128)S(1)}, u32[]{:S(2)}, u32[]{:S(2)}) collective-permute-start(f32[32,256]{1,0:T(8,128)S(1)} %get-tuple-element.144), channel_id=1, source_target_pairs={{0,4},{4,8},{8,12},{12,16},{16,20},{20,24},{24,28},{28,32},{32,36}... | collective-permute-start | bytes 98312 | tf_op jit(solution)/shard_map/ppermute | solution.py:119
  137.8 8.9 %collective-permute-start.29 = (f32[32,256]{1,0:T(8,128)S(1)}, f32[32,256]{1,0:T(8,128)S(1)}, u32[]{:S(2)}, u32[]{:S(2)}) collective-permute-start(f32[32,256]{1,0:T(8,128)S(1)} %get-tuple-element.145), channel_id=1, source_target_pairs={{0,60},{4,0},{8,4},{12,8},{16,12},{20,16},{24,20},{28,24},{32,28},... | collective-permute-start | bytes 98312 | tf_op jit(solution)/shard_map/ppermute | solution.py:119
  143.5 3.2 %collective-permute-start.31 = (f32[16,256]{1,0:T(8,128)S(1)}, f32[16,256]{1,0:T(8,128)S(1)}, u32[]{:S(2)}, u32[]{:S(2)}) collective-permute-start(f32[16,256]{1,0:T(8,128)S(1)} %get-tuple-element.147), channel_id=1, source_target_pairs={{0,3},{1,0},{2,1},{3,2},{4,7},{5,4},{6,5},{7,6},{8,11},{9,8},{10,9... | collective-permute-start | bytes 49160 | tf_op jit(solution)/shard_map/ppermute | solution.py:119
  148.2 11.8 %collective-permute-start.34 = (f32[8,32,256]{2,1,0:T(8,128)S(1)}, f32[8,32,256]{2,1,0:T(8,128)S(1)}, u32[]{:S(2)}, u32[]{:S(2)}) collective-permute-start(f32[8,32,256]{2,1,0:T(8,128)S(1)} %get-tuple-element.152.fa), channel_id=1, source_target_pairs={{0,64},{64,0},{128,192},{192,128},{1,65},{65,1},{129,193},{193,129... | collective-permute-start | bytes 786440 | tf_op jit(solution)/shard_map/ppermute | solution.py:534
  150.0 10.0 %collective-permute-start.35 = (f32[8,32,256]{2,1,0:T(8,128)S(1)}, f32[8,32,256]{2,1,0:T(8,128)S(1)}, u32[]{:S(2)}, u32[]{:S(2)}) collective-permute-start(f32[8,32,256]{2,1,0:T(8,128)S(1)} %get-tuple-element.153.fb), channel_id=1, source_target_pairs={{0,192},{192,0},{64,128},{128,64},{1,193},{193,1},{65,129},{129,65... | collective-permute-start | bytes 786440 | tf_op jit(solution)/shard_map/ppermute | solution.py:535
  159.4 6.7 %collective-permute-start.40 = (f32[41,8,256]{2,1,0:T(8,128)S(1)}, f32[41,8,256]{2,1,0:T(8,128)S(1)}, u32[]{:S(2)}, u32[]{:S(2)}) collective-permute-start(f32[41,8,256]{2,1,0:T(8,128)S(1)} %get-tuple-element.161), channel_id=1, source_target_pairs={{0,1},{1,2},{2,3},{3,0},{4,5},{5,6},{6,7},{7,4},{8,9},{9,10},{10,1... | collective-permute-start | bytes 1007624 | tf_op jit(solution)/shard_map/ppermute | solution.py:119
  160.0 9.6 %collective-permute-start.41 = (f32[41,8,256]{2,1,0:T(8,128)S(1)}, f32[41,8,256]{2,1,0:T(8,128)S(1)}, u32[]{:S(2)}, u32[]{:S(2)}) collective-permute-start(f32[41,8,256]{2,1,0:T(8,128)S(1)} %get-tuple-element.162), channel_id=1, source_target_pairs={{0,3},{1,0},{2,1},{3,2},{4,7},{5,4},{6,5},{7,6},{8,11},{9,8},{10,9... | collective-permute-start | bytes 1007624 | tf_op jit(solution)/shard_map/ppermute | solution.py:119
  160.7 9.6 %collective-permute-start.36 = (f32[8,32,256]{2,1,0:T(8,128)S(1)}, f32[8,32,256]{2,1,0:T(8,128)S(1)}, u32[]{:S(2)}, u32[]{:S(2)}) collective-permute-start(f32[8,32,256]{2,1,0:T(8,128)S(1)} %get-tuple-element.156), channel_id=1, source_target_pairs={{0,192},{192,0},{64,128},{128,64},{1,193},{193,1},{65,129},{129,65... | collective-permute-start | bytes 786440 | tf_op jit(solution)/shard_map/ppermute | solution.py:544
  162.9 7.4 %collective-permute-start.37 = (f32[8,32,256]{2,1,0:T(8,128)S(1)}, f32[8,32,256]{2,1,0:T(8,128)S(1)}, u32[]{:S(2)}, u32[]{:S(2)}) collective-permute-start(f32[8,32,256]{2,1,0:T(8,128)S(1)} %get-tuple-element.157), channel_id=1, source_target_pairs={{0,64},{64,0},{128,192},{192,128},{1,65},{65,1},{129,193},{193,129... | collective-permute-start | bytes 786440 | tf_op jit(solution)/shard_map/ppermute | solution.py:545
  179.1 8.5 %collective-permute-start.42 = (f32[41,8,256]{2,1,0:T(8,128)S(1)}, f32[41,8,256]{2,1,0:T(8,128)S(1)}, u32[]{:S(2)}, u32[]{:S(2)}) collective-permute-start(f32[41,8,256]{2,1,0:T(8,128)S(1)} %get-tuple-element.168), channel_id=1, source_target_pairs={{0,1},{1,2},{2,3},{3,0},{4,5},{5,6},{6,7},{7,4},{8,9},{9,10},{10,1... | collective-permute-start | bytes 1007624 | tf_op jit(solution)/shard_map/ppermute | solution.py:119
  181.2 21.5 %collective-permute-start.43 = (f32[41,8,256]{2,1,0:T(8,128)S(1)}, f32[41,8,256]{2,1,0:T(8,128)S(1)}, u32[]{:S(2)}, u32[]{:S(2)}) collective-permute-start(f32[41,8,256]{2,1,0:T(8,128)S(1)} %get-tuple-element.169), channel_id=1, source_target_pairs={{0,3},{1,0},{2,1},{3,2},{4,7},{5,4},{6,5},{7,6},{8,11},{9,8},{10,9... | collective-permute-start | bytes 1007624 | tf_op jit(solution)/shard_map/ppermute | solution.py:119
  181.2 28.0 %collective-permute-start.47 = (f32[12,32,256]{2,1,0:T(8,128)S(1)}, f32[12,32,256]{2,1,0:T(8,128)S(1)}, u32[]{:S(2)}, u32[]{:S(2)}) collective-permute-start(f32[12,32,256]{2,1,0:T(8,128)S(1)} %get-tuple-element.163), channel_id=1, source_target_pairs={{0,60},{4,0},{8,4},{12,8},{16,12},{20,16},{24,20},{28,24},{32,28},... | collective-permute-start | bytes 1179656 | tf_op jit(solution)/shard_map/ppermute | solution.py:119
  187.2 28.3 %collective-permute-start.46 = (f32[12,32,256]{2,1,0:T(8,128)S(1)}, f32[12,32,256]{2,1,0:T(8,128)S(1)}, u32[]{:S(2)}, u32[]{:S(2)}) collective-permute-start(f32[12,32,256]{2,1,0:T(8,128)S(1)} %get-tuple-element.164), channel_id=1, source_target_pairs={{0,4},{4,8},{8,12},{12,16},{16,20},{20,24},{24,28},{28,32},{32,36}... | collective-permute-start | bytes 1179656 | tf_op jit(solution)/shard_map/ppermute | solution.py:119
  203.4 25.3 %collective-permute-start.44 = (f32[12,32,256]{2,1,0:T(8,128)S(1)}, f32[12,32,256]{2,1,0:T(8,128)S(1)}, u32[]{:S(2)}, u32[]{:S(2)}) collective-permute-start(f32[12,32,256]{2,1,0:T(8,128)S(1)} %get-tuple-element.171), channel_id=1, source_target_pairs={{0,4},{4,8},{8,12},{12,16},{16,20},{20,24},{24,28},{28,32},{32,36}... | collective-permute-start | bytes 1179656 | tf_op jit(solution)/shard_map/ppermute | solution.py:119
  203.5 25.2 %collective-permute-start.45 = (f32[12,32,256]{2,1,0:T(8,128)S(1)}, f32[12,32,256]{2,1,0:T(8,128)S(1)}, u32[]{:S(2)}, u32[]{:S(2)}) collective-permute-start(f32[12,32,256]{2,1,0:T(8,128)S(1)} %get-tuple-element.172), channel_id=1, source_target_pairs={{0,60},{4,0},{8,4},{12,8},{16,12},{20,16},{24,20},{28,24},{32,28},... | collective-permute-start | bytes 1179656 | tf_op jit(solution)/shard_map/ppermute | solution.py:119
